TPU v7x, 512 devices: a whole 4x8x8 slice. The times are simulated.
512 devices in a mesh: aux: 16 (over x_lo, z), pair: 32 (over y, x_hi, core).
Axes of the slice: x: 4 (x_hi: 2, x_lo: 2; x = x_hi * 2 + x_lo), y: 8, z: 8, core: 2. Of those that a mesh axis runs over, the one named last changes fastest.
Arguments:
- metric: bfloat16 [4096, 4096], P('aux', 'pair'), may hold values from -0.09375 to 0.09375
- amplitudes: bfloat16 [4096, 16384], P('aux', 'pair'), may hold values from -0.59765625 to 0.59765625
- virt_coef: bfloat16 [1024, 1280], replicated, may hold values from -1.5 to 1.5
Outputs:
- density: float32 [4096, 4096], P('aux', 'pair')
- fitted_ao: bfloat16 [4096, 20480], P(('aux', 'pair'))
All inputs are finite; a program needn't handle non-finite values.
Results may differ from a plain program's by a relative error of at most 0.012.
Values may be sent and summed in bfloat16 or wider, within the bound.
No kernel may reach another device: no remote copies, remote signals or barrier semaphores. Data moves between devices by JAX's collectives and lax.ppermute only.
A program may use at most 64 MiB of HBM per device.

v0:
```python
import jax
import jax.numpy as jnp
from jax import lax
from jax.sharding import Mesh
from jax.sharding import PartitionSpec as P

PAIR = ("pair_0", "pair_1", "pair_2")
AUX = ("aux_0", "aux_1")
AUX_PAIR = ("aux_0", "aux_1", "pair_0", "pair_1", "pair_2")


def copy_for_each(x, axis):
    copies = jnp.broadcast_to(x, (lax.axis_size(axis), *x.shape))
    return lax.all_to_all(copies, axis, split_axis=0, concat_axis=0, tiled=True)


def in_order(parts, dim):
    shape = list(parts.shape[1:])
    shape[dim] *= parts.shape[0]
    return jnp.moveaxis(parts, 0, dim).reshape(shape)


def whole_of(x, axes, dim):
    far, near = axes
    first = copy_for_each(x, far)
    parts = jnp.swapaxes(copy_for_each(first, near), 0, 1)
    return in_order(parts.reshape(-1, *x.shape), dim)


def all_blocks(x, axes, order):
    parts = x
    for k in order:
        parts = lax.all_gather(parts, axes[k])
    done = order[::-1]
    back = [done.index(k) for k in range(len(axes))]
    parts = parts.transpose(*back, *range(len(axes), parts.ndim))
    return parts.reshape(-1, *x.shape)


def gather_axes(x, axes, order, dim):
    return in_order(all_blocks(x, axes, order), dim)


def in_blocks(x, dim, size):
    before, after = (x.shape[:dim], x.shape[dim + 1 :])
    return jnp.moveaxis(x.reshape(*before, size, -1, *after), dim, 0)


def sent_and_summed(x, axis, dim):
    size = lax.axis_size(axis)
    parts = lax.all_to_all(in_blocks(x, dim, size), axis, 0, 0, tiled=True)
    return jnp.sum(parts.astype(jnp.float32), axis=0)


def sum_in_two_steps(x, axes, dim):
    far, near = axes
    parts = in_blocks(x, dim, lax.axis_size(far))
    nearer = sent_and_summed(parts, near, dim + 1)
    arrived = lax.all_to_all(
        nearer.astype(jnp.bfloat16), far, split_axis=0, concat_axis=0, tiled=True
    )
    return arrived.astype(jnp.float32).sum(axis=0)


def shards(metric, amplitudes, virt_coef):
    rows_metric = whole_of(metric, (("pair_0", "pair_1"), "pair_2"), 1)
    full_amp = gather_axes(amplitudes, AUX, (0, 1), 0)
    fitted = jnp.dot(rows_metric, full_amp, preferred_element_type=jnp.float32).astype(jnp.bfloat16)
    partial_value = lax.dot_general(
        fitted, full_amp, (((1,), (1,)), ((), ())), preferred_element_type=jnp.float32
    )
    density = sum_in_two_steps(
        partial_value.astype(jnp.bfloat16), (("pair_0", "pair_1"), "pair_2"), 1
    )
    regrouped = lax.all_to_all(fitted, PAIR, split_axis=0, concat_axis=1, tiled=True)
    row_count = regrouped.shape[0]
    virt_count = virt_coef.shape[0]
    ao_count = virt_coef.shape[1]
    occ_count = regrouped.shape[1] // virt_count
    blocks = regrouped.reshape(row_count * occ_count, virt_count)
    fitted_ao = jnp.dot(blocks, virt_coef, preferred_element_type=jnp.float32).astype(jnp.bfloat16)
    return (density, fitted_ao.reshape(row_count, occ_count * ao_count))


def solution(mesh):
    split = Mesh(
        mesh.devices.reshape(2, 8, 8, 2, 2), ("aux_0", "aux_1", "pair_0", "pair_1", "pair_2")
    )
    return jax.shard_map(
        shards,
        mesh=split,
        in_specs=(P(AUX, PAIR), P(AUX, PAIR), P()),
        out_specs=(P(AUX, PAIR), P(AUX_PAIR, None)),
        check_vma=False,
    )
```

profile of v0, /device:TPU:1, one launch (start us, length us, event | category | flops | bytes accessed | tf_op | source)
XLA Modules:
  0.0 170.4 jit_solution(5360390549793918562)
XLA Ops:
  7.2 0.0 copy-start
  7.2 0.0 all-gather.4.cloned.1.call-start
  7.2 8.6 %all-gather = bf16[512,512]{1,0:T(8,128)(2,1)} all-gather(bf16[256,512]{1,0:T(8,128)(2,1)} %param.4), channel_id=2, replica_groups=mesh['aux_0'=2,'aux_1'=8,'pair_0'=8,'pair_1'=2,'pair_2'=2] {'aux_0'}, dimensions={0}, use_global_device_ids=true | all-gather | bytes 786432 | tf_op jit(solution)/shard_map/all_gather | solution.py:33
  15.8 0.0 all-gather.4.cloned.1.call-update
  15.8 1.0 broadcast_in_dim.6
  16.8 39.3 %all_to_all.36 = bf16[16,256,128]{2,1,0:T(8,128)(2,1)S(1)} all-to-all(bf16[16,256,128]{2,1,0:T(8,128)(2,1)S(1)} %broadcast_in_dim.6), channel_id=1, replica_groups=mesh['aux_0'=2,'aux_1'=8,'pair_0'=8,'pair_1'=2,'pair_2'=2] {'pair_0','pa..., dimensions={0} | all-to-all | bytes 2097152 | tf_op jit(solution)/shard_map/all_to_all | solution.py:14
  56.1 0.6 broadcast_in_dim.7
  56.7 7.8 %all_to_all.37 = bf16[2,16,256,128]{3,2,1,0:T(8,128)(2,1)S(1)} all-to-all(bf16[2,16,256,128]{3,2,1,0:T(8,128)(2,1)S(1)} %broadcast_in_dim.7), channel_id=1, replica_groups=mesh['aux_0'=2,'aux_1'=8,'pair_0'=8,'pair_1'=2,'pair_2'=2] {'pair_2'}, dimensions={0} | all-to-all | bytes 4194304 | tf_op jit(solution)/shard_map/all_to_all | solution.py:14
  64.6 1.5 copy.22
  66.1 4.1 %copy.23 = bf16[256,32,128]{0,2,1:T(8,128)(2,1)} copy(bf16[256,32,128]{2,0,1:T(8,128)(2,1)} %bitcast.28) | data formatting | bytes 4194304 | tf_op jit(solution)/shard_map/transpose | solution.py:20
  70.1 11.0 %all-gather.4.cloned.1.call-done = bf16[16,256,512]{2,1,0:T(8,128)(2,1)} async-done(((bf16[2,256,512]{2,1,0:T(8,128)(2,1)}), bf16[16,256,512]{2,1,0:T(8,128)(2,1)}) %all-gather.4.cloned.1.call-update) | async-done | bytes 4194320 | tf_op jit(solution)/shard_map/all_gather | solution.py:33
  81.2 0.0 copy-start.1
  81.2 2.8 %copy.24 = bf16[2,8,256,512]{3,2,1,0:T(8,128)(2,1)S(1)} copy(bf16[2,8,256,512]{3,2,0,1:T(8,128)(2,1)} %bitcast.30) | data formatting | bytes 8388608 | tf_op jit(solution)/shard_map/transpose | solution.py:36
  83.9 0.1 copy-done.1
  84.0 2.0 %convolution_convert_fusion.2 = bf16[256,512]{1,0:T(8,128)(2,1)} fusion(bf16[256,4096]{0,1:T(8,128)(2,1)S(1)} %bitcast.31, bf16[4096,512]{1,0:T(8,128)(2,1)S(1)} %bitcast.26), kind=kOutput, calls=%fused_computation.3 | convolution fusion | flops 1073872896 | bytes 6553600 | tf_op jit(solution)/shard_map/dot_general | solution.py:68
  86.0 3.5 %convolution_convert_fusion = bf16[256,4096]{1,0:T(8,128)(2,1)} fusion(bf16[256,512]{1,0:T(8,128)(2,1)} %convolution_convert_fusion.2, bf16[4096,512]{1,0:T(8,128)(2,1)S(1)} %bitcast.27), kind=kOutput, calls=%fused_computation | convolution fusion | flops 1074790400 | bytes 6553600 | tf_op jit(solution)/shard_map/dot_general | solution.py:69
  89.5 4.1 %copy.30 = bf16[256,4096]{0,1:T(8,128)(2,1)} copy(bf16[256,4096]{1,0:T(8,128)(2,1)} %convolution_convert_fusion) | data formatting | bytes 4194304 | tf_op jit(solution)/shard_map/reshape | solution.py:46
  93.6 4.5 %copy.26 = bf16[2,16,256,128]{3,1,2,0:T(8,128)(2,1)} copy(bf16[2,16,256,128]{2,3,0,1:T(8,128)(2,1)} %bitcast.29) | data formatting | bytes 4194304 | tf_op jit(solution)/shard_map/transpose | solution.py:46
  98.1 9.0 %all_to_all.38 = bf16[2,16,256,128]{3,1,2,0:T(8,128)(2,1)} all-to-all(bf16[2,16,256,128]{3,1,2,0:T(8,128)(2,1)} %copy.26), channel_id=1, replica_groups=mesh['aux_0'=2,'aux_1'=8,'pair_0'=8,'pair_1'=2,'pair_2'=2] {'pair_2'}, dimensions={0} | all-to-all | bytes 4194304 | tf_op jit(solution)/shard_map/all_to_all | solution.py:51
  107.1 9.7 %all-to-all-start.4 = ((bf16[32,8,512]{2,1,0:T(8,128)(2,1)}), bf16[32,8,512]{2,1,0:T(8,128)(2,1)S(1)}, u32[]{:S(2)}, u32[]{:S(2)}) async-start(bf16[32,8,512]{2,1,0:T(8,128)(2,1)} %bitcast.12), calls=%async_computation.4 | async-start | bytes 524288 | tf_op jit(solution)/shard_map/all_to_all | solution.py:75
  116.8 3.3 %reduce_sum.21 = bf16[16,256,128]{2,0,1:T(8,128)(2,1)} reduce(bf16[2,16,256,128]{3,1,2,0:T(8,128)(2,1)} %all_to_all.38, bf16[]{:T(256)} %constant.2.clone.1), dimensions={0}, to_apply=%region_0.0 | reduce | flops 524288 | bytes 3145730 | tf_op jit(solution)/shard_map/reduce_sum | solution.py:52
  120.1 2.5 %copy.28 = bf16[16,256,128]{2,1,0:T(8,128)(2,1)} copy(bf16[16,256,128]{2,0,1:T(8,128)(2,1)} %reduce_sum.21) | data formatting | bytes 2097152 | tf_op jit(solution)/shard_map/reduce_sum | solution.py:52
  122.5 7.2 %all-to-all-done.4 = bf16[32,8,512]{2,1,0:T(8,128)(2,1)S(1)} async-done(((bf16[32,8,512]{2,1,0:T(8,128)(2,1)}), bf16[32,8,512]{2,1,0:T(8,128)(2,1)S(1)}, u32[]{:S(2)}, u32[]{:S(2)}) %all-to-all-start.4) | async-done | bytes 262176 | tf_op jit(solution)/shard_map/all_to_all | solution.py:75
  129.7 4.3 %all-to-all-start.3 = ((bf16[16,256,128]{2,1,0:T(8,128)(2,1)}), bf16[16,256,128]{2,1,0:T(8,128)(2,1)}, u32[]{:S(2)}, u32[]{:S(2)}) async-start(bf16[16,256,128]{2,1,0:T(8,128)(2,1)} %copy.28), calls=%async_computation.3 | async-start | bytes 2097152 | tf_op jit(solution)/shard_map/all_to_all | solution.py:59
  134.1 0.1 copy.29
  134.2 0.1 reshape.30
  134.3 0.0 copy-done
  134.3 0.5 convolution_convert_fusion.1
  134.8 0.9 reshape.31
  135.7 25.8 %all-to-all-done.3 = bf16[16,256,128]{2,1,0:T(8,128)(2,1)} async-done(((bf16[16,256,128]{2,1,0:T(8,128)(2,1)}), bf16[16,256,128]{2,1,0:T(8,128)(2,1)}, u32[]{:S(2)}, u32[]{:S(2)}) %all-to-all-start.3) | async-done | bytes 1048608 | tf_op jit(solution)/shard_map/all_to_all | solution.py:59
  161.5 2.0 %convert_reduce_fusion = f32[256,128]{1,0:T(8,128)} fusion(bf16[16,256,128]{2,1,0:T(8,128)(2,1)} %all-to-all-done.3), kind=kLoop, calls=%fused_computation.2 | loop fusion | flops 1015808 | bytes 1179648 | tf_op jit(solution)/shard_map/reduce_sum | solution.py:62
Async XLA Ops:
  7.2 127.1 %copy-start = (bf16[1024,1280]{1,0:T(8,128)(2,1)S(1)}, bf16[1024,1280]{1,0:T(8,128)(2,1)}, u32[]{:S(2)}) copy-start(bf16[1024,1280]{1,0:T(8,128)(2,1)} %param.5) | copy-start | bytes 7864324
  7.2 74.0 %all-gather.4.cloned.1.call-start = ((), (), s32[]{:S(2)}) async-start(), calls=%async_computation.5 | async-start | bytes 4718592 | tf_op jit(solution)/shard_map/all_gather | solution.py:33
  81.2 2.9 %copy-start.1 = (bf16[256,32,128]{0,2,1:T(8,128)(2,1)S(1)}, bf16[256,32,128]{0,2,1:T(8,128)(2,1)}, u32[]{:S(2)}) copy-start(bf16[256,32,128]{0,2,1:T(8,128)(2,1)} %copy.23) | copy-start | bytes 6291460
  107.1 22.6 %all-to-all-start.4 = ((bf16[32,8,512]{2,1,0:T(8,128)(2,1)}), bf16[32,8,512]{2,1,0:T(8,128)(2,1)S(1)}, u32[]{:S(2)}, u32[]{:S(2)}) async-start(bf16[32,8,512]{2,1,0:T(8,128)(2,1)} %bitcast.12), calls=%async_computation.4 | async-start | bytes 524288 | tf_op jit(solution)/shard_map/all_to_all | solution.py:75
  129.7 31.8 %all-to-all-start.3 = ((bf16[16,256,128]{2,1,0:T(8,128)(2,1)}), bf16[16,256,128]{2,1,0:T(8,128)(2,1)}, u32[]{:S(2)}, u32[]{:S(2)}) async-start(bf16[16,256,128]{2,1,0:T(8,128)(2,1)} %copy.28), calls=%async_computation.3 | async-start | bytes 2097152 | tf_op jit(solution)/shard_map/all_to_all | solution.py:59
Sparse Core Ops, SparseCore 0:
  15.9 65.1 all-gather.3
where the time goes:
time: 173 us; the launch traced here: 170 us
  blocking collectives  64.7 us (37%)
  waiting for transfers between devices  44.1 us (25%)
  local copies, waits for them, and re-layouts  22.1 us (13%)
  starting transfers between devices  14.1 us (8%)
  between operations  14.1 us (8%)
  matrix products  6.03 us (3%)
  other arithmetic  5.3 us (3%)
    all_to_all x2, blocking collectives, copy_for_each(): return lax.all_to_all(copies, axis, split_axis=0, concat_axis=0, tiled=True)  47.1 us
    all_to_all x1, waiting for transfers between devices, sum_in_two_steps(): lax.all_to_all(nearer.astype(jnp.bfloat16), far, split_axis=0, concat_axi...  25.8 us
    all_gather x1, waiting for transfers between devices, all_blocks(): parts = lax.all_gather(parts, axes[k])  11 us
    all_to_all x1, starting transfers between devices, shards(): lax.all_to_all(fitted, PAIR, split_axis=0, concat_axis=1, tiled=True)  9.68 us
    all_to_all x1, blocking collectives, sent_and_summed(): parts = lax.all_to_all(in_blocks(x, dim, size), axis, 0, 0, tiled=True)  9.01 us
    all_gather x1, blocking collectives, all_blocks(): parts = lax.all_gather(parts, axes[k])  8.55 us
    all_to_all x1, waiting for transfers between devices, shards(): lax.all_to_all(fitted, PAIR, split_axis=0, concat_axis=1, tiled=True)  7.2 us
    transpose x1, local copies, waits for them, and re-layouts, in_blocks(): return jnp.moveaxis(x.reshape(*before, size, -1, *after), dim, 0)  4.49 us
  transfers between devices with their start and end apart: 3, of which 3 were waited for; matrix products, arithmetic and copies ran while one was open for 9% of the time, Pallas kernels for 0%

commit v1 on v0

v1 whole, which is shorter than its diff:
```python
import functools

import jax
import jax.numpy as jnp
from jax import lax
from jax.experimental import pallas as pl
from jax.experimental.pallas import tpu as pltpu
from jax.sharding import Mesh
from jax.sharding import PartitionSpec as P

AUX = ("xl", "z")
PAIR = ("y", "xh", "c")
ALL = AUX + PAIR
CHUNKS = 1
VMEM = pl.BlockSpec(memory_space=pltpu.VMEM)


def shifted(x, axis, by):
    n = lax.axis_size(axis)
    return lax.ppermute(x, axis, [(i, (i + by) % n) for i in range(n)])


def exchange(x, axes):
    return lax.all_to_all(x, axes, split_axis=0, concat_axis=0, tiled=True)


def ring_blocks(x):
    n = lax.axis_size("z")
    half = x.shape[1] // 2
    right, left = x, x
    blocks, offsets = [x], [0]
    for s in range(1, n // 2):
        right, left = shifted(right, "z", 1), shifted(left, "z", -1)
        blocks += [right, left]
        offsets += [n - s, s]
    far = [shifted(right[:, :half], "z", 1), shifted(left[:, half:], "z", -1)]
    return blocks, offsets, far, n // 2


def loaded(refs, offsets, far_refs, far_offset):
    values = [(o, r[...]) for o, r in zip(offsets, refs)]
    far = jnp.concatenate([r[...] for r in far_refs], axis=1)
    return values + [(far_offset, far)]


def fitted_kernel(offsets, far_offset, chunks, own_ref, other_ref, *refs):
    count = len(offsets)
    blocks = loaded(refs[:count], offsets, refs[count : count + 2], far_offset)
    wide_refs = refs[count + 2 : count + 2 + chunks]
    narrow_refs = refs[count + 2 + chunks :]
    n = 8
    z, c = lax.axis_index("z"), lax.axis_index("c")
    half = own_ref.shape[-1]
    right = []
    for i, (_, block) in enumerate(blocks):
        first, second = block[:half], block[half:]
        right += [jnp.where(c == 0, first, second), jnp.where(c == 0, second, first)]
    rhs = jnp.concatenate(right, axis=0)
    for h in range(2):
        left = []
        for offset, _ in blocks:
            at = lax.rem(z + offset, n)
            far, near = lax.rem(at, 2), lax.div(at, 2)
            left += [own_ref[h, far, near], other_ref[h, far, near]]
        lhs = jnp.concatenate(left, axis=1)
        out = jnp.dot(lhs, rhs, preferred_element_type=jnp.float32)
        rows = out.shape[0] // chunks
        for j in range(chunks):
            part = out[j * rows : (j + 1) * rows]
            wide_refs[j][h] = part
            narrow_refs[j][h] = part.astype(jnp.bfloat16)


def density_kernel(offsets, far_offset, wide_ref, arrived_ref, *refs):
    count = len(offsets)
    blocks = loaded(refs[:count], offsets, refs[count : count + 2], far_offset)
    keep_ref, send_ref, fitted_ref = refs[count + 2 :]
    n = 8
    z, c, xl = lax.axis_index("z"), lax.axis_index("c"), lax.axis_index("xl")
    fitted_ref[...] = (wide_ref[xl] + arrived_ref[xl].astype(jnp.float32)).astype(jnp.bfloat16)
    rows = wide_ref.shape[1]
    whole = (wide_ref[...] + arrived_ref[...].astype(jnp.float32)).astype(jnp.bfloat16)
    lhs = whole.reshape(2 * rows, whole.shape[2])
    for offset, block in blocks:
        at = lax.rem(z + offset, n)
        far, near = lax.rem(at, 2), lax.div(at, 2)
        out = lax.dot_general(
            lhs, block, (((1,), (1,)), ((), ())), preferred_element_type=jnp.float32
        ).astype(jnp.bfloat16)
        half = out.shape[1] // 2
        first, second = out[:, :half], out[:, half:]
        keep = jnp.where(c == 0, first, second)
        send = jnp.where(c == 0, second, first)
        for h in range(2):
            keep_ref[h, far, near] = keep[h * rows : (h + 1) * rows]
            send_ref[h, far, near] = send[h * rows : (h + 1) * rows]


def shards(metric, amplitudes, virt_coef):
    xl = lax.axis_index("xl")
    ys = exchange(jnp.broadcast_to(metric, (8, *metric.shape)), "y")
    ys = ys.reshape(2, 1, 4, *metric.shape)
    wanted = jnp.broadcast_to(ys, (2, 2, 4, *metric.shape))
    own = exchange(wanted.reshape(4, 4, *metric.shape), ("xl", "xh"))
    own = own.reshape(2, 2, 4, *metric.shape)
    other = shifted(own, "c", 1)

    blocks, offsets, far, far_offset = ring_blocks(amplitudes)
    rows, cols = metric.shape[0], amplitudes.shape[1]
    part = rows // CHUNKS
    outs = pl.pallas_call(
        functools.partial(fitted_kernel, offsets, far_offset, CHUNKS),
        in_specs=[VMEM] * (2 + len(blocks) + 2),
        out_specs=[VMEM] * (2 * CHUNKS),
        out_shape=[jax.ShapeDtypeStruct((2, part, cols), jnp.float32)] * CHUNKS
        + [jax.ShapeDtypeStruct((2, part, cols), jnp.bfloat16)] * CHUNKS,
    )(own, other, *blocks, *far)
    wides, narrows = outs[:CHUNKS], outs[CHUNKS:]

    results, fitteds = [], []
    for wide, narrow in zip(wides, narrows):
        arrived = shifted(narrow, "xl", 1)
        keep, send, fitted = pl.pallas_call(
            functools.partial(density_kernel, offsets, far_offset),
            in_specs=[VMEM] * (2 + len(blocks) + 2),
            out_specs=[VMEM] * 3,
            out_shape=[jax.ShapeDtypeStruct((2, 2, 4, part, 128), jnp.bfloat16)] * 2
            + [jax.ShapeDtypeStruct((part, cols), jnp.bfloat16)],
        )(wide, arrived, *blocks, *far)
        fitteds.append(fitted)
        got = shifted(send, "c", 1)
        both = (keep.astype(jnp.float32) + got.astype(jnp.float32)).astype(jnp.bfloat16)
        xs = exchange(both.reshape(4, 4, part, 128), ("xl", "xh")).reshape(2, 2, 4, part, 128)
        xs = jnp.sum(xs.astype(jnp.float32), axis=1).astype(jnp.bfloat16)
        ysum = exchange(xs.reshape(8, part, 128), "y")
        results.append(jnp.sum(ysum.astype(jnp.float32), axis=0))
    density = results[0] if CHUNKS == 1 else jnp.concatenate(results, axis=0)

    fitted = fitteds[0] if CHUNKS == 1 else jnp.concatenate(fitteds, axis=0)
    got = exchange(fitted.reshape(32, 8, cols), PAIR)
    got = got.reshape(16, 2, 8, cols).transpose(0, 2, 1, 3).reshape(128, 2 * cols)
    ao = jnp.dot(got, virt_coef, preferred_element_type=jnp.float32).astype(jnp.bfloat16)
    ao_count = virt_coef.shape[1]
    ao = ao.reshape(16, 8, ao_count).transpose(1, 0, 2).reshape(8, 16 * ao_count)
    return density, ao


def solution(mesh):
    split = Mesh(mesh.devices.reshape(2, 8, 8, 2, 2), ALL)
    return jax.shard_map(
        shards,
        mesh=split,
        in_specs=(P(AUX, PAIR), P(AUX, PAIR), P()),
        out_specs=(P(AUX, PAIR), P(ALL, None)),
        check_vma=False,
    )
```

time: 173 us -> 187 us (1.081); the launches traced: 170 us -> 186 us
  starting transfers between devices: 14.1 us -> 57.3 us
  local copies, waits for them, and re-layouts: 22.1 us -> 3.09 us
  between operations: 14.1 us -> 0.91 us
  Pallas kernels: 0 us -> 9.36 us
  waiting for transfers between devices: 44.1 us -> 52.7 us
  blocking collectives: 64.7 us -> 57.2 us
  matrix products: 6.03 us -> 1.24 us
    ppermute x0 -> x11, starting transfers between devices: none -> 48.7 us  [shifted(): return lax.ppermute(x, axis, [(i, (i + by) % n) for i in range(n)])]
    ppermute x0 -> x11, waiting for transfers between devices: none -> 25.4 us  [shifted(): return lax.ppermute(x, axis, [(i, (i + by) % n) for i in range(n)])]
    transpose x3 -> x0, local copies, waits for them, and re-layouts: 11.3 us -> none  [the longest x1 4.49 us: in_blocks(): return jnp.moveaxis(x.reshape(*before, size, -1, *after), dim, 0)]
    all_gather x1 -> x0, waiting for transfers between devices: 11 us -> none  [all_blocks(): parts = lax.all_gather(parts, axes[k])]
    pallas_call x0 -> x2, Pallas kernels: none -> 9.36 us  [the longest x1 4.82 us: shards(): pl.pallas_call(functools.partial(density_kernel, offsets, far_offset), in...]
    all_gather x1 -> x0, blocking collectives: 8.55 us -> none  [all_blocks(): parts = lax.all_gather(parts, axes[k])]
    all_to_all x2, waiting for transfers between devices: 33 us -> 27.2 us  [exchange(): return lax.all_to_all(x, axes, split_axis=0, concat_axis=0, tiled=True)]
    all_to_all x2, starting transfers between devices: 14 us -> 8.64 us  [exchange(): return lax.all_to_all(x, axes, split_axis=0, concat_axis=0, tiled=True)]
  transfers between devices with their start and end apart: 3 -> 13, of which waited for: 3 -> 8; matrix products, arithmetic and copies ran while one was open for 9% -> 2% of each run, Pallas kernels for 0% -> 0%
where the time goes in v1:
time: 187 us; the launch traced here: 186 us
  starting transfers between devices  57.3 us (31%)
  blocking collectives  57.2 us (31%)
  waiting for transfers between devices  52.7 us (28%)
  Pallas kernels  9.36 us (5%)
  other arithmetic  4.56 us (2%)
  local copies, waits for them, and re-layouts  3.09 us (2%)
    all_to_all x3, blocking collectives, exchange(): return lax.all_to_all(x, axes, split_axis=0, concat_axis=0, tiled=True)  57.2 us
    ppermute x11, starting transfers between devices, shifted(): return lax.ppermute(x, axis, [(i, (i + by) % n) for i in range(n)])  48.7 us
    all_to_all x2, waiting for transfers between devices, exchange(): return lax.all_to_all(x, axes, split_axis=0, concat_axis=0, tiled=True)  27.2 us
    ppermute x11, waiting for transfers between devices, shifted(): return lax.ppermute(x, axis, [(i, (i + by) % n) for i in range(n)])  25.4 us
    all_to_all x2, starting transfers between devices, exchange(): return lax.all_to_all(x, axes, split_axis=0, concat_axis=0, tiled=True)  8.64 us
    pallas_call x1, Pallas kernels, shards(): pl.pallas_call(functools.partial(density_kernel, offsets, far_offset), in...  4.82 us
    pallas_call x1, Pallas kernels, shards(): pl.pallas_call(functools.partial(fitted_kernel, offsets, far_offset, CHUN...  4.54 us
  transfers between devices with their start and end apart: 13, of which 8 were waited for; matrix products, arithmetic and copies ran while one was open for 2% of the time, Pallas kernels for 0%

profile of v1, /device:TPU:1, one launch (start us, length us, event | category | flops | bytes accessed | tf_op | source)
XLA Modules:
  0.0 186.3 jit_solution(13475399327408758200)
XLA Ops:
  0.6 0.0 copy-start
  0.6 0.0 copy-start.4
  0.7 1.1 broadcast_in_dim.10
  1.7 22.3 %all_to_all.25 = bf16[8,256,128]{2,1,0:T(8,128)(2,1)S(1)} all-to-all(bf16[8,256,128]{2,1,0:T(8,128)(2,1)S(1)} %broadcast_in_dim.10), channel_id=1, replica_groups=mesh['xl'=2,'z'=8,'y'=8,'xh'=2,'c'=2] {'y'}, dimensions={0} | all-to-all | bytes 1048576 | tf_op jit(solution)/shard_map/all_to_all | solution.py:24
  24.1 0.2 broadcast_in_dim.12
  24.3 17.2 %all_to_all.26 = bf16[4,4,256,128]{3,2,1,0:T(8,128)(2,1)S(1)} all-to-all(bf16[4,4,256,128]{3,2,1,0:T(8,128)(2,1)S(1)} %bitcast.21), channel_id=1, replica_groups=mesh['xl'=2,'z'=8,'y'=8,'xh'=2,'c'=2] {'xl','xh'}, dimensions={0} | all-to-all | bytes 2097152 | tf_op jit(solution)/shard_map/all_to_all | solution.py:24
  41.4 0.0 copy-start.1
  41.5 1.0 copy-done.1
  42.4 5.5 %collective-permute-start = (bf16[2,2,4,256,128]{4,3,2,1,0:T(8,128)(2,1)S(1)}, bf16[2,2,4,256,128]{4,3,2,1,0:T(8,128)(2,1)}, u32[]{:S(2)}, u32[]{:S(2)}) collective-permute-start(bf16[2,2,4,256,128]{4,3,2,1,0:T(8,128)(2,1)S(1)} %bitcast.22), channel_id=1, source_target_pairs={{0,1},{1,0},{2,3},{3,2},{4,5},{5,4},{6,7},{7,6},{8,9},{9,8},{10,11... | collective-permute-start | bytes 3145736 | tf_op jit(solution)/shard_map/ppermute | solution.py:20
  47.9 0.0 copy-done.4
  47.9 10.7 %collective-permute-start.2 = (bf16[256,512]{1,0:T(8,128)(2,1)S(1)}, bf16[256,512]{1,0:T(8,128)(2,1)S(1)}, u32[]{:S(2)}, u32[]{:S(2)}) collective-permute-start(bf16[256,512]{1,0:T(8,128)(2,1)S(1)} %copy-done.4), channel_id=1, source_target_pairs={{0,224},{32,0},{64,32},{96,64},{128,96},{160,128},{192,160},{224,1... | collective-permute-start | bytes 786440 | tf_op jit(solution)/shard_map/ppermute | solution.py:20
  58.6 1.9 %collective-permute-start.1 = (bf16[256,512]{1,0:T(8,128)(2,1)S(1)}, bf16[256,512]{1,0:T(8,128)(2,1)S(1)}, u32[]{:S(2)}, u32[]{:S(2)}) collective-permute-start(bf16[256,512]{1,0:T(8,128)(2,1)S(1)} %copy-done.4), channel_id=1, source_target_pairs={{0,32},{32,64},{64,96},{96,128},{128,160},{160,192},{192,224},{224... | collective-permute-start | bytes 786440 | tf_op jit(solution)/shard_map/ppermute | solution.py:20
  60.5 3.7 %collective-permute-done.2.refs_2_ = bf16[256,512]{1,0:T(8,128)(2,1)S(1)} collective-permute-done((bf16[256,512]{1,0:T(8,128)(2,1)S(1)}, bf16[256,512]{1,0:T(8,128)(2,1)S(1)}, u32[]{:S(2)}, u32[]{:S(2)}) %collective-permute-start.2) | collective-permute-done | bytes 262176 | tf_op jit(solution)/shard_map/ppermute | solution.py:20
  64.2 0.0 copy-start.5
  64.2 5.3 %collective-permute-start.4 = (bf16[256,512]{1,0:T(8,128)(2,1)S(1)}, bf16[256,512]{1,0:T(8,128)(2,1)S(1)}, u32[]{:S(2)}, u32[]{:S(2)}) collective-permute-start(bf16[256,512]{1,0:T(8,128)(2,1)S(1)} %collective-permute-done.2.refs_2_), channel_id=1, source_target_pairs={{0,224},{32,0},{64,32},{96,64},{128,96},{160,128},{192,160},{224,1... | collective-permute-start | bytes 786440 | tf_op jit(solution)/shard_map/ppermute | solution.py:20
  69.6 0.0 collective-permute-done.1.refs_1_
  69.6 0.0 copy-start.6
  69.6 1.9 %collective-permute-start.3 = (bf16[256,512]{1,0:T(8,128)(2,1)S(1)}, bf16[256,512]{1,0:T(8,128)(2,1)S(1)}, u32[]{:S(2)}, u32[]{:S(2)}) collective-permute-start(bf16[256,512]{1,0:T(8,128)(2,1)S(1)} %collective-permute-done.1.refs_1_), channel_id=1, source_target_pairs={{0,32},{32,64},{64,96},{96,128},{128,160},{160,192},{192,224},{224... | collective-permute-start | bytes 786440 | tf_op jit(solution)/shard_map/ppermute | solution.py:20
  71.5 2.8 %collective-permute-done.4.refs_4_ = bf16[256,512]{1,0:T(8,128)(2,1)S(1)} collective-permute-done((bf16[256,512]{1,0:T(8,128)(2,1)S(1)}, bf16[256,512]{1,0:T(8,128)(2,1)S(1)}, u32[]{:S(2)}, u32[]{:S(2)}) %collective-permute-start.4) | collective-permute-done | bytes 262176 | tf_op jit(solution)/shard_map/ppermute | solution.py:20
  74.3 0.0 copy-start.7
  74.3 5.3 %collective-permute-start.6 = (bf16[256,512]{1,0:T(8,128)(2,1)S(1)}, bf16[256,512]{1,0:T(8,128)(2,1)S(1)}, u32[]{:S(2)}, u32[]{:S(2)}) collective-permute-start(bf16[256,512]{1,0:T(8,128)(2,1)S(1)} %collective-permute-done.4.refs_4_), channel_id=1, source_target_pairs={{0,224},{32,0},{64,32},{96,64},{128,96},{160,128},{192,160},{224,1... | collective-permute-start | bytes 786440 | tf_op jit(solution)/shard_map/ppermute | solution.py:20
  79.6 0.0 copy-done.6
  79.7 0.0 collective-permute-done.3.refs_3_
  79.7 0.0 copy-done.5
  79.7 0.0 copy-start.8
  79.7 1.9 %collective-permute-start.5 = (bf16[256,512]{1,0:T(8,128)(2,1)S(1)}, bf16[256,512]{1,0:T(8,128)(2,1)S(1)}, u32[]{:S(2)}, u32[]{:S(2)}) collective-permute-start(bf16[256,512]{1,0:T(8,128)(2,1)S(1)} %collective-permute-done.3.refs_3_), channel_id=1, source_target_pairs={{0,32},{32,64},{64,96},{96,128},{128,160},{160,192},{192,224},{224... | collective-permute-start | bytes 786440 | tf_op jit(solution)/shard_map/ppermute | solution.py:20
  81.6 0.0 copy-done.7
  81.6 1.9 %collective-permute-done.6.refs_6_ = bf16[256,512]{1,0:T(8,128)(2,1)S(1)} collective-permute-done((bf16[256,512]{1,0:T(8,128)(2,1)S(1)}, bf16[256,512]{1,0:T(8,128)(2,1)S(1)}, u32[]{:S(2)}, u32[]{:S(2)}) %collective-permute-start.6) | collective-permute-done | bytes 262176 | tf_op jit(solution)/shard_map/ppermute | solution.py:20
  83.6 0.0 copy-start.2
  83.6 5.3 %collective-permute-start.8 = (bf16[256,256]{1,0:T(8,128)(2,1)S(1)}, bf16[256,256]{1,0:T(8,128)(2,1)S(1)}, u32[]{:S(2)}, u32[]{:S(2)}) collective-permute-start(bf16[256,256]{1,0:T(8,128)(2,1)S(1)} %slice.9), channel_id=1, source_target_pairs={{0,224},{32,0},{64,32},{96,64},{128,96},{160,128},{192,160},{224,1... | collective-permute-start | bytes 393224 | tf_op jit(solution)/shard_map/ppermute | solution.py:20
  88.9 0.0 collective-permute-done.5.refs_5_
  88.9 0.0 copy-start.3
  88.9 1.9 %collective-permute-start.7 = (bf16[256,256]{1,0:T(8,128)(2,1)S(1)}, bf16[256,256]{1,0:T(8,128)(2,1)}, u32[]{:S(2)}, u32[]{:S(2)}) collective-permute-start(bf16[256,256]{1,0:T(8,128)(2,1)S(1)} %slice.8), channel_id=1, source_target_pairs={{0,32},{32,64},{64,96},{96,128},{128,160},{160,192},{192,224},{224... | collective-permute-start | bytes 393224 | tf_op jit(solution)/shard_map/ppermute | solution.py:20
  90.9 0.0 collective-permute-done.8.refs_8_
  90.9 0.0 copy-start.10
  90.9 5.1 %collective-permute-done.7.refs_7_ = bf16[256,256]{1,0:T(8,128)(2,1)} collective-permute-done((bf16[256,256]{1,0:T(8,128)(2,1)S(1)}, bf16[256,256]{1,0:T(8,128)(2,1)}, u32[]{:S(2)}, u32[]{:S(2)}) %collective-permute-start.7) | collective-permute-done | bytes 131104 | tf_op jit(solution)/shard_map/ppermute | solution.py:20
  96.0 0.0 collective-permute-done.other_ref
  96.0 0.0 copy-done.8
  96.0 0.0 copy-done.2
  96.0 0.0 copy-done.3
  96.0 0.0 copy-done.10
  96.0 4.5 %shard_map.50 = (f32[2,256,512]{2,1,0:T(8,128)}, bf16[2,256,512]{2,1,0:T(8,128)(2,1)}) custom-call(bf16[2,2,4,256,128]{4,3,2,1,0:T(8,128)(2,1)} %bitcast.23, bf16[2,2,4,256,128]{4,3,2,1,0:T(8,128)(2,1)} %collective-permute-done.other_ref, bf16[256,512]{1,0:T(8,128)(2,1)} %refs_0_.3, bf16[256,512]{1,0:T(8,128)(2,1)} %copy-done.6, bf16[256,512]{1,0:T(8,128)(2,1)} %copy-done.5, ...), custom_call_target="tpu_custom_call" | custom-call | tf_op jit(solution)/shard_map/pallas_call | solution.py:111
  100.5 2.1 %collective-permute-start.9 = (bf16[2,256,512]{2,1,0:T(8,128)(2,1)}, bf16[2,256,512]{2,1,0:T(8,128)(2,1)S(1)}, u32[]{:S(2)}, u32[]{:S(2)}) collective-permute-start(bf16[2,256,512]{2,1,0:T(8,128)(2,1)} %get-tuple-element.8), channel_id=1, source_target_pairs={{0,256},{256,0},{1,257},{257,1},{2,258},{258,2},{3,259},{259,3},{4... | collective-permute-start | bytes 1572872 | tf_op jit(solution)/shard_map/ppermute | solution.py:20
  102.7 9.4 %collective-permute-done.9.arrived_ref = bf16[2,256,512]{2,1,0:T(8,128)(2,1)S(1)} collective-permute-done((bf16[2,256,512]{2,1,0:T(8,128)(2,1)}, bf16[2,256,512]{2,1,0:T(8,128)(2,1)S(1)}, u32[]{:S(2)}, u32[]{:S(2)}) %collective-permute-start.9) | collective-permute-done | bytes 524320 | tf_op jit(solution)/shard_map/ppermute | solution.py:20
  112.1 0.0 copy-start.9
  112.1 0.8 copy-done.9
  112.9 4.8 %shard_map.51 = (bf16[2,2,4,256,128]{4,3,2,1,0:T(8,128)(2,1)}, bf16[2,2,4,256,128]{4,3,2,1,0:T(8,128)(2,1)}, bf16[256,512]{1,0:T(8,128)(2,1)}) custom-call(f32[2,256,512]{2,1,0:T(8,128)} %get-tuple-element.7.wide_ref, bf16[2,256,512]{2,1,0:T(8,128)(2,1)} %copy-done.9, bf16[256,512]{1,0:T(8,128)(2,1)} %refs_0_.3, bf16[256,512]{1,0:T(8,128)(2,1)} %copy-done.6, ...), custom_call_target="tpu_custom_call" | custom-call | tf_op jit(solution)/shard_map/pallas_call | solution.py:123
  117.7 6.8 %collective-permute-start.10 = (bf16[2,2,4,256,128]{4,3,2,1,0:T(8,128)(2,1)}, bf16[2,2,4,256,128]{4,3,2,1,0:T(8,128)(2,1)S(1)}, u32[]{:S(2)}, u32[]{:S(2)}) collective-permute-start(bf16[2,2,4,256,128]{4,3,2,1,0:T(8,128)(2,1)} %get-tuple-element.10), channel_id=1, source_target_pairs={{0,1},{1,0},{2,3},{3,2},{4,5},{5,4},{6,7},{7,6},{8,9},{9,8},{10,11... | collective-permute-start | bytes 3145736 | tf_op jit(solution)/shard_map/ppermute | solution.py:20
  124.5 2.5 %collective-permute-done.10 = bf16[2,2,4,256,128]{4,3,2,1,0:T(8,128)(2,1)S(1)} collective-permute-done((bf16[2,2,4,256,128]{4,3,2,1,0:T(8,128)(2,1)}, bf16[2,2,4,256,128]{4,3,2,1,0:T(8,128)(2,1)S(1)}, u32[]{:S(2)}, u32[]{:S(2)}) %collective-permute-start.10) | collective-permute-done | bytes 1048608 | tf_op jit(solution)/shard_map/ppermute | solution.py:20
  127.0 1.5 add_convert_fusion
  128.5 17.7 %all_to_all.27 = bf16[4,4,256,128]{3,2,1,0:T(8,128)(2,1)} all-to-all(bf16[4,4,256,128]{3,2,1,0:T(8,128)(2,1)S(1)} %bitcast.20), channel_id=1, replica_groups=mesh['xl'=2,'z'=8,'y'=8,'xh'=2,'c'=2] {'xl','xh'}, dimensions={0} | all-to-all | bytes 2097152 | tf_op jit(solution)/shard_map/all_to_all | solution.py:24
  146.1 5.1 %all-to-all-start.4 = ((bf16[32,8,512]{2,1,0:T(8,128)(2,1)}), bf16[32,8,512]{2,1,0:T(8,128)(2,1)S(1)}, u32[]{:S(2)}, u32[]{:S(2)}) async-start(bf16[32,8,512]{2,1,0:T(8,128)(2,1)} %bitcast.6), calls=%async_computation.4 | async-start | bytes 524288 | tf_op jit(solution)/shard_map/all_to_all | solution.py:24
  151.3 2.3 %bitcast_reduce_fusion = bf16[2,4,256,128]{3,2,1,0:T(8,128)(2,1)} fusion(bf16[4,4,256,128]{3,2,1,0:T(8,128)(2,1)} %all_to_all.27), kind=kLoop, calls=%fused_computation.2 | loop fusion | flops 262144 | bytes 1572864 | tf_op jit(solution)/shard_map/reduce_sum | solution.py:134
  153.6 10.6 %all-to-all-done.4 = bf16[32,8,512]{2,1,0:T(8,128)(2,1)S(1)} async-done(((bf16[32,8,512]{2,1,0:T(8,128)(2,1)}), bf16[32,8,512]{2,1,0:T(8,128)(2,1)S(1)}, u32[]{:S(2)}, u32[]{:S(2)}) %all-to-all-start.4) | async-done | bytes 262176 | tf_op jit(solution)/shard_map/all_to_all | solution.py:24
  164.2 3.5 %all-to-all-start.3 = ((bf16[8,256,128]{2,1,0:T(8,128)(2,1)}), bf16[8,256,128]{2,1,0:T(8,128)(2,1)S(1)}, u32[]{:S(2)}, u32[]{:S(2)}) async-start(bf16[8,256,128]{2,1,0:T(8,128)(2,1)} %bitcast.5), calls=%async_computation.3 | async-start | bytes 1048576 | tf_op jit(solution)/shard_map/all_to_all | solution.py:24
  167.7 0.0 copy-done
  167.7 1.2 convolution_convert_fusion
  169.0 16.6 %all-to-all-done.3 = bf16[8,256,128]{2,1,0:T(8,128)(2,1)S(1)} async-done(((bf16[8,256,128]{2,1,0:T(8,128)(2,1)}), bf16[8,256,128]{2,1,0:T(8,128)(2,1)S(1)}, u32[]{:S(2)}, u32[]{:S(2)}) %all-to-all-start.3) | async-done | bytes 524320 | tf_op jit(solution)/shard_map/all_to_all | solution.py:24
  185.6 0.7 convert_reduce_fusion
  (2 shorter events, 0.0 us)
Async XLA Ops:
  0.6 167.1 %copy-start = (bf16[1024,1280]{1,0:T(8,128)(2,1)S(1)}, bf16[1024,1280]{1,0:T(8,128)(2,1)}, u32[]{:S(2)}) copy-start(bf16[1024,1280]{1,0:T(8,128)(2,1)} %param.5) | copy-start | bytes 7864324
  0.6 47.3 %copy-start.4 = (bf16[256,512]{1,0:T(8,128)(2,1)S(1)}, bf16[256,512]{1,0:T(8,128)(2,1)}, u32[]{:S(2)}) copy-start(bf16[256,512]{1,0:T(8,128)(2,1)} %refs_0_.3) | copy-start | bytes 786436
  41.4 1.0 copy-start.1
  42.4 53.6 %collective-permute-start = (bf16[2,2,4,256,128]{4,3,2,1,0:T(8,128)(2,1)S(1)}, bf16[2,2,4,256,128]{4,3,2,1,0:T(8,128)(2,1)}, u32[]{:S(2)}, u32[]{:S(2)}) collective-permute-start(bf16[2,2,4,256,128]{4,3,2,1,0:T(8,128)(2,1)S(1)} %bitcast.22), channel_id=1, source_target_pairs={{0,1},{1,0},{2,3},{3,2},{4,5},{5,4},{6,7},{7,6},{8,9},{9,8},{10,11... | collective-permute-start | bytes 3145736 | tf_op jit(solution)/shard_map/ppermute | solution.py:20
  47.9 16.3 %collective-permute-start.2 = (bf16[256,512]{1,0:T(8,128)(2,1)S(1)}, bf16[256,512]{1,0:T(8,128)(2,1)S(1)}, u32[]{:S(2)}, u32[]{:S(2)}) collective-permute-start(bf16[256,512]{1,0:T(8,128)(2,1)S(1)} %copy-done.4), channel_id=1, source_target_pairs={{0,224},{32,0},{64,32},{96,64},{128,96},{160,128},{192,160},{224,1... | collective-permute-start | bytes 786440 | tf_op jit(solution)/shard_map/ppermute | solution.py:20
  58.6 10.9 %collective-permute-start.1 = (bf16[256,512]{1,0:T(8,128)(2,1)S(1)}, bf16[256,512]{1,0:T(8,128)(2,1)S(1)}, u32[]{:S(2)}, u32[]{:S(2)}) collective-permute-start(bf16[256,512]{1,0:T(8,128)(2,1)S(1)} %copy-done.4), channel_id=1, source_target_pairs={{0,32},{32,64},{64,96},{96,128},{128,160},{160,192},{192,224},{224... | collective-permute-start | bytes 786440 | tf_op jit(solution)/shard_map/ppermute | solution.py:20
  64.2 15.4 %copy-start.5 = (bf16[256,512]{1,0:T(8,128)(2,1)}, bf16[256,512]{1,0:T(8,128)(2,1)S(1)}, u32[]{:S(2)}) copy-start(bf16[256,512]{1,0:T(8,128)(2,1)S(1)} %collective-permute-done.2.refs_2_) | copy-start | bytes 786436
  64.2 10.1 %collective-permute-start.4 = (bf16[256,512]{1,0:T(8,128)(2,1)S(1)}, bf16[256,512]{1,0:T(8,128)(2,1)S(1)}, u32[]{:S(2)}, u32[]{:S(2)}) collective-permute-start(bf16[256,512]{1,0:T(8,128)(2,1)S(1)} %collective-permute-done.2.refs_2_), channel_id=1, source_target_pairs={{0,224},{32,0},{64,32},{96,64},{128,96},{160,128},{192,160},{224,1... | collective-permute-start | bytes 786440 | tf_op jit(solution)/shard_map/ppermute | solution.py:20
  69.6 10.1 %copy-start.6 = (bf16[256,512]{1,0:T(8,128)(2,1)}, bf16[256,512]{1,0:T(8,128)(2,1)S(1)}, u32[]{:S(2)}) copy-start(bf16[256,512]{1,0:T(8,128)(2,1)S(1)} %collective-permute-done.1.refs_1_) | copy-start | bytes 786436
  69.6 10.1 %collective-permute-start.3 = (bf16[256,512]{1,0:T(8,128)(2,1)S(1)}, bf16[256,512]{1,0:T(8,128)(2,1)S(1)}, u32[]{:S(2)}, u32[]{:S(2)}) collective-permute-start(bf16[256,512]{1,0:T(8,128)(2,1)S(1)} %collective-permute-done.1.refs_1_), channel_id=1, source_target_pairs={{0,32},{32,64},{64,96},{96,128},{128,160},{160,192},{192,224},{224... | collective-permute-start | bytes 786440 | tf_op jit(solution)/shard_map/ppermute | solution.py:20
  74.3 7.3 %copy-start.7 = (bf16[256,512]{1,0:T(8,128)(2,1)}, bf16[256,512]{1,0:T(8,128)(2,1)S(1)}, u32[]{:S(2)}) copy-start(bf16[256,512]{1,0:T(8,128)(2,1)S(1)} %collective-permute-done.4.refs_4_) | copy-start | bytes 786436
  74.3 9.2 %collective-permute-start.6 = (bf16[256,512]{1,0:T(8,128)(2,1)S(1)}, bf16[256,512]{1,0:T(8,128)(2,1)S(1)}, u32[]{:S(2)}, u32[]{:S(2)}) collective-permute-start(bf16[256,512]{1,0:T(8,128)(2,1)S(1)} %collective-permute-done.4.refs_4_), channel_id=1, source_target_pairs={{0,224},{32,0},{64,32},{96,64},{128,96},{160,128},{192,160},{224,1... | collective-permute-start | bytes 786440 | tf_op jit(solution)/shard_map/ppermute | solution.py:20
  79.7 16.3 %copy-start.8 = (bf16[256,512]{1,0:T(8,128)(2,1)}, bf16[256,512]{1,0:T(8,128)(2,1)S(1)}, u32[]{:S(2)}) copy-start(bf16[256,512]{1,0:T(8,128)(2,1)S(1)} %collective-permute-done.3.refs_3_) | copy-start | bytes 786436
  79.7 9.2 %collective-permute-start.5 = (bf16[256,512]{1,0:T(8,128)(2,1)S(1)}, bf16[256,512]{1,0:T(8,128)(2,1)S(1)}, u32[]{:S(2)}, u32[]{:S(2)}) collective-permute-start(bf16[256,512]{1,0:T(8,128)(2,1)S(1)} %collective-permute-done.3.refs_3_), channel_id=1, source_target_pairs={{0,32},{32,64},{64,96},{96,128},{128,160},{160,192},{192,224},{224... | collective-permute-start | bytes 786440 | tf_op jit(solution)/shard_map/ppermute | solution.py:20
  83.6 12.4 %copy-start.2 = (bf16[256,512]{1,0:T(8,128)(2,1)}, bf16[256,512]{1,0:T(8,128)(2,1)S(1)}, u32[]{:S(2)}) copy-start(bf16[256,512]{1,0:T(8,128)(2,1)S(1)} %collective-permute-done.6.refs_6_) | copy-start | bytes 786436
  83.6 7.3 %collective-permute-start.8 = (bf16[256,256]{1,0:T(8,128)(2,1)S(1)}, bf16[256,256]{1,0:T(8,128)(2,1)S(1)}, u32[]{:S(2)}, u32[]{:S(2)}) collective-permute-start(bf16[256,256]{1,0:T(8,128)(2,1)S(1)} %slice.9), channel_id=1, source_target_pairs={{0,224},{32,0},{64,32},{96,64},{128,96},{160,128},{192,160},{224,1... | collective-permute-start | bytes 393224 | tf_op jit(solution)/shard_map/ppermute | solution.py:20
  88.9 7.1 %copy-start.3 = (bf16[256,512]{1,0:T(8,128)(2,1)}, bf16[256,512]{1,0:T(8,128)(2,1)S(1)}, u32[]{:S(2)}) copy-start(bf16[256,512]{1,0:T(8,128)(2,1)S(1)} %collective-permute-done.5.refs_5_) | copy-start | bytes 786436
  88.9 7.0 %collective-permute-start.7 = (bf16[256,256]{1,0:T(8,128)(2,1)S(1)}, bf16[256,256]{1,0:T(8,128)(2,1)}, u32[]{:S(2)}, u32[]{:S(2)}) collective-permute-start(bf16[256,256]{1,0:T(8,128)(2,1)S(1)} %slice.8), channel_id=1, source_target_pairs={{0,32},{32,64},{64,96},{96,128},{128,160},{160,192},{192,224},{224... | collective-permute-start | bytes 393224 | tf_op jit(solution)/shard_map/ppermute | solution.py:20
  90.9 5.1 %copy-start.10 = (bf16[256,256]{1,0:T(8,128)(2,1)}, bf16[256,256]{1,0:T(8,128)(2,1)S(1)}, u32[]{:S(2)}) copy-start(bf16[256,256]{1,0:T(8,128)(2,1)S(1)} %collective-permute-done.8.refs_8_) | copy-start | bytes 393220
  100.5 11.6 %collective-permute-start.9 = (bf16[2,256,512]{2,1,0:T(8,128)(2,1)}, bf16[2,256,512]{2,1,0:T(8,128)(2,1)S(1)}, u32[]{:S(2)}, u32[]{:S(2)}) collective-permute-start(bf16[2,256,512]{2,1,0:T(8,128)(2,1)} %get-tuple-element.8), channel_id=1, source_target_pairs={{0,256},{256,0},{1,257},{257,1},{2,258},{258,2},{3,259},{259,3},{4... | collective-permute-start | bytes 1572872 | tf_op jit(solution)/shard_map/ppermute | solution.py:20
  112.1 0.8 copy-start.9
  117.7 9.2 %collective-permute-start.10 = (bf16[2,2,4,256,128]{4,3,2,1,0:T(8,128)(2,1)}, bf16[2,2,4,256,128]{4,3,2,1,0:T(8,128)(2,1)S(1)}, u32[]{:S(2)}, u32[]{:S(2)}) collective-permute-start(bf16[2,2,4,256,128]{4,3,2,1,0:T(8,128)(2,1)} %get-tuple-element.10), channel_id=1, source_target_pairs={{0,1},{1,0},{2,3},{3,2},{4,5},{5,4},{6,7},{7,6},{8,9},{9,8},{10,11... | collective-permute-start | bytes 3145736 | tf_op jit(solution)/shard_map/ppermute | solution.py:20
  146.1 18.1 %all-to-all-start.4 = ((bf16[32,8,512]{2,1,0:T(8,128)(2,1)}), bf16[32,8,512]{2,1,0:T(8,128)(2,1)S(1)}, u32[]{:S(2)}, u32[]{:S(2)}) async-start(bf16[32,8,512]{2,1,0:T(8,128)(2,1)} %bitcast.6), calls=%async_computation.4 | async-start | bytes 524288 | tf_op jit(solution)/shard_map/all_to_all | solution.py:24
  164.2 21.4 %all-to-all-start.3 = ((bf16[8,256,128]{2,1,0:T(8,128)(2,1)}), bf16[8,256,128]{2,1,0:T(8,128)(2,1)S(1)}, u32[]{:S(2)}, u32[]{:S(2)}) async-start(bf16[8,256,128]{2,1,0:T(8,128)(2,1)} %bitcast.5), calls=%async_computation.3 | async-start | bytes 1048576 | tf_op jit(solution)/shard_map/all_to_all | solution.py:24

commit v2 on v1

v2 whole, which is shorter than its diff:
```python
import functools

import jax
import jax.numpy as jnp
from jax import lax
from jax.experimental import pallas as pl
from jax.experimental.pallas import tpu as pltpu
from jax.sharding import Mesh
from jax.sharding import PartitionSpec as P


AUX = ("xl", "z")
PAIR = ("y", "xh", "c")
ALL = AUX + PAIR
CHUNKS = 1
VMEM = pl.BlockSpec(memory_space=pltpu.VMEM)
PARAMS = pltpu.CompilerParams(vmem_limit_bytes=24 * 1024 * 1024)


def in_vmem(kernel, outs, *args):
    args = [pltpu.with_memory_space_constraint(a, pltpu.VMEM) for a in args]
    return pl.pallas_call(
        kernel,
        in_specs=[VMEM] * len(args),
        out_specs=[VMEM] * len(outs),
        out_shape=[pltpu.VMEM(shape, dtype) for shape, dtype in outs],
        compiler_params=PARAMS,
    )(*args)


def shifted(x, axis, by):
    n = lax.axis_size(axis)
    return lax.ppermute(x, axis, [(i, (i + by) % n) for i in range(n)])


def exchange(x, axes):
    return lax.all_to_all(x, axes, split_axis=0, concat_axis=0, tiled=True)


def ring_blocks(x):
    n = lax.axis_size("z")
    half = x.shape[1] // 2
    right, left = x, x
    blocks, offsets = [x], [0]
    for s in range(1, n // 2):
        right, left = shifted(right, "z", 1), shifted(left, "z", -1)
        blocks += [right, left]
        offsets += [n - s, s]
    far = [shifted(right[:, :half], "z", 1), shifted(left[:, half:], "z", -1)]
    return blocks, offsets, far, n // 2


def loaded(refs, offsets, far_refs, far_offset):
    values = [(o, r[...]) for o, r in zip(offsets, refs)]
    far = jnp.concatenate([r[...] for r in far_refs], axis=1)
    return values + [(far_offset, far)]


def fitted_kernel(offsets, far_offset, chunks, own_ref, other_ref, *refs):
    count = len(offsets)
    blocks = loaded(refs[:count], offsets, refs[count : count + 2], far_offset)
    wide_refs = refs[count + 2 : count + 2 + chunks]
    narrow_refs = refs[count + 2 + chunks :]
    n = 8
    z, c = lax.axis_index("z"), lax.axis_index("c")
    half = own_ref.shape[-1]
    right = []
    for _, block in blocks:
        first, second = block[:half], block[half:]
        right += [jnp.where(c == 0, first, second), jnp.where(c == 0, second, first)]
    rhs = jnp.concatenate(right, axis=0)
    for h in range(2):
        left = []
        for offset, _ in blocks:
            at = lax.rem(z + offset, n)
            far, near = lax.rem(at, 2), lax.div(at, 2)
            left += [own_ref[h, far, near], other_ref[h, far, near]]
        lhs = jnp.concatenate(left, axis=1)
        out = jnp.dot(lhs, rhs, preferred_element_type=jnp.float32)
        rows = out.shape[0] // chunks
        for j in range(chunks):
            part = out[j * rows : (j + 1) * rows]
            wide_refs[j][h] = part
            narrow_refs[j][h] = part.astype(jnp.bfloat16)


def join_kernel(wide_ref, arrived_ref, whole_ref, own_ref):
    xl = lax.axis_index("xl")
    rows = wide_ref.shape[1]
    for h in range(2):
        whole = wide_ref[h] + arrived_ref[h].astype(jnp.float32)
        whole_ref[h * rows : (h + 1) * rows] = whole.astype(jnp.bfloat16)
    start = pl.multiple_of(xl * rows, rows)
    own_ref[...] = whole_ref[pl.ds(start, rows)]


def density_kernel(offsets, far_offset, whole_ref, *refs):
    count = len(offsets)
    blocks = loaded(refs[:count], offsets, refs[count : count + 2], far_offset)
    keep_ref, send_ref = refs[count + 2 :]
    n = 8
    z, c = lax.axis_index("z"), lax.axis_index("c")
    x = 2 * lax.axis_index("xh") + lax.axis_index("xl")
    lhs = whole_ref[...]
    rows = lhs.shape[0] // 2
    for offset, block in blocks:
        at = lax.rem(z + offset, n)
        far, near = lax.rem(at, 2), lax.div(at, 2)
        out = lax.dot_general(
            lhs, block, (((1,), (1,)), ((), ())), preferred_element_type=jnp.float32
        ).astype(jnp.bfloat16)
        half = out.shape[1] // 2
        first, second = out[:, :half], out[:, half:]
        keep = jnp.where(c == 0, first, second)
        send = jnp.where(c == 0, second, first)
        for h in range(2):
            slot = lax.rem(2 * far + h + 4 - x, 4)
            keep_ref[slot, near] = keep[h * rows : (h + 1) * rows]
            send_ref[slot, near] = send[h * rows : (h + 1) * rows]


def add_kernel(count, *refs):
    keeps, gots, outs = refs[:count], refs[count : 2 * count], refs[2 * count :]
    part = keeps[0].shape[2]
    for j in range(count):
        for s, out in enumerate(outs):
            both = keeps[j][s].astype(jnp.float32) + gots[j][s].astype(jnp.float32)
            out[:, j * part : (j + 1) * part] = both.astype(jnp.bfloat16)


def half_sum_kernel(here_ref, far_ref, left_ref, right_ref, out_ref):
    xl = lax.axis_index("xl")
    ours = here_ref[...].astype(jnp.float32) + far_ref[...].astype(jnp.float32)
    theirs = left_ref[...].astype(jnp.float32) + right_ref[...].astype(jnp.float32)
    n = here_ref.shape[0]
    out_ref[pl.ds(xl * n, n)] = ours.astype(jnp.bfloat16)
    out_ref[pl.ds((1 - xl) * n, n)] = theirs.astype(jnp.bfloat16)


def ao_kernel(got_ref, coef_ref, out_ref):
    n, rows, _ = got_ref.shape
    both = [
        jnp.concatenate([got_ref[2 * i + c].astype(jnp.float32) for i in range(n // 2)], axis=0)
        for c in range(2)
    ]
    lhs = jnp.concatenate(both, axis=1).astype(jnp.bfloat16)
    out = jnp.dot(lhs, coef_ref[...], preferred_element_type=jnp.float32)
    count = out.shape[1]
    for i in range(n // 2):
        part = out[i * rows : (i + 1) * rows].astype(jnp.bfloat16)
        out_ref[:, i * count : (i + 1) * count] = part


def work(metric, amplitudes, virt_coef):
    ys = exchange(jnp.broadcast_to(metric, (8, *metric.shape)), "y")
    ys = ys.reshape(2, 1, 4, *metric.shape)
    wanted = jnp.broadcast_to(ys, (2, 2, 4, *metric.shape))
    own = exchange(wanted.reshape(4, 4, *metric.shape), ("xl", "xh"))
    own = own.reshape(2, 2, 4, *metric.shape)
    other = shifted(own, "c", 1)

    blocks, offsets, far, far_offset = ring_blocks(amplitudes)
    rows, cols = metric.shape[0], amplitudes.shape[1]
    part = rows // CHUNKS
    f32, bf16 = jnp.float32, jnp.bfloat16
    outs = in_vmem(
        functools.partial(fitted_kernel, offsets, far_offset, CHUNKS),
        [((2, part, cols), f32)] * CHUNKS + [((2, part, cols), bf16)] * CHUNKS,
        own, other, *blocks, *far,
    )
    wides, narrows = outs[:CHUNKS], outs[CHUNKS:]

    keeps, gots, fitteds = [], [], []
    for wide, narrow in zip(wides, narrows):
        arrived = shifted(narrow, "xl", 1)
        whole, mine = in_vmem(
            join_kernel, [((2 * part, cols), bf16), ((part, cols), bf16)], wide, arrived
        )
        fitteds.append(mine)
        keep, send = in_vmem(
            functools.partial(density_kernel, offsets, far_offset),
            [((4, 4, part, 128), bf16)] * 2,
            whole, *blocks, *far,
        )
        keeps.append(keep)
        gots.append(shifted(send, "c", 1))

    slots = in_vmem(
        functools.partial(add_kernel, CHUNKS), [((4, rows, 128), bf16)] * 4, *keeps, *gots
    )

    def sent(s):
        at = lambda x: (x % 2) * 2 + x // 2
        return lax.ppermute(slots[s], ("xl", "xh"), [(at(x), at((x + s) % 4)) for x in range(4)])

    arrived = [sent(s) for s in (2, 1, 3)]
    (xs,) = in_vmem(half_sum_kernel, [((8, rows, 128), bf16)], slots[0], *arrived)
    ysum = exchange(xs, "y")
    density = jnp.sum(ysum.astype(f32), axis=0)

    fitted = fitteds[0] if CHUNKS == 1 else jnp.concatenate(fitteds, axis=0)
    got = exchange(fitted.reshape(32, 8, cols), PAIR)
    ao_count = virt_coef.shape[1]
    ao = pl.pallas_call(
        ao_kernel,
        in_specs=[VMEM] * 2,
        out_specs=VMEM,
        out_shape=jax.ShapeDtypeStruct((8, 16 * ao_count), bf16),
        compiler_params=PARAMS,
    )(got, virt_coef)
    return density, ao


def solution(mesh):
    split = Mesh(mesh.devices.reshape(2, 8, 8, 2, 2), ALL)
    return jax.shard_map(
        work,
        mesh=split,
        in_specs=(P(AUX, PAIR), P(AUX, PAIR), P()),
        out_specs=(P(AUX, PAIR), P(ALL, None)),
        check_vma=False,
    )
```

time: 187 us -> 170 us (0.909)
  blocking collectives: 57.2 us -> 39.5 us
  starting transfers between devices: 57.3 us -> 69.7 us
  waiting for transfers between devices: 52.7 us -> 46.7 us
  other arithmetic: 4.56 us -> 0.72 us
    all_to_all x3 -> x2, blocking collectives: 57.2 us -> 39.5 us  [exchange(): return lax.all_to_all(x, axes, split_axis=0, concat_axis=0, tiled=True)]
    ppermute x0 -> x3, starting transfers between devices: none -> 11.3 us  [sent(): lax.ppermute(slots[s], ('xl', 'xh'), [(at(x), at((x + s) % 4)) for x in r...]
    all_to_all x2, waiting for transfers between devices: 27.2 us -> 16.7 us  [exchange(): return lax.all_to_all(x, axes, split_axis=0, concat_axis=0, tiled=True)]
    ppermute x0 -> x3, waiting for transfers between devices: none -> 7.2 us  [sent(): lax.ppermute(slots[s], ('xl', 'xh'), [(at(x), at((x + s) % 4)) for x in r...]
    ppermute x11, waiting for transfers between devices: 25.4 us -> 22.7 us  [shifted(): return lax.ppermute(x, axis, [(i, (i + by) % n) for i in range(n)])]
    reduce_sum x2 -> x1, other arithmetic: 3.06 us -> 0.72 us  [work(): density = jnp.sum(ysum.astype(f32), axis=0)]
    pallas_call x2 -> x6, Pallas kernels: 9.36 us -> 8.22 us  [the longest x5 6.98 us: in_vmem(): pl.pallas_call(kernel, in_specs=[VMEM] * len(args), out_specs=[VMEM] * le...]
  transfers between devices with their start and end apart: 13 -> 16, of which waited for: 8 -> 8; matrix products, arithmetic and copies ran while one was open for 2% -> 0% of each run, Pallas kernels for 0% -> 2%
where the time goes in v2:
time: 170 us; the launch traced here: 169 us
  starting transfers between devices  69.7 us (41%)
  waiting for transfers between devices  46.7 us (27%)
  blocking collectives  39.5 us (23%)
  Pallas kernels  8.22 us (5%)
  local copies, waits for them, and re-layouts  3.36 us (2%)
    ppermute x11, starting transfers between devices, shifted(): return lax.ppermute(x, axis, [(i, (i + by) % n) for i in range(n)])  48.7 us
    all_to_all x2, blocking collectives, exchange(): return lax.all_to_all(x, axes, split_axis=0, concat_axis=0, tiled=True)  39.5 us
    ppermute x11, waiting for transfers between devices, shifted(): return lax.ppermute(x, axis, [(i, (i + by) % n) for i in range(n)])  22.7 us
    all_to_all x2, waiting for transfers between devices, exchange(): return lax.all_to_all(x, axes, split_axis=0, concat_axis=0, tiled=True)  16.7 us
    ppermute x3, starting transfers between devices, sent(): lax.ppermute(slots[s], ('xl', 'xh'), [(at(x), at((x + s) % 4)) for x in r...  11.3 us
    all_to_all x2, starting transfers between devices, exchange(): return lax.all_to_all(x, axes, split_axis=0, concat_axis=0, tiled=True)  9.74 us
    ppermute x3, waiting for transfers between devices, sent(): lax.ppermute(slots[s], ('xl', 'xh'), [(at(x), at((x + s) % 4)) for x in r...  7.2 us
    pallas_call x5, Pallas kernels, in_vmem(): pl.pallas_call(kernel, in_specs=[VMEM] * len(args), out_specs=[VMEM] * le...  6.98 us
  transfers between devices with their start and end apart: 16, of which 8 were waited for; matrix products, arithmetic and copies ran while one was open for 0% of the time, Pallas kernels for 2%

profile of v2, /device:TPU:1, one launch (start us, length us, event | category | flops | bytes accessed | tf_op | source)
XLA Modules:
  0.0 169.0 jit_solution(10791240233560233678)
XLA Ops:
  0.6 0.0 copy-start.1
  0.6 0.9 broadcast_in_dim.10
  1.6 22.3 %all_to_all.20 = bf16[8,256,128]{2,1,0:T(8,128)(2,1)S(1)} all-to-all(bf16[8,256,128]{2,1,0:T(8,128)(2,1)S(1)} %broadcast_in_dim.10), channel_id=1, replica_groups=mesh['xl'=2,'z'=8,'y'=8,'xh'=2,'c'=2] {'y'}, dimensions={0} | all-to-all | bytes 1048576 | tf_op jit(solution)/shard_map/all_to_all | solution.py:37
  23.9 0.2 broadcast_in_dim.12
  24.1 17.2 %all_to_all.21 = bf16[4,4,256,128]{3,2,1,0:T(8,128)(2,1)S(1)} all-to-all(bf16[4,4,256,128]{3,2,1,0:T(8,128)(2,1)S(1)} %bitcast.6), channel_id=1, replica_groups=mesh['xl'=2,'z'=8,'y'=8,'xh'=2,'c'=2] {'xl','xh'}, dimensions={0} | all-to-all | bytes 2097152 | tf_op jit(solution)/shard_map/all_to_all | solution.py:37
  41.3 5.5 %collective-permute-start = (bf16[2,2,4,256,128]{4,3,2,1,0:T(8,128)(2,1)S(1)}, bf16[2,2,4,256,128]{4,3,2,1,0:T(8,128)(2,1)S(1)}, u32[]{:S(2)}, u32[]{:S(2)}) collective-permute-start(bf16[2,2,4,256,128]{4,3,2,1,0:T(8,128)(2,1)S(1)} %bitcast.4), channel_id=1, source_target_pairs={{0,1},{1,0},{2,3},{3,2},{4,5},{5,4},{6,7},{7,6},{8,9},{9,8},{10,11... | collective-permute-start | bytes 3145736 | tf_op jit(solution)/shard_map/ppermute | solution.py:33
  46.8 0.0 copy-done.1
  46.8 10.7 %collective-permute-start.2 = (bf16[256,512]{1,0:T(8,128)(2,1)S(1)}, bf16[256,512]{1,0:T(8,128)(2,1)S(1)}, u32[]{:S(2)}, u32[]{:S(2)}) collective-permute-start(bf16[256,512]{1,0:T(8,128)(2,1)S(1)} %copy-done.1), channel_id=1, source_target_pairs={{0,224},{32,0},{64,32},{96,64},{128,96},{160,128},{192,160},{224,1... | collective-permute-start | bytes 786440 | tf_op jit(solution)/shard_map/ppermute | solution.py:33
  57.5 1.9 %collective-permute-start.1 = (bf16[256,512]{1,0:T(8,128)(2,1)S(1)}, bf16[256,512]{1,0:T(8,128)(2,1)S(1)}, u32[]{:S(2)}, u32[]{:S(2)}) collective-permute-start(bf16[256,512]{1,0:T(8,128)(2,1)S(1)} %copy-done.1), channel_id=1, source_target_pairs={{0,32},{32,64},{64,96},{96,128},{128,160},{160,192},{192,224},{224... | collective-permute-start | bytes 786440 | tf_op jit(solution)/shard_map/ppermute | solution.py:33
  59.4 3.7 %collective-permute-done.2.refs_2_ = bf16[256,512]{1,0:T(8,128)(2,1)S(1)} collective-permute-done((bf16[256,512]{1,0:T(8,128)(2,1)S(1)}, bf16[256,512]{1,0:T(8,128)(2,1)S(1)}, u32[]{:S(2)}, u32[]{:S(2)}) %collective-permute-start.2) | collective-permute-done | bytes 262176 | tf_op jit(solution)/shard_map/ppermute | solution.py:33
  63.1 5.3 %collective-permute-start.4 = (bf16[256,512]{1,0:T(8,128)(2,1)S(1)}, bf16[256,512]{1,0:T(8,128)(2,1)S(1)}, u32[]{:S(2)}, u32[]{:S(2)}) collective-permute-start(bf16[256,512]{1,0:T(8,128)(2,1)S(1)} %collective-permute-done.2.refs_2_), channel_id=1, source_target_pairs={{0,224},{32,0},{64,32},{96,64},{128,96},{160,128},{192,160},{224,1... | collective-permute-start | bytes 786440 | tf_op jit(solution)/shard_map/ppermute | solution.py:33
  68.5 0.0 collective-permute-done.1.refs_1_
  68.5 1.9 %collective-permute-start.3 = (bf16[256,512]{1,0:T(8,128)(2,1)S(1)}, bf16[256,512]{1,0:T(8,128)(2,1)S(1)}, u32[]{:S(2)}, u32[]{:S(2)}) collective-permute-start(bf16[256,512]{1,0:T(8,128)(2,1)S(1)} %collective-permute-done.1.refs_1_), channel_id=1, source_target_pairs={{0,32},{32,64},{64,96},{96,128},{128,160},{160,192},{192,224},{224... | collective-permute-start | bytes 786440 | tf_op jit(solution)/shard_map/ppermute | solution.py:33
  70.4 2.8 %collective-permute-done.4.refs_4_ = bf16[256,512]{1,0:T(8,128)(2,1)S(1)} collective-permute-done((bf16[256,512]{1,0:T(8,128)(2,1)S(1)}, bf16[256,512]{1,0:T(8,128)(2,1)S(1)}, u32[]{:S(2)}, u32[]{:S(2)}) %collective-permute-start.4) | collective-permute-done | bytes 262176 | tf_op jit(solution)/shard_map/ppermute | solution.py:33
  73.2 5.3 %collective-permute-start.6 = (bf16[256,512]{1,0:T(8,128)(2,1)S(1)}, bf16[256,512]{1,0:T(8,128)(2,1)S(1)}, u32[]{:S(2)}, u32[]{:S(2)}) collective-permute-start(bf16[256,512]{1,0:T(8,128)(2,1)S(1)} %collective-permute-done.4.refs_4_), channel_id=1, source_target_pairs={{0,224},{32,0},{64,32},{96,64},{128,96},{160,128},{192,160},{224,1... | collective-permute-start | bytes 786440 | tf_op jit(solution)/shard_map/ppermute | solution.py:33
  78.5 0.0 collective-permute-done.3.refs_3_
  78.5 1.9 %collective-permute-start.5 = (bf16[256,512]{1,0:T(8,128)(2,1)S(1)}, bf16[256,512]{1,0:T(8,128)(2,1)S(1)}, u32[]{:S(2)}, u32[]{:S(2)}) collective-permute-start(bf16[256,512]{1,0:T(8,128)(2,1)S(1)} %collective-permute-done.3.refs_3_), channel_id=1, source_target_pairs={{0,32},{32,64},{64,96},{96,128},{128,160},{160,192},{192,224},{224... | collective-permute-start | bytes 786440 | tf_op jit(solution)/shard_map/ppermute | solution.py:33
  80.5 2.0 %collective-permute-done.6.refs_6_ = bf16[256,512]{1,0:T(8,128)(2,1)S(1)} collective-permute-done((bf16[256,512]{1,0:T(8,128)(2,1)S(1)}, bf16[256,512]{1,0:T(8,128)(2,1)S(1)}, u32[]{:S(2)}, u32[]{:S(2)}) %collective-permute-start.6) | collective-permute-done | bytes 262176 | tf_op jit(solution)/shard_map/ppermute | solution.py:33
  82.5 5.3 %collective-permute-start.8 = (bf16[256,256]{1,0:T(8,128)(2,1)S(1)}, bf16[256,256]{1,0:T(8,128)(2,1)S(1)}, u32[]{:S(2)}, u32[]{:S(2)}) collective-permute-start(bf16[256,256]{1,0:T(8,128)(2,1)S(1)} %slice.9), channel_id=1, source_target_pairs={{0,224},{32,0},{64,32},{96,64},{128,96},{160,128},{192,160},{224,1... | collective-permute-start | bytes 393224 | tf_op jit(solution)/shard_map/ppermute | solution.py:33
  87.8 0.0 collective-permute-done.5.refs_5_
  87.8 1.9 %collective-permute-start.7 = (bf16[256,256]{1,0:T(8,128)(2,1)S(1)}, bf16[256,256]{1,0:T(8,128)(2,1)S(1)}, u32[]{:S(2)}, u32[]{:S(2)}) collective-permute-start(bf16[256,256]{1,0:T(8,128)(2,1)S(1)} %slice.8), channel_id=1, source_target_pairs={{0,32},{32,64},{64,96},{96,128},{128,160},{160,192},{192,224},{224... | collective-permute-start | bytes 393224 | tf_op jit(solution)/shard_map/ppermute | solution.py:33
  89.8 0.0 collective-permute-done.8.refs_8_
  89.8 5.0 %collective-permute-done.7.refs_7_ = bf16[256,256]{1,0:T(8,128)(2,1)S(1)} collective-permute-done((bf16[256,256]{1,0:T(8,128)(2,1)S(1)}, bf16[256,256]{1,0:T(8,128)(2,1)S(1)}, u32[]{:S(2)}, u32[]{:S(2)}) %collective-permute-start.7) | collective-permute-done | bytes 131104 | tf_op jit(solution)/shard_map/ppermute | solution.py:33
  94.7 0.0 collective-permute-done.other_ref
  94.7 1.3 shard_map.50
  96.0 2.1 %collective-permute-start.9 = (bf16[2,256,512]{2,1,0:T(8,128)(2,1)S(1)}, bf16[2,256,512]{2,1,0:T(8,128)(2,1)S(1)}, u32[]{:S(2)}, u32[]{:S(2)}) collective-permute-start(bf16[2,256,512]{2,1,0:T(8,128)(2,1)S(1)} %get-tuple-element.13), channel_id=1, source_target_pairs={{0,256},{256,0},{1,257},{257,1},{2,258},{258,2},{3,259},{259,3},{4... | collective-permute-start | bytes 1572872 | tf_op jit(solution)/shard_map/ppermute | solution.py:33
  98.2 9.2 %collective-permute-done.9.arrived_ref = bf16[2,256,512]{2,1,0:T(8,128)(2,1)S(1)} collective-permute-done((bf16[2,256,512]{2,1,0:T(8,128)(2,1)S(1)}, bf16[2,256,512]{2,1,0:T(8,128)(2,1)S(1)}, u32[]{:S(2)}, u32[]{:S(2)}) %collective-permute-start.9) | collective-permute-done | bytes 524320 | tf_op jit(solution)/shard_map/ppermute | solution.py:33
  107.4 0.9 shard_map.51
  108.3 2.4 %shard_map.52 = (bf16[4,4,256,128]{3,2,1,0:T(8,128)(2,1)S(1)}, bf16[4,4,256,128]{3,2,1,0:T(8,128)(2,1)}) custom-call(bf16[512,512]{1,0:T(8,128)(2,1)S(1)} %get-tuple-element.14.whole_ref, bf16[256,512]{1,0:T(8,128)(2,1)S(1)} %copy-done.1, bf16[256,512]{1,0:T(8,128)(2,1)S(1)} %collective-permute-done.1.refs_1_, ...), custom_call_target="tpu_custom_call" | custom-call | tf_op jit(solution)/shard_map/pallas_call | solution.py:22
  110.7 0.0 copy-start.2
  110.7 1.0 copy-done.2
  111.7 6.7 %collective-permute-start.10 = (bf16[4,4,256,128]{3,2,1,0:T(8,128)(2,1)}, bf16[4,4,256,128]{3,2,1,0:T(8,128)(2,1)}, u32[]{:S(2)}, u32[]{:S(2)}) collective-permute-start(bf16[4,4,256,128]{3,2,1,0:T(8,128)(2,1)} %get-tuple-element.16), channel_id=1, source_target_pairs={{0,1},{1,0},{2,3},{3,2},{4,5},{5,4},{6,7},{7,6},{8,9},{9,8},{10,11... | collective-permute-start | bytes 3145736 | tf_op jit(solution)/shard_map/ppermute | solution.py:33
  118.4 0.0 copy-start
  118.5 4.2 %all-to-all-start.3 = ((bf16[32,8,512]{2,1,0:T(8,128)(2,1)}), bf16[32,8,512]{2,1,0:T(8,128)(2,1)S(1)}, u32[]{:S(2)}, u32[]{:S(2)}) async-start(bf16[32,8,512]{2,1,0:T(8,128)(2,1)} %bitcast.3), calls=%async_computation.3 | async-start | bytes 524288 | tf_op jit(solution)/shard_map/all_to_all | solution.py:37
  122.6 0.0 collective-permute-done.10.refs_1_
  122.6 0.0 copy-start.3
  122.6 1.2 copy-done.3
  123.9 1.5 shard_map.53
  125.3 4.8 %collective-permute-start.11 = (bf16[4,256,128]{2,1,0:T(8,128)(2,1)S(1)}, bf16[4,256,128]{2,1,0:T(8,128)(2,1)S(1)}, u32[]{:S(2)}, u32[]{:S(2)}) collective-permute-start(bf16[4,256,128]{2,1,0:T(8,128)(2,1)S(1)} %get-tuple-element.18), channel_id=1, source_target_pairs={{0,2},{256,258},{2,0},{258,256},{1,3},{257,259},{3,1},{259,257},{4... | collective-permute-start | bytes 786440 | tf_op jit(solution)/shard_map/ppermute | solution.py:194
  130.1 2.1 %collective-permute-start.12 = (bf16[4,256,128]{2,1,0:T(8,128)(2,1)S(1)}, bf16[4,256,128]{2,1,0:T(8,128)(2,1)S(1)}, u32[]{:S(2)}, u32[]{:S(2)}) collective-permute-start(bf16[4,256,128]{2,1,0:T(8,128)(2,1)S(1)} %get-tuple-element.19), channel_id=1, source_target_pairs={{0,256},{256,2},{2,258},{258,0},{1,257},{257,3},{3,259},{259,1},{4... | collective-permute-start | bytes 786440 | tf_op jit(solution)/shard_map/ppermute | solution.py:194
  132.2 4.4 %collective-permute-start.13 = (bf16[4,256,128]{2,1,0:T(8,128)(2,1)S(1)}, bf16[4,256,128]{2,1,0:T(8,128)(2,1)S(1)}, u32[]{:S(2)}, u32[]{:S(2)}) collective-permute-start(bf16[4,256,128]{2,1,0:T(8,128)(2,1)S(1)} %get-tuple-element.20), channel_id=1, source_target_pairs={{0,258},{256,0},{2,256},{258,2},{1,259},{257,1},{3,257},{259,3},{4... | collective-permute-start | bytes 786440 | tf_op jit(solution)/shard_map/ppermute | solution.py:194
  136.6 1.3 collective-permute-done.11.far_ref
  137.9 5.9 %collective-permute-done.12.left_ref = bf16[4,256,128]{2,1,0:T(8,128)(2,1)S(1)} collective-permute-done((bf16[4,256,128]{2,1,0:T(8,128)(2,1)S(1)}, bf16[4,256,128]{2,1,0:T(8,128)(2,1)S(1)}, u32[]{:S(2)}, u32[]{:S(2)}) %collective-permute-start.12) | collective-permute-done | bytes 262176 | tf_op jit(solution)/shard_map/ppermute | solution.py:194
  143.8 0.0 collective-permute-done.13.right_ref
  143.8 0.9 shard_map.54
  144.7 0.0 all-to-all-done.3.got_ref
  144.7 5.6 %all-to-all-start.2 = ((bf16[8,256,128]{2,1,0:T(8,128)(2,1)}), bf16[8,256,128]{2,1,0:T(8,128)(2,1)S(1)}, u32[]{:S(2)}, u32[]{:S(2)}) async-start(bf16[8,256,128]{2,1,0:T(8,128)(2,1)} %shard_map.54), calls=%async_computation.2 | async-start | bytes 1048576 | tf_op jit(solution)/shard_map/all_to_all | solution.py:37
  150.3 0.0 copy-done
  150.3 1.2 shard_map.55
  151.6 16.7 %all-to-all-done.2 = bf16[8,256,128]{2,1,0:T(8,128)(2,1)S(1)} async-done(((bf16[8,256,128]{2,1,0:T(8,128)(2,1)}), bf16[8,256,128]{2,1,0:T(8,128)(2,1)S(1)}, u32[]{:S(2)}, u32[]{:S(2)}) %all-to-all-start.2) | async-done | bytes 524320 | tf_op jit(solution)/shard_map/all_to_all | solution.py:37
  168.3 0.7 convert_reduce_fusion
  (2 shorter events, 0.0 us)
Async XLA Ops:
  0.6 46.2 %copy-start.1 = (bf16[256,512]{1,0:T(8,128)(2,1)S(1)}, bf16[256,512]{1,0:T(8,128)(2,1)}, u32[]{:S(2)}) copy-start(bf16[256,512]{1,0:T(8,128)(2,1)} %refs_0_.3) | copy-start | bytes 786436
  41.3 53.4 %collective-permute-start = (bf16[2,2,4,256,128]{4,3,2,1,0:T(8,128)(2,1)S(1)}, bf16[2,2,4,256,128]{4,3,2,1,0:T(8,128)(2,1)S(1)}, u32[]{:S(2)}, u32[]{:S(2)}) collective-permute-start(bf16[2,2,4,256,128]{4,3,2,1,0:T(8,128)(2,1)S(1)} %bitcast.4), channel_id=1, source_target_pairs={{0,1},{1,0},{2,3},{3,2},{4,5},{5,4},{6,7},{7,6},{8,9},{9,8},{10,11... | collective-permute-start | bytes 3145736 | tf_op jit(solution)/shard_map/ppermute | solution.py:33
  46.8 16.3 %collective-permute-start.2 = (bf16[256,512]{1,0:T(8,128)(2,1)S(1)}, bf16[256,512]{1,0:T(8,128)(2,1)S(1)}, u32[]{:S(2)}, u32[]{:S(2)}) collective-permute-start(bf16[256,512]{1,0:T(8,128)(2,1)S(1)} %copy-done.1), channel_id=1, source_target_pairs={{0,224},{32,0},{64,32},{96,64},{128,96},{160,128},{192,160},{224,1... | collective-permute-start | bytes 786440 | tf_op jit(solution)/shard_map/ppermute | solution.py:33
  57.5 10.9 %collective-permute-start.1 = (bf16[256,512]{1,0:T(8,128)(2,1)S(1)}, bf16[256,512]{1,0:T(8,128)(2,1)S(1)}, u32[]{:S(2)}, u32[]{:S(2)}) collective-permute-start(bf16[256,512]{1,0:T(8,128)(2,1)S(1)} %copy-done.1), channel_id=1, source_target_pairs={{0,32},{32,64},{64,96},{96,128},{128,160},{160,192},{192,224},{224... | collective-permute-start | bytes 786440 | tf_op jit(solution)/shard_map/ppermute | solution.py:33
  63.1 10.1 %collective-permute-start.4 = (bf16[256,512]{1,0:T(8,128)(2,1)S(1)}, bf16[256,512]{1,0:T(8,128)(2,1)S(1)}, u32[]{:S(2)}, u32[]{:S(2)}) collective-permute-start(bf16[256,512]{1,0:T(8,128)(2,1)S(1)} %collective-permute-done.2.refs_2_), channel_id=1, source_target_pairs={{0,224},{32,0},{64,32},{96,64},{128,96},{160,128},{192,160},{224,1... | collective-permute-start | bytes 786440 | tf_op jit(solution)/shard_map/ppermute | solution.py:33
  68.5 10.1 %collective-permute-start.3 = (bf16[256,512]{1,0:T(8,128)(2,1)S(1)}, bf16[256,512]{1,0:T(8,128)(2,1)S(1)}, u32[]{:S(2)}, u32[]{:S(2)}) collective-permute-start(bf16[256,512]{1,0:T(8,128)(2,1)S(1)} %collective-permute-done.1.refs_1_), channel_id=1, source_target_pairs={{0,32},{32,64},{64,96},{96,128},{128,160},{160,192},{192,224},{224... | collective-permute-start | bytes 786440 | tf_op jit(solution)/shard_map/ppermute | solution.py:33
  73.2 9.2 %collective-permute-start.6 = (bf16[256,512]{1,0:T(8,128)(2,1)S(1)}, bf16[256,512]{1,0:T(8,128)(2,1)S(1)}, u32[]{:S(2)}, u32[]{:S(2)}) collective-permute-start(bf16[256,512]{1,0:T(8,128)(2,1)S(1)} %collective-permute-done.4.refs_4_), channel_id=1, source_target_pairs={{0,224},{32,0},{64,32},{96,64},{128,96},{160,128},{192,160},{224,1... | collective-permute-start | bytes 786440 | tf_op jit(solution)/shard_map/ppermute | solution.py:33
  78.5 9.2 %collective-permute-start.5 = (bf16[256,512]{1,0:T(8,128)(2,1)S(1)}, bf16[256,512]{1,0:T(8,128)(2,1)S(1)}, u32[]{:S(2)}, u32[]{:S(2)}) collective-permute-start(bf16[256,512]{1,0:T(8,128)(2,1)S(1)} %collective-permute-done.3.refs_3_), channel_id=1, source_target_pairs={{0,32},{32,64},{64,96},{96,128},{128,160},{160,192},{192,224},{224... | collective-permute-start | bytes 786440 | tf_op jit(solution)/shard_map/ppermute | solution.py:33
  82.5 7.3 %collective-permute-start.8 = (bf16[256,256]{1,0:T(8,128)(2,1)S(1)}, bf16[256,256]{1,0:T(8,128)(2,1)S(1)}, u32[]{:S(2)}, u32[]{:S(2)}) collective-permute-start(bf16[256,256]{1,0:T(8,128)(2,1)S(1)} %slice.9), channel_id=1, source_target_pairs={{0,224},{32,0},{64,32},{96,64},{128,96},{160,128},{192,160},{224,1... | collective-permute-start | bytes 393224 | tf_op jit(solution)/shard_map/ppermute | solution.py:33
  87.8 6.9 %collective-permute-start.7 = (bf16[256,256]{1,0:T(8,128)(2,1)S(1)}, bf16[256,256]{1,0:T(8,128)(2,1)S(1)}, u32[]{:S(2)}, u32[]{:S(2)}) collective-permute-start(bf16[256,256]{1,0:T(8,128)(2,1)S(1)} %slice.8), channel_id=1, source_target_pairs={{0,32},{32,64},{64,96},{96,128},{128,160},{160,192},{192,224},{224... | collective-permute-start | bytes 393224 | tf_op jit(solution)/shard_map/ppermute | solution.py:33
  96.0 11.4 %collective-permute-start.9 = (bf16[2,256,512]{2,1,0:T(8,128)(2,1)S(1)}, bf16[2,256,512]{2,1,0:T(8,128)(2,1)S(1)}, u32[]{:S(2)}, u32[]{:S(2)}) collective-permute-start(bf16[2,256,512]{2,1,0:T(8,128)(2,1)S(1)} %get-tuple-element.13), channel_id=1, source_target_pairs={{0,256},{256,0},{1,257},{257,1},{2,258},{258,2},{3,259},{259,3},{4... | collective-permute-start | bytes 1572872 | tf_op jit(solution)/shard_map/ppermute | solution.py:33
  110.7 1.0 copy-start.2
  111.7 10.9 %collective-permute-start.10 = (bf16[4,4,256,128]{3,2,1,0:T(8,128)(2,1)}, bf16[4,4,256,128]{3,2,1,0:T(8,128)(2,1)}, u32[]{:S(2)}, u32[]{:S(2)}) collective-permute-start(bf16[4,4,256,128]{3,2,1,0:T(8,128)(2,1)} %get-tuple-element.16), channel_id=1, source_target_pairs={{0,1},{1,0},{2,3},{3,2},{4,5},{5,4},{6,7},{7,6},{8,9},{9,8},{10,11... | collective-permute-start | bytes 3145736 | tf_op jit(solution)/shard_map/ppermute | solution.py:33
  118.4 31.9 %copy-start = (bf16[1024,1280]{1,0:T(8,128)(2,1)S(1)}, bf16[1024,1280]{1,0:T(8,128)(2,1)}, u32[]{:S(2)}) copy-start(bf16[1024,1280]{1,0:T(8,128)(2,1)} %coef_ref.1) | copy-start | bytes 7864324
  118.5 26.3 %all-to-all-start.3 = ((bf16[32,8,512]{2,1,0:T(8,128)(2,1)}), bf16[32,8,512]{2,1,0:T(8,128)(2,1)S(1)}, u32[]{:S(2)}, u32[]{:S(2)}) async-start(bf16[32,8,512]{2,1,0:T(8,128)(2,1)} %bitcast.3), calls=%async_computation.3 | async-start | bytes 524288 | tf_op jit(solution)/shard_map/all_to_all | solution.py:37
  122.6 1.2 copy-start.3
  125.3 12.6 %collective-permute-start.11 = (bf16[4,256,128]{2,1,0:T(8,128)(2,1)S(1)}, bf16[4,256,128]{2,1,0:T(8,128)(2,1)S(1)}, u32[]{:S(2)}, u32[]{:S(2)}) collective-permute-start(bf16[4,256,128]{2,1,0:T(8,128)(2,1)S(1)} %get-tuple-element.18), channel_id=1, source_target_pairs={{0,2},{256,258},{2,0},{258,256},{1,3},{257,259},{3,1},{259,257},{4... | collective-permute-start | bytes 786440 | tf_op jit(solution)/shard_map/ppermute | solution.py:194
  130.1 13.7 %collective-permute-start.12 = (bf16[4,256,128]{2,1,0:T(8,128)(2,1)S(1)}, bf16[4,256,128]{2,1,0:T(8,128)(2,1)S(1)}, u32[]{:S(2)}, u32[]{:S(2)}) collective-permute-start(bf16[4,256,128]{2,1,0:T(8,128)(2,1)S(1)} %get-tuple-element.19), channel_id=1, source_target_pairs={{0,256},{256,2},{2,258},{258,0},{1,257},{257,3},{3,259},{259,1},{4... | collective-permute-start | bytes 786440 | tf_op jit(solution)/shard_map/ppermute | solution.py:194
  132.2 11.6 %collective-permute-start.13 = (bf16[4,256,128]{2,1,0:T(8,128)(2,1)S(1)}, bf16[4,256,128]{2,1,0:T(8,128)(2,1)S(1)}, u32[]{:S(2)}, u32[]{:S(2)}) collective-permute-start(bf16[4,256,128]{2,1,0:T(8,128)(2,1)S(1)} %get-tuple-element.20), channel_id=1, source_target_pairs={{0,258},{256,0},{2,256},{258,2},{1,259},{257,1},{3,257},{259,3},{4... | collective-permute-start | bytes 786440 | tf_op jit(solution)/shard_map/ppermute | solution.py:194
  144.7 23.5 %all-to-all-start.2 = ((bf16[8,256,128]{2,1,0:T(8,128)(2,1)}), bf16[8,256,128]{2,1,0:T(8,128)(2,1)S(1)}, u32[]{:S(2)}, u32[]{:S(2)}) async-start(bf16[8,256,128]{2,1,0:T(8,128)(2,1)} %shard_map.54), calls=%async_computation.2 | async-start | bytes 1048576 | tf_op jit(solution)/shard_map/all_to_all | solution.py:37

commit v3 on v2

v3 whole, which is shorter than its diff:
```python
import functools

import jax
import jax.numpy as jnp
from jax import lax
from jax.experimental import pallas as pl
from jax.experimental.pallas import tpu as pltpu
from jax.sharding import Mesh
from jax.sharding import PartitionSpec as P


AUX = ("xl", "z")
PAIR = ("y", "xh", "c")
ALL = AUX + PAIR
VMEM = pl.BlockSpec(memory_space=pltpu.VMEM)
PARAMS = pltpu.CompilerParams(vmem_limit_bytes=24 * 1024 * 1024)
F32, BF16 = jnp.float32, jnp.bfloat16


def in_vmem(kernel, outs, *args):
    args = [pltpu.with_memory_space_constraint(a, pltpu.VMEM) for a in args]
    return pl.pallas_call(
        kernel,
        in_specs=[VMEM] * len(args),
        out_specs=[VMEM] * len(outs),
        out_shape=[pltpu.VMEM(shape, dtype) for shape, dtype in outs],
        compiler_params=PARAMS,
    )(*args)


def shifted(x, axis, by):
    n = lax.axis_size(axis)
    return lax.ppermute(x, axis, [(i, (i + by) % n) for i in range(n)])


def shifted_x(x, by):
    at = lambda i: (i % 2) * 2 + i // 2
    return lax.ppermute(x, ("xl", "xh"), [(at(i), at((i + by) % 4)) for i in range(4)])


def exchange(x, axes):
    return lax.all_to_all(x, axes, split_axis=0, concat_axis=0, tiled=True)


def ring_blocks(x):
    n = lax.axis_size("z")
    half = x.shape[1] // 2
    right, left = x, x
    blocks, offsets = [x], [0]
    for s in range(1, n // 2):
        right, left = shifted(right, "z", 1), shifted(left, "z", -1)
        blocks += [right, left]
        offsets += [n - s, s]
    far = [shifted(right[:, :half], "z", 1), shifted(left[:, half:], "z", -1)]
    return blocks + far, offsets + [n // 2]


def values_of(refs):
    far = jnp.concatenate([refs[-2][...], refs[-1][...]], axis=1)
    return [r[...] for r in refs[:-2]] + [far]


def place(offset):
    at = lax.rem(lax.axis_index("z") + offset, 8)
    return lax.rem(at, 2), lax.div(at, 2)


def pack_kernel(amp_ref, got_ref, out_ref):
    rows, cols = got_ref.shape
    c = lax.axis_index("c")
    out_ref[:, :cols] = amp_ref[pl.ds(pl.multiple_of(c * rows, rows), rows)]
    out_ref[:, cols:] = got_ref[...]


def fitted_kernel(offsets, metric_ref, *refs):
    blocks = values_of(refs[:-2])
    keep_ref, send_ref = refs[-2:]
    rhs = jnp.concatenate(blocks, axis=0)
    cols = keep_ref.shape[2]
    for h in range(2):
        lhs = jnp.concatenate([metric_ref[(h, *place(o))] for o in offsets], axis=1)
        out = jnp.dot(lhs, rhs, preferred_element_type=F32)
        keep_ref[h] = out[:, :cols]
        send_ref[h] = out[:, cols:].astype(BF16)


def add_kernel(keep_ref, got_ref, own_ref, other_ref):
    xl = lax.axis_index("xl")
    own_ref[...] = keep_ref[xl] + got_ref[xl].astype(F32)
    other_ref[...] = (keep_ref[1 - xl] + got_ref[1 - xl].astype(F32)).astype(BF16)


def join_kernel(own_ref, arrived_ref, out_ref):
    out_ref[...] = (own_ref[...] + arrived_ref[...].astype(F32)).astype(BF16)


def density_kernel(offsets, own_ref, own_next_ref, other_ref, other_next_ref, *refs):
    blocks = values_of(refs[:-4])
    slots = refs[-4:]
    xl = lax.axis_index("xl")
    x = 2 * lax.axis_index("xh") + xl
    own = jnp.concatenate([own_ref[...], own_next_ref[...]], axis=1)
    other = jnp.concatenate([other_ref[...], other_next_ref[...]], axis=1)
    lhs = jnp.concatenate([own, other], axis=0)
    rows, width = own.shape[0], blocks[0].shape[0]
    for i in range(0, len(blocks), 2):
        rhs = jnp.concatenate(blocks[i : i + 2], axis=0)
        out = lax.dot_general(
            lhs, rhs, (((1,), (1,)), ((), ())), preferred_element_type=F32
        ).astype(BF16)
        for j in range(2):
            far, near = place(offsets[i + j])
            cols = slice(j * width, (j + 1) * width)
            same = far == lax.axis_index("xh")
            mine, theirs = out[:rows, cols], out[rows:, cols]

            @pl.when(same)
            def _():
                slots[0][near] = mine

            @pl.when(jnp.logical_not(same))
            def _():
                slots[2][near] = mine

            next_one = lax.rem(2 * far + (1 - xl) + 4 - x, 4) == 1

            @pl.when(next_one)
            def _():
                slots[1][near] = theirs

            @pl.when(jnp.logical_not(next_one))
            def _():
                slots[3][near] = theirs


def half_sum_kernel(here_ref, far_ref, left_ref, right_ref, out_ref):
    xl = lax.axis_index("xl")
    n = here_ref.shape[0]
    ours = here_ref[...].astype(F32) + far_ref[...].astype(F32)
    theirs = left_ref[...].astype(F32) + right_ref[...].astype(F32)
    out_ref[pl.ds(xl * n, n)] = ours.astype(BF16)
    out_ref[pl.ds((1 - xl) * n, n)] = theirs.astype(BF16)


def ao_kernel(got_ref, coef_ref, out_ref):
    n, rows, _ = got_ref.shape
    both = [
        jnp.concatenate([got_ref[2 * i + c].astype(F32) for i in range(n // 2)], axis=0)
        for c in range(2)
    ]
    lhs = jnp.concatenate(both, axis=1).astype(BF16)
    out = jnp.dot(lhs, coef_ref[...], preferred_element_type=F32)
    count = out.shape[1]
    for i in range(n // 2):
        part = out[i * rows : (i + 1) * rows].astype(BF16)
        out_ref[:, i * count : (i + 1) * count] = part


def work(metric, amplitudes, virt_coef):
    rows, cols = amplitudes.shape
    c = lax.axis_index("c")
    ys = exchange(jnp.broadcast_to(metric, (8, *metric.shape)), "y")
    ys = ys.reshape(2, 1, 4, *metric.shape)
    wanted = jnp.broadcast_to(ys, (2, 2, 4, *metric.shape))
    part = exchange(wanted.reshape(4, 4, *metric.shape), ("xl", "xh"))
    part = part.reshape(2, 2, 4, *metric.shape)

    half = rows // 2
    away = lax.dynamic_slice_in_dim(amplitudes, (1 - c) * half, half, 0)
    got = shifted(away, "c", 1)
    (packed,) = in_vmem(pack_kernel, [((half, 2 * cols), BF16)], amplitudes, got)
    blocks, offsets = ring_blocks(packed)

    keep, send = in_vmem(
        functools.partial(fitted_kernel, offsets),
        [((2, rows, cols), F32), ((2, rows, cols), BF16)],
        part, *blocks,
    )
    got = shifted(send, "c", 1)
    own, away = in_vmem(add_kernel, [((rows, cols), F32), ((rows, cols), BF16)], keep, got)
    arrived = shifted(away, "xl", 1)
    (fitted,) = in_vmem(join_kernel, [((rows, cols), BF16)], own, arrived)
    other = shifted(fitted, "xl", 1)
    fitted_next = shifted(fitted, "c", 1)
    other_next = shifted(other, "c", 1)
    slots = in_vmem(
        functools.partial(density_kernel, offsets),
        [((4, rows, half), BF16)] * 4,
        fitted, fitted_next, other, other_next, *blocks,
    )
    arrived = [shifted_x(slots[s], s) for s in (2, 1, 3)]
    (xs,) = in_vmem(half_sum_kernel, [((8, rows, half), BF16)], slots[0], *arrived)
    ysum = exchange(xs, "y")
    density = jnp.sum(ysum.astype(F32), axis=0)

    got = exchange(fitted.reshape(32, 8, cols), PAIR)
    ao_count = virt_coef.shape[1]
    ao = pl.pallas_call(
        ao_kernel,
        in_specs=[VMEM] * 2,
        out_specs=VMEM,
        out_shape=jax.ShapeDtypeStruct((8, 16 * ao_count), BF16),
        compiler_params=PARAMS,
    )(got, virt_coef)
    return density, ao


def solution(mesh):
    split = Mesh(mesh.devices.reshape(2, 8, 8, 2, 2), ALL)
    return jax.shard_map(
        work,
        mesh=split,
        in_specs=(P(AUX, PAIR), P(AUX, PAIR), P()),
        out_specs=(P(AUX, PAIR), P(ALL, None)),
        check_vma=False,
    )
```

time: 170 us -> 160 us (0.941)
  blocking collectives: 39.5 us -> 0 us
  starting transfers between devices: 69.7 us -> 95.6 us
  local copies, waits for them, and re-layouts: 3.36 us -> 9.63 us
  waiting for transfers between devices: 46.7 us -> 40.9 us
    all_to_all x2 -> x0, blocking collectives: 39.5 us -> none  [exchange(): return lax.all_to_all(x, axes, split_axis=0, concat_axis=0, tiled=True)]
    all_to_all x2 -> x4, starting transfers between devices: 9.74 us -> 22.8 us  [exchange(): return lax.all_to_all(x, axes, split_axis=0, concat_axis=0, tiled=True)]
    ppermute x11 -> x14, starting transfers between devices: 48.7 us -> 61.5 us  [shifted(): return lax.ppermute(x, axis, [(i, (i + by) % n) for i in range(n)])]
    unnamed x8 -> x24, local copies, waits for them, and re-layouts: 2.19 us -> 5.82 us
    all_to_all x2 -> x4, waiting for transfers between devices: 16.7 us -> 14.2 us  [exchange(): return lax.all_to_all(x, axes, split_axis=0, concat_axis=0, tiled=True)]
    ppermute x11 -> x14, waiting for transfers between devices: 22.7 us -> 21.1 us  [shifted(): return lax.ppermute(x, axis, [(i, (i + by) % n) for i in range(n)])]
    pallas_call x5 -> x6, Pallas kernels: 6.98 us -> 7.46 us  [in_vmem(): pl.pallas_call(kernel, in_specs=[VMEM] * len(args), out_specs=[VMEM] * le...]
  transfers between devices with their start and end apart: 16 -> 21, of which waited for: 8 -> 9; matrix products, arithmetic and copies ran while one was open for 0% -> 1% of each run, Pallas kernels for 2% -> 5%
where the time goes in v3:
time: 160 us; the launch traced here: 157 us
  starting transfers between devices  95.6 us (60%)
  waiting for transfers between devices  40.9 us (26%)
  Pallas kernels  9.65 us (6%)
  local copies, waits for them, and re-layouts  9.63 us (6%)
    ppermute x14, starting transfers between devices, shifted(): return lax.ppermute(x, axis, [(i, (i + by) % n) for i in range(n)])  61.5 us
    all_to_all x4, starting transfers between devices, exchange(): return lax.all_to_all(x, axes, split_axis=0, concat_axis=0, tiled=True)  22.8 us
    ppermute x14, waiting for transfers between devices, shifted(): return lax.ppermute(x, axis, [(i, (i + by) % n) for i in range(n)])  21.1 us
    all_to_all x4, waiting for transfers between devices, exchange(): return lax.all_to_all(x, axes, split_axis=0, concat_axis=0, tiled=True)  14.2 us
    ppermute x3, starting transfers between devices, shifted_x(): lax.ppermute(x, ('xl', 'xh'), [(at(i), at((i + by) % 4)) for i in range(4)])  11.3 us
    pallas_call x6, Pallas kernels, in_vmem(): pl.pallas_call(kernel, in_specs=[VMEM] * len(args), out_specs=[VMEM] * le...  7.46 us
    unnamed x24, local copies, waits for them, and re-layouts  5.82 us
    ppermute x3, waiting for transfers between devices, shifted_x(): lax.ppermute(x, ('xl', 'xh'), [(at(i), at((i + by) % 4)) for i in range(4)])  5.67 us
  transfers between devices with their start and end apart: 21, of which 9 were waited for; matrix products, arithmetic and copies ran while one was open for 1% of the time, Pallas kernels for 5%

profile of v3, /device:TPU:1, one launch (start us, length us, event | category | flops | bytes accessed | tf_op | source)
XLA Modules:
  0.0 157.5 jit_solution(12176317054225063478)
XLA Ops:
  0.6 1.7 %broadcast_in_dim.10 = bf16[8,256,128]{2,1,0:T(8,128)(2,1)} broadcast(bf16[256,128]{1,0:T(8,128)(2,1)} %param.3), dimensions={1,2} | broadcast | bytes 589824 | tf_op jit(solution)/shard_map/broadcast_in_dim | solution.py:162
  2.3 7.6 %all-to-all-start = ((bf16[8,256,128]{2,1,0:T(8,128)(2,1)}), bf16[8,256,128]{2,1,0:T(8,128)(2,1)S(1)}, u32[]{:S(2)}, u32[]{:S(2)}) async-start(bf16[8,256,128]{2,1,0:T(8,128)(2,1)} %broadcast_in_dim.10), calls=%async_computation | async-start | bytes 1048576 | tf_op jit(solution)/shard_map/all_to_all | solution.py:42
  10.0 0.9 constant_dynamic-slice_fusion
  10.9 4.6 %collective-permute-start = (bf16[128,512]{1,0:T(8,128)(2,1)S(1)}, bf16[128,512]{1,0:T(8,128)(2,1)S(1)}, u32[]{:S(2)}, u32[]{:S(2)}) collective-permute-start(bf16[128,512]{1,0:T(8,128)(2,1)S(1)} %constant_dynamic-slice_fusion), channel_id=1, source_target_pairs={{0,1},{1,0},{2,3},{3,2},{4,5},{5,4},{6,7},{7,6},{8,9},{9,8},{10,11... | collective-permute-start | bytes 393224 | tf_op jit(solution)/shard_map/ppermute | solution.py:33
  15.5 1.0 collective-permute-done.got_ref
  16.5 0.9 copy-done.9
  17.4 8.9 %collective-permute-start.2 = (bf16[128,1024]{1,0:T(8,128)(2,1)S(1)}, bf16[128,1024]{1,0:T(8,128)(2,1)S(1)}, u32[]{:S(2)}, u32[]{:S(2)}) collective-permute-start(bf16[128,1024]{1,0:T(8,128)(2,1)S(1)} %shard_map.50.refs_0_), channel_id=1, source_target_pairs={{0,224},{32,0},{64,32},{96,64},{128,96},{160,128},{192,160},{224,1... | collective-permute-start | bytes 786440 | tf_op jit(solution)/shard_map/ppermute | solution.py:33
  26.4 1.9 %collective-permute-start.1 = (bf16[128,1024]{1,0:T(8,128)(2,1)S(1)}, bf16[128,1024]{1,0:T(8,128)(2,1)S(1)}, u32[]{:S(2)}, u32[]{:S(2)}) collective-permute-start(bf16[128,1024]{1,0:T(8,128)(2,1)S(1)} %shard_map.50.refs_0_), channel_id=1, source_target_pairs={{0,32},{32,64},{64,96},{96,128},{128,160},{160,192},{192,224},{224... | collective-permute-start | bytes 786440 | tf_op jit(solution)/shard_map/ppermute | solution.py:33
  28.3 0.0 all-to-all-done
  28.3 1.2 broadcast_in_dim.12
  29.5 4.0 %all-to-all-start.1 = ((bf16[4,4,256,128]{3,2,1,0:T(8,128)(2,1)}), bf16[4,4,256,128]{3,2,1,0:T(8,128)(2,1)S(1)}, u32[]{:S(2)}, u32[]{:S(2)}) async-start(bf16[4,4,256,128]{3,2,1,0:T(8,128)(2,1)} %bitcast.1), calls=%async_computation.1 | async-start | bytes 2097152 | tf_op jit(solution)/shard_map/all_to_all | solution.py:42
  33.5 0.0 collective-permute-done.2.refs_2_
  33.5 10.3 %collective-permute-start.4 = (bf16[128,1024]{1,0:T(8,128)(2,1)S(1)}, bf16[128,1024]{1,0:T(8,128)(2,1)S(1)}, u32[]{:S(2)}, u32[]{:S(2)}) collective-permute-start(bf16[128,1024]{1,0:T(8,128)(2,1)S(1)} %collective-permute-done.2.refs_2_), channel_id=1, source_target_pairs={{0,224},{32,0},{64,32},{96,64},{128,96},{160,128},{192,160},{224,1... | collective-permute-start | bytes 786440 | tf_op jit(solution)/shard_map/ppermute | solution.py:33
  43.8 0.0 collective-permute-done.1.refs_1_
  43.8 0.0 copy-start.3
  43.8 1.9 %collective-permute-start.3 = (bf16[128,1024]{1,0:T(8,128)(2,1)S(1)}, bf16[128,1024]{1,0:T(8,128)(2,1)S(1)}, u32[]{:S(2)}, u32[]{:S(2)}) collective-permute-start(bf16[128,1024]{1,0:T(8,128)(2,1)S(1)} %collective-permute-done.1.refs_1_), channel_id=1, source_target_pairs={{0,32},{32,64},{64,96},{96,128},{128,160},{160,192},{192,224},{224... | collective-permute-start | bytes 786440 | tf_op jit(solution)/shard_map/ppermute | solution.py:33
  45.7 2.9 %collective-permute-done.4.refs_4_ = bf16[128,1024]{1,0:T(8,128)(2,1)S(1)} collective-permute-done((bf16[128,1024]{1,0:T(8,128)(2,1)S(1)}, bf16[128,1024]{1,0:T(8,128)(2,1)S(1)}, u32[]{:S(2)}, u32[]{:S(2)}) %collective-permute-start.4) | collective-permute-done | bytes 262176 | tf_op jit(solution)/shard_map/ppermute | solution.py:33
  48.7 5.3 %collective-permute-start.6 = (bf16[128,1024]{1,0:T(8,128)(2,1)S(1)}, bf16[128,1024]{1,0:T(8,128)(2,1)S(1)}, u32[]{:S(2)}, u32[]{:S(2)}) collective-permute-start(bf16[128,1024]{1,0:T(8,128)(2,1)S(1)} %collective-permute-done.4.refs_4_), channel_id=1, source_target_pairs={{0,224},{32,0},{64,32},{96,64},{128,96},{160,128},{192,160},{224,1... | collective-permute-start | bytes 786440 | tf_op jit(solution)/shard_map/ppermute | solution.py:33
  54.0 0.0 collective-permute-done.3.refs_3_
  54.0 0.0 copy-start.7
  54.0 1.9 %collective-permute-start.5 = (bf16[128,1024]{1,0:T(8,128)(2,1)S(1)}, bf16[128,1024]{1,0:T(8,128)(2,1)S(1)}, u32[]{:S(2)}, u32[]{:S(2)}) collective-permute-start(bf16[128,1024]{1,0:T(8,128)(2,1)S(1)} %collective-permute-done.3.refs_3_), channel_id=1, source_target_pairs={{0,32},{32,64},{64,96},{96,128},{128,160},{160,192},{192,224},{224... | collective-permute-start | bytes 786440 | tf_op jit(solution)/shard_map/ppermute | solution.py:33
  55.9 2.1 %collective-permute-done.6.refs_6_ = bf16[128,1024]{1,0:T(8,128)(2,1)S(1)} collective-permute-done((bf16[128,1024]{1,0:T(8,128)(2,1)S(1)}, bf16[128,1024]{1,0:T(8,128)(2,1)S(1)}, u32[]{:S(2)}, u32[]{:S(2)}) %collective-permute-start.6) | collective-permute-done | bytes 262176 | tf_op jit(solution)/shard_map/ppermute | solution.py:33
  58.0 5.3 %collective-permute-start.8 = (bf16[128,512]{1,0:T(8,128)(2,1)S(1)}, bf16[128,512]{1,0:T(8,128)(2,1)S(1)}, u32[]{:S(2)}, u32[]{:S(2)}) collective-permute-start(bf16[128,512]{1,0:T(8,128)(2,1)S(1)} %slice.9), channel_id=1, source_target_pairs={{0,224},{32,0},{64,32},{96,64},{128,96},{160,128},{192,160},{224,1... | collective-permute-start | bytes 393224 | tf_op jit(solution)/shard_map/ppermute | solution.py:33
  63.3 0.0 collective-permute-done.5.refs_5_
  63.4 1.9 %collective-permute-start.7 = (bf16[128,512]{1,0:T(8,128)(2,1)S(1)}, bf16[128,512]{1,0:T(8,128)(2,1)S(1)}, u32[]{:S(2)}, u32[]{:S(2)}) collective-permute-start(bf16[128,512]{1,0:T(8,128)(2,1)S(1)} %slice.8), channel_id=1, source_target_pairs={{0,32},{32,64},{64,96},{96,128},{128,160},{160,192},{192,224},{224... | collective-permute-start | bytes 393224 | tf_op jit(solution)/shard_map/ppermute | solution.py:33
  65.3 0.0 collective-permute-done.8.refs_8_
  65.3 5.0 %collective-permute-done.7.refs_7_ = bf16[128,512]{1,0:T(8,128)(2,1)S(1)} collective-permute-done((bf16[128,512]{1,0:T(8,128)(2,1)S(1)}, bf16[128,512]{1,0:T(8,128)(2,1)S(1)}, u32[]{:S(2)}, u32[]{:S(2)}) %collective-permute-start.7) | collective-permute-done | bytes 131104 | tf_op jit(solution)/shard_map/ppermute | solution.py:33
  70.3 0.0 all-to-all-done.1
  70.3 1.2 shard_map.51
  71.5 0.0 copy-done.10
  71.6 5.8 %collective-permute-start.9 = (bf16[2,256,512]{2,1,0:T(8,128)(2,1)S(1)}, bf16[2,256,512]{2,1,0:T(8,128)(2,1)S(1)}, u32[]{:S(2)}, u32[]{:S(2)}) collective-permute-start(bf16[2,256,512]{2,1,0:T(8,128)(2,1)S(1)} %get-tuple-element.11), channel_id=1, source_target_pairs={{0,1},{1,0},{2,3},{3,2},{4,5},{5,4},{6,7},{7,6},{8,9},{9,8},{10,11... | collective-permute-start | bytes 1572872 | tf_op jit(solution)/shard_map/ppermute | solution.py:33
  77.4 1.5 collective-permute-done.9.got_ref
  78.9 0.1 shard_map.52
  79.0 0.0 copy-done.1
  79.0 0.0 copy-done.3
  79.0 3.1 %collective-permute-start.10 = (bf16[256,512]{1,0:T(8,128)(2,1)S(1)}, bf16[256,512]{1,0:T(8,128)(2,1)S(1)}, u32[]{:S(2)}, u32[]{:S(2)}) collective-permute-start(bf16[256,512]{1,0:T(8,128)(2,1)S(1)} %get-tuple-element.13), channel_id=1, source_target_pairs={{0,256},{256,0},{1,257},{257,1},{2,258},{258,2},{3,259},{259,3},{4... | collective-permute-start | bytes 786440 | tf_op jit(solution)/shard_map/ppermute | solution.py:33
  82.1 6.3 %collective-permute-done.10.arrived_ref = bf16[256,512]{1,0:T(8,128)(2,1)S(1)} collective-permute-done((bf16[256,512]{1,0:T(8,128)(2,1)S(1)}, bf16[256,512]{1,0:T(8,128)(2,1)S(1)}, u32[]{:S(2)}, u32[]{:S(2)}) %collective-permute-start.10) | collective-permute-done | bytes 262176 | tf_op jit(solution)/shard_map/ppermute | solution.py:33
  88.4 0.7 shard_map.53.own_ref
  89.2 3.1 %collective-permute-start.12 = (bf16[256,512]{1,0:T(8,128)(2,1)}, bf16[256,512]{1,0:T(8,128)(2,1)}, u32[]{:S(2)}, u32[]{:S(2)}) collective-permute-start(bf16[256,512]{1,0:T(8,128)(2,1)} %shard_map.53.own_ref), channel_id=1, source_target_pairs={{0,256},{256,0},{1,257},{257,1},{2,258},{258,2},{3,259},{259,3},{4... | collective-permute-start | bytes 786440 | tf_op jit(solution)/shard_map/ppermute | solution.py:33
  92.3 3.4 %collective-permute-start.11 = (bf16[256,512]{1,0:T(8,128)(2,1)}, bf16[256,512]{1,0:T(8,128)(2,1)}, u32[]{:S(2)}, u32[]{:S(2)}) collective-permute-start(bf16[256,512]{1,0:T(8,128)(2,1)} %shard_map.53.own_ref), channel_id=1, source_target_pairs={{0,1},{1,0},{2,3},{3,2},{4,5},{5,4},{6,7},{7,6},{8,9},{9,8},{10,11... | collective-permute-start | bytes 786440 | tf_op jit(solution)/shard_map/ppermute | solution.py:33
  95.7 2.3 %collective-permute-done.12.other_ref = bf16[256,512]{1,0:T(8,128)(2,1)} collective-permute-done((bf16[256,512]{1,0:T(8,128)(2,1)}, bf16[256,512]{1,0:T(8,128)(2,1)}, u32[]{:S(2)}, u32[]{:S(2)}) %collective-permute-start.12) | collective-permute-done | bytes 262176 | tf_op jit(solution)/shard_map/ppermute | solution.py:33
  98.0 4.0 %collective-permute-start.13 = (bf16[256,512]{1,0:T(8,128)(2,1)}, bf16[256,512]{1,0:T(8,128)(2,1)}, u32[]{:S(2)}, u32[]{:S(2)}) collective-permute-start(bf16[256,512]{1,0:T(8,128)(2,1)} %collective-permute-done.12.other_ref), channel_id=1, source_target_pairs={{0,1},{1,0},{2,3},{3,2},{4,5},{5,4},{6,7},{7,6},{8,9},{9,8},{10,11... | collective-permute-start | bytes 786440 | tf_op jit(solution)/shard_map/ppermute | solution.py:33
  102.0 4.6 %all-to-all-start.3 = ((bf16[32,8,512]{2,1,0:T(8,128)(2,1)}), bf16[32,8,512]{2,1,0:T(8,128)(2,1)}, u32[]{:S(2)}, u32[]{:S(2)}) async-start(bf16[32,8,512]{2,1,0:T(8,128)(2,1)} %bitcast.3), calls=%async_computation.3 | async-start | bytes 524288 | tf_op jit(solution)/shard_map/all_to_all | solution.py:42
  106.6 0.0 copy-start
  106.6 0.0 collective-permute-done.11.own_next_ref
  106.6 0.0 collective-permute-done.13.other_next_ref
  106.6 1.1 copy-done.2
  107.7 0.9 copy-done.4
  108.7 0.9 copy-done.6
  109.6 0.9 copy-done.8
  110.6 0.9 copy-done.11
  111.5 4.4 %shard_map.54 = (bf16[4,256,128]{2,1,0:T(8,128)(2,1)S(1)}, bf16[4,256,128]{2,1,0:T(8,128)(2,1)S(1)}, bf16[4,256,128]{2,1,0:T(8,128)(2,1)S(1)}, bf16[4,256,128]{2,1,0:T(8,128)(2,1)S(1)}) custom-call(bf16[256,512]{1,0:T(8,128)(2,1)} %shard_map.53.own_ref, bf16[256,512]{1,0:T(8,128)(2,1)} %collective-permute-done.11.own_next_ref, ...), custom_call_target="tpu_custom_call" | custom-call | tf_op jit(solution)/shard_map/pallas_call | solution.py:22
  115.9 4.8 %collective-permute-start.14 = (bf16[4,256,128]{2,1,0:T(8,128)(2,1)S(1)}, bf16[4,256,128]{2,1,0:T(8,128)(2,1)S(1)}, u32[]{:S(2)}, u32[]{:S(2)}) collective-permute-start(bf16[4,256,128]{2,1,0:T(8,128)(2,1)S(1)} %get-tuple-element.15), channel_id=1, source_target_pairs={{0,2},{256,258},{2,0},{258,256},{1,3},{257,259},{3,1},{259,257},{4... | collective-permute-start | bytes 786440 | tf_op jit(solution)/shard_map/ppermute | solution.py:38
  120.7 2.7 %collective-permute-start.15 = (bf16[4,256,128]{2,1,0:T(8,128)(2,1)S(1)}, bf16[4,256,128]{2,1,0:T(8,128)(2,1)S(1)}, u32[]{:S(2)}, u32[]{:S(2)}) collective-permute-start(bf16[4,256,128]{2,1,0:T(8,128)(2,1)S(1)} %get-tuple-element.16), channel_id=1, source_target_pairs={{0,256},{256,2},{2,258},{258,0},{1,257},{257,3},{3,259},{259,1},{4... | collective-permute-start | bytes 786440 | tf_op jit(solution)/shard_map/ppermute | solution.py:38
  123.4 3.8 %collective-permute-start.16 = (bf16[4,256,128]{2,1,0:T(8,128)(2,1)S(1)}, bf16[4,256,128]{2,1,0:T(8,128)(2,1)S(1)}, u32[]{:S(2)}, u32[]{:S(2)}) collective-permute-start(bf16[4,256,128]{2,1,0:T(8,128)(2,1)S(1)} %get-tuple-element.17), channel_id=1, source_target_pairs={{0,258},{256,0},{2,256},{258,2},{1,259},{257,1},{3,257},{259,3},{4... | collective-permute-start | bytes 786440 | tf_op jit(solution)/shard_map/ppermute | solution.py:38
  127.2 0.0 collective-permute-done.14.far_ref
  127.2 5.7 %collective-permute-done.15.left_ref = bf16[4,256,128]{2,1,0:T(8,128)(2,1)S(1)} collective-permute-done((bf16[4,256,128]{2,1,0:T(8,128)(2,1)S(1)}, bf16[4,256,128]{2,1,0:T(8,128)(2,1)S(1)}, u32[]{:S(2)}, u32[]{:S(2)}) %collective-permute-start.15) | collective-permute-done | bytes 262176 | tf_op jit(solution)/shard_map/ppermute | solution.py:38
  132.9 0.0 collective-permute-done.16.right_ref
  132.9 0.9 shard_map.55
  133.8 0.0 all-to-all-done.3.got_ref
  133.8 6.6 %all-to-all-start.2 = ((bf16[8,256,128]{2,1,0:T(8,128)(2,1)}), bf16[8,256,128]{2,1,0:T(8,128)(2,1)S(1)}, u32[]{:S(2)}, u32[]{:S(2)}) async-start(bf16[8,256,128]{2,1,0:T(8,128)(2,1)} %shard_map.55), calls=%async_computation.2 | async-start | bytes 1048576 | tf_op jit(solution)/shard_map/all_to_all | solution.py:42
  140.4 2.2 %shard_map.56 = bf16[8,20480]{1,0:T(8,128)(2,1)} custom-call(bf16[32,8,512]{2,1,0:T(8,128)(2,1)} %all-to-all-done.3.got_ref, bf16[1024,1280]{1,0:T(8,128)(2,1)S(1)} %copy-done), custom_call_target="tpu_custom_call" | custom-call | tf_op jit(solution)/shard_map/pallas_call | solution.py:198
  142.6 14.2 %all-to-all-done.2 = bf16[8,256,128]{2,1,0:T(8,128)(2,1)S(1)} async-done(((bf16[8,256,128]{2,1,0:T(8,128)(2,1)}), bf16[8,256,128]{2,1,0:T(8,128)(2,1)S(1)}, u32[]{:S(2)}, u32[]{:S(2)}) %all-to-all-start.2) | async-done | bytes 524320 | tf_op jit(solution)/shard_map/all_to_all | solution.py:42
  156.7 0.7 convert_reduce_fusion
  (15 shorter events, 0.1 us)
Async XLA Ops:
  2.3 26.0 %all-to-all-start = ((bf16[8,256,128]{2,1,0:T(8,128)(2,1)}), bf16[8,256,128]{2,1,0:T(8,128)(2,1)S(1)}, u32[]{:S(2)}, u32[]{:S(2)}) async-start(bf16[8,256,128]{2,1,0:T(8,128)(2,1)} %broadcast_in_dim.10), calls=%async_computation | async-start | bytes 1048576 | tf_op jit(solution)/shard_map/all_to_all | solution.py:42
  10.9 5.6 %collective-permute-start = (bf16[128,512]{1,0:T(8,128)(2,1)S(1)}, bf16[128,512]{1,0:T(8,128)(2,1)S(1)}, u32[]{:S(2)}, u32[]{:S(2)}) collective-permute-start(bf16[128,512]{1,0:T(8,128)(2,1)S(1)} %constant_dynamic-slice_fusion), channel_id=1, source_target_pairs={{0,1},{1,0},{2,3},{3,2},{4,5},{5,4},{6,7},{7,6},{8,9},{9,8},{10,11... | collective-permute-start | bytes 393224 | tf_op jit(solution)/shard_map/ppermute | solution.py:33
  16.5 0.9 copy-start.9
  17.4 16.1 %collective-permute-start.2 = (bf16[128,1024]{1,0:T(8,128)(2,1)S(1)}, bf16[128,1024]{1,0:T(8,128)(2,1)S(1)}, u32[]{:S(2)}, u32[]{:S(2)}) collective-permute-start(bf16[128,1024]{1,0:T(8,128)(2,1)S(1)} %shard_map.50.refs_0_), channel_id=1, source_target_pairs={{0,224},{32,0},{64,32},{96,64},{128,96},{160,128},{192,160},{224,1... | collective-permute-start | bytes 786440 | tf_op jit(solution)/shard_map/ppermute | solution.py:33
  26.4 17.4 %collective-permute-start.1 = (bf16[128,1024]{1,0:T(8,128)(2,1)S(1)}, bf16[128,1024]{1,0:T(8,128)(2,1)S(1)}, u32[]{:S(2)}, u32[]{:S(2)}) collective-permute-start(bf16[128,1024]{1,0:T(8,128)(2,1)S(1)} %shard_map.50.refs_0_), channel_id=1, source_target_pairs={{0,32},{32,64},{64,96},{96,128},{128,160},{160,192},{192,224},{224... | collective-permute-start | bytes 786440 | tf_op jit(solution)/shard_map/ppermute | solution.py:33
  29.5 40.8 %all-to-all-start.1 = ((bf16[4,4,256,128]{3,2,1,0:T(8,128)(2,1)}), bf16[4,4,256,128]{3,2,1,0:T(8,128)(2,1)S(1)}, u32[]{:S(2)}, u32[]{:S(2)}) async-start(bf16[4,4,256,128]{3,2,1,0:T(8,128)(2,1)} %bitcast.1), calls=%async_computation.1 | async-start | bytes 2097152 | tf_op jit(solution)/shard_map/all_to_all | solution.py:42
  33.5 45.5 %copy-start.1 = (bf16[128,1024]{1,0:T(8,128)(2,1)}, bf16[128,1024]{1,0:T(8,128)(2,1)S(1)}, u32[]{:S(2)}) copy-start(bf16[128,1024]{1,0:T(8,128)(2,1)S(1)} %collective-permute-done.2.refs_2_) | copy-start | bytes 786436
  33.5 15.2 %collective-permute-start.4 = (bf16[128,1024]{1,0:T(8,128)(2,1)S(1)}, bf16[128,1024]{1,0:T(8,128)(2,1)S(1)}, u32[]{:S(2)}, u32[]{:S(2)}) collective-permute-start(bf16[128,1024]{1,0:T(8,128)(2,1)S(1)} %collective-permute-done.2.refs_2_), channel_id=1, source_target_pairs={{0,224},{32,0},{64,32},{96,64},{128,96},{160,128},{192,160},{224,1... | collective-permute-start | bytes 786440 | tf_op jit(solution)/shard_map/ppermute | solution.py:33
  43.8 35.2 %copy-start.3 = (bf16[128,1024]{1,0:T(8,128)(2,1)}, bf16[128,1024]{1,0:T(8,128)(2,1)S(1)}, u32[]{:S(2)}) copy-start(bf16[128,1024]{1,0:T(8,128)(2,1)S(1)} %collective-permute-done.1.refs_1_) | copy-start | bytes 786436
  43.8 10.2 %collective-permute-start.3 = (bf16[128,1024]{1,0:T(8,128)(2,1)S(1)}, bf16[128,1024]{1,0:T(8,128)(2,1)S(1)}, u32[]{:S(2)}, u32[]{:S(2)}) collective-permute-start(bf16[128,1024]{1,0:T(8,128)(2,1)S(1)} %collective-permute-done.1.refs_1_), channel_id=1, source_target_pairs={{0,32},{32,64},{64,96},{96,128},{128,160},{160,192},{192,224},{224... | collective-permute-start | bytes 786440 | tf_op jit(solution)/shard_map/ppermute | solution.py:33
  48.7 30.4 %copy-start.5 = (bf16[128,1024]{1,0:T(8,128)(2,1)}, bf16[128,1024]{1,0:T(8,128)(2,1)S(1)}, u32[]{:S(2)}) copy-start(bf16[128,1024]{1,0:T(8,128)(2,1)S(1)} %collective-permute-done.4.refs_4_) | copy-start | bytes 786436
  48.7 9.3 %collective-permute-start.6 = (bf16[128,1024]{1,0:T(8,128)(2,1)S(1)}, bf16[128,1024]{1,0:T(8,128)(2,1)S(1)}, u32[]{:S(2)}, u32[]{:S(2)}) collective-permute-start(bf16[128,1024]{1,0:T(8,128)(2,1)S(1)} %collective-permute-done.4.refs_4_), channel_id=1, source_target_pairs={{0,224},{32,0},{64,32},{96,64},{128,96},{160,128},{192,160},{224,1... | collective-permute-start | bytes 786440 | tf_op jit(solution)/shard_map/ppermute | solution.py:33
  54.0 25.0 %copy-start.7 = (bf16[128,1024]{1,0:T(8,128)(2,1)}, bf16[128,1024]{1,0:T(8,128)(2,1)S(1)}, u32[]{:S(2)}) copy-start(bf16[128,1024]{1,0:T(8,128)(2,1)S(1)} %collective-permute-done.3.refs_3_) | copy-start | bytes 786436
  54.0 9.3 %collective-permute-start.5 = (bf16[128,1024]{1,0:T(8,128)(2,1)S(1)}, bf16[128,1024]{1,0:T(8,128)(2,1)S(1)}, u32[]{:S(2)}, u32[]{:S(2)}) collective-permute-start(bf16[128,1024]{1,0:T(8,128)(2,1)S(1)} %collective-permute-done.3.refs_3_), channel_id=1, source_target_pairs={{0,32},{32,64},{64,96},{96,128},{128,160},{160,192},{192,224},{224... | collective-permute-start | bytes 786440 | tf_op jit(solution)/shard_map/ppermute | solution.py:33
  58.0 7.3 %collective-permute-start.8 = (bf16[128,512]{1,0:T(8,128)(2,1)S(1)}, bf16[128,512]{1,0:T(8,128)(2,1)S(1)}, u32[]{:S(2)}, u32[]{:S(2)}) collective-permute-start(bf16[128,512]{1,0:T(8,128)(2,1)S(1)} %slice.9), channel_id=1, source_target_pairs={{0,224},{32,0},{64,32},{96,64},{128,96},{160,128},{192,160},{224,1... | collective-permute-start | bytes 393224 | tf_op jit(solution)/shard_map/ppermute | solution.py:33
  63.4 6.9 %collective-permute-start.7 = (bf16[128,512]{1,0:T(8,128)(2,1)S(1)}, bf16[128,512]{1,0:T(8,128)(2,1)S(1)}, u32[]{:S(2)}, u32[]{:S(2)}) collective-permute-start(bf16[128,512]{1,0:T(8,128)(2,1)S(1)} %slice.8), channel_id=1, source_target_pairs={{0,32},{32,64},{64,96},{96,128},{128,160},{160,192},{192,224},{224... | collective-permute-start | bytes 393224 | tf_op jit(solution)/shard_map/ppermute | solution.py:33
  70.3 1.3 copy-start.10
  71.6 7.3 %collective-permute-start.9 = (bf16[2,256,512]{2,1,0:T(8,128)(2,1)S(1)}, bf16[2,256,512]{2,1,0:T(8,128)(2,1)S(1)}, u32[]{:S(2)}, u32[]{:S(2)}) collective-permute-start(bf16[2,256,512]{2,1,0:T(8,128)(2,1)S(1)} %get-tuple-element.11), channel_id=1, source_target_pairs={{0,1},{1,0},{2,3},{3,2},{4,5},{5,4},{6,7},{7,6},{8,9},{9,8},{10,11... | collective-permute-start | bytes 1572872 | tf_op jit(solution)/shard_map/ppermute | solution.py:33
  79.0 9.4 %collective-permute-start.10 = (bf16[256,512]{1,0:T(8,128)(2,1)S(1)}, bf16[256,512]{1,0:T(8,128)(2,1)S(1)}, u32[]{:S(2)}, u32[]{:S(2)}) collective-permute-start(bf16[256,512]{1,0:T(8,128)(2,1)S(1)} %get-tuple-element.13), channel_id=1, source_target_pairs={{0,256},{256,0},{1,257},{257,1},{2,258},{258,2},{3,259},{259,3},{4... | collective-permute-start | bytes 786440 | tf_op jit(solution)/shard_map/ppermute | solution.py:33
  89.2 8.8 %collective-permute-start.12 = (bf16[256,512]{1,0:T(8,128)(2,1)}, bf16[256,512]{1,0:T(8,128)(2,1)}, u32[]{:S(2)}, u32[]{:S(2)}) collective-permute-start(bf16[256,512]{1,0:T(8,128)(2,1)} %shard_map.53.own_ref), channel_id=1, source_target_pairs={{0,256},{256,0},{1,257},{257,1},{2,258},{258,2},{3,259},{259,3},{4... | collective-permute-start | bytes 786440 | tf_op jit(solution)/shard_map/ppermute | solution.py:33
  92.3 14.3 %collective-permute-start.11 = (bf16[256,512]{1,0:T(8,128)(2,1)}, bf16[256,512]{1,0:T(8,128)(2,1)}, u32[]{:S(2)}, u32[]{:S(2)}) collective-permute-start(bf16[256,512]{1,0:T(8,128)(2,1)} %shard_map.53.own_ref), channel_id=1, source_target_pairs={{0,1},{1,0},{2,3},{3,2},{4,5},{5,4},{6,7},{7,6},{8,9},{9,8},{10,11... | collective-permute-start | bytes 786440 | tf_op jit(solution)/shard_map/ppermute | solution.py:33
  98.0 8.6 %collective-permute-start.13 = (bf16[256,512]{1,0:T(8,128)(2,1)}, bf16[256,512]{1,0:T(8,128)(2,1)}, u32[]{:S(2)}, u32[]{:S(2)}) collective-permute-start(bf16[256,512]{1,0:T(8,128)(2,1)} %collective-permute-done.12.other_ref), channel_id=1, source_target_pairs={{0,1},{1,0},{2,3},{3,2},{4,5},{5,4},{6,7},{7,6},{8,9},{9,8},{10,11... | collective-permute-start | bytes 786440 | tf_op jit(solution)/shard_map/ppermute | solution.py:33
  102.0 31.8 %all-to-all-start.3 = ((bf16[32,8,512]{2,1,0:T(8,128)(2,1)}), bf16[32,8,512]{2,1,0:T(8,128)(2,1)}, u32[]{:S(2)}, u32[]{:S(2)}) async-start(bf16[32,8,512]{2,1,0:T(8,128)(2,1)} %bitcast.3), calls=%async_computation.3 | async-start | bytes 524288 | tf_op jit(solution)/shard_map/all_to_all | solution.py:42
  106.6 33.8 %copy-start = (bf16[1024,1280]{1,0:T(8,128)(2,1)S(1)}, bf16[1024,1280]{1,0:T(8,128)(2,1)}, u32[]{:S(2)}) copy-start(bf16[1024,1280]{1,0:T(8,128)(2,1)} %coef_ref.1) | copy-start | bytes 7864324
  106.6 1.1 copy-start.2
  107.7 0.9 copy-start.4
  108.7 0.9 copy-start.6
  109.6 0.9 copy-start.8
  110.6 0.9 copy-start.11
  115.9 11.3 %collective-permute-start.14 = (bf16[4,256,128]{2,1,0:T(8,128)(2,1)S(1)}, bf16[4,256,128]{2,1,0:T(8,128)(2,1)S(1)}, u32[]{:S(2)}, u32[]{:S(2)}) collective-permute-start(bf16[4,256,128]{2,1,0:T(8,128)(2,1)S(1)} %get-tuple-element.15), channel_id=1, source_target_pairs={{0,2},{256,258},{2,0},{258,256},{1,3},{257,259},{3,1},{259,257},{4... | collective-permute-start | bytes 786440 | tf_op jit(solution)/shard_map/ppermute | solution.py:38
  120.7 12.2 %collective-permute-start.15 = (bf16[4,256,128]{2,1,0:T(8,128)(2,1)S(1)}, bf16[4,256,128]{2,1,0:T(8,128)(2,1)S(1)}, u32[]{:S(2)}, u32[]{:S(2)}) collective-permute-start(bf16[4,256,128]{2,1,0:T(8,128)(2,1)S(1)} %get-tuple-element.16), channel_id=1, source_target_pairs={{0,256},{256,2},{2,258},{258,0},{1,257},{257,3},{3,259},{259,1},{4... | collective-permute-start | bytes 786440 | tf_op jit(solution)/shard_map/ppermute | solution.py:38
  123.4 9.5 %collective-permute-start.16 = (bf16[4,256,128]{2,1,0:T(8,128)(2,1)S(1)}, bf16[4,256,128]{2,1,0:T(8,128)(2,1)S(1)}, u32[]{:S(2)}, u32[]{:S(2)}) collective-permute-start(bf16[4,256,128]{2,1,0:T(8,128)(2,1)S(1)} %get-tuple-element.17), channel_id=1, source_target_pairs={{0,258},{256,0},{2,256},{258,2},{1,259},{257,1},{3,257},{259,3},{4... | collective-permute-start | bytes 786440 | tf_op jit(solution)/shard_map/ppermute | solution.py:38
  133.8 22.9 %all-to-all-start.2 = ((bf16[8,256,128]{2,1,0:T(8,128)(2,1)}), bf16[8,256,128]{2,1,0:T(8,128)(2,1)S(1)}, u32[]{:S(2)}, u32[]{:S(2)}) async-start(bf16[8,256,128]{2,1,0:T(8,128)(2,1)} %shard_map.55), calls=%async_computation.2 | async-start | bytes 1048576 | tf_op jit(solution)/shard_map/all_to_all | solution.py:42

commit v4 on v3

--- a/solution.py
+++ b/solution.py
@@ -31,11 +31,6 @@
 def shifted(x, axis, by):
     n = lax.axis_size(axis)
     return lax.ppermute(x, axis, [(i, (i + by) % n) for i in range(n)])
-
-
-def shifted_x(x, by):
-    at = lambda i: (i % 2) * 2 + i // 2
-    return lax.ppermute(x, ("xl", "xh"), [(at(i), at((i + by) % 4)) for i in range(4)])
 
 
 def exchange(x, axes):
@@ -95,10 +90,9 @@
 
 
 def density_kernel(offsets, own_ref, own_next_ref, other_ref, other_next_ref, *refs):
-    blocks = values_of(refs[:-4])
-    slots = refs[-4:]
+    blocks = values_of(refs[:-1])
+    out_ref = refs[-1]
     xl = lax.axis_index("xl")
-    x = 2 * lax.axis_index("xh") + xl
     own = jnp.concatenate([own_ref[...], own_next_ref[...]], axis=1)
     other = jnp.concatenate([other_ref[...], other_next_ref[...]], axis=1)
     lhs = jnp.concatenate([own, other], axis=0)
@@ -111,35 +105,15 @@
         for j in range(2):
             far, near = place(offsets[i + j])
             cols = slice(j * width, (j + 1) * width)
-            same = far == lax.axis_index("xh")
-            mine, theirs = out[:rows, cols], out[rows:, cols]
-
-            @pl.when(same)
-            def _():
-                slots[0][near] = mine
-
-            @pl.when(jnp.logical_not(same))
-            def _():
-                slots[2][near] = mine
-
-            next_one = lax.rem(2 * far + (1 - xl) + 4 - x, 4) == 1
-
-            @pl.when(next_one)
-            def _():
-                slots[1][near] = theirs
-
-            @pl.when(jnp.logical_not(next_one))
-            def _():
-                slots[3][near] = theirs
+            out_ref[2 * xl + far, near] = out[:rows, cols]
+            out_ref[2 * (1 - xl) + far, near] = out[rows:, cols]
 
 
-def half_sum_kernel(here_ref, far_ref, left_ref, right_ref, out_ref):
-    xl = lax.axis_index("xl")
-    n = here_ref.shape[0]
-    ours = here_ref[...].astype(F32) + far_ref[...].astype(F32)
-    theirs = left_ref[...].astype(F32) + right_ref[...].astype(F32)
-    out_ref[pl.ds(xl * n, n)] = ours.astype(BF16)
-    out_ref[pl.ds((1 - xl) * n, n)] = theirs.astype(BF16)
+def half_sum_kernel(in_ref, out_ref):
+    n = in_ref.shape[1]
+    for h in range(2):
+        both = in_ref[2 * h].astype(F32) + in_ref[2 * h + 1].astype(F32)
+        out_ref[h * n : (h + 1) * n] = both.astype(BF16)
 
 
 def ao_kernel(got_ref, coef_ref, out_ref):
@@ -183,13 +157,13 @@
     other = shifted(fitted, "xl", 1)
     fitted_next = shifted(fitted, "c", 1)
     other_next = shifted(other, "c", 1)
-    slots = in_vmem(
+    (parts,) = in_vmem(
         functools.partial(density_kernel, offsets),
-        [((4, rows, half), BF16)] * 4,
+        [((4, 4, rows, half), BF16)],
         fitted, fitted_next, other, other_next, *blocks,
     )
-    arrived = [shifted_x(slots[s], s) for s in (2, 1, 3)]
-    (xs,) = in_vmem(half_sum_kernel, [((8, rows, half), BF16)], slots[0], *arrived)
+    parts = exchange(parts, ("xl", "xh"))
+    (xs,) = in_vmem(half_sum_kernel, [((8, rows, half), BF16)], parts)
     ysum = exchange(xs, "y")
     density = jnp.sum(ysum.astype(F32), axis=0)
 

time: 160 us -> 164 us (1.025); the launches traced: 157 us -> 163 us
  blocking collectives: 0 us -> 17.8 us
  starting transfers between devices: 95.6 us -> 81.9 us
  waiting for transfers between devices: 40.9 us -> 49.1 us
  local copies, waits for them, and re-layouts: 9.63 us -> 6.53 us
  Pallas kernels: 9.65 us -> 6.56 us
    all_to_all x0 -> x1, blocking collectives: none -> 17.8 us  [exchange(): return lax.all_to_all(x, axes, split_axis=0, concat_axis=0, tiled=True)]
    all_to_all x4, waiting for transfers between devices: 14.2 us -> 27 us  [exchange(): return lax.all_to_all(x, axes, split_axis=0, concat_axis=0, tiled=True)]
    ppermute x3 -> x0, starting transfers between devices: 11.3 us -> none  [shifted_x(): lax.ppermute(x, ('xl', 'xh'), [(at(i), at((i + by) % 4)) for i in range(4)])]
    ppermute x3 -> x0, waiting for transfers between devices: 5.67 us -> none  [shifted_x(): lax.ppermute(x, ('xl', 'xh'), [(at(i), at((i + by) % 4)) for i in range(4)])]
    unnamed x24 -> x4, local copies, waits for them, and re-layouts: 5.82 us -> 2.68 us
    all_to_all x4, starting transfers between devices: 22.8 us -> 20.4 us  [exchange(): return lax.all_to_all(x, axes, split_axis=0, concat_axis=0, tiled=True)]
    pallas_call x6, Pallas kernels: 7.46 us -> 5.33 us  [in_vmem(): pl.pallas_call(kernel, in_specs=[VMEM] * len(args), out_specs=[VMEM] * le...]
  transfers between devices with their start and end apart: 21 -> 18, of which waited for: 9 -> 10; matrix products, arithmetic and copies ran while one was open for 1% -> 1% of each run, Pallas kernels for 5% -> 1%
where the time goes in v4:
time: 164 us; the launch traced here: 163 us
  starting transfers between devices  81.9 us (50%)
  waiting for transfers between devices  49.1 us (30%)
  blocking collectives  17.8 us (11%)
  Pallas kernels  6.56 us (4%)
  local copies, waits for them, and re-layouts  6.53 us (4%)
    ppermute x14, starting transfers between devices, shifted(): return lax.ppermute(x, axis, [(i, (i + by) % n) for i in range(n)])  61.5 us
    all_to_all x4, waiting for transfers between devices, exchange(): return lax.all_to_all(x, axes, split_axis=0, concat_axis=0, tiled=True)  27 us
    ppermute x14, waiting for transfers between devices, shifted(): return lax.ppermute(x, axis, [(i, (i + by) % n) for i in range(n)])  22.1 us
    all_to_all x4, starting transfers between devices, exchange(): return lax.all_to_all(x, axes, split_axis=0, concat_axis=0, tiled=True)  20.4 us
    all_to_all x1, blocking collectives, exchange(): return lax.all_to_all(x, axes, split_axis=0, concat_axis=0, tiled=True)  17.8 us
    pallas_call x6, Pallas kernels, in_vmem(): pl.pallas_call(kernel, in_specs=[VMEM] * len(args), out_specs=[VMEM] * le...  5.33 us
  transfers between devices with their start and end apart: 18, of which 10 were waited for; matrix products, arithmetic and copies ran while one was open for 1% of the time, Pallas kernels for 1%

profile of v4, /device:TPU:1, one launch (start us, length us, event | category | flops | bytes accessed | tf_op | source)
XLA Modules:
  0.0 163.4 jit_solution(12561475916409401638)
XLA Ops:
  0.6 1.7 %broadcast_in_dim.10 = bf16[8,256,128]{2,1,0:T(8,128)(2,1)} broadcast(bf16[256,128]{1,0:T(8,128)(2,1)} %param.3), dimensions={1,2} | broadcast | bytes 589824 | tf_op jit(solution)/shard_map/broadcast_in_dim | solution.py:136
  2.3 7.6 %all-to-all-start = ((bf16[8,256,128]{2,1,0:T(8,128)(2,1)}), bf16[8,256,128]{2,1,0:T(8,128)(2,1)S(1)}, u32[]{:S(2)}, u32[]{:S(2)}) async-start(bf16[8,256,128]{2,1,0:T(8,128)(2,1)} %broadcast_in_dim.10), calls=%async_computation | async-start | bytes 1048576 | tf_op jit(solution)/shard_map/all_to_all | solution.py:37
  10.0 0.9 constant_dynamic-slice_fusion
  10.9 4.6 %collective-permute-start = (bf16[128,512]{1,0:T(8,128)(2,1)S(1)}, bf16[128,512]{1,0:T(8,128)(2,1)S(1)}, u32[]{:S(2)}, u32[]{:S(2)}) collective-permute-start(bf16[128,512]{1,0:T(8,128)(2,1)S(1)} %constant_dynamic-slice_fusion), channel_id=1, source_target_pairs={{0,1},{1,0},{2,3},{3,2},{4,5},{5,4},{6,7},{7,6},{8,9},{9,8},{10,11... | collective-permute-start | bytes 393224 | tf_op jit(solution)/shard_map/ppermute | solution.py:33
  15.5 1.0 collective-permute-done.got_ref
  16.5 0.0 copy-start.1
  16.5 0.9 copy-done.1
  17.5 8.9 %collective-permute-start.2 = (bf16[128,1024]{1,0:T(8,128)(2,1)S(1)}, bf16[128,1024]{1,0:T(8,128)(2,1)S(1)}, u32[]{:S(2)}, u32[]{:S(2)}) collective-permute-start(bf16[128,1024]{1,0:T(8,128)(2,1)S(1)} %shard_map.50.refs_0_), channel_id=1, source_target_pairs={{0,224},{32,0},{64,32},{96,64},{128,96},{160,128},{192,160},{224,1... | collective-permute-start | bytes 786440 | tf_op jit(solution)/shard_map/ppermute | solution.py:33
  26.4 1.9 %collective-permute-start.1 = (bf16[128,1024]{1,0:T(8,128)(2,1)S(1)}, bf16[128,1024]{1,0:T(8,128)(2,1)S(1)}, u32[]{:S(2)}, u32[]{:S(2)}) collective-permute-start(bf16[128,1024]{1,0:T(8,128)(2,1)S(1)} %shard_map.50.refs_0_), channel_id=1, source_target_pairs={{0,32},{32,64},{64,96},{96,128},{128,160},{160,192},{192,224},{224... | collective-permute-start | bytes 786440 | tf_op jit(solution)/shard_map/ppermute | solution.py:33
  28.3 0.0 all-to-all-done
  28.3 1.2 broadcast_in_dim.12
  29.5 4.0 %all-to-all-start.1 = ((bf16[4,4,256,128]{3,2,1,0:T(8,128)(2,1)}), bf16[4,4,256,128]{3,2,1,0:T(8,128)(2,1)S(1)}, u32[]{:S(2)}, u32[]{:S(2)}) async-start(bf16[4,4,256,128]{3,2,1,0:T(8,128)(2,1)} %bitcast.1), calls=%async_computation.1 | async-start | bytes 2097152 | tf_op jit(solution)/shard_map/all_to_all | solution.py:37
  33.5 0.0 collective-permute-done.2.refs_2_
  33.5 10.3 %collective-permute-start.4 = (bf16[128,1024]{1,0:T(8,128)(2,1)S(1)}, bf16[128,1024]{1,0:T(8,128)(2,1)S(1)}, u32[]{:S(2)}, u32[]{:S(2)}) collective-permute-start(bf16[128,1024]{1,0:T(8,128)(2,1)S(1)} %collective-permute-done.2.refs_2_), channel_id=1, source_target_pairs={{0,224},{32,0},{64,32},{96,64},{128,96},{160,128},{192,160},{224,1... | collective-permute-start | bytes 786440 | tf_op jit(solution)/shard_map/ppermute | solution.py:33
  43.8 0.0 collective-permute-done.1.refs_1_
  43.8 1.9 %collective-permute-start.3 = (bf16[128,1024]{1,0:T(8,128)(2,1)S(1)}, bf16[128,1024]{1,0:T(8,128)(2,1)S(1)}, u32[]{:S(2)}, u32[]{:S(2)}) collective-permute-start(bf16[128,1024]{1,0:T(8,128)(2,1)S(1)} %collective-permute-done.1.refs_1_), channel_id=1, source_target_pairs={{0,32},{32,64},{64,96},{96,128},{128,160},{160,192},{192,224},{224... | collective-permute-start | bytes 786440 | tf_op jit(solution)/shard_map/ppermute | solution.py:33
  45.8 2.9 %collective-permute-done.4.refs_4_ = bf16[128,1024]{1,0:T(8,128)(2,1)S(1)} collective-permute-done((bf16[128,1024]{1,0:T(8,128)(2,1)S(1)}, bf16[128,1024]{1,0:T(8,128)(2,1)S(1)}, u32[]{:S(2)}, u32[]{:S(2)}) %collective-permute-start.4) | collective-permute-done | bytes 262176 | tf_op jit(solution)/shard_map/ppermute | solution.py:33
  48.7 5.3 %collective-permute-start.6 = (bf16[128,1024]{1,0:T(8,128)(2,1)S(1)}, bf16[128,1024]{1,0:T(8,128)(2,1)S(1)}, u32[]{:S(2)}, u32[]{:S(2)}) collective-permute-start(bf16[128,1024]{1,0:T(8,128)(2,1)S(1)} %collective-permute-done.4.refs_4_), channel_id=1, source_target_pairs={{0,224},{32,0},{64,32},{96,64},{128,96},{160,128},{192,160},{224,1... | collective-permute-start | bytes 786440 | tf_op jit(solution)/shard_map/ppermute | solution.py:33
  54.0 0.0 collective-permute-done.3.refs_3_
  54.0 1.9 %collective-permute-start.5 = (bf16[128,1024]{1,0:T(8,128)(2,1)S(1)}, bf16[128,1024]{1,0:T(8,128)(2,1)S(1)}, u32[]{:S(2)}, u32[]{:S(2)}) collective-permute-start(bf16[128,1024]{1,0:T(8,128)(2,1)S(1)} %collective-permute-done.3.refs_3_), channel_id=1, source_target_pairs={{0,32},{32,64},{64,96},{96,128},{128,160},{160,192},{192,224},{224... | collective-permute-start | bytes 786440 | tf_op jit(solution)/shard_map/ppermute | solution.py:33
  55.9 2.1 %collective-permute-done.6.refs_6_ = bf16[128,1024]{1,0:T(8,128)(2,1)S(1)} collective-permute-done((bf16[128,1024]{1,0:T(8,128)(2,1)S(1)}, bf16[128,1024]{1,0:T(8,128)(2,1)S(1)}, u32[]{:S(2)}, u32[]{:S(2)}) %collective-permute-start.6) | collective-permute-done | bytes 262176 | tf_op jit(solution)/shard_map/ppermute | solution.py:33
  58.0 5.3 %collective-permute-start.8 = (bf16[128,512]{1,0:T(8,128)(2,1)S(1)}, bf16[128,512]{1,0:T(8,128)(2,1)S(1)}, u32[]{:S(2)}, u32[]{:S(2)}) collective-permute-start(bf16[128,512]{1,0:T(8,128)(2,1)S(1)} %slice.9), channel_id=1, source_target_pairs={{0,224},{32,0},{64,32},{96,64},{128,96},{160,128},{192,160},{224,1... | collective-permute-start | bytes 393224 | tf_op jit(solution)/shard_map/ppermute | solution.py:33
  63.4 0.0 collective-permute-done.5.refs_5_
  63.4 1.9 %collective-permute-start.7 = (bf16[128,512]{1,0:T(8,128)(2,1)S(1)}, bf16[128,512]{1,0:T(8,128)(2,1)S(1)}, u32[]{:S(2)}, u32[]{:S(2)}) collective-permute-start(bf16[128,512]{1,0:T(8,128)(2,1)S(1)} %slice.8), channel_id=1, source_target_pairs={{0,32},{32,64},{64,96},{96,128},{128,160},{160,192},{192,224},{224... | collective-permute-start | bytes 393224 | tf_op jit(solution)/shard_map/ppermute | solution.py:33
  65.3 0.0 collective-permute-done.8.refs_8_
  65.3 5.0 %collective-permute-done.7.refs_7_ = bf16[128,512]{1,0:T(8,128)(2,1)S(1)} collective-permute-done((bf16[128,512]{1,0:T(8,128)(2,1)S(1)}, bf16[128,512]{1,0:T(8,128)(2,1)S(1)}, u32[]{:S(2)}, u32[]{:S(2)}) %collective-permute-start.7) | collective-permute-done | bytes 131104 | tf_op jit(solution)/shard_map/ppermute | solution.py:33
  70.3 0.0 all-to-all-done.1
  70.3 1.2 shard_map.51
  71.6 5.8 %collective-permute-start.9 = (bf16[2,256,512]{2,1,0:T(8,128)(2,1)S(1)}, bf16[2,256,512]{2,1,0:T(8,128)(2,1)S(1)}, u32[]{:S(2)}, u32[]{:S(2)}) collective-permute-start(bf16[2,256,512]{2,1,0:T(8,128)(2,1)S(1)} %get-tuple-element.7), channel_id=1, source_target_pairs={{0,1},{1,0},{2,3},{3,2},{4,5},{5,4},{6,7},{7,6},{8,9},{9,8},{10,11... | collective-permute-start | bytes 1572872 | tf_op jit(solution)/shard_map/ppermute | solution.py:33
  77.4 1.5 collective-permute-done.9.got_ref
  78.9 0.1 shard_map.52
  79.0 3.1 %collective-permute-start.10 = (bf16[256,512]{1,0:T(8,128)(2,1)S(1)}, bf16[256,512]{1,0:T(8,128)(2,1)S(1)}, u32[]{:S(2)}, u32[]{:S(2)}) collective-permute-start(bf16[256,512]{1,0:T(8,128)(2,1)S(1)} %get-tuple-element.9), channel_id=1, source_target_pairs={{0,256},{256,0},{1,257},{257,1},{2,258},{258,2},{3,259},{259,3},{4... | collective-permute-start | bytes 786440 | tf_op jit(solution)/shard_map/ppermute | solution.py:33
  82.1 6.3 %collective-permute-done.10.arrived_ref = bf16[256,512]{1,0:T(8,128)(2,1)S(1)} collective-permute-done((bf16[256,512]{1,0:T(8,128)(2,1)S(1)}, bf16[256,512]{1,0:T(8,128)(2,1)S(1)}, u32[]{:S(2)}, u32[]{:S(2)}) %collective-permute-start.10) | collective-permute-done | bytes 262176 | tf_op jit(solution)/shard_map/ppermute | solution.py:33
  88.4 0.7 shard_map.53.own_ref
  89.1 3.1 %collective-permute-start.12 = (bf16[256,512]{1,0:T(8,128)(2,1)}, bf16[256,512]{1,0:T(8,128)(2,1)S(1)}, u32[]{:S(2)}, u32[]{:S(2)}) collective-permute-start(bf16[256,512]{1,0:T(8,128)(2,1)} %shard_map.53.own_ref), channel_id=1, source_target_pairs={{0,256},{256,0},{1,257},{257,1},{2,258},{258,2},{3,259},{259,3},{4... | collective-permute-start | bytes 786440 | tf_op jit(solution)/shard_map/ppermute | solution.py:33
  92.2 3.4 %collective-permute-start.11 = (bf16[256,512]{1,0:T(8,128)(2,1)}, bf16[256,512]{1,0:T(8,128)(2,1)S(1)}, u32[]{:S(2)}, u32[]{:S(2)}) collective-permute-start(bf16[256,512]{1,0:T(8,128)(2,1)} %shard_map.53.own_ref), channel_id=1, source_target_pairs={{0,1},{1,0},{2,3},{3,2},{4,5},{5,4},{6,7},{7,6},{8,9},{9,8},{10,11... | collective-permute-start | bytes 786440 | tf_op jit(solution)/shard_map/ppermute | solution.py:33
  95.6 2.2 %collective-permute-done.12.other_ref = bf16[256,512]{1,0:T(8,128)(2,1)S(1)} collective-permute-done((bf16[256,512]{1,0:T(8,128)(2,1)}, bf16[256,512]{1,0:T(8,128)(2,1)S(1)}, u32[]{:S(2)}, u32[]{:S(2)}) %collective-permute-start.12) | collective-permute-done | bytes 262176 | tf_op jit(solution)/shard_map/ppermute | solution.py:33
  97.9 4.0 %collective-permute-start.13 = (bf16[256,512]{1,0:T(8,128)(2,1)S(1)}, bf16[256,512]{1,0:T(8,128)(2,1)S(1)}, u32[]{:S(2)}, u32[]{:S(2)}) collective-permute-start(bf16[256,512]{1,0:T(8,128)(2,1)S(1)} %collective-permute-done.12.other_ref), channel_id=1, source_target_pairs={{0,1},{1,0},{2,3},{3,2},{4,5},{5,4},{6,7},{7,6},{8,9},{9,8},{10,11... | collective-permute-start | bytes 786440 | tf_op jit(solution)/shard_map/ppermute | solution.py:33
  101.9 0.0 collective-permute-done.11.own_next_ref
  101.9 1.1 collective-permute-done.13.other_next_ref
  103.0 2.3 %shard_map.54 = bf16[4,4,256,128]{3,2,1,0:T(8,128)(2,1)S(1)} custom-call(bf16[256,512]{1,0:T(8,128)(2,1)} %shard_map.53.own_ref, bf16[256,512]{1,0:T(8,128)(2,1)S(1)} %collective-permute-done.11.own_next_ref, bf16[256,512]{1,0:T(8,128)(2,1)S(1)} %collective-permute-done.12.other_ref, bf16[256,512]{1,0:T(8,128)(2,1)S(1)} %collective-permute-done.13.other_next_ref, ...), custom_call_target="tpu_custom_call" | custom-call | tf_op jit(solution)/shard_map/pallas_call | solution.py:22
  105.3 17.8 %all_to_all.25.in_ref = bf16[4,4,256,128]{3,2,1,0:T(8,128)(2,1)S(1)} all-to-all(bf16[4,4,256,128]{3,2,1,0:T(8,128)(2,1)S(1)} %shard_map.54), channel_id=1, replica_groups=mesh['xl'=2,'z'=8,'y'=8,'xh'=2,'c'=2] {'xl','xh'}, dimensions={0} | all-to-all | bytes 2097152 | tf_op jit(solution)/shard_map/all_to_all | solution.py:37
  123.1 5.2 %all-to-all-start.4 = ((bf16[32,8,512]{2,1,0:T(8,128)(2,1)}), bf16[32,8,512]{2,1,0:T(8,128)(2,1)S(1)}, u32[]{:S(2)}, u32[]{:S(2)}) async-start(bf16[32,8,512]{2,1,0:T(8,128)(2,1)} %bitcast.3), calls=%async_computation.4 | async-start | bytes 524288 | tf_op jit(solution)/shard_map/all_to_all | solution.py:37
  128.3 0.9 shard_map.55
  129.3 12.1 %all-to-all-done.4.got_ref = bf16[32,8,512]{2,1,0:T(8,128)(2,1)S(1)} async-done(((bf16[32,8,512]{2,1,0:T(8,128)(2,1)}), bf16[32,8,512]{2,1,0:T(8,128)(2,1)S(1)}, u32[]{:S(2)}, u32[]{:S(2)}) %all-to-all-start.4) | async-done | bytes 262176 | tf_op jit(solution)/shard_map/all_to_all | solution.py:37
  141.3 3.5 %all-to-all-start.3 = ((bf16[8,256,128]{2,1,0:T(8,128)(2,1)}), bf16[8,256,128]{2,1,0:T(8,128)(2,1)S(1)}, u32[]{:S(2)}, u32[]{:S(2)}) async-start(bf16[8,256,128]{2,1,0:T(8,128)(2,1)} %shard_map.55), calls=%async_computation.3 | async-start | bytes 1048576 | tf_op jit(solution)/shard_map/all_to_all | solution.py:37
  144.8 0.0 copy-start
  144.8 1.7 %copy-done = bf16[1024,1280]{1,0:T(8,128)(2,1)S(1)} copy-done((bf16[1024,1280]{1,0:T(8,128)(2,1)S(1)}, bf16[1024,1280]{1,0:T(8,128)(2,1)}, u32[]{:S(2)}) %copy-start) | copy-done | bytes 2621464
  146.6 1.2 shard_map.56
  147.8 14.9 %all-to-all-done.3 = bf16[8,256,128]{2,1,0:T(8,128)(2,1)S(1)} async-done(((bf16[8,256,128]{2,1,0:T(8,128)(2,1)}), bf16[8,256,128]{2,1,0:T(8,128)(2,1)S(1)}, u32[]{:S(2)}, u32[]{:S(2)}) %all-to-all-start.3) | async-done | bytes 524320 | tf_op jit(solution)/shard_map/all_to_all | solution.py:37
  162.7 0.7 convert_reduce_fusion
  (3 shorter events, 0.0 us)
Async XLA Ops:
  2.3 26.0 %all-to-all-start = ((bf16[8,256,128]{2,1,0:T(8,128)(2,1)}), bf16[8,256,128]{2,1,0:T(8,128)(2,1)S(1)}, u32[]{:S(2)}, u32[]{:S(2)}) async-start(bf16[8,256,128]{2,1,0:T(8,128)(2,1)} %broadcast_in_dim.10), calls=%async_computation | async-start | bytes 1048576 | tf_op jit(solution)/shard_map/all_to_all | solution.py:37
  10.9 5.6 %collective-permute-start = (bf16[128,512]{1,0:T(8,128)(2,1)S(1)}, bf16[128,512]{1,0:T(8,128)(2,1)S(1)}, u32[]{:S(2)}, u32[]{:S(2)}) collective-permute-start(bf16[128,512]{1,0:T(8,128)(2,1)S(1)} %constant_dynamic-slice_fusion), channel_id=1, source_target_pairs={{0,1},{1,0},{2,3},{3,2},{4,5},{5,4},{6,7},{7,6},{8,9},{9,8},{10,11... | collective-permute-start | bytes 393224 | tf_op jit(solution)/shard_map/ppermute | solution.py:33
  16.5 0.9 copy-start.1
  17.5 16.1 %collective-permute-start.2 = (bf16[128,1024]{1,0:T(8,128)(2,1)S(1)}, bf16[128,1024]{1,0:T(8,128)(2,1)S(1)}, u32[]{:S(2)}, u32[]{:S(2)}) collective-permute-start(bf16[128,1024]{1,0:T(8,128)(2,1)S(1)} %shard_map.50.refs_0_), channel_id=1, source_target_pairs={{0,224},{32,0},{64,32},{96,64},{128,96},{160,128},{192,160},{224,1... | collective-permute-start | bytes 786440 | tf_op jit(solution)/shard_map/ppermute | solution.py:33
  26.4 17.4 %collective-permute-start.1 = (bf16[128,1024]{1,0:T(8,128)(2,1)S(1)}, bf16[128,1024]{1,0:T(8,128)(2,1)S(1)}, u32[]{:S(2)}, u32[]{:S(2)}) collective-permute-start(bf16[128,1024]{1,0:T(8,128)(2,1)S(1)} %shard_map.50.refs_0_), channel_id=1, source_target_pairs={{0,32},{32,64},{64,96},{96,128},{128,160},{160,192},{192,224},{224... | collective-permute-start | bytes 786440 | tf_op jit(solution)/shard_map/ppermute | solution.py:33
  29.5 40.8 %all-to-all-start.1 = ((bf16[4,4,256,128]{3,2,1,0:T(8,128)(2,1)}), bf16[4,4,256,128]{3,2,1,0:T(8,128)(2,1)S(1)}, u32[]{:S(2)}, u32[]{:S(2)}) async-start(bf16[4,4,256,128]{3,2,1,0:T(8,128)(2,1)} %bitcast.1), calls=%async_computation.1 | async-start | bytes 2097152 | tf_op jit(solution)/shard_map/all_to_all | solution.py:37
  33.5 15.2 %collective-permute-start.4 = (bf16[128,1024]{1,0:T(8,128)(2,1)S(1)}, bf16[128,1024]{1,0:T(8,128)(2,1)S(1)}, u32[]{:S(2)}, u32[]{:S(2)}) collective-permute-start(bf16[128,1024]{1,0:T(8,128)(2,1)S(1)} %collective-permute-done.2.refs_2_), channel_id=1, source_target_pairs={{0,224},{32,0},{64,32},{96,64},{128,96},{160,128},{192,160},{224,1... | collective-permute-start | bytes 786440 | tf_op jit(solution)/shard_map/ppermute | solution.py:33
  43.8 10.2 %collective-permute-start.3 = (bf16[128,1024]{1,0:T(8,128)(2,1)S(1)}, bf16[128,1024]{1,0:T(8,128)(2,1)S(1)}, u32[]{:S(2)}, u32[]{:S(2)}) collective-permute-start(bf16[128,1024]{1,0:T(8,128)(2,1)S(1)} %collective-permute-done.1.refs_1_), channel_id=1, source_target_pairs={{0,32},{32,64},{64,96},{96,128},{128,160},{160,192},{192,224},{224... | collective-permute-start | bytes 786440 | tf_op jit(solution)/shard_map/ppermute | solution.py:33
  48.7 9.3 %collective-permute-start.6 = (bf16[128,1024]{1,0:T(8,128)(2,1)S(1)}, bf16[128,1024]{1,0:T(8,128)(2,1)S(1)}, u32[]{:S(2)}, u32[]{:S(2)}) collective-permute-start(bf16[128,1024]{1,0:T(8,128)(2,1)S(1)} %collective-permute-done.4.refs_4_), channel_id=1, source_target_pairs={{0,224},{32,0},{64,32},{96,64},{128,96},{160,128},{192,160},{224,1... | collective-permute-start | bytes 786440 | tf_op jit(solution)/shard_map/ppermute | solution.py:33
  54.0 9.3 %collective-permute-start.5 = (bf16[128,1024]{1,0:T(8,128)(2,1)S(1)}, bf16[128,1024]{1,0:T(8,128)(2,1)S(1)}, u32[]{:S(2)}, u32[]{:S(2)}) collective-permute-start(bf16[128,1024]{1,0:T(8,128)(2,1)S(1)} %collective-permute-done.3.refs_3_), channel_id=1, source_target_pairs={{0,32},{32,64},{64,96},{96,128},{128,160},{160,192},{192,224},{224... | collective-permute-start | bytes 786440 | tf_op jit(solution)/shard_map/ppermute | solution.py:33
  58.0 7.3 %collective-permute-start.8 = (bf16[128,512]{1,0:T(8,128)(2,1)S(1)}, bf16[128,512]{1,0:T(8,128)(2,1)S(1)}, u32[]{:S(2)}, u32[]{:S(2)}) collective-permute-start(bf16[128,512]{1,0:T(8,128)(2,1)S(1)} %slice.9), channel_id=1, source_target_pairs={{0,224},{32,0},{64,32},{96,64},{128,96},{160,128},{192,160},{224,1... | collective-permute-start | bytes 393224 | tf_op jit(solution)/shard_map/ppermute | solution.py:33
  63.4 6.9 %collective-permute-start.7 = (bf16[128,512]{1,0:T(8,128)(2,1)S(1)}, bf16[128,512]{1,0:T(8,128)(2,1)S(1)}, u32[]{:S(2)}, u32[]{:S(2)}) collective-permute-start(bf16[128,512]{1,0:T(8,128)(2,1)S(1)} %slice.8), channel_id=1, source_target_pairs={{0,32},{32,64},{64,96},{96,128},{128,160},{160,192},{192,224},{224... | collective-permute-start | bytes 393224 | tf_op jit(solution)/shard_map/ppermute | solution.py:33
  71.6 7.3 %collective-permute-start.9 = (bf16[2,256,512]{2,1,0:T(8,128)(2,1)S(1)}, bf16[2,256,512]{2,1,0:T(8,128)(2,1)S(1)}, u32[]{:S(2)}, u32[]{:S(2)}) collective-permute-start(bf16[2,256,512]{2,1,0:T(8,128)(2,1)S(1)} %get-tuple-element.7), channel_id=1, source_target_pairs={{0,1},{1,0},{2,3},{3,2},{4,5},{5,4},{6,7},{7,6},{8,9},{9,8},{10,11... | collective-permute-start | bytes 1572872 | tf_op jit(solution)/shard_map/ppermute | solution.py:33
  79.0 9.4 %collective-permute-start.10 = (bf16[256,512]{1,0:T(8,128)(2,1)S(1)}, bf16[256,512]{1,0:T(8,128)(2,1)S(1)}, u32[]{:S(2)}, u32[]{:S(2)}) collective-permute-start(bf16[256,512]{1,0:T(8,128)(2,1)S(1)} %get-tuple-element.9), channel_id=1, source_target_pairs={{0,256},{256,0},{1,257},{257,1},{2,258},{258,2},{3,259},{259,3},{4... | collective-permute-start | bytes 786440 | tf_op jit(solution)/shard_map/ppermute | solution.py:33
  89.1 8.7 %collective-permute-start.12 = (bf16[256,512]{1,0:T(8,128)(2,1)}, bf16[256,512]{1,0:T(8,128)(2,1)S(1)}, u32[]{:S(2)}, u32[]{:S(2)}) collective-permute-start(bf16[256,512]{1,0:T(8,128)(2,1)} %shard_map.53.own_ref), channel_id=1, source_target_pairs={{0,256},{256,0},{1,257},{257,1},{2,258},{258,2},{3,259},{259,3},{4... | collective-permute-start | bytes 786440 | tf_op jit(solution)/shard_map/ppermute | solution.py:33
  92.2 9.6 %collective-permute-start.11 = (bf16[256,512]{1,0:T(8,128)(2,1)}, bf16[256,512]{1,0:T(8,128)(2,1)S(1)}, u32[]{:S(2)}, u32[]{:S(2)}) collective-permute-start(bf16[256,512]{1,0:T(8,128)(2,1)} %shard_map.53.own_ref), channel_id=1, source_target_pairs={{0,1},{1,0},{2,3},{3,2},{4,5},{5,4},{6,7},{7,6},{8,9},{9,8},{10,11... | collective-permute-start | bytes 786440 | tf_op jit(solution)/shard_map/ppermute | solution.py:33
  97.9 5.1 %collective-permute-start.13 = (bf16[256,512]{1,0:T(8,128)(2,1)S(1)}, bf16[256,512]{1,0:T(8,128)(2,1)S(1)}, u32[]{:S(2)}, u32[]{:S(2)}) collective-permute-start(bf16[256,512]{1,0:T(8,128)(2,1)S(1)} %collective-permute-done.12.other_ref), channel_id=1, source_target_pairs={{0,1},{1,0},{2,3},{3,2},{4,5},{5,4},{6,7},{7,6},{8,9},{9,8},{10,11... | collective-permute-start | bytes 786440 | tf_op jit(solution)/shard_map/ppermute | solution.py:33
  123.1 18.2 %all-to-all-start.4 = ((bf16[32,8,512]{2,1,0:T(8,128)(2,1)}), bf16[32,8,512]{2,1,0:T(8,128)(2,1)S(1)}, u32[]{:S(2)}, u32[]{:S(2)}) async-start(bf16[32,8,512]{2,1,0:T(8,128)(2,1)} %bitcast.3), calls=%async_computation.4 | async-start | bytes 524288 | tf_op jit(solution)/shard_map/all_to_all | solution.py:37
  141.3 21.4 %all-to-all-start.3 = ((bf16[8,256,128]{2,1,0:T(8,128)(2,1)}), bf16[8,256,128]{2,1,0:T(8,128)(2,1)S(1)}, u32[]{:S(2)}, u32[]{:S(2)}) async-start(bf16[8,256,128]{2,1,0:T(8,128)(2,1)} %shard_map.55), calls=%async_computation.3 | async-start | bytes 1048576 | tf_op jit(solution)/shard_map/all_to_all | solution.py:37
  144.8 1.7 %copy-start = (bf16[1024,1280]{1,0:T(8,128)(2,1)S(1)}, bf16[1024,1280]{1,0:T(8,128)(2,1)}, u32[]{:S(2)}) copy-start(bf16[1024,1280]{1,0:T(8,128)(2,1)} %coef_ref.1) | copy-start | bytes 7864324

commit v5 on v4

v5 whole, which is shorter than its diff:
```python
import jax
import jax.numpy as jnp
from jax import lax
from jax.experimental import pallas as pl
from jax.experimental.pallas import tpu as pltpu
from jax.sharding import Mesh
from jax.sharding import PartitionSpec as P


AUX = ("xl", "z")
PAIR = ("y", "xh", "c")
ALL = AUX + PAIR
VMEM = pl.BlockSpec(memory_space=pltpu.VMEM)
PARAMS = pltpu.CompilerParams(vmem_limit_bytes=24 * 1024 * 1024)
F32, BF16 = jnp.float32, jnp.bfloat16


def in_vmem(kernel, outs, *args):
    args = [pltpu.with_memory_space_constraint(a, pltpu.VMEM) for a in args]
    return pl.pallas_call(
        kernel,
        in_specs=[VMEM] * len(args),
        out_specs=[VMEM] * len(outs),
        out_shape=[pltpu.VMEM(shape, dtype) for shape, dtype in outs],
        compiler_params=PARAMS,
    )(*args)


def shifted(x, axis, by):
    n = lax.axis_size(axis)
    return lax.ppermute(x, axis, [(i, (i + by) % n) for i in range(n)])


def exchange(x, axes):
    return lax.all_to_all(x, axes, split_axis=0, concat_axis=0, tiled=True)


def ring_step(x):
    n = lax.axis_size("z")
    moves = [(2 * i, 2 * ((i + 1) % n)) for i in range(n)]
    moves += [(2 * i + 1, 2 * ((i - 1) % n) + 1) for i in range(n)]
    return lax.ppermute(x, ("z", "c"), moves)


def shifted_x(x, by):
    at = lambda i: (i % 2) * 2 + i // 2
    return lax.ppermute(x, ("xl", "xh"), [(at(i), at((i + by) % 4)) for i in range(4)])


def blocks_of(refs):
    c = lax.axis_index("c")
    toward = 2 * c - 1
    blocks = [(0, refs[0][...])]
    for s in range(1, 4):
        blocks += [(toward * s, refs[s][...]), (-toward * s, refs[3 + s][...])]
    mine, got = refs[7][...], refs[8][...]
    first = jnp.where(c == 0, mine, got)
    second = jnp.where(c == 0, got, mine)
    return blocks + [(4, jnp.concatenate([first, second], axis=0))]


def place(offset):
    at = lax.rem(lax.axis_index("z") + offset + 8, 8)
    return lax.rem(at, 2), lax.div(at, 2)


def pack_kernel(amp_ref, got_ref, out_ref):
    cols = got_ref.shape[1]
    first = lax.axis_index("c") == 0
    own, got = amp_ref[...], got_ref[...]
    out_ref[:, :cols] = jnp.where(first, own, got)
    out_ref[:, cols:] = jnp.where(first, got, own)


def half_kernel(in_ref, out_ref):
    rows = out_ref.shape[0]
    out_ref[...] = in_ref[pl.ds(pl.multiple_of(lax.axis_index("c") * rows, rows), rows)]


def fitted_kernel(metric_ref, *refs):
    blocks = blocks_of(refs[:-2])
    own_ref, away_ref = refs[-2:]
    xl = lax.axis_index("xl")
    rhs = jnp.concatenate([b for _, b in blocks], axis=0)
    for h, ref in ((xl, own_ref), (1 - xl, away_ref)):
        lhs = [metric_ref[(h, *place(o), j)] for o, _ in blocks for j in range(2)]
        out = jnp.dot(jnp.concatenate(lhs, axis=1), rhs, preferred_element_type=F32)
        ref[...] = out.astype(ref.dtype)


def join_kernel(own_ref, arrived_ref, out_ref):
    out_ref[...] = (own_ref[...] + arrived_ref[...].astype(F32)).astype(BF16)


def density_kernel(own_ref, other_ref, *refs):
    blocks = blocks_of(refs[:-5])
    outs, all_ref = refs[-5:-1], refs[-1]
    xl = lax.axis_index("xl")
    x = 2 * lax.axis_index("xh") + xl
    lhs = jnp.concatenate([own_ref[...], other_ref[...]], axis=0)
    rows = own_ref.shape[0]
    for offset, block in blocks:
        out = lax.dot_general(
            lhs, block, (((1,), (1,)), ((), ())), preferred_element_type=F32
        ).astype(BF16)
        far, near = place(offset)
        half = out.shape[1] // 2
        for h, part in ((xl, out[:rows]), (1 - xl, out[rows:])):
            slot = lax.rem(2 * far + h + 4 - x, 4)
            for j in range(2):
                all_ref[slot, near, j] = part[:, j * half : (j + 1) * half]
    for s in range(4):
        outs[s][...] = all_ref[s]


def half_sum_kernel(here_ref, far_ref, left_ref, right_ref, out_ref):
    xl = lax.axis_index("xl")
    n = here_ref.shape[0]
    ours = here_ref[...].astype(F32) + far_ref[...].astype(F32)
    theirs = left_ref[...].astype(F32) + right_ref[...].astype(F32)
    out_ref[pl.ds(xl * n, n)] = ours.astype(BF16)
    out_ref[pl.ds((1 - xl) * n, n)] = theirs.astype(BF16)


def last_sum_kernel(in_ref, out_ref):
    groups, _, rows, _ = out_ref.shape
    for c in range(2):
        total = in_ref[0, c].astype(F32)
        for y in range(1, in_ref.shape[0]):
            total += in_ref[y, c].astype(F32)
        for g in range(groups):
            out_ref[g, c] = total[g * rows : (g + 1) * rows]


def ao_kernel(got_ref, coef_ref, out_ref):
    n, rows, _ = got_ref.shape
    lhs = jnp.concatenate([got_ref[i].astype(F32) for i in range(n)], axis=0).astype(BF16)
    out = jnp.dot(lhs, coef_ref[...], preferred_element_type=F32)
    count = out.shape[1]
    for i in range(n):
        part = out[i * rows : (i + 1) * rows].astype(BF16)
        out_ref[:, i * count : (i + 1) * count] = part


def work(metric, amplitudes, virt_coef):
    rows, cols = amplitudes.shape
    half, width = rows // 2, metric.shape[1]
    by_core = metric.reshape(rows // 16, 2, 8, width).swapaxes(0, 1).reshape(2, half, width)
    ys = exchange(jnp.tile(by_core, (8, 1, 1)), ("y", "c"))
    ys = ys.reshape(2, 1, 4, 2, half, width)
    wanted = jnp.broadcast_to(ys, (2, 2, 4, 2, half, width))
    part = exchange(wanted.reshape(4, 4, 2, half, width), ("xl", "xh"))
    part = part.reshape(2, 2, 4, 2, half, width)

    got = shifted(amplitudes, "c", 1)
    (packed,) = in_vmem(pack_kernel, [((rows, 2 * cols), BF16)], amplitudes, got)
    steps = [packed]
    for _ in range(1, 4):
        steps.append(ring_step(steps[-1]))
    swaps = [shifted(steps[s], "c", 1) for s in range(1, 4)]
    (farther,) = in_vmem(half_kernel, [((half, 2 * cols), BF16)], steps[3])
    far = ring_step(farther)
    blocks = steps + swaps + [far, shifted(far, "c", 1)]

    own, away = in_vmem(
        fitted_kernel, [((half, 2 * cols), F32), ((half, 2 * cols), BF16)], part, *blocks
    )
    arrived = shifted(away, "xl", 1)
    (fitted,) = in_vmem(join_kernel, [((half, 2 * cols), BF16)], own, arrived)
    other = shifted(fitted, "xl", 1)
    args = [pltpu.with_memory_space_constraint(a, pltpu.VMEM) for a in (fitted, other, *blocks)]
    piece = (4, 2, half, half)
    slots = pl.pallas_call(
        density_kernel,
        in_specs=[VMEM] * len(args),
        out_specs=[VMEM] * 4,
        out_shape=[pltpu.VMEM(piece, BF16)] * 4,
        scratch_shapes=[pltpu.VMEM((4, *piece), BF16)],
        compiler_params=PARAMS,
    )(*args)
    arrived = [shifted_x(slots[s], s) for s in (2, 1, 3)]
    (xs,) = in_vmem(half_sum_kernel, [((8, 2, half, half), BF16)], slots[0], *arrived)
    got = exchange(xs.reshape(16, half, half), ("y", "c"))
    density = pl.pallas_call(
        last_sum_kernel,
        in_specs=[VMEM],
        out_specs=VMEM,
        out_shape=jax.ShapeDtypeStruct((rows // 16, 2, 8, half), F32),
        compiler_params=PARAMS,
    )(got.reshape(8, 2, half, half))

    got = exchange(fitted.reshape(16, 8, 2 * cols), ("y", "xh"))
    ao_count = virt_coef.shape[1]
    ao = pl.pallas_call(
        ao_kernel,
        in_specs=[VMEM] * 2,
        out_specs=VMEM,
        out_shape=jax.ShapeDtypeStruct((8, 16 * ao_count), BF16),
        compiler_params=PARAMS,
    )(got, virt_coef)
    return density.reshape(rows, half), ao


def solution(mesh):
    split = Mesh(mesh.devices.reshape(2, 8, 8, 2, 2), ALL)
    return jax.shard_map(
        work,
        mesh=split,
        in_specs=(P(AUX, PAIR), P(AUX, PAIR), P()),
        out_specs=(P(AUX, PAIR), P(ALL, None)),
        check_vma=False,
    )
```

time: 164 us -> 139 us (0.85)
  blocking collectives: 17.8 us -> 0 us
  starting transfers between devices: 81.9 us -> 76 us
  waiting for transfers between devices: 49.1 us -> 43.9 us
  Pallas kernels: 6.56 us -> 9.91 us
    ppermute x14 -> x7, starting transfers between devices: 61.5 us -> 25.7 us  [shifted(): return lax.ppermute(x, axis, [(i, (i + by) % n) for i in range(n)])]
    ppermute x0 -> x7, starting transfers between devices: none -> 24.5 us  [the longest x4 13.1 us: ring_step(): return lax.ppermute(x, ('z', 'c'), moves)]
    all_to_all x1 -> x0, blocking collectives: 17.8 us -> none  [exchange(): return lax.all_to_all(x, axes, split_axis=0, concat_axis=0, tiled=True)]
    ppermute x0 -> x7, waiting for transfers between devices: none -> 17.5 us  [the longest x4 11.3 us: ring_step(): return lax.ppermute(x, ('z', 'c'), moves)]
    ppermute x14 -> x7, waiting for transfers between devices: 22.1 us -> 7.83 us  [shifted(): return lax.ppermute(x, axis, [(i, (i + by) % n) for i in range(n)])]
    all_to_all x4, waiting for transfers between devices: 27 us -> 18.6 us  [exchange(): return lax.all_to_all(x, axes, split_axis=0, concat_axis=0, tiled=True)]
    all_to_all x4, starting transfers between devices: 20.4 us -> 25.8 us  [exchange(): return lax.all_to_all(x, axes, split_axis=0, concat_axis=0, tiled=True)]
    pallas_call x0 -> x2, Pallas kernels: none -> 3.43 us  [the longest x1 2.71 us: work(): pl.pallas_call(density_kernel, in_specs=[VMEM] * len(args), out_specs=[VM...]
  transfers between devices with their start and end apart: 18 -> 18, of which waited for: 10 -> 9; matrix products, arithmetic and copies ran while one was open for 1% -> 2% of each run, Pallas kernels for 1% -> 4%
where the time goes in v5:
time: 139 us; the launch traced here: 138 us
  starting transfers between devices  76 us (55%)
  waiting for transfers between devices  43.9 us (32%)
  Pallas kernels  9.91 us (7%)
  local copies, waits for them, and re-layouts  6.85 us (5%)
    all_to_all x4, starting transfers between devices, exchange(): return lax.all_to_all(x, axes, split_axis=0, concat_axis=0, tiled=True)  25.8 us
    ppermute x7, starting transfers between devices, shifted(): return lax.ppermute(x, axis, [(i, (i + by) % n) for i in range(n)])  25.7 us
    all_to_all x4, waiting for transfers between devices, exchange(): return lax.all_to_all(x, axes, split_axis=0, concat_axis=0, tiled=True)  18.6 us
    ppermute x4, starting transfers between devices, ring_step(): return lax.ppermute(x, ('z', 'c'), moves)  13.1 us
    ppermute x3, starting transfers between devices, shifted_x(): lax.ppermute(x, ('xl', 'xh'), [(at(i), at((i + by) % 4)) for i in range(4)])  11.5 us
    ppermute x4, waiting for transfers between devices, ring_step(): return lax.ppermute(x, ('z', 'c'), moves)  11.3 us
    ppermute x7, waiting for transfers between devices, shifted(): return lax.ppermute(x, axis, [(i, (i + by) % n) for i in range(n)])  7.83 us
    ppermute x3, waiting for transfers between devices, shifted_x(): lax.ppermute(x, ('xl', 'xh'), [(at(i), at((i + by) % 4)) for i in range(4)])  6.14 us
  transfers between devices with their start and end apart: 18, of which 9 were waited for; matrix products, arithmetic and copies ran while one was open for 2% of the time, Pallas kernels for 4%

profile of v5, /device:TPU:1, one launch (start us, length us, event | category | flops | bytes accessed | tf_op | source)
XLA Modules:
  0.0 137.5 jit_solution(13630712534878721007)
XLA Ops:
  0.6 8.7 %collective-permute-start = (bf16[256,512]{1,0:T(8,128)(2,1)}, bf16[256,512]{1,0:T(8,128)(2,1)S(1)}, u32[]{:S(2)}, u32[]{:S(2)}) collective-permute-start(bf16[256,512]{1,0:T(8,128)(2,1)} %amp_ref.1), channel_id=1, source_target_pairs={{0,1},{1,0},{2,3},{3,2},{4,5},{5,4},{6,7},{7,6},{8,9},{9,8},{10,11... | collective-permute-start | bytes 786440 | tf_op jit(solution)/shard_map/ppermute | solution.py:31
  9.4 1.4 collective-permute-done.got_ref
  10.7 0.0 copy-start.4
  10.7 0.9 copy-done.4
  11.7 0.1 shard_map.50.refs_0_
  11.7 5.3 %collective-permute-start.1 = (bf16[256,1024]{1,0:T(8,128)(2,1)S(1)}, bf16[256,1024]{1,0:T(8,128)(2,1)S(1)}, u32[]{:S(2)}, u32[]{:S(2)}) collective-permute-start(bf16[256,1024]{1,0:T(8,128)(2,1)S(1)} %shard_map.50.refs_0_), channel_id=1, source_target_pairs={{0,32},{32,64},{64,96},{96,128},{128,160},{160,192},{192,224},{224... | collective-permute-start | bytes 1572872 | tf_op jit(solution)/shard_map/ppermute | solution.py:42
  17.1 0.9 copy.7
  17.9 0.9 tile.11
  18.8 7.2 %all-to-all-start = ((bf16[16,128,128]{2,1,0:T(8,128)(2,1)}), bf16[16,128,128]{2,1,0:T(8,128)(2,1)S(1)}, u32[]{:S(2)}, u32[]{:S(2)}) async-start(bf16[16,128,128]{2,1,0:T(8,128)(2,1)} %bitcast.3), calls=%async_computation | async-start | bytes 1048576 | tf_op jit(solution)/shard_map/all_to_all | solution.py:35
  26.1 0.0 collective-permute-done.1.refs_1_
  26.1 2.2 %collective-permute-start.2 = (bf16[256,1024]{1,0:T(8,128)(2,1)S(1)}, bf16[256,1024]{1,0:T(8,128)(2,1)S(1)}, u32[]{:S(2)}, u32[]{:S(2)}) collective-permute-start(bf16[256,1024]{1,0:T(8,128)(2,1)S(1)} %collective-permute-done.1.refs_1_), channel_id=1, source_target_pairs={{0,32},{32,64},{64,96},{96,128},{128,160},{160,192},{192,224},{224... | collective-permute-start | bytes 1572872 | tf_op jit(solution)/shard_map/ppermute | solution.py:42
  28.3 8.0 %collective-permute-done.2.refs_2_ = bf16[256,1024]{1,0:T(8,128)(2,1)S(1)} collective-permute-done((bf16[256,1024]{1,0:T(8,128)(2,1)S(1)}, bf16[256,1024]{1,0:T(8,128)(2,1)S(1)}, u32[]{:S(2)}, u32[]{:S(2)}) %collective-permute-start.2) | collective-permute-done | bytes 524320 | tf_op jit(solution)/shard_map/ppermute | solution.py:42
  36.3 3.4 %collective-permute-start.3 = (bf16[256,1024]{1,0:T(8,128)(2,1)S(1)}, bf16[256,1024]{1,0:T(8,128)(2,1)S(1)}, u32[]{:S(2)}, u32[]{:S(2)}) collective-permute-start(bf16[256,1024]{1,0:T(8,128)(2,1)S(1)} %collective-permute-done.2.refs_2_), channel_id=1, source_target_pairs={{0,32},{32,64},{64,96},{96,128},{128,160},{160,192},{192,224},{224... | collective-permute-start | bytes 1572872 | tf_op jit(solution)/shard_map/ppermute | solution.py:42
  39.7 3.6 %all-to-all-done = bf16[16,128,128]{2,1,0:T(8,128)(2,1)S(1)} async-done(((bf16[16,128,128]{2,1,0:T(8,128)(2,1)}), bf16[16,128,128]{2,1,0:T(8,128)(2,1)S(1)}, u32[]{:S(2)}, u32[]{:S(2)}) %all-to-all-start) | async-done | bytes 524320 | tf_op jit(solution)/shard_map/all_to_all | solution.py:35
  43.3 1.2 broadcast_in_dim.8
  44.5 4.0 %all-to-all-start.1 = ((bf16[4,4,2,128,128]{4,3,2,1,0:T(8,128)(2,1)}), bf16[4,4,2,128,128]{4,3,2,1,0:T(8,128)(2,1)S(1)}, u32[]{:S(2)}, u32[]{:S(2)}) async-start(bf16[4,4,2,128,128]{4,3,2,1,0:T(8,128)(2,1)} %bitcast.16), calls=%async_computation.1 | async-start | bytes 2097152 | tf_op jit(solution)/shard_map/all_to_all | solution.py:35
  48.5 1.9 %collective-permute-start.4 = (bf16[256,1024]{1,0:T(8,128)(2,1)S(1)}, bf16[256,1024]{1,0:T(8,128)(2,1)S(1)}, u32[]{:S(2)}, u32[]{:S(2)}) collective-permute-start(bf16[256,1024]{1,0:T(8,128)(2,1)S(1)} %collective-permute-done.1.refs_1_), channel_id=1, source_target_pairs={{0,1},{1,0},{2,3},{3,2},{4,5},{5,4},{6,7},{7,6},{8,9},{9,8},{10,11... | collective-permute-start | bytes 1572872 | tf_op jit(solution)/shard_map/ppermute | solution.py:31
  50.5 2.4 %collective-permute-start.5 = (bf16[256,1024]{1,0:T(8,128)(2,1)S(1)}, bf16[256,1024]{1,0:T(8,128)(2,1)}, u32[]{:S(2)}, u32[]{:S(2)}) collective-permute-start(bf16[256,1024]{1,0:T(8,128)(2,1)S(1)} %collective-permute-done.2.refs_2_), channel_id=1, source_target_pairs={{0,1},{1,0},{2,3},{3,2},{4,5},{5,4},{6,7},{7,6},{8,9},{9,8},{10,11... | collective-permute-start | bytes 1572872 | tf_op jit(solution)/shard_map/ppermute | solution.py:31
  52.9 0.0 collective-permute-done.3.in_ref.refs_3_
  52.9 2.2 %collective-permute-start.7 = (bf16[128,1024]{1,0:T(8,128)(2,1)S(1)}, bf16[128,1024]{1,0:T(8,128)(2,1)S(1)}, u32[]{:S(2)}, u32[]{:S(2)}) collective-permute-start(bf16[128,1024]{1,0:T(8,128)(2,1)S(1)} %shard_map.51), channel_id=1, source_target_pairs={{0,32},{32,64},{64,96},{96,128},{128,160},{160,192},{192,224},{224... | collective-permute-start | bytes 786440 | tf_op jit(solution)/shard_map/ppermute | solution.py:42
  55.1 1.9 %collective-permute-start.6 = (bf16[256,1024]{1,0:T(8,128)(2,1)S(1)}, bf16[256,1024]{1,0:T(8,128)(2,1)}, u32[]{:S(2)}, u32[]{:S(2)}) collective-permute-start(bf16[256,1024]{1,0:T(8,128)(2,1)S(1)} %collective-permute-done.3.in_ref.refs_3_), channel_id=1, source_target_pairs={{0,1},{1,0},{2,3},{3,2},{4,5},{5,4},{6,7},{7,6},{8,9},{9,8},{10,11... | collective-permute-start | bytes 1572872 | tf_op jit(solution)/shard_map/ppermute | solution.py:31
  57.0 3.3 %collective-permute-done.7.refs_7_ = bf16[128,1024]{1,0:T(8,128)(2,1)S(1)} collective-permute-done((bf16[128,1024]{1,0:T(8,128)(2,1)S(1)}, bf16[128,1024]{1,0:T(8,128)(2,1)S(1)}, u32[]{:S(2)}, u32[]{:S(2)}) %collective-permute-start.7) | collective-permute-done | bytes 262176 | tf_op jit(solution)/shard_map/ppermute | solution.py:42
  60.3 4.0 %collective-permute-start.8 = (bf16[128,1024]{1,0:T(8,128)(2,1)S(1)}, bf16[128,1024]{1,0:T(8,128)(2,1)}, u32[]{:S(2)}, u32[]{:S(2)}) collective-permute-start(bf16[128,1024]{1,0:T(8,128)(2,1)S(1)} %collective-permute-done.7.refs_7_), channel_id=1, source_target_pairs={{0,1},{1,0},{2,3},{3,2},{4,5},{5,4},{6,7},{7,6},{8,9},{9,8},{10,11... | collective-permute-start | bytes 786440 | tf_op jit(solution)/shard_map/ppermute | solution.py:31
  64.3 0.0 collective-permute-done.4.refs_4_
  64.3 0.0 copy-start.1
  64.3 0.8 copy-done.1
  65.1 0.0 all-to-all-done.1
  65.1 0.0 collective-permute-done.5.refs_5_
  65.1 0.4 collective-permute-done.8.refs_8_
  65.6 0.0 collective-permute-done.6.refs_6_
  65.6 0.0 copy-start.2
  65.6 1.0 copy-done.2
  66.6 2.5 %shard_map.52 = (f32[128,1024]{1,0:T(8,128)S(1)}, bf16[128,1024]{1,0:T(8,128)(2,1)S(1)}) custom-call(bf16[2,2,4,2,128,128]{5,4,3,2,1,0:T(8,128)(2,1)S(1)} %bitcast.14, bf16[256,1024]{1,0:T(8,128)(2,1)S(1)} %shard_map.50.refs_0_, bf16[256,1024]{1,0:T(8,128)(2,1)S(1)} %collective-permute-done.1.refs_1_, bf16[256,1024]{1,0:T(8,128)(2,1)S(1)} %collective-permute-done.2.refs_2_, ...), custom_call_target="tpu_custom_call" | custom-call | tf_op jit(solution)/shard_map/pallas_call | solution.py:20
  69.2 3.4 %collective-permute-start.9 = (bf16[128,1024]{1,0:T(8,128)(2,1)S(1)}, bf16[128,1024]{1,0:T(8,128)(2,1)S(1)}, u32[]{:S(2)}, u32[]{:S(2)}) collective-permute-start(bf16[128,1024]{1,0:T(8,128)(2,1)S(1)} %get-tuple-element.9), channel_id=1, source_target_pairs={{0,256},{256,0},{1,257},{257,1},{2,258},{258,2},{3,259},{259,3},{4... | collective-permute-start | bytes 786440 | tf_op jit(solution)/shard_map/ppermute | solution.py:31
  72.5 6.0 %collective-permute-done.9.arrived_ref = bf16[128,1024]{1,0:T(8,128)(2,1)S(1)} collective-permute-done((bf16[128,1024]{1,0:T(8,128)(2,1)S(1)}, bf16[128,1024]{1,0:T(8,128)(2,1)S(1)}, u32[]{:S(2)}, u32[]{:S(2)}) %collective-permute-start.9) | collective-permute-done | bytes 262176 | tf_op jit(solution)/shard_map/ppermute | solution.py:31
  78.6 0.7 shard_map.53.own_ref
  79.3 3.3 %collective-permute-start.10 = (bf16[128,1024]{1,0:T(8,128)(2,1)}, bf16[128,1024]{1,0:T(8,128)(2,1)S(1)}, u32[]{:S(2)}, u32[]{:S(2)}) collective-permute-start(bf16[128,1024]{1,0:T(8,128)(2,1)} %shard_map.53.own_ref), channel_id=1, source_target_pairs={{0,256},{256,0},{1,257},{257,1},{2,258},{258,2},{3,259},{259,3},{4... | collective-permute-start | bytes 786440 | tf_op jit(solution)/shard_map/ppermute | solution.py:31
  82.7 6.8 %all-to-all-start.3 = ((bf16[16,8,1024]{2,1,0:T(8,128)(2,1)}), bf16[16,8,1024]{2,1,0:T(8,128)(2,1)}, u32[]{:S(2)}, u32[]{:S(2)}) async-start(bf16[16,8,1024]{2,1,0:T(8,128)(2,1)} %bitcast.10), calls=%async_computation.3 | async-start | bytes 524288 | tf_op jit(solution)/shard_map/all_to_all | solution.py:35
  89.4 0.0 collective-permute-done.10.other_ref
  89.5 0.0 copy-start.3
  89.5 1.0 copy-done.3
  90.5 2.7 %shard_map.54 = (bf16[4,2,128,128]{3,2,1,0:T(8,128)(2,1)S(1)}, bf16[4,2,128,128]{3,2,1,0:T(8,128)(2,1)S(1)}, bf16[4,2,128,128]{3,2,1,0:T(8,128)(2,1)S(1)}, bf16[4,2,128,128]{3,2,1,0:T(8,128)(2,1)S(1)}) custom-call(bf16[128,1024]{1,0:T(8,128)(2,1)} %shard_map.53.own_ref, bf16[128,1024]{1,0:T(8,128)(2,1)S(1)} %collective-permute-done.10.other_ref, ...), custom_call_target="tpu_custom_call" | custom-call | tf_op jit(solution)/shard_map/pallas_call | solution.py:173
  93.2 0.0 copy-start
  93.2 5.0 %collective-permute-start.11 = (bf16[4,2,128,128]{3,2,1,0:T(8,128)(2,1)S(1)}, bf16[4,2,128,128]{3,2,1,0:T(8,128)(2,1)S(1)}, u32[]{:S(2)}, u32[]{:S(2)}) collective-permute-start(bf16[4,2,128,128]{3,2,1,0:T(8,128)(2,1)S(1)} %get-tuple-element.11), channel_id=1, source_target_pairs={{0,2},{256,258},{2,0},{258,256},{1,3},{257,259},{3,1},{259,257},{4... | collective-permute-start | bytes 786440 | tf_op jit(solution)/shard_map/ppermute | solution.py:47
  98.2 1.9 %collective-permute-start.12 = (bf16[4,2,128,128]{3,2,1,0:T(8,128)(2,1)S(1)}, bf16[4,2,128,128]{3,2,1,0:T(8,128)(2,1)S(1)}, u32[]{:S(2)}, u32[]{:S(2)}) collective-permute-start(bf16[4,2,128,128]{3,2,1,0:T(8,128)(2,1)S(1)} %get-tuple-element.12), channel_id=1, source_target_pairs={{0,256},{256,2},{2,258},{258,0},{1,257},{257,3},{3,259},{259,1},{4... | collective-permute-start | bytes 786440 | tf_op jit(solution)/shard_map/ppermute | solution.py:47
  100.2 4.6 %collective-permute-start.13 = (bf16[4,2,128,128]{3,2,1,0:T(8,128)(2,1)S(1)}, bf16[4,2,128,128]{3,2,1,0:T(8,128)(2,1)S(1)}, u32[]{:S(2)}, u32[]{:S(2)}) collective-permute-start(bf16[4,2,128,128]{3,2,1,0:T(8,128)(2,1)S(1)} %get-tuple-element.13), channel_id=1, source_target_pairs={{0,258},{256,0},{2,256},{258,2},{1,259},{257,1},{3,257},{259,3},{4... | collective-permute-start | bytes 786440 | tf_op jit(solution)/shard_map/ppermute | solution.py:47
  104.7 0.1 collective-permute-done.11.far_ref
  104.8 6.1 %collective-permute-done.12.left_ref = bf16[4,2,128,128]{3,2,1,0:T(8,128)(2,1)S(1)} collective-permute-done((bf16[4,2,128,128]{3,2,1,0:T(8,128)(2,1)S(1)}, bf16[4,2,128,128]{3,2,1,0:T(8,128)(2,1)S(1)}, u32[]{:S(2)}, u32[]{:S(2)}) %collective-permute-start.12) | collective-permute-done | bytes 262176 | tf_op jit(solution)/shard_map/ppermute | solution.py:47
  110.9 0.0 collective-permute-done.13.right_ref
  110.9 0.9 shard_map.55
  111.8 0.0 all-to-all-done.3.got_ref
  111.8 7.8 %all-to-all-start.2 = ((bf16[16,128,128]{2,1,0:T(8,128)(2,1)}), bf16[16,128,128]{2,1,0:T(8,128)(2,1)S(1)}, u32[]{:S(2)}, u32[]{:S(2)}) async-start(bf16[16,128,128]{2,1,0:T(8,128)(2,1)} %bitcast.7), calls=%async_computation.2 | async-start | bytes 1048576 | tf_op jit(solution)/shard_map/all_to_all | solution.py:35
  119.6 0.0 copy-done
  119.6 2.2 %shard_map.57 = bf16[8,20480]{1,0:T(8,128)(2,1)} custom-call(bf16[16,8,1024]{2,1,0:T(8,128)(2,1)} %all-to-all-done.3.got_ref, bf16[1024,1280]{1,0:T(8,128)(2,1)S(1)} %copy-done), custom_call_target="tpu_custom_call" | custom-call | tf_op jit(solution)/shard_map/pallas_call | solution.py:194
  121.8 15.0 %all-to-all-done.2 = bf16[16,128,128]{2,1,0:T(8,128)(2,1)S(1)} async-done(((bf16[16,128,128]{2,1,0:T(8,128)(2,1)}), bf16[16,128,128]{2,1,0:T(8,128)(2,1)S(1)}, u32[]{:S(2)}, u32[]{:S(2)}) %all-to-all-start.2) | async-done | bytes 524320 | tf_op jit(solution)/shard_map/all_to_all | solution.py:35
  136.8 0.7 shard_map.56
  (1 shorter events, 0.0 us)
Async XLA Ops:
  0.6 10.1 %collective-permute-start = (bf16[256,512]{1,0:T(8,128)(2,1)}, bf16[256,512]{1,0:T(8,128)(2,1)S(1)}, u32[]{:S(2)}, u32[]{:S(2)}) collective-permute-start(bf16[256,512]{1,0:T(8,128)(2,1)} %amp_ref.1), channel_id=1, source_target_pairs={{0,1},{1,0},{2,3},{3,2},{4,5},{5,4},{6,7},{7,6},{8,9},{9,8},{10,11... | collective-permute-start | bytes 786440 | tf_op jit(solution)/shard_map/ppermute | solution.py:31
  10.7 0.9 copy-start.4
  11.7 14.3 %collective-permute-start.1 = (bf16[256,1024]{1,0:T(8,128)(2,1)S(1)}, bf16[256,1024]{1,0:T(8,128)(2,1)S(1)}, u32[]{:S(2)}, u32[]{:S(2)}) collective-permute-start(bf16[256,1024]{1,0:T(8,128)(2,1)S(1)} %shard_map.50.refs_0_), channel_id=1, source_target_pairs={{0,32},{32,64},{64,96},{96,128},{128,160},{160,192},{192,224},{224... | collective-permute-start | bytes 1572872 | tf_op jit(solution)/shard_map/ppermute | solution.py:42
  18.8 24.4 %all-to-all-start = ((bf16[16,128,128]{2,1,0:T(8,128)(2,1)}), bf16[16,128,128]{2,1,0:T(8,128)(2,1)S(1)}, u32[]{:S(2)}, u32[]{:S(2)}) async-start(bf16[16,128,128]{2,1,0:T(8,128)(2,1)} %bitcast.3), calls=%async_computation | async-start | bytes 1048576 | tf_op jit(solution)/shard_map/all_to_all | solution.py:35
  26.1 10.2 %collective-permute-start.2 = (bf16[256,1024]{1,0:T(8,128)(2,1)S(1)}, bf16[256,1024]{1,0:T(8,128)(2,1)S(1)}, u32[]{:S(2)}, u32[]{:S(2)}) collective-permute-start(bf16[256,1024]{1,0:T(8,128)(2,1)S(1)} %collective-permute-done.1.refs_1_), channel_id=1, source_target_pairs={{0,32},{32,64},{64,96},{96,128},{128,160},{160,192},{192,224},{224... | collective-permute-start | bytes 1572872 | tf_op jit(solution)/shard_map/ppermute | solution.py:42
  36.3 16.6 %collective-permute-start.3 = (bf16[256,1024]{1,0:T(8,128)(2,1)S(1)}, bf16[256,1024]{1,0:T(8,128)(2,1)S(1)}, u32[]{:S(2)}, u32[]{:S(2)}) collective-permute-start(bf16[256,1024]{1,0:T(8,128)(2,1)S(1)} %collective-permute-done.2.refs_2_), channel_id=1, source_target_pairs={{0,32},{32,64},{64,96},{96,128},{128,160},{160,192},{192,224},{224... | collective-permute-start | bytes 1572872 | tf_op jit(solution)/shard_map/ppermute | solution.py:42
  44.5 20.6 %all-to-all-start.1 = ((bf16[4,4,2,128,128]{4,3,2,1,0:T(8,128)(2,1)}), bf16[4,4,2,128,128]{4,3,2,1,0:T(8,128)(2,1)S(1)}, u32[]{:S(2)}, u32[]{:S(2)}) async-start(bf16[4,4,2,128,128]{4,3,2,1,0:T(8,128)(2,1)} %bitcast.16), calls=%async_computation.1 | async-start | bytes 2097152 | tf_op jit(solution)/shard_map/all_to_all | solution.py:35
  48.5 15.8 %collective-permute-start.4 = (bf16[256,1024]{1,0:T(8,128)(2,1)S(1)}, bf16[256,1024]{1,0:T(8,128)(2,1)S(1)}, u32[]{:S(2)}, u32[]{:S(2)}) collective-permute-start(bf16[256,1024]{1,0:T(8,128)(2,1)S(1)} %collective-permute-done.1.refs_1_), channel_id=1, source_target_pairs={{0,1},{1,0},{2,3},{3,2},{4,5},{5,4},{6,7},{7,6},{8,9},{9,8},{10,11... | collective-permute-start | bytes 1572872 | tf_op jit(solution)/shard_map/ppermute | solution.py:31
  50.5 14.7 %collective-permute-start.5 = (bf16[256,1024]{1,0:T(8,128)(2,1)S(1)}, bf16[256,1024]{1,0:T(8,128)(2,1)}, u32[]{:S(2)}, u32[]{:S(2)}) collective-permute-start(bf16[256,1024]{1,0:T(8,128)(2,1)S(1)} %collective-permute-done.2.refs_2_), channel_id=1, source_target_pairs={{0,1},{1,0},{2,3},{3,2},{4,5},{5,4},{6,7},{7,6},{8,9},{9,8},{10,11... | collective-permute-start | bytes 1572872 | tf_op jit(solution)/shard_map/ppermute | solution.py:31
  52.9 7.4 %collective-permute-start.7 = (bf16[128,1024]{1,0:T(8,128)(2,1)S(1)}, bf16[128,1024]{1,0:T(8,128)(2,1)S(1)}, u32[]{:S(2)}, u32[]{:S(2)}) collective-permute-start(bf16[128,1024]{1,0:T(8,128)(2,1)S(1)} %shard_map.51), channel_id=1, source_target_pairs={{0,32},{32,64},{64,96},{96,128},{128,160},{160,192},{192,224},{224... | collective-permute-start | bytes 786440 | tf_op jit(solution)/shard_map/ppermute | solution.py:42
  55.1 10.5 %collective-permute-start.6 = (bf16[256,1024]{1,0:T(8,128)(2,1)S(1)}, bf16[256,1024]{1,0:T(8,128)(2,1)}, u32[]{:S(2)}, u32[]{:S(2)}) collective-permute-start(bf16[256,1024]{1,0:T(8,128)(2,1)S(1)} %collective-permute-done.3.in_ref.refs_3_), channel_id=1, source_target_pairs={{0,1},{1,0},{2,3},{3,2},{4,5},{5,4},{6,7},{7,6},{8,9},{9,8},{10,11... | collective-permute-start | bytes 1572872 | tf_op jit(solution)/shard_map/ppermute | solution.py:31
  60.3 5.3 %collective-permute-start.8 = (bf16[128,1024]{1,0:T(8,128)(2,1)S(1)}, bf16[128,1024]{1,0:T(8,128)(2,1)}, u32[]{:S(2)}, u32[]{:S(2)}) collective-permute-start(bf16[128,1024]{1,0:T(8,128)(2,1)S(1)} %collective-permute-done.7.refs_7_), channel_id=1, source_target_pairs={{0,1},{1,0},{2,3},{3,2},{4,5},{5,4},{6,7},{7,6},{8,9},{9,8},{10,11... | collective-permute-start | bytes 786440 | tf_op jit(solution)/shard_map/ppermute | solution.py:31
  64.3 0.8 copy-start.1
  65.6 1.0 copy-start.2
  69.2 9.4 %collective-permute-start.9 = (bf16[128,1024]{1,0:T(8,128)(2,1)S(1)}, bf16[128,1024]{1,0:T(8,128)(2,1)S(1)}, u32[]{:S(2)}, u32[]{:S(2)}) collective-permute-start(bf16[128,1024]{1,0:T(8,128)(2,1)S(1)} %get-tuple-element.9), channel_id=1, source_target_pairs={{0,256},{256,0},{1,257},{257,1},{2,258},{258,2},{3,259},{259,3},{4... | collective-permute-start | bytes 786440 | tf_op jit(solution)/shard_map/ppermute | solution.py:31
  79.3 10.1 %collective-permute-start.10 = (bf16[128,1024]{1,0:T(8,128)(2,1)}, bf16[128,1024]{1,0:T(8,128)(2,1)S(1)}, u32[]{:S(2)}, u32[]{:S(2)}) collective-permute-start(bf16[128,1024]{1,0:T(8,128)(2,1)} %shard_map.53.own_ref), channel_id=1, source_target_pairs={{0,256},{256,0},{1,257},{257,1},{2,258},{258,2},{3,259},{259,3},{4... | collective-permute-start | bytes 786440 | tf_op jit(solution)/shard_map/ppermute | solution.py:31
  82.7 29.1 %all-to-all-start.3 = ((bf16[16,8,1024]{2,1,0:T(8,128)(2,1)}), bf16[16,8,1024]{2,1,0:T(8,128)(2,1)}, u32[]{:S(2)}, u32[]{:S(2)}) async-start(bf16[16,8,1024]{2,1,0:T(8,128)(2,1)} %bitcast.10), calls=%async_computation.3 | async-start | bytes 524288 | tf_op jit(solution)/shard_map/all_to_all | solution.py:35
  89.5 1.0 copy-start.3
  93.2 26.4 %copy-start = (bf16[1024,1280]{1,0:T(8,128)(2,1)S(1)}, bf16[1024,1280]{1,0:T(8,128)(2,1)}, u32[]{:S(2)}) copy-start(bf16[1024,1280]{1,0:T(8,128)(2,1)} %coef_ref.1) | copy-start | bytes 7864324
  93.2 11.6 %collective-permute-start.11 = (bf16[4,2,128,128]{3,2,1,0:T(8,128)(2,1)S(1)}, bf16[4,2,128,128]{3,2,1,0:T(8,128)(2,1)S(1)}, u32[]{:S(2)}, u32[]{:S(2)}) collective-permute-start(bf16[4,2,128,128]{3,2,1,0:T(8,128)(2,1)S(1)} %get-tuple-element.11), channel_id=1, source_target_pairs={{0,2},{256,258},{2,0},{258,256},{1,3},{257,259},{3,1},{259,257},{4... | collective-permute-start | bytes 786440 | tf_op jit(solution)/shard_map/ppermute | solution.py:47
  98.2 12.7 %collective-permute-start.12 = (bf16[4,2,128,128]{3,2,1,0:T(8,128)(2,1)S(1)}, bf16[4,2,128,128]{3,2,1,0:T(8,128)(2,1)S(1)}, u32[]{:S(2)}, u32[]{:S(2)}) collective-permute-start(bf16[4,2,128,128]{3,2,1,0:T(8,128)(2,1)S(1)} %get-tuple-element.12), channel_id=1, source_target_pairs={{0,256},{256,2},{2,258},{258,0},{1,257},{257,3},{3,259},{259,1},{4... | collective-permute-start | bytes 786440 | tf_op jit(solution)/shard_map/ppermute | solution.py:47
  100.2 10.7 %collective-permute-start.13 = (bf16[4,2,128,128]{3,2,1,0:T(8,128)(2,1)S(1)}, bf16[4,2,128,128]{3,2,1,0:T(8,128)(2,1)S(1)}, u32[]{:S(2)}, u32[]{:S(2)}) collective-permute-start(bf16[4,2,128,128]{3,2,1,0:T(8,128)(2,1)S(1)} %get-tuple-element.13), channel_id=1, source_target_pairs={{0,258},{256,0},{2,256},{258,2},{1,259},{257,1},{3,257},{259,3},{4... | collective-permute-start | bytes 786440 | tf_op jit(solution)/shard_map/ppermute | solution.py:47
  111.8 25.0 %all-to-all-start.2 = ((bf16[16,128,128]{2,1,0:T(8,128)(2,1)}), bf16[16,128,128]{2,1,0:T(8,128)(2,1)S(1)}, u32[]{:S(2)}, u32[]{:S(2)}) async-start(bf16[16,128,128]{2,1,0:T(8,128)(2,1)} %bitcast.7), calls=%async_computation.2 | async-start | bytes 1048576 | tf_op jit(solution)/shard_map/all_to_all | solution.py:35

commit v6 on v5

--- a/solution.py
+++ b/solution.py
@@ -70,6 +70,15 @@
     own, got = amp_ref[...], got_ref[...]
     out_ref[:, :cols] = jnp.where(first, own, got)
     out_ref[:, cols:] = jnp.where(first, got, own)
+
+
+def split_kernel(in_ref, out_ref):
+    n, cores, rows, cols = out_ref.shape
+    groups = in_ref[...].astype(F32).reshape(rows // 8, cores, 8, cols)
+    for c in range(cores):
+        part = groups[:, c].reshape(rows, cols).astype(BF16)
+        for i in range(n):
+            out_ref[i, c] = part
 
 
 def half_kernel(in_ref, out_ref):
@@ -145,8 +154,14 @@
 def work(metric, amplitudes, virt_coef):
     rows, cols = amplitudes.shape
     half, width = rows // 2, metric.shape[1]
-    by_core = metric.reshape(rows // 16, 2, 8, width).swapaxes(0, 1).reshape(2, half, width)
-    ys = exchange(jnp.tile(by_core, (8, 1, 1)), ("y", "c"))
+    by_core = pl.pallas_call(
+        split_kernel,
+        in_specs=[VMEM],
+        out_specs=VMEM,
+        out_shape=jax.ShapeDtypeStruct((8, 2, half, width), BF16),
+        compiler_params=PARAMS,
+    )(metric)
+    ys = exchange(by_core.reshape(16, half, width), ("y", "c"))
     ys = ys.reshape(2, 1, 4, 2, half, width)
     wanted = jnp.broadcast_to(ys, (2, 2, 4, 2, half, width))
     part = exchange(wanted.reshape(4, 4, 2, half, width), ("xl", "xh"))
@@ -197,7 +212,7 @@
         out_specs=VMEM,
         out_shape=jax.ShapeDtypeStruct((8, 16 * ao_count), BF16),
         compiler_params=PARAMS,
-    )(got, virt_coef)
+    )(got, pltpu.with_memory_space_constraint(virt_coef, pltpu.HBM))
     return density.reshape(rows, half), ao
 
 

time: 139 us -> 138 us (level)
  Pallas kernels: 9.91 us -> 11.6 us
  transfers between devices with their start and end apart: 18 -> 18, of which waited for: 9 -> 8; matrix products, arithmetic and copies ran while one was open for 2% -> 1% of each run, Pallas kernels for 4% -> 5%
where the time goes in v6:
time: 138 us; the launch traced here: 137 us
  starting transfers between devices  75.8 us (55%)
  waiting for transfers between devices  43 us (31%)
  Pallas kernels  11.6 us (8%)
  local copies, waits for them, and re-layouts  5.91 us (4%)
    all_to_all x4, starting transfers between devices, exchange(): return lax.all_to_all(x, axes, split_axis=0, concat_axis=0, tiled=True)  25.8 us
    ppermute x7, starting transfers between devices, shifted(): return lax.ppermute(x, axis, [(i, (i + by) % n) for i in range(n)])  25.7 us
    all_to_all x4, waiting for transfers between devices, exchange(): return lax.all_to_all(x, axes, split_axis=0, concat_axis=0, tiled=True)  17.8 us
    ppermute x4, starting transfers between devices, ring_step(): return lax.ppermute(x, ('z', 'c'), moves)  13.1 us
    ppermute x4, waiting for transfers between devices, ring_step(): return lax.ppermute(x, ('z', 'c'), moves)  11.3 us
    ppermute x3, starting transfers between devices, shifted_x(): lax.ppermute(x, ('xl', 'xh'), [(at(i), at((i + by) % 4)) for i in range(4)])  11.3 us
    ppermute x7, waiting for transfers between devices, shifted(): return lax.ppermute(x, axis, [(i, (i + by) % n) for i in range(n)])  7.83 us
    ppermute x3, waiting for transfers between devices, shifted_x(): lax.ppermute(x, ('xl', 'xh'), [(at(i), at((i + by) % 4)) for i in range(4)])  6.03 us
  transfers between devices with their start and end apart: 18, of which 8 were waited for; matrix products, arithmetic and copies ran while one was open for 1% of the time, Pallas kernels for 5%

profile of v6, /device:TPU:1, one launch (start us, length us, event | category | flops | bytes accessed | tf_op | source)
XLA Modules:
  0.0 137.2 jit_solution(5331241149409413576)
XLA Ops:
  0.6 8.7 %collective-permute-start = (bf16[256,512]{1,0:T(8,128)(2,1)}, bf16[256,512]{1,0:T(8,128)(2,1)S(1)}, u32[]{:S(2)}, u32[]{:S(2)}) collective-permute-start(bf16[256,512]{1,0:T(8,128)(2,1)} %amp_ref.1), channel_id=1, source_target_pairs={{0,1},{1,0},{2,3},{3,2},{4,5},{5,4},{6,7},{7,6},{8,9},{9,8},{10,11... | collective-permute-start | bytes 786440 | tf_op jit(solution)/shard_map/ppermute | solution.py:31
  9.4 1.4 collective-permute-done.got_ref
  10.7 0.0 copy-start.3
  10.7 0.9 copy-done.3
  11.7 0.1 shard_map.51.refs_0_
  11.7 5.3 %collective-permute-start.1 = (bf16[256,1024]{1,0:T(8,128)(2,1)S(1)}, bf16[256,1024]{1,0:T(8,128)(2,1)S(1)}, u32[]{:S(2)}, u32[]{:S(2)}) collective-permute-start(bf16[256,1024]{1,0:T(8,128)(2,1)S(1)} %shard_map.51.refs_0_), channel_id=1, source_target_pairs={{0,32},{32,64},{64,96},{96,128},{128,160},{160,192},{192,224},{224... | collective-permute-start | bytes 1572872 | tf_op jit(solution)/shard_map/ppermute | solution.py:42
  17.1 0.0 copy-start.4
  17.1 0.8 copy-done.4
  17.9 0.9 shard_map.50
  18.8 7.2 %all-to-all-start = ((bf16[16,128,128]{2,1,0:T(8,128)(2,1)}), bf16[16,128,128]{2,1,0:T(8,128)(2,1)S(1)}, u32[]{:S(2)}, u32[]{:S(2)}) async-start(bf16[16,128,128]{2,1,0:T(8,128)(2,1)} %bitcast), calls=%async_computation | async-start | bytes 1048576 | tf_op jit(solution)/shard_map/all_to_all | solution.py:35
  26.0 0.0 collective-permute-done.1.refs_1_
  26.0 2.2 %collective-permute-start.2 = (bf16[256,1024]{1,0:T(8,128)(2,1)S(1)}, bf16[256,1024]{1,0:T(8,128)(2,1)S(1)}, u32[]{:S(2)}, u32[]{:S(2)}) collective-permute-start(bf16[256,1024]{1,0:T(8,128)(2,1)S(1)} %collective-permute-done.1.refs_1_), channel_id=1, source_target_pairs={{0,32},{32,64},{64,96},{96,128},{128,160},{160,192},{192,224},{224... | collective-permute-start | bytes 1572872 | tf_op jit(solution)/shard_map/ppermute | solution.py:42
  28.2 8.0 %collective-permute-done.2.refs_2_ = bf16[256,1024]{1,0:T(8,128)(2,1)S(1)} collective-permute-done((bf16[256,1024]{1,0:T(8,128)(2,1)S(1)}, bf16[256,1024]{1,0:T(8,128)(2,1)S(1)}, u32[]{:S(2)}, u32[]{:S(2)}) %collective-permute-start.2) | collective-permute-done | bytes 524320 | tf_op jit(solution)/shard_map/ppermute | solution.py:42
  36.2 3.4 %collective-permute-start.3 = (bf16[256,1024]{1,0:T(8,128)(2,1)S(1)}, bf16[256,1024]{1,0:T(8,128)(2,1)S(1)}, u32[]{:S(2)}, u32[]{:S(2)}) collective-permute-start(bf16[256,1024]{1,0:T(8,128)(2,1)S(1)} %collective-permute-done.2.refs_2_), channel_id=1, source_target_pairs={{0,32},{32,64},{64,96},{96,128},{128,160},{160,192},{192,224},{224... | collective-permute-start | bytes 1572872 | tf_op jit(solution)/shard_map/ppermute | solution.py:42
  39.6 3.6 %all-to-all-done = bf16[16,128,128]{2,1,0:T(8,128)(2,1)S(1)} async-done(((bf16[16,128,128]{2,1,0:T(8,128)(2,1)}), bf16[16,128,128]{2,1,0:T(8,128)(2,1)S(1)}, u32[]{:S(2)}, u32[]{:S(2)}) %all-to-all-start) | async-done | bytes 524320 | tf_op jit(solution)/shard_map/all_to_all | solution.py:35
  43.2 1.2 broadcast_in_dim.8
  44.5 4.0 %all-to-all-start.1 = ((bf16[4,4,2,128,128]{4,3,2,1,0:T(8,128)(2,1)}), bf16[4,4,2,128,128]{4,3,2,1,0:T(8,128)(2,1)S(1)}, u32[]{:S(2)}, u32[]{:S(2)}) async-start(bf16[4,4,2,128,128]{4,3,2,1,0:T(8,128)(2,1)} %bitcast.10), calls=%async_computation.1 | async-start | bytes 2097152 | tf_op jit(solution)/shard_map/all_to_all | solution.py:35
  48.5 1.9 %collective-permute-start.4 = (bf16[256,1024]{1,0:T(8,128)(2,1)S(1)}, bf16[256,1024]{1,0:T(8,128)(2,1)S(1)}, u32[]{:S(2)}, u32[]{:S(2)}) collective-permute-start(bf16[256,1024]{1,0:T(8,128)(2,1)S(1)} %collective-permute-done.1.refs_1_), channel_id=1, source_target_pairs={{0,1},{1,0},{2,3},{3,2},{4,5},{5,4},{6,7},{7,6},{8,9},{9,8},{10,11... | collective-permute-start | bytes 1572872 | tf_op jit(solution)/shard_map/ppermute | solution.py:31
  50.4 2.4 %collective-permute-start.5 = (bf16[256,1024]{1,0:T(8,128)(2,1)S(1)}, bf16[256,1024]{1,0:T(8,128)(2,1)}, u32[]{:S(2)}, u32[]{:S(2)}) collective-permute-start(bf16[256,1024]{1,0:T(8,128)(2,1)S(1)} %collective-permute-done.2.refs_2_), channel_id=1, source_target_pairs={{0,1},{1,0},{2,3},{3,2},{4,5},{5,4},{6,7},{7,6},{8,9},{9,8},{10,11... | collective-permute-start | bytes 1572872 | tf_op jit(solution)/shard_map/ppermute | solution.py:31
  52.8 0.0 collective-permute-done.3.in_ref.refs_3_
  52.9 2.2 %collective-permute-start.7 = (bf16[128,1024]{1,0:T(8,128)(2,1)S(1)}, bf16[128,1024]{1,0:T(8,128)(2,1)S(1)}, u32[]{:S(2)}, u32[]{:S(2)}) collective-permute-start(bf16[128,1024]{1,0:T(8,128)(2,1)S(1)} %shard_map.52), channel_id=1, source_target_pairs={{0,32},{32,64},{64,96},{96,128},{128,160},{160,192},{192,224},{224... | collective-permute-start | bytes 786440 | tf_op jit(solution)/shard_map/ppermute | solution.py:42
  55.1 1.9 %collective-permute-start.6 = (bf16[256,1024]{1,0:T(8,128)(2,1)S(1)}, bf16[256,1024]{1,0:T(8,128)(2,1)}, u32[]{:S(2)}, u32[]{:S(2)}) collective-permute-start(bf16[256,1024]{1,0:T(8,128)(2,1)S(1)} %collective-permute-done.3.in_ref.refs_3_), channel_id=1, source_target_pairs={{0,1},{1,0},{2,3},{3,2},{4,5},{5,4},{6,7},{7,6},{8,9},{9,8},{10,11... | collective-permute-start | bytes 1572872 | tf_op jit(solution)/shard_map/ppermute | solution.py:31
  57.0 3.3 %collective-permute-done.7.refs_7_ = bf16[128,1024]{1,0:T(8,128)(2,1)S(1)} collective-permute-done((bf16[128,1024]{1,0:T(8,128)(2,1)S(1)}, bf16[128,1024]{1,0:T(8,128)(2,1)S(1)}, u32[]{:S(2)}, u32[]{:S(2)}) %collective-permute-start.7) | collective-permute-done | bytes 262176 | tf_op jit(solution)/shard_map/ppermute | solution.py:42
  60.3 4.0 %collective-permute-start.8 = (bf16[128,1024]{1,0:T(8,128)(2,1)S(1)}, bf16[128,1024]{1,0:T(8,128)(2,1)}, u32[]{:S(2)}, u32[]{:S(2)}) collective-permute-start(bf16[128,1024]{1,0:T(8,128)(2,1)S(1)} %collective-permute-done.7.refs_7_), channel_id=1, source_target_pairs={{0,1},{1,0},{2,3},{3,2},{4,5},{5,4},{6,7},{7,6},{8,9},{9,8},{10,11... | collective-permute-start | bytes 786440 | tf_op jit(solution)/shard_map/ppermute | solution.py:31
  64.3 0.0 collective-permute-done.4.refs_4_
  64.3 0.0 copy-start
  64.3 0.8 copy-done
  65.1 0.0 all-to-all-done.1
  65.1 0.0 collective-permute-done.5.refs_5_
  65.1 0.4 collective-permute-done.8.refs_8_
  65.5 0.0 collective-permute-done.6.refs_6_
  65.5 0.0 copy-start.1
  65.5 1.0 copy-done.1
  66.6 2.5 %shard_map.53 = (f32[128,1024]{1,0:T(8,128)S(1)}, bf16[128,1024]{1,0:T(8,128)(2,1)S(1)}) custom-call(bf16[2,2,4,2,128,128]{5,4,3,2,1,0:T(8,128)(2,1)S(1)} %bitcast.8, bf16[256,1024]{1,0:T(8,128)(2,1)S(1)} %shard_map.51.refs_0_, bf16[256,1024]{1,0:T(8,128)(2,1)S(1)} %collective-permute-done.1.refs_1_, bf16[256,1024]{1,0:T(8,128)(2,1)S(1)} %collective-permute-done.2.refs_2_, ...), custom_call_target="tpu_custom_call" | custom-call | tf_op jit(solution)/shard_map/pallas_call | solution.py:20
  69.1 3.4 %collective-permute-start.9 = (bf16[128,1024]{1,0:T(8,128)(2,1)S(1)}, bf16[128,1024]{1,0:T(8,128)(2,1)S(1)}, u32[]{:S(2)}, u32[]{:S(2)}) collective-permute-start(bf16[128,1024]{1,0:T(8,128)(2,1)S(1)} %get-tuple-element.9), channel_id=1, source_target_pairs={{0,256},{256,0},{1,257},{257,1},{2,258},{258,2},{3,259},{259,3},{4... | collective-permute-start | bytes 786440 | tf_op jit(solution)/shard_map/ppermute | solution.py:31
  72.5 6.0 %collective-permute-done.9.arrived_ref = bf16[128,1024]{1,0:T(8,128)(2,1)S(1)} collective-permute-done((bf16[128,1024]{1,0:T(8,128)(2,1)S(1)}, bf16[128,1024]{1,0:T(8,128)(2,1)S(1)}, u32[]{:S(2)}, u32[]{:S(2)}) %collective-permute-start.9) | collective-permute-done | bytes 262176 | tf_op jit(solution)/shard_map/ppermute | solution.py:31
  78.5 0.7 shard_map.54.own_ref
  79.3 3.3 %collective-permute-start.10 = (bf16[128,1024]{1,0:T(8,128)(2,1)}, bf16[128,1024]{1,0:T(8,128)(2,1)S(1)}, u32[]{:S(2)}, u32[]{:S(2)}) collective-permute-start(bf16[128,1024]{1,0:T(8,128)(2,1)} %shard_map.54.own_ref), channel_id=1, source_target_pairs={{0,256},{256,0},{1,257},{257,1},{2,258},{258,2},{3,259},{259,3},{4... | collective-permute-start | bytes 786440 | tf_op jit(solution)/shard_map/ppermute | solution.py:31
  82.6 6.7 %all-to-all-start.3 = ((bf16[16,8,1024]{2,1,0:T(8,128)(2,1)}), bf16[16,8,1024]{2,1,0:T(8,128)(2,1)S(1)}, u32[]{:S(2)}, u32[]{:S(2)}) async-start(bf16[16,8,1024]{2,1,0:T(8,128)(2,1)} %bitcast.7), calls=%async_computation.3 | async-start | bytes 524288 | tf_op jit(solution)/shard_map/all_to_all | solution.py:35
  89.3 0.0 collective-permute-done.10.other_ref
  89.3 0.0 copy-start.2
  89.4 1.0 copy-done.2
  90.4 2.7 %shard_map.55 = (bf16[4,2,128,128]{3,2,1,0:T(8,128)(2,1)S(1)}, bf16[4,2,128,128]{3,2,1,0:T(8,128)(2,1)S(1)}, bf16[4,2,128,128]{3,2,1,0:T(8,128)(2,1)S(1)}, bf16[4,2,128,128]{3,2,1,0:T(8,128)(2,1)S(1)}) custom-call(bf16[128,1024]{1,0:T(8,128)(2,1)} %shard_map.54.own_ref, bf16[128,1024]{1,0:T(8,128)(2,1)S(1)} %collective-permute-done.10.other_ref, ...), custom_call_target="tpu_custom_call" | custom-call | tf_op jit(solution)/shard_map/pallas_call | solution.py:188
  93.1 4.8 %collective-permute-start.11 = (bf16[4,2,128,128]{3,2,1,0:T(8,128)(2,1)S(1)}, bf16[4,2,128,128]{3,2,1,0:T(8,128)(2,1)S(1)}, u32[]{:S(2)}, u32[]{:S(2)}) collective-permute-start(bf16[4,2,128,128]{3,2,1,0:T(8,128)(2,1)S(1)} %get-tuple-element.11), channel_id=1, source_target_pairs={{0,2},{256,258},{2,0},{258,256},{1,3},{257,259},{3,1},{259,257},{4... | collective-permute-start | bytes 786440 | tf_op jit(solution)/shard_map/ppermute | solution.py:47
  97.9 1.9 %collective-permute-start.12 = (bf16[4,2,128,128]{3,2,1,0:T(8,128)(2,1)S(1)}, bf16[4,2,128,128]{3,2,1,0:T(8,128)(2,1)S(1)}, u32[]{:S(2)}, u32[]{:S(2)}) collective-permute-start(bf16[4,2,128,128]{3,2,1,0:T(8,128)(2,1)S(1)} %get-tuple-element.12), channel_id=1, source_target_pairs={{0,256},{256,2},{2,258},{258,0},{1,257},{257,3},{3,259},{259,1},{4... | collective-permute-start | bytes 786440 | tf_op jit(solution)/shard_map/ppermute | solution.py:47
  99.8 4.6 %collective-permute-start.13 = (bf16[4,2,128,128]{3,2,1,0:T(8,128)(2,1)S(1)}, bf16[4,2,128,128]{3,2,1,0:T(8,128)(2,1)S(1)}, u32[]{:S(2)}, u32[]{:S(2)}) collective-permute-start(bf16[4,2,128,128]{3,2,1,0:T(8,128)(2,1)S(1)} %get-tuple-element.13), channel_id=1, source_target_pairs={{0,258},{256,0},{2,256},{258,2},{1,259},{257,1},{3,257},{259,3},{4... | collective-permute-start | bytes 786440 | tf_op jit(solution)/shard_map/ppermute | solution.py:47
  104.4 0.0 collective-permute-done.11.far_ref
  104.4 6.0 %collective-permute-done.12.left_ref = bf16[4,2,128,128]{3,2,1,0:T(8,128)(2,1)S(1)} collective-permute-done((bf16[4,2,128,128]{3,2,1,0:T(8,128)(2,1)S(1)}, bf16[4,2,128,128]{3,2,1,0:T(8,128)(2,1)S(1)}, u32[]{:S(2)}, u32[]{:S(2)}) %collective-permute-start.12) | collective-permute-done | bytes 262176 | tf_op jit(solution)/shard_map/ppermute | solution.py:47
  110.4 0.0 collective-permute-done.13.right_ref
  110.4 0.9 shard_map.56
  111.4 0.0 all-to-all-done.3.got_ref
  111.4 7.9 %all-to-all-start.2 = ((bf16[16,128,128]{2,1,0:T(8,128)(2,1)}), bf16[16,128,128]{2,1,0:T(8,128)(2,1)S(1)}, u32[]{:S(2)}, u32[]{:S(2)}) async-start(bf16[16,128,128]{2,1,0:T(8,128)(2,1)} %bitcast.4), calls=%async_computation.2 | async-start | bytes 1048576 | tf_op jit(solution)/shard_map/all_to_all | solution.py:35
  119.2 3.0 %shard_map.58 = bf16[8,20480]{1,0:T(8,128)(2,1)} custom-call(bf16[16,8,1024]{2,1,0:T(8,128)(2,1)S(1)} %all-to-all-done.3.got_ref, bf16[1024,1280]{1,0:T(8,128)(2,1)} %coef_ref.1), custom_call_target="tpu_custom_call" | custom-call | tf_op jit(solution)/shard_map/pallas_call | solution.py:209
  122.2 14.2 %all-to-all-done.2 = bf16[16,128,128]{2,1,0:T(8,128)(2,1)S(1)} async-done(((bf16[16,128,128]{2,1,0:T(8,128)(2,1)}), bf16[16,128,128]{2,1,0:T(8,128)(2,1)S(1)}, u32[]{:S(2)}, u32[]{:S(2)}) %all-to-all-start.2) | async-done | bytes 524320 | tf_op jit(solution)/shard_map/all_to_all | solution.py:35
  136.4 0.7 shard_map.57
  (1 shorter events, 0.0 us)
Async XLA Ops:
  0.6 10.1 %collective-permute-start = (bf16[256,512]{1,0:T(8,128)(2,1)}, bf16[256,512]{1,0:T(8,128)(2,1)S(1)}, u32[]{:S(2)}, u32[]{:S(2)}) collective-permute-start(bf16[256,512]{1,0:T(8,128)(2,1)} %amp_ref.1), channel_id=1, source_target_pairs={{0,1},{1,0},{2,3},{3,2},{4,5},{5,4},{6,7},{7,6},{8,9},{9,8},{10,11... | collective-permute-start | bytes 786440 | tf_op jit(solution)/shard_map/ppermute | solution.py:31
  10.7 0.9 copy-start.3
  11.7 14.3 %collective-permute-start.1 = (bf16[256,1024]{1,0:T(8,128)(2,1)S(1)}, bf16[256,1024]{1,0:T(8,128)(2,1)S(1)}, u32[]{:S(2)}, u32[]{:S(2)}) collective-permute-start(bf16[256,1024]{1,0:T(8,128)(2,1)S(1)} %shard_map.51.refs_0_), channel_id=1, source_target_pairs={{0,32},{32,64},{64,96},{96,128},{128,160},{160,192},{192,224},{224... | collective-permute-start | bytes 1572872 | tf_op jit(solution)/shard_map/ppermute | solution.py:42
  17.1 0.8 copy-start.4
  18.8 24.4 %all-to-all-start = ((bf16[16,128,128]{2,1,0:T(8,128)(2,1)}), bf16[16,128,128]{2,1,0:T(8,128)(2,1)S(1)}, u32[]{:S(2)}, u32[]{:S(2)}) async-start(bf16[16,128,128]{2,1,0:T(8,128)(2,1)} %bitcast), calls=%async_computation | async-start | bytes 1048576 | tf_op jit(solution)/shard_map/all_to_all | solution.py:35
  26.0 10.2 %collective-permute-start.2 = (bf16[256,1024]{1,0:T(8,128)(2,1)S(1)}, bf16[256,1024]{1,0:T(8,128)(2,1)S(1)}, u32[]{:S(2)}, u32[]{:S(2)}) collective-permute-start(bf16[256,1024]{1,0:T(8,128)(2,1)S(1)} %collective-permute-done.1.refs_1_), channel_id=1, source_target_pairs={{0,32},{32,64},{64,96},{96,128},{128,160},{160,192},{192,224},{224... | collective-permute-start | bytes 1572872 | tf_op jit(solution)/shard_map/ppermute | solution.py:42
  36.2 16.6 %collective-permute-start.3 = (bf16[256,1024]{1,0:T(8,128)(2,1)S(1)}, bf16[256,1024]{1,0:T(8,128)(2,1)S(1)}, u32[]{:S(2)}, u32[]{:S(2)}) collective-permute-start(bf16[256,1024]{1,0:T(8,128)(2,1)S(1)} %collective-permute-done.2.refs_2_), channel_id=1, source_target_pairs={{0,32},{32,64},{64,96},{96,128},{128,160},{160,192},{192,224},{224... | collective-permute-start | bytes 1572872 | tf_op jit(solution)/shard_map/ppermute | solution.py:42
  44.5 20.6 %all-to-all-start.1 = ((bf16[4,4,2,128,128]{4,3,2,1,0:T(8,128)(2,1)}), bf16[4,4,2,128,128]{4,3,2,1,0:T(8,128)(2,1)S(1)}, u32[]{:S(2)}, u32[]{:S(2)}) async-start(bf16[4,4,2,128,128]{4,3,2,1,0:T(8,128)(2,1)} %bitcast.10), calls=%async_computation.1 | async-start | bytes 2097152 | tf_op jit(solution)/shard_map/all_to_all | solution.py:35
  48.5 15.8 %collective-permute-start.4 = (bf16[256,1024]{1,0:T(8,128)(2,1)S(1)}, bf16[256,1024]{1,0:T(8,128)(2,1)S(1)}, u32[]{:S(2)}, u32[]{:S(2)}) collective-permute-start(bf16[256,1024]{1,0:T(8,128)(2,1)S(1)} %collective-permute-done.1.refs_1_), channel_id=1, source_target_pairs={{0,1},{1,0},{2,3},{3,2},{4,5},{5,4},{6,7},{7,6},{8,9},{9,8},{10,11... | collective-permute-start | bytes 1572872 | tf_op jit(solution)/shard_map/ppermute | solution.py:31
  50.4 14.7 %collective-permute-start.5 = (bf16[256,1024]{1,0:T(8,128)(2,1)S(1)}, bf16[256,1024]{1,0:T(8,128)(2,1)}, u32[]{:S(2)}, u32[]{:S(2)}) collective-permute-start(bf16[256,1024]{1,0:T(8,128)(2,1)S(1)} %collective-permute-done.2.refs_2_), channel_id=1, source_target_pairs={{0,1},{1,0},{2,3},{3,2},{4,5},{5,4},{6,7},{7,6},{8,9},{9,8},{10,11... | collective-permute-start | bytes 1572872 | tf_op jit(solution)/shard_map/ppermute | solution.py:31
  52.9 7.4 %collective-permute-start.7 = (bf16[128,1024]{1,0:T(8,128)(2,1)S(1)}, bf16[128,1024]{1,0:T(8,128)(2,1)S(1)}, u32[]{:S(2)}, u32[]{:S(2)}) collective-permute-start(bf16[128,1024]{1,0:T(8,128)(2,1)S(1)} %shard_map.52), channel_id=1, source_target_pairs={{0,32},{32,64},{64,96},{96,128},{128,160},{160,192},{192,224},{224... | collective-permute-start | bytes 786440 | tf_op jit(solution)/shard_map/ppermute | solution.py:42
  55.1 10.5 %collective-permute-start.6 = (bf16[256,1024]{1,0:T(8,128)(2,1)S(1)}, bf16[256,1024]{1,0:T(8,128)(2,1)}, u32[]{:S(2)}, u32[]{:S(2)}) collective-permute-start(bf16[256,1024]{1,0:T(8,128)(2,1)S(1)} %collective-permute-done.3.in_ref.refs_3_), channel_id=1, source_target_pairs={{0,1},{1,0},{2,3},{3,2},{4,5},{5,4},{6,7},{7,6},{8,9},{9,8},{10,11... | collective-permute-start | bytes 1572872 | tf_op jit(solution)/shard_map/ppermute | solution.py:31
  60.3 5.3 %collective-permute-start.8 = (bf16[128,1024]{1,0:T(8,128)(2,1)S(1)}, bf16[128,1024]{1,0:T(8,128)(2,1)}, u32[]{:S(2)}, u32[]{:S(2)}) collective-permute-start(bf16[128,1024]{1,0:T(8,128)(2,1)S(1)} %collective-permute-done.7.refs_7_), channel_id=1, source_target_pairs={{0,1},{1,0},{2,3},{3,2},{4,5},{5,4},{6,7},{7,6},{8,9},{9,8},{10,11... | collective-permute-start | bytes 786440 | tf_op jit(solution)/shard_map/ppermute | solution.py:31
  64.3 0.8 copy-start
  65.5 1.0 copy-start.1
  69.1 9.4 %collective-permute-start.9 = (bf16[128,1024]{1,0:T(8,128)(2,1)S(1)}, bf16[128,1024]{1,0:T(8,128)(2,1)S(1)}, u32[]{:S(2)}, u32[]{:S(2)}) collective-permute-start(bf16[128,1024]{1,0:T(8,128)(2,1)S(1)} %get-tuple-element.9), channel_id=1, source_target_pairs={{0,256},{256,0},{1,257},{257,1},{2,258},{258,2},{3,259},{259,3},{4... | collective-permute-start | bytes 786440 | tf_op jit(solution)/shard_map/ppermute | solution.py:31
  79.3 10.1 %collective-permute-start.10 = (bf16[128,1024]{1,0:T(8,128)(2,1)}, bf16[128,1024]{1,0:T(8,128)(2,1)S(1)}, u32[]{:S(2)}, u32[]{:S(2)}) collective-permute-start(bf16[128,1024]{1,0:T(8,128)(2,1)} %shard_map.54.own_ref), channel_id=1, source_target_pairs={{0,256},{256,0},{1,257},{257,1},{2,258},{258,2},{3,259},{259,3},{4... | collective-permute-start | bytes 786440 | tf_op jit(solution)/shard_map/ppermute | solution.py:31
  82.6 28.8 %all-to-all-start.3 = ((bf16[16,8,1024]{2,1,0:T(8,128)(2,1)}), bf16[16,8,1024]{2,1,0:T(8,128)(2,1)S(1)}, u32[]{:S(2)}, u32[]{:S(2)}) async-start(bf16[16,8,1024]{2,1,0:T(8,128)(2,1)} %bitcast.7), calls=%async_computation.3 | async-start | bytes 524288 | tf_op jit(solution)/shard_map/all_to_all | solution.py:35
  89.3 1.0 copy-start.2
  93.1 11.3 %collective-permute-start.11 = (bf16[4,2,128,128]{3,2,1,0:T(8,128)(2,1)S(1)}, bf16[4,2,128,128]{3,2,1,0:T(8,128)(2,1)S(1)}, u32[]{:S(2)}, u32[]{:S(2)}) collective-permute-start(bf16[4,2,128,128]{3,2,1,0:T(8,128)(2,1)S(1)} %get-tuple-element.11), channel_id=1, source_target_pairs={{0,2},{256,258},{2,0},{258,256},{1,3},{257,259},{3,1},{259,257},{4... | collective-permute-start | bytes 786440 | tf_op jit(solution)/shard_map/ppermute | solution.py:47
  97.9 12.5 %collective-permute-start.12 = (bf16[4,2,128,128]{3,2,1,0:T(8,128)(2,1)S(1)}, bf16[4,2,128,128]{3,2,1,0:T(8,128)(2,1)S(1)}, u32[]{:S(2)}, u32[]{:S(2)}) collective-permute-start(bf16[4,2,128,128]{3,2,1,0:T(8,128)(2,1)S(1)} %get-tuple-element.12), channel_id=1, source_target_pairs={{0,256},{256,2},{2,258},{258,0},{1,257},{257,3},{3,259},{259,1},{4... | collective-permute-start | bytes 786440 | tf_op jit(solution)/shard_map/ppermute | solution.py:47
  99.8 10.6 %collective-permute-start.13 = (bf16[4,2,128,128]{3,2,1,0:T(8,128)(2,1)S(1)}, bf16[4,2,128,128]{3,2,1,0:T(8,128)(2,1)S(1)}, u32[]{:S(2)}, u32[]{:S(2)}) collective-permute-start(bf16[4,2,128,128]{3,2,1,0:T(8,128)(2,1)S(1)} %get-tuple-element.13), channel_id=1, source_target_pairs={{0,258},{256,0},{2,256},{258,2},{1,259},{257,1},{3,257},{259,3},{4... | collective-permute-start | bytes 786440 | tf_op jit(solution)/shard_map/ppermute | solution.py:47
  111.4 25.1 %all-to-all-start.2 = ((bf16[16,128,128]{2,1,0:T(8,128)(2,1)}), bf16[16,128,128]{2,1,0:T(8,128)(2,1)S(1)}, u32[]{:S(2)}, u32[]{:S(2)}) async-start(bf16[16,128,128]{2,1,0:T(8,128)(2,1)} %bitcast.4), calls=%async_computation.2 | async-start | bytes 1048576 | tf_op jit(solution)/shard_map/all_to_all | solution.py:35

commit v7 on v6

--- a/solution.py
+++ b/solution.py
@@ -47,16 +47,18 @@
     return lax.ppermute(x, ("xl", "xh"), [(at(i), at((i + by) % 4)) for i in range(4)])
 
 
-def blocks_of(refs):
-    c = lax.axis_index("c")
-    toward = 2 * c - 1
-    blocks = [(0, refs[0][...])]
-    for s in range(1, 4):
-        blocks += [(toward * s, refs[s][...]), (-toward * s, refs[3 + s][...])]
-    mine, got = refs[7][...], refs[8][...]
-    first = jnp.where(c == 0, mine, got)
-    second = jnp.where(c == 0, got, mine)
-    return blocks + [(4, jnp.concatenate([first, second], axis=0))]
+def with_blocks(near_refs, swap_refs, bufs, sems, use):
+    toward = 2 * lax.axis_index("c") - 1
+    copies = [
+        pltpu.make_async_copy(ref, bufs.at[i], sems.at[i]) for i, ref in enumerate(swap_refs)
+    ]
+    for copy in copies:
+        copy.start()
+    near = [(toward * s, ref[...]) for s, ref in enumerate(near_refs)]
+    use(near)
+    for copy in copies:
+        copy.wait()
+    use([(-toward * (i + 1), bufs[i]) for i in range(len(copies))])
 
 
 def place(offset):
@@ -81,43 +83,51 @@
             out_ref[i, c] = part
 
 
-def half_kernel(in_ref, out_ref):
-    rows = out_ref.shape[0]
-    out_ref[...] = in_ref[pl.ds(pl.multiple_of(lax.axis_index("c") * rows, rows), rows)]
-
-
 def fitted_kernel(metric_ref, *refs):
-    blocks = blocks_of(refs[:-2])
-    own_ref, away_ref = refs[-2:]
+    near_refs, swap_refs = refs[:5], refs[5:8]
+    wide_refs, narrow_refs, (bufs, sems) = refs[8:10], refs[10:12], refs[12:]
     xl = lax.axis_index("xl")
-    rhs = jnp.concatenate([b for _, b in blocks], axis=0)
-    for h, ref in ((xl, own_ref), (1 - xl, away_ref)):
-        lhs = [metric_ref[(h, *place(o), j)] for o, _ in blocks for j in range(2)]
-        out = jnp.dot(jnp.concatenate(lhs, axis=1), rhs, preferred_element_type=F32)
-        ref[...] = out.astype(ref.dtype)
+    sums = [None, None]
+
+    def use(blocks):
+        rhs = jnp.concatenate([b for _, b in blocks], axis=0)
+        for i, h in enumerate((xl, 1 - xl)):
+            lhs = [metric_ref[(h, *place(o), j)] for o, _ in blocks for j in range(2)]
+            out = jnp.dot(jnp.concatenate(lhs, axis=1), rhs, preferred_element_type=F32)
+            sums[i] = out if sums[i] is None else sums[i] + out
+
+    with_blocks(near_refs, swap_refs, bufs, sems, use)
+    for i in range(2):
+        wide_refs[i][...] = sums[i]
+        narrow_refs[i][...] = sums[i].astype(BF16)
 
 
 def join_kernel(own_ref, arrived_ref, out_ref):
     out_ref[...] = (own_ref[...] + arrived_ref[...].astype(F32)).astype(BF16)
 
 
-def density_kernel(own_ref, other_ref, *refs):
-    blocks = blocks_of(refs[:-5])
-    outs, all_ref = refs[-5:-1], refs[-1]
+def density_kernel(own_ref, other_ref, arrived_ref, *refs):
+    near_refs, swap_refs, outs = refs[:5], refs[5:8], refs[8:12]
+    all_ref, bufs, sems = refs[12:]
     xl = lax.axis_index("xl")
     x = 2 * lax.axis_index("xh") + xl
-    lhs = jnp.concatenate([own_ref[...], other_ref[...]], axis=0)
+    other = (other_ref[...] + arrived_ref[...].astype(F32)).astype(BF16)
+    lhs = jnp.concatenate([own_ref[...], other], axis=0)
     rows = own_ref.shape[0]
-    for offset, block in blocks:
-        out = lax.dot_general(
-            lhs, block, (((1,), (1,)), ((), ())), preferred_element_type=F32
-        ).astype(BF16)
-        far, near = place(offset)
-        half = out.shape[1] // 2
-        for h, part in ((xl, out[:rows]), (1 - xl, out[rows:])):
-            slot = lax.rem(2 * far + h + 4 - x, 4)
-            for j in range(2):
-                all_ref[slot, near, j] = part[:, j * half : (j + 1) * half]
+
+    def use(blocks):
+        for offset, block in blocks:
+            out = lax.dot_general(
+                lhs, block, (((1,), (1,)), ((), ())), preferred_element_type=F32
+            ).astype(BF16)
+            far, near = place(offset)
+            half = out.shape[1] // 2
+            for h, part in ((xl, out[:rows]), (1 - xl, out[rows:])):
+                slot = lax.rem(2 * far + h + 4 - x, 4)
+                for j in range(2):
+                    all_ref[slot, near, j] = part[:, j * half : (j + 1) * half]
+
+    with_blocks(near_refs, swap_refs, bufs, sems, use)
     for s in range(4):
         outs[s][...] = all_ref[s]
 
@@ -173,27 +183,41 @@
     for _ in range(1, 4):
         steps.append(ring_step(steps[-1]))
     swaps = [shifted(steps[s], "c", 1) for s in range(1, 4)]
-    (farther,) = in_vmem(half_kernel, [((half, 2 * cols), BF16)], steps[3])
-    far = ring_step(farther)
-    blocks = steps + swaps + [far, shifted(far, "c", 1)]
-
-    own, away = in_vmem(
-        fitted_kernel, [((half, 2 * cols), F32), ((half, 2 * cols), BF16)], part, *blocks
+    steps.append(ring_step(steps[3]))
+    in_hbm = [pltpu.with_memory_space_constraint(a, pltpu.HBM) for a in swaps]
+    shape = (half, 2 * cols)
+    buffers = [pltpu.VMEM((3, rows, 2 * cols), BF16), pltpu.SemaphoreType.DMA((3,))]
+
+    def on_blocks(kernel, outs, scratch, *args):
+        spaces = [pltpu.HBM if a.dtype == F32 else pltpu.VMEM for a in args] + [pltpu.VMEM] * 5
+        args = map(pltpu.with_memory_space_constraint, (*args, *steps), spaces)
+        args = list(args)
+        return pl.pallas_call(
+            kernel,
+            in_specs=[VMEM] * len(args) + [pl.BlockSpec(memory_space=pl.ANY)] * 3,
+            out_specs=[VMEM] * len(outs),
+            out_shape=[space(shape, dtype) for space, shape, dtype in outs],
+            scratch_shapes=scratch + buffers,
+            compiler_params=PARAMS,
+        )(*args, *in_hbm)
+
+    own, other, own_sent, other_sent = on_blocks(
+        fitted_kernel,
+        [(pltpu.VMEM, shape, F32), (pltpu.HBM, shape, F32)] + [(pltpu.VMEM, shape, BF16)] * 2,
+        [],
+        part,
     )
-    arrived = shifted(away, "xl", 1)
-    (fitted,) = in_vmem(join_kernel, [((half, 2 * cols), BF16)], own, arrived)
-    other = shifted(fitted, "xl", 1)
-    args = [pltpu.with_memory_space_constraint(a, pltpu.VMEM) for a in (fitted, other, *blocks)]
+    own_arrived = shifted(other_sent, "xl", 1)
+    other_arrived = shifted(own_sent, "xl", 1)
+    (fitted,) = in_vmem(join_kernel, [(shape, BF16)], own, own_arrived)
     piece = (4, 2, half, half)
-    slots = pl.pallas_call(
+    slots = on_blocks(
         density_kernel,
-        in_specs=[VMEM] * len(args),
-        out_specs=[VMEM] * 4,
-        out_shape=[pltpu.VMEM(piece, BF16)] * 4,
-        scratch_shapes=[pltpu.VMEM((4, *piece), BF16)],
-        compiler_params=PARAMS,
-    )(*args)
-    arrived = [shifted_x(slots[s], s) for s in (2, 1, 3)]
+        [(pltpu.VMEM, piece, BF16)] * 4,
+        [pltpu.VMEM((4, *piece), BF16)],
+        fitted, other, other_arrived,
+    )
+    arrived = [shifted_x(slots[s], s) for s in (2, 3, 1)]
     (xs,) = in_vmem(half_sum_kernel, [((8, 2, half, half), BF16)], slots[0], *arrived)
     got = exchange(xs.reshape(16, half, half), ("y", "c"))
     density = pl.pallas_call(

time: 138 us -> 139 us (level)
  Pallas kernels: 11.6 us -> 15.1 us
  local copies, waits for them, and re-layouts: 5.91 us -> 3.01 us
    all_to_all x4, waiting for transfers between devices: 17.8 us -> 24.3 us  [exchange(): return lax.all_to_all(x, axes, split_axis=0, concat_axis=0, tiled=True)]
    pallas_call x1 -> x2, Pallas kernels: 2.71 us -> 8.85 us  [on_blocks(): pl.pallas_call(kernel, in_specs=[VMEM] * len(args) + [pl.BlockSpec(memory...]
    all_to_all x4, starting transfers between devices: 25.8 us -> 31.7 us  [exchange(): return lax.all_to_all(x, axes, split_axis=0, concat_axis=0, tiled=True)]
    ppermute x7 -> x6, starting transfers between devices: 25.7 us -> 20.3 us  [shifted(): return lax.ppermute(x, axis, [(i, (i + by) % n) for i in range(n)])]
    ppermute x7 -> x6, waiting for transfers between devices: 7.83 us -> 3.18 us  [shifted(): return lax.ppermute(x, axis, [(i, (i + by) % n) for i in range(n)])]
    unnamed x10 -> x4, local copies, waits for them, and re-layouts: 4.66 us -> 1.78 us
    pallas_call x5 -> x3, Pallas kernels: 4.29 us -> 1.73 us  [in_vmem(): pl.pallas_call(kernel, in_specs=[VMEM] * len(args), out_specs=[VMEM] * le...]
    ppermute x4, waiting for transfers between devices: 11.3 us -> 9.59 us  [ring_step(): return lax.ppermute(x, ('z', 'c'), moves)]
  transfers between devices with their start and end apart: 18 -> 17, of which waited for: 8 -> 10; matrix products, arithmetic and copies ran while one was open for 1% -> 1% of each run, Pallas kernels for 5% -> 7%
where the time goes in v7:
time: 139 us; the launch traced here: 138 us
  starting transfers between devices  75.2 us (54%)
  waiting for transfers between devices  43.8 us (32%)
  Pallas kernels  15.1 us (11%)
  local copies, waits for them, and re-layouts  3.01 us (2%)
    all_to_all x4, starting transfers between devices, exchange(): return lax.all_to_all(x, axes, split_axis=0, concat_axis=0, tiled=True)  31.7 us
    all_to_all x4, waiting for transfers between devices, exchange(): return lax.all_to_all(x, axes, split_axis=0, concat_axis=0, tiled=True)  24.3 us
    ppermute x6, starting transfers between devices, shifted(): return lax.ppermute(x, axis, [(i, (i + by) % n) for i in range(n)])  20.3 us
    ppermute x4, starting transfers between devices, ring_step(): return lax.ppermute(x, ('z', 'c'), moves)  13.1 us
    ppermute x3, starting transfers between devices, shifted_x(): lax.ppermute(x, ('xl', 'xh'), [(at(i), at((i + by) % 4)) for i in range(4)])  10.1 us
    ppermute x4, waiting for transfers between devices, ring_step(): return lax.ppermute(x, ('z', 'c'), moves)  9.59 us
    pallas_call x2, Pallas kernels, on_blocks(): pl.pallas_call(kernel, in_specs=[VMEM] * len(args) + [pl.BlockSpec(memory...  8.85 us
    ppermute x3, waiting for transfers between devices, shifted_x(): lax.ppermute(x, ('xl', 'xh'), [(at(i), at((i + by) % 4)) for i in range(4)])  6.68 us
  transfers between devices with their start and end apart: 17, of which 10 were waited for; matrix products, arithmetic and copies ran while one was open for 1% of the time, Pallas kernels for 7%

profile of v7, /device:TPU:1, one launch (start us, length us, event | category | flops | bytes accessed | tf_op | source)
XLA Modules:
  0.0 137.9 jit_solution(14707991758060783451)
XLA Ops:
  0.6 8.7 %collective-permute-start = (bf16[256,512]{1,0:T(8,128)(2,1)}, bf16[256,512]{1,0:T(8,128)(2,1)S(1)}, u32[]{:S(2)}, u32[]{:S(2)}) collective-permute-start(bf16[256,512]{1,0:T(8,128)(2,1)} %amp_ref.1), channel_id=1, source_target_pairs={{0,1},{1,0},{2,3},{3,2},{4,5},{5,4},{6,7},{7,6},{8,9},{9,8},{10,11... | collective-permute-start | bytes 786440 | tf_op jit(solution)/shard_map/ppermute | solution.py:31
  9.4 1.4 collective-permute-done.got_ref
  10.7 0.0 copy-start
  10.7 0.9 copy-done
  11.7 0.1 shard_map.51.refs_0_
  11.7 5.3 %collective-permute-start.1 = (bf16[256,1024]{1,0:T(8,128)(2,1)S(1)}, bf16[256,1024]{1,0:T(8,128)(2,1)S(1)}, u32[]{:S(2)}, u32[]{:S(2)}) collective-permute-start(bf16[256,1024]{1,0:T(8,128)(2,1)S(1)} %shard_map.51.refs_0_), channel_id=1, source_target_pairs={{0,32},{32,64},{64,96},{96,128},{128,160},{160,192},{192,224},{224... | collective-permute-start | bytes 1572872 | tf_op jit(solution)/shard_map/ppermute | solution.py:42
  17.1 0.0 copy-start.1
  17.1 0.8 copy-done.1
  17.9 0.9 shard_map.50
  18.8 7.2 %all-to-all-start = ((bf16[16,128,128]{2,1,0:T(8,128)(2,1)}), bf16[16,128,128]{2,1,0:T(8,128)(2,1)S(1)}, u32[]{:S(2)}, u32[]{:S(2)}) async-start(bf16[16,128,128]{2,1,0:T(8,128)(2,1)} %bitcast), calls=%async_computation | async-start | bytes 1048576 | tf_op jit(solution)/shard_map/all_to_all | solution.py:35
  26.0 0.0 collective-permute-done.1.refs_1_
  26.0 2.2 %collective-permute-start.2 = (bf16[256,1024]{1,0:T(8,128)(2,1)S(1)}, bf16[256,1024]{1,0:T(8,128)(2,1)S(1)}, u32[]{:S(2)}, u32[]{:S(2)}) collective-permute-start(bf16[256,1024]{1,0:T(8,128)(2,1)S(1)} %collective-permute-done.1.refs_1_), channel_id=1, source_target_pairs={{0,32},{32,64},{64,96},{96,128},{128,160},{160,192},{192,224},{224... | collective-permute-start | bytes 1572872 | tf_op jit(solution)/shard_map/ppermute | solution.py:42
  28.2 8.0 %collective-permute-done.2.refs_2_ = bf16[256,1024]{1,0:T(8,128)(2,1)S(1)} collective-permute-done((bf16[256,1024]{1,0:T(8,128)(2,1)S(1)}, bf16[256,1024]{1,0:T(8,128)(2,1)S(1)}, u32[]{:S(2)}, u32[]{:S(2)}) %collective-permute-start.2) | collective-permute-done | bytes 524320 | tf_op jit(solution)/shard_map/ppermute | solution.py:42
  36.2 3.4 %collective-permute-start.3 = (bf16[256,1024]{1,0:T(8,128)(2,1)S(1)}, bf16[256,1024]{1,0:T(8,128)(2,1)S(1)}, u32[]{:S(2)}, u32[]{:S(2)}) collective-permute-start(bf16[256,1024]{1,0:T(8,128)(2,1)S(1)} %collective-permute-done.2.refs_2_), channel_id=1, source_target_pairs={{0,32},{32,64},{64,96},{96,128},{128,160},{160,192},{192,224},{224... | collective-permute-start | bytes 1572872 | tf_op jit(solution)/shard_map/ppermute | solution.py:42
  39.6 3.6 %all-to-all-done = bf16[16,128,128]{2,1,0:T(8,128)(2,1)S(1)} async-done(((bf16[16,128,128]{2,1,0:T(8,128)(2,1)}), bf16[16,128,128]{2,1,0:T(8,128)(2,1)S(1)}, u32[]{:S(2)}, u32[]{:S(2)}) %all-to-all-start) | async-done | bytes 524320 | tf_op jit(solution)/shard_map/all_to_all | solution.py:35
  43.2 1.2 broadcast_in_dim.8
  44.5 4.0 %all-to-all-start.1 = ((bf16[4,4,2,128,128]{4,3,2,1,0:T(8,128)(2,1)}), bf16[4,4,2,128,128]{4,3,2,1,0:T(8,128)(2,1)S(1)}, u32[]{:S(2)}, u32[]{:S(2)}) async-start(bf16[4,4,2,128,128]{4,3,2,1,0:T(8,128)(2,1)} %bitcast.10), calls=%async_computation.1 | async-start | bytes 2097152 | tf_op jit(solution)/shard_map/all_to_all | solution.py:35
  48.5 1.9 %collective-permute-start.5 = (bf16[256,1024]{1,0:T(8,128)(2,1)S(1)}, bf16[256,1024]{1,0:T(8,128)(2,1)}, u32[]{:S(2)}, u32[]{:S(2)}) collective-permute-start(bf16[256,1024]{1,0:T(8,128)(2,1)S(1)} %collective-permute-done.1.refs_1_), channel_id=1, source_target_pairs={{0,1},{1,0},{2,3},{3,2},{4,5},{5,4},{6,7},{7,6},{8,9},{9,8},{10,11... | collective-permute-start | bytes 1572872 | tf_op jit(solution)/shard_map/ppermute | solution.py:31
  50.4 2.4 %collective-permute-start.6 = (bf16[256,1024]{1,0:T(8,128)(2,1)S(1)}, bf16[256,1024]{1,0:T(8,128)(2,1)}, u32[]{:S(2)}, u32[]{:S(2)}) collective-permute-start(bf16[256,1024]{1,0:T(8,128)(2,1)S(1)} %collective-permute-done.2.refs_2_), channel_id=1, source_target_pairs={{0,1},{1,0},{2,3},{3,2},{4,5},{5,4},{6,7},{7,6},{8,9},{9,8},{10,11... | collective-permute-start | bytes 1572872 | tf_op jit(solution)/shard_map/ppermute | solution.py:31
  52.8 0.0 collective-permute-done.3.refs_3_
  52.8 1.9 %collective-permute-start.7 = (bf16[256,1024]{1,0:T(8,128)(2,1)S(1)}, bf16[256,1024]{1,0:T(8,128)(2,1)}, u32[]{:S(2)}, u32[]{:S(2)}) collective-permute-start(bf16[256,1024]{1,0:T(8,128)(2,1)S(1)} %collective-permute-done.3.refs_3_), channel_id=1, source_target_pairs={{0,1},{1,0},{2,3},{3,2},{4,5},{5,4},{6,7},{7,6},{8,9},{9,8},{10,11... | collective-permute-start | bytes 1572872 | tf_op jit(solution)/shard_map/ppermute | solution.py:31
  54.7 2.2 %collective-permute-start.4 = (bf16[256,1024]{1,0:T(8,128)(2,1)S(1)}, bf16[256,1024]{1,0:T(8,128)(2,1)}, u32[]{:S(2)}, u32[]{:S(2)}) collective-permute-start(bf16[256,1024]{1,0:T(8,128)(2,1)S(1)} %collective-permute-done.3.refs_3_), channel_id=1, source_target_pairs={{0,32},{32,64},{64,96},{96,128},{128,160},{160,192},{192,224},{224... | collective-permute-start | bytes 1572872 | tf_op jit(solution)/shard_map/ppermute | solution.py:42
  57.0 0.0 collective-permute-done.5.refs_5_
  57.0 6.5 %all-to-all-done.1 = bf16[4,4,2,128,128]{4,3,2,1,0:T(8,128)(2,1)S(1)} async-done(((bf16[4,4,2,128,128]{4,3,2,1,0:T(8,128)(2,1)}), bf16[4,4,2,128,128]{4,3,2,1,0:T(8,128)(2,1)S(1)}, u32[]{:S(2)}, u32[]{:S(2)}) %all-to-all-start.1) | async-done | bytes 1048608 | tf_op jit(solution)/shard_map/all_to_all | solution.py:35
  63.5 0.0 collective-permute-done.6.refs_6_
  63.5 0.0 collective-permute-done.7.refs_7_
  63.5 1.6 %collective-permute-done.4.refs_4_ = bf16[256,1024]{1,0:T(8,128)(2,1)} collective-permute-done((bf16[256,1024]{1,0:T(8,128)(2,1)S(1)}, bf16[256,1024]{1,0:T(8,128)(2,1)}, u32[]{:S(2)}, u32[]{:S(2)}) %collective-permute-start.4) | collective-permute-done | bytes 524320 | tf_op jit(solution)/shard_map/ppermute | solution.py:42
  65.1 4.6 %shard_map.52 = (f32[128,1024]{1,0:T(8,128)S(1)}, f32[128,1024]{1,0:T(8,128)}, bf16[128,1024]{1,0:T(8,128)(2,1)S(1)}, bf16[128,1024]{1,0:T(8,128)(2,1)S(1)}) custom-call(bf16[2,2,4,2,128,128]{5,4,3,2,1,0:T(8,128)(2,1)S(1)} %bitcast.8, bf16[256,1024]{1,0:T(8,128)(2,1)S(1)} %shard_map.51.refs_0_, bf16[256,1024]{1,0:T(8,128)(2,1)S(1)} %collective-permute-done.1.refs_1_, ...), custom_call_target="tpu_custom_call" | custom-call | tf_op jit(solution)/shard_map/pallas_call | solution.py:195
  69.7 3.4 %collective-permute-start.8 = (bf16[128,1024]{1,0:T(8,128)(2,1)S(1)}, bf16[128,1024]{1,0:T(8,128)(2,1)S(1)}, u32[]{:S(2)}, u32[]{:S(2)}) collective-permute-start(bf16[128,1024]{1,0:T(8,128)(2,1)S(1)} %get-tuple-element.11), channel_id=1, source_target_pairs={{0,256},{256,0},{1,257},{257,1},{2,258},{258,2},{3,259},{259,3},{4... | collective-permute-start | bytes 786440 | tf_op jit(solution)/shard_map/ppermute | solution.py:31
  73.1 1.9 %collective-permute-start.9 = (bf16[128,1024]{1,0:T(8,128)(2,1)S(1)}, bf16[128,1024]{1,0:T(8,128)(2,1)S(1)}, u32[]{:S(2)}, u32[]{:S(2)}) collective-permute-start(bf16[128,1024]{1,0:T(8,128)(2,1)S(1)} %get-tuple-element.13), channel_id=1, source_target_pairs={{0,256},{256,0},{1,257},{257,1},{2,258},{258,2},{3,259},{259,3},{4... | collective-permute-start | bytes 786440 | tf_op jit(solution)/shard_map/ppermute | solution.py:31
  75.0 1.8 %collective-permute-done.8.arrived_ref = bf16[128,1024]{1,0:T(8,128)(2,1)S(1)} collective-permute-done((bf16[128,1024]{1,0:T(8,128)(2,1)S(1)}, bf16[128,1024]{1,0:T(8,128)(2,1)S(1)}, u32[]{:S(2)}, u32[]{:S(2)}) %collective-permute-start.8) | collective-permute-done | bytes 262176 | tf_op jit(solution)/shard_map/ppermute | solution.py:31
  76.8 0.7 shard_map.53.own_ref
  77.6 9.1 %all-to-all-start.3 = ((bf16[16,8,1024]{2,1,0:T(8,128)(2,1)}), bf16[16,8,1024]{2,1,0:T(8,128)(2,1)S(1)}, u32[]{:S(2)}, u32[]{:S(2)}) async-start(bf16[16,8,1024]{2,1,0:T(8,128)(2,1)} %bitcast.7), calls=%async_computation.3 | async-start | bytes 524288 | tf_op jit(solution)/shard_map/all_to_all | solution.py:35
  86.7 0.0 collective-permute-done.9.arrived_ref
  86.7 4.2 %shard_map.54 = (bf16[4,2,128,128]{3,2,1,0:T(8,128)(2,1)S(1)}, bf16[4,2,128,128]{3,2,1,0:T(8,128)(2,1)S(1)}, bf16[4,2,128,128]{3,2,1,0:T(8,128)(2,1)S(1)}, bf16[4,2,128,128]{3,2,1,0:T(8,128)(2,1)S(1)}) custom-call(bf16[128,1024]{1,0:T(8,128)(2,1)} %shard_map.53.own_ref, f32[128,1024]{1,0:T(8,128)} %get-tuple-element.12.other_ref, ...), custom_call_target="tpu_custom_call" | custom-call | tf_op jit(solution)/shard_map/pallas_call | solution.py:195
  90.9 4.8 %collective-permute-start.10 = (bf16[4,2,128,128]{3,2,1,0:T(8,128)(2,1)S(1)}, bf16[4,2,128,128]{3,2,1,0:T(8,128)(2,1)S(1)}, u32[]{:S(2)}, u32[]{:S(2)}) collective-permute-start(bf16[4,2,128,128]{3,2,1,0:T(8,128)(2,1)S(1)} %get-tuple-element.15), channel_id=1, source_target_pairs={{0,2},{256,258},{2,0},{258,256},{1,3},{257,259},{3,1},{259,257},{4... | collective-permute-start | bytes 786440 | tf_op jit(solution)/shard_map/ppermute | solution.py:47
  95.7 1.9 %collective-permute-start.11 = (bf16[4,2,128,128]{3,2,1,0:T(8,128)(2,1)S(1)}, bf16[4,2,128,128]{3,2,1,0:T(8,128)(2,1)S(1)}, u32[]{:S(2)}, u32[]{:S(2)}) collective-permute-start(bf16[4,2,128,128]{3,2,1,0:T(8,128)(2,1)S(1)} %get-tuple-element.16), channel_id=1, source_target_pairs={{0,258},{256,0},{2,256},{258,2},{1,259},{257,1},{3,257},{259,3},{4... | collective-permute-start | bytes 786440 | tf_op jit(solution)/shard_map/ppermute | solution.py:47
  97.6 3.4 %collective-permute-start.12 = (bf16[4,2,128,128]{3,2,1,0:T(8,128)(2,1)S(1)}, bf16[4,2,128,128]{3,2,1,0:T(8,128)(2,1)S(1)}, u32[]{:S(2)}, u32[]{:S(2)}) collective-permute-start(bf16[4,2,128,128]{3,2,1,0:T(8,128)(2,1)S(1)} %get-tuple-element.17), channel_id=1, source_target_pairs={{0,256},{256,2},{2,258},{258,0},{1,257},{257,3},{3,259},{259,1},{4... | collective-permute-start | bytes 786440 | tf_op jit(solution)/shard_map/ppermute | solution.py:47
  101.0 0.1 collective-permute-done.10.far_ref
  101.1 3.4 %collective-permute-done.11.left_ref = bf16[4,2,128,128]{3,2,1,0:T(8,128)(2,1)S(1)} collective-permute-done((bf16[4,2,128,128]{3,2,1,0:T(8,128)(2,1)S(1)}, bf16[4,2,128,128]{3,2,1,0:T(8,128)(2,1)S(1)}, u32[]{:S(2)}, u32[]{:S(2)}) %collective-permute-start.11) | collective-permute-done | bytes 262176 | tf_op jit(solution)/shard_map/ppermute | solution.py:47
  104.5 3.2 %collective-permute-done.12.right_ref = bf16[4,2,128,128]{3,2,1,0:T(8,128)(2,1)S(1)} collective-permute-done((bf16[4,2,128,128]{3,2,1,0:T(8,128)(2,1)S(1)}, bf16[4,2,128,128]{3,2,1,0:T(8,128)(2,1)S(1)}, u32[]{:S(2)}, u32[]{:S(2)}) %collective-permute-start.12) | collective-permute-done | bytes 262176 | tf_op jit(solution)/shard_map/ppermute | solution.py:47
  107.7 0.9 shard_map.55
  108.6 0.0 all-to-all-done.3.got_ref
  108.6 11.4 %all-to-all-start.2 = ((bf16[16,128,128]{2,1,0:T(8,128)(2,1)}), bf16[16,128,128]{2,1,0:T(8,128)(2,1)S(1)}, u32[]{:S(2)}, u32[]{:S(2)}) async-start(bf16[16,128,128]{2,1,0:T(8,128)(2,1)} %bitcast.4), calls=%async_computation.2 | async-start | bytes 1048576 | tf_op jit(solution)/shard_map/all_to_all | solution.py:35
  120.0 3.0 %shard_map.57 = bf16[8,20480]{1,0:T(8,128)(2,1)} custom-call(bf16[16,8,1024]{2,1,0:T(8,128)(2,1)S(1)} %all-to-all-done.3.got_ref, bf16[1024,1280]{1,0:T(8,128)(2,1)} %coef_ref.1), custom_call_target="tpu_custom_call" | custom-call | tf_op jit(solution)/shard_map/pallas_call | solution.py:233
  123.0 14.2 %all-to-all-done.2 = bf16[16,128,128]{2,1,0:T(8,128)(2,1)S(1)} async-done(((bf16[16,128,128]{2,1,0:T(8,128)(2,1)}), bf16[16,128,128]{2,1,0:T(8,128)(2,1)S(1)}, u32[]{:S(2)}, u32[]{:S(2)}) %all-to-all-start.2) | async-done | bytes 524320 | tf_op jit(solution)/shard_map/all_to_all | solution.py:35
  137.2 0.7 shard_map.56
Async XLA Ops:
  0.6 10.1 %collective-permute-start = (bf16[256,512]{1,0:T(8,128)(2,1)}, bf16[256,512]{1,0:T(8,128)(2,1)S(1)}, u32[]{:S(2)}, u32[]{:S(2)}) collective-permute-start(bf16[256,512]{1,0:T(8,128)(2,1)} %amp_ref.1), channel_id=1, source_target_pairs={{0,1},{1,0},{2,3},{3,2},{4,5},{5,4},{6,7},{7,6},{8,9},{9,8},{10,11... | collective-permute-start | bytes 786440 | tf_op jit(solution)/shard_map/ppermute | solution.py:31
  10.7 0.9 copy-start
  11.7 14.3 %collective-permute-start.1 = (bf16[256,1024]{1,0:T(8,128)(2,1)S(1)}, bf16[256,1024]{1,0:T(8,128)(2,1)S(1)}, u32[]{:S(2)}, u32[]{:S(2)}) collective-permute-start(bf16[256,1024]{1,0:T(8,128)(2,1)S(1)} %shard_map.51.refs_0_), channel_id=1, source_target_pairs={{0,32},{32,64},{64,96},{96,128},{128,160},{160,192},{192,224},{224... | collective-permute-start | bytes 1572872 | tf_op jit(solution)/shard_map/ppermute | solution.py:42
  17.1 0.8 copy-start.1
  18.8 24.4 %all-to-all-start = ((bf16[16,128,128]{2,1,0:T(8,128)(2,1)}), bf16[16,128,128]{2,1,0:T(8,128)(2,1)S(1)}, u32[]{:S(2)}, u32[]{:S(2)}) async-start(bf16[16,128,128]{2,1,0:T(8,128)(2,1)} %bitcast), calls=%async_computation | async-start | bytes 1048576 | tf_op jit(solution)/shard_map/all_to_all | solution.py:35
  26.0 10.2 %collective-permute-start.2 = (bf16[256,1024]{1,0:T(8,128)(2,1)S(1)}, bf16[256,1024]{1,0:T(8,128)(2,1)S(1)}, u32[]{:S(2)}, u32[]{:S(2)}) collective-permute-start(bf16[256,1024]{1,0:T(8,128)(2,1)S(1)} %collective-permute-done.1.refs_1_), channel_id=1, source_target_pairs={{0,32},{32,64},{64,96},{96,128},{128,160},{160,192},{192,224},{224... | collective-permute-start | bytes 1572872 | tf_op jit(solution)/shard_map/ppermute | solution.py:42
  36.2 16.6 %collective-permute-start.3 = (bf16[256,1024]{1,0:T(8,128)(2,1)S(1)}, bf16[256,1024]{1,0:T(8,128)(2,1)S(1)}, u32[]{:S(2)}, u32[]{:S(2)}) collective-permute-start(bf16[256,1024]{1,0:T(8,128)(2,1)S(1)} %collective-permute-done.2.refs_2_), channel_id=1, source_target_pairs={{0,32},{32,64},{64,96},{96,128},{128,160},{160,192},{192,224},{224... | collective-permute-start | bytes 1572872 | tf_op jit(solution)/shard_map/ppermute | solution.py:42
  44.5 19.1 %all-to-all-start.1 = ((bf16[4,4,2,128,128]{4,3,2,1,0:T(8,128)(2,1)}), bf16[4,4,2,128,128]{4,3,2,1,0:T(8,128)(2,1)S(1)}, u32[]{:S(2)}, u32[]{:S(2)}) async-start(bf16[4,4,2,128,128]{4,3,2,1,0:T(8,128)(2,1)} %bitcast.10), calls=%async_computation.1 | async-start | bytes 2097152 | tf_op jit(solution)/shard_map/all_to_all | solution.py:35
  48.5 8.5 %collective-permute-start.5 = (bf16[256,1024]{1,0:T(8,128)(2,1)S(1)}, bf16[256,1024]{1,0:T(8,128)(2,1)}, u32[]{:S(2)}, u32[]{:S(2)}) collective-permute-start(bf16[256,1024]{1,0:T(8,128)(2,1)S(1)} %collective-permute-done.1.refs_1_), channel_id=1, source_target_pairs={{0,1},{1,0},{2,3},{3,2},{4,5},{5,4},{6,7},{7,6},{8,9},{9,8},{10,11... | collective-permute-start | bytes 1572872 | tf_op jit(solution)/shard_map/ppermute | solution.py:31
  50.4 13.1 %collective-permute-start.6 = (bf16[256,1024]{1,0:T(8,128)(2,1)S(1)}, bf16[256,1024]{1,0:T(8,128)(2,1)}, u32[]{:S(2)}, u32[]{:S(2)}) collective-permute-start(bf16[256,1024]{1,0:T(8,128)(2,1)S(1)} %collective-permute-done.2.refs_2_), channel_id=1, source_target_pairs={{0,1},{1,0},{2,3},{3,2},{4,5},{5,4},{6,7},{7,6},{8,9},{9,8},{10,11... | collective-permute-start | bytes 1572872 | tf_op jit(solution)/shard_map/ppermute | solution.py:31
  52.8 10.7 %collective-permute-start.7 = (bf16[256,1024]{1,0:T(8,128)(2,1)S(1)}, bf16[256,1024]{1,0:T(8,128)(2,1)}, u32[]{:S(2)}, u32[]{:S(2)}) collective-permute-start(bf16[256,1024]{1,0:T(8,128)(2,1)S(1)} %collective-permute-done.3.refs_3_), channel_id=1, source_target_pairs={{0,1},{1,0},{2,3},{3,2},{4,5},{5,4},{6,7},{7,6},{8,9},{9,8},{10,11... | collective-permute-start | bytes 1572872 | tf_op jit(solution)/shard_map/ppermute | solution.py:31
  54.7 10.3 %collective-permute-start.4 = (bf16[256,1024]{1,0:T(8,128)(2,1)S(1)}, bf16[256,1024]{1,0:T(8,128)(2,1)}, u32[]{:S(2)}, u32[]{:S(2)}) collective-permute-start(bf16[256,1024]{1,0:T(8,128)(2,1)S(1)} %collective-permute-done.3.refs_3_), channel_id=1, source_target_pairs={{0,32},{32,64},{64,96},{96,128},{128,160},{160,192},{192,224},{224... | collective-permute-start | bytes 1572872 | tf_op jit(solution)/shard_map/ppermute | solution.py:42
  69.7 7.1 %collective-permute-start.8 = (bf16[128,1024]{1,0:T(8,128)(2,1)S(1)}, bf16[128,1024]{1,0:T(8,128)(2,1)S(1)}, u32[]{:S(2)}, u32[]{:S(2)}) collective-permute-start(bf16[128,1024]{1,0:T(8,128)(2,1)S(1)} %get-tuple-element.11), channel_id=1, source_target_pairs={{0,256},{256,0},{1,257},{257,1},{2,258},{258,2},{3,259},{259,3},{4... | collective-permute-start | bytes 786440 | tf_op jit(solution)/shard_map/ppermute | solution.py:31
  73.1 13.6 %collective-permute-start.9 = (bf16[128,1024]{1,0:T(8,128)(2,1)S(1)}, bf16[128,1024]{1,0:T(8,128)(2,1)S(1)}, u32[]{:S(2)}, u32[]{:S(2)}) collective-permute-start(bf16[128,1024]{1,0:T(8,128)(2,1)S(1)} %get-tuple-element.13), channel_id=1, source_target_pairs={{0,256},{256,0},{1,257},{257,1},{2,258},{258,2},{3,259},{259,3},{4... | collective-permute-start | bytes 786440 | tf_op jit(solution)/shard_map/ppermute | solution.py:31
  77.6 31.0 %all-to-all-start.3 = ((bf16[16,8,1024]{2,1,0:T(8,128)(2,1)}), bf16[16,8,1024]{2,1,0:T(8,128)(2,1)S(1)}, u32[]{:S(2)}, u32[]{:S(2)}) async-start(bf16[16,8,1024]{2,1,0:T(8,128)(2,1)} %bitcast.7), calls=%async_computation.3 | async-start | bytes 524288 | tf_op jit(solution)/shard_map/all_to_all | solution.py:35
  90.9 10.1 %collective-permute-start.10 = (bf16[4,2,128,128]{3,2,1,0:T(8,128)(2,1)S(1)}, bf16[4,2,128,128]{3,2,1,0:T(8,128)(2,1)S(1)}, u32[]{:S(2)}, u32[]{:S(2)}) collective-permute-start(bf16[4,2,128,128]{3,2,1,0:T(8,128)(2,1)S(1)} %get-tuple-element.15), channel_id=1, source_target_pairs={{0,2},{256,258},{2,0},{258,256},{1,3},{257,259},{3,1},{259,257},{4... | collective-permute-start | bytes 786440 | tf_op jit(solution)/shard_map/ppermute | solution.py:47
  95.7 8.8 %collective-permute-start.11 = (bf16[4,2,128,128]{3,2,1,0:T(8,128)(2,1)S(1)}, bf16[4,2,128,128]{3,2,1,0:T(8,128)(2,1)S(1)}, u32[]{:S(2)}, u32[]{:S(2)}) collective-permute-start(bf16[4,2,128,128]{3,2,1,0:T(8,128)(2,1)S(1)} %get-tuple-element.16), channel_id=1, source_target_pairs={{0,258},{256,0},{2,256},{258,2},{1,259},{257,1},{3,257},{259,3},{4... | collective-permute-start | bytes 786440 | tf_op jit(solution)/shard_map/ppermute | solution.py:47
  97.6 10.1 %collective-permute-start.12 = (bf16[4,2,128,128]{3,2,1,0:T(8,128)(2,1)S(1)}, bf16[4,2,128,128]{3,2,1,0:T(8,128)(2,1)S(1)}, u32[]{:S(2)}, u32[]{:S(2)}) collective-permute-start(bf16[4,2,128,128]{3,2,1,0:T(8,128)(2,1)S(1)} %get-tuple-element.17), channel_id=1, source_target_pairs={{0,256},{256,2},{2,258},{258,0},{1,257},{257,3},{3,259},{259,1},{4... | collective-permute-start | bytes 786440 | tf_op jit(solution)/shard_map/ppermute | solution.py:47
  108.6 28.6 %all-to-all-start.2 = ((bf16[16,128,128]{2,1,0:T(8,128)(2,1)}), bf16[16,128,128]{2,1,0:T(8,128)(2,1)S(1)}, u32[]{:S(2)}, u32[]{:S(2)}) async-start(bf16[16,128,128]{2,1,0:T(8,128)(2,1)} %bitcast.4), calls=%async_computation.2 | async-start | bytes 1048576 | tf_op jit(solution)/shard_map/all_to_all | solution.py:35

commit v8 on v7

--- a/solution.py
+++ b/solution.py
@@ -47,18 +47,10 @@
     return lax.ppermute(x, ("xl", "xh"), [(at(i), at((i + by) % 4)) for i in range(4)])
 
 
-def with_blocks(near_refs, swap_refs, bufs, sems, use):
+def blocks_of(refs):
     toward = 2 * lax.axis_index("c") - 1
-    copies = [
-        pltpu.make_async_copy(ref, bufs.at[i], sems.at[i]) for i, ref in enumerate(swap_refs)
-    ]
-    for copy in copies:
-        copy.start()
-    near = [(toward * s, ref[...]) for s, ref in enumerate(near_refs)]
-    use(near)
-    for copy in copies:
-        copy.wait()
-    use([(-toward * (i + 1), bufs[i]) for i in range(len(copies))])
+    near = [(toward * s, ref[...]) for s, ref in enumerate(refs[:5])]
+    return near + [(-toward * (i + 1), ref[...]) for i, ref in enumerate(refs[5:])]
 
 
 def place(offset):
@@ -84,22 +76,15 @@
 
 
 def fitted_kernel(metric_ref, *refs):
-    near_refs, swap_refs = refs[:5], refs[5:8]
-    wide_refs, narrow_refs, (bufs, sems) = refs[8:10], refs[10:12], refs[12:]
+    blocks = blocks_of(refs[:8])
+    wide_refs, narrow_refs = refs[8:10], refs[10:12]
     xl = lax.axis_index("xl")
-    sums = [None, None]
-
-    def use(blocks):
-        rhs = jnp.concatenate([b for _, b in blocks], axis=0)
-        for i, h in enumerate((xl, 1 - xl)):
-            lhs = [metric_ref[(h, *place(o), j)] for o, _ in blocks for j in range(2)]
-            out = jnp.dot(jnp.concatenate(lhs, axis=1), rhs, preferred_element_type=F32)
-            sums[i] = out if sums[i] is None else sums[i] + out
-
-    with_blocks(near_refs, swap_refs, bufs, sems, use)
-    for i in range(2):
-        wide_refs[i][...] = sums[i]
-        narrow_refs[i][...] = sums[i].astype(BF16)
+    rhs = jnp.concatenate([b for _, b in blocks], axis=0)
+    for i, h in enumerate((xl, 1 - xl)):
+        lhs = [metric_ref[(h, *place(o), j)] for o, _ in blocks for j in range(2)]
+        out = jnp.dot(jnp.concatenate(lhs, axis=1), rhs, preferred_element_type=F32)
+        wide_refs[i][...] = out
+        narrow_refs[i][...] = out.astype(BF16)
 
 
 def join_kernel(own_ref, arrived_ref, out_ref):
@@ -107,27 +92,22 @@
 
 
 def density_kernel(own_ref, other_ref, arrived_ref, *refs):
-    near_refs, swap_refs, outs = refs[:5], refs[5:8], refs[8:12]
-    all_ref, bufs, sems = refs[12:]
+    blocks, outs, all_ref = blocks_of(refs[:8]), refs[8:12], refs[12]
     xl = lax.axis_index("xl")
     x = 2 * lax.axis_index("xh") + xl
     other = (other_ref[...] + arrived_ref[...].astype(F32)).astype(BF16)
-    lhs = jnp.concatenate([own_ref[...], other], axis=0)
+    fitted = jnp.concatenate([own_ref[...], other], axis=0)
     rows = own_ref.shape[0]
-
-    def use(blocks):
-        for offset, block in blocks:
-            out = lax.dot_general(
-                lhs, block, (((1,), (1,)), ((), ())), preferred_element_type=F32
-            ).astype(BF16)
-            far, near = place(offset)
-            half = out.shape[1] // 2
-            for h, part in ((xl, out[:rows]), (1 - xl, out[rows:])):
-                slot = lax.rem(2 * far + h + 4 - x, 4)
-                for j in range(2):
-                    all_ref[slot, near, j] = part[:, j * half : (j + 1) * half]
-
-    with_blocks(near_refs, swap_refs, bufs, sems, use)
+    for offset, block in blocks:
+        out = lax.dot_general(
+            block, fitted, (((1,), (1,)), ((), ())), preferred_element_type=F32
+        ).astype(BF16)
+        far, near = place(offset)
+        half = out.shape[0] // 2
+        for h, part in ((xl, out[:, :rows]), (1 - xl, out[:, rows:])):
+            slot = lax.rem(2 * far + h + 4 - x, 4)
+            for j in range(2):
+                all_ref[slot, near, j] = part[j * half : (j + 1) * half]
     for s in range(4):
         outs[s][...] = all_ref[s]
 
@@ -147,6 +127,7 @@
         total = in_ref[0, c].astype(F32)
         for y in range(1, in_ref.shape[0]):
             total += in_ref[y, c].astype(F32)
+        total = total.T
         for g in range(groups):
             out_ref[g, c] = total[g * rows : (g + 1) * rows]
 
@@ -184,22 +165,19 @@
         steps.append(ring_step(steps[-1]))
     swaps = [shifted(steps[s], "c", 1) for s in range(1, 4)]
     steps.append(ring_step(steps[3]))
-    in_hbm = [pltpu.with_memory_space_constraint(a, pltpu.HBM) for a in swaps]
     shape = (half, 2 * cols)
-    buffers = [pltpu.VMEM((3, rows, 2 * cols), BF16), pltpu.SemaphoreType.DMA((3,))]
 
     def on_blocks(kernel, outs, scratch, *args):
-        spaces = [pltpu.HBM if a.dtype == F32 else pltpu.VMEM for a in args] + [pltpu.VMEM] * 5
-        args = map(pltpu.with_memory_space_constraint, (*args, *steps), spaces)
-        args = list(args)
+        spaces = [pltpu.HBM if a.dtype == F32 else pltpu.VMEM for a in args] + [pltpu.VMEM] * 5 + [pltpu.HBM] * 3
+        args = list(map(pltpu.with_memory_space_constraint, (*args, *steps, *swaps), spaces))
         return pl.pallas_call(
             kernel,
-            in_specs=[VMEM] * len(args) + [pl.BlockSpec(memory_space=pl.ANY)] * 3,
+            in_specs=[VMEM] * len(args),
             out_specs=[VMEM] * len(outs),
             out_shape=[space(shape, dtype) for space, shape, dtype in outs],
-            scratch_shapes=scratch + buffers,
+            scratch_shapes=scratch,
             compiler_params=PARAMS,
-        )(*args, *in_hbm)
+        )(*args)
 
     own, other, own_sent, other_sent = on_blocks(
         fitted_kernel,

time: 139 us -> 137 us (0.986)
  Pallas kernels: 15.1 us -> 13.1 us
    pallas_call x2, Pallas kernels: 8.85 us -> 6.75 us  [on_blocks(): pl.pallas_call(kernel, in_specs=[VMEM] * len(args), out_specs=[VMEM] * le...]
  transfers between devices with their start and end apart: 17 -> 17, of which waited for: 10 -> 9; matrix products, arithmetic and copies ran while one was open for 1% -> 1% of each run, Pallas kernels for 7% -> 6%
where the time goes in v8:
time: 137 us; the launch traced here: 136 us
  starting transfers between devices  75.1 us (55%)
  waiting for transfers between devices  43.9 us (32%)
  Pallas kernels  13.1 us (10%)
  local copies, waits for them, and re-layouts  3.01 us (2%)
    all_to_all x4, starting transfers between devices, exchange(): return lax.all_to_all(x, axes, split_axis=0, concat_axis=0, tiled=True)  31.7 us
    all_to_all x4, waiting for transfers between devices, exchange(): return lax.all_to_all(x, axes, split_axis=0, concat_axis=0, tiled=True)  24.3 us
    ppermute x6, starting transfers between devices, shifted(): return lax.ppermute(x, axis, [(i, (i + by) % n) for i in range(n)])  20.3 us
    ppermute x4, starting transfers between devices, ring_step(): return lax.ppermute(x, ('z', 'c'), moves)  13.1 us
    ppermute x3, starting transfers between devices, shifted_x(): lax.ppermute(x, ('xl', 'xh'), [(at(i), at((i + by) % 4)) for i in range(4)])  10.1 us
    ppermute x4, waiting for transfers between devices, ring_step(): return lax.ppermute(x, ('z', 'c'), moves)  9.59 us
    ppermute x3, waiting for transfers between devices, shifted_x(): lax.ppermute(x, ('xl', 'xh'), [(at(i), at((i + by) % 4)) for i in range(4)])  6.77 us
    pallas_call x2, Pallas kernels, on_blocks(): pl.pallas_call(kernel, in_specs=[VMEM] * len(args), out_specs=[VMEM] * le...  6.75 us
  transfers between devices with their start and end apart: 17, of which 9 were waited for; matrix products, arithmetic and copies ran while one was open for 1% of the time, Pallas kernels for 6%

profile of v8, /device:TPU:1, one launch (start us, length us, event | category | flops | bytes accessed | tf_op | source)
XLA Modules:
  0.0 135.9 jit_solution(15322182355191021131)
XLA Ops:
  0.6 8.7 %collective-permute-start = (bf16[256,512]{1,0:T(8,128)(2,1)}, bf16[256,512]{1,0:T(8,128)(2,1)S(1)}, u32[]{:S(2)}, u32[]{:S(2)}) collective-permute-start(bf16[256,512]{1,0:T(8,128)(2,1)} %amp_ref.1), channel_id=1, source_target_pairs={{0,1},{1,0},{2,3},{3,2},{4,5},{5,4},{6,7},{7,6},{8,9},{9,8},{10,11... | collective-permute-start | bytes 786440 | tf_op jit(solution)/shard_map/ppermute | solution.py:31
  9.4 1.4 collective-permute-done.got_ref
  10.7 0.0 copy-start
  10.7 0.9 copy-done
  11.7 0.1 shard_map.51.refs_0_
  11.7 5.3 %collective-permute-start.1 = (bf16[256,1024]{1,0:T(8,128)(2,1)S(1)}, bf16[256,1024]{1,0:T(8,128)(2,1)S(1)}, u32[]{:S(2)}, u32[]{:S(2)}) collective-permute-start(bf16[256,1024]{1,0:T(8,128)(2,1)S(1)} %shard_map.51.refs_0_), channel_id=1, source_target_pairs={{0,32},{32,64},{64,96},{96,128},{128,160},{160,192},{192,224},{224... | collective-permute-start | bytes 1572872 | tf_op jit(solution)/shard_map/ppermute | solution.py:42
  17.1 0.0 copy-start.1
  17.1 0.8 copy-done.1
  17.9 0.9 shard_map.50
  18.8 7.2 %all-to-all-start = ((bf16[16,128,128]{2,1,0:T(8,128)(2,1)}), bf16[16,128,128]{2,1,0:T(8,128)(2,1)S(1)}, u32[]{:S(2)}, u32[]{:S(2)}) async-start(bf16[16,128,128]{2,1,0:T(8,128)(2,1)} %bitcast), calls=%async_computation | async-start | bytes 1048576 | tf_op jit(solution)/shard_map/all_to_all | solution.py:35
  26.0 0.0 collective-permute-done.1.refs_1_
  26.0 2.2 %collective-permute-start.2 = (bf16[256,1024]{1,0:T(8,128)(2,1)S(1)}, bf16[256,1024]{1,0:T(8,128)(2,1)S(1)}, u32[]{:S(2)}, u32[]{:S(2)}) collective-permute-start(bf16[256,1024]{1,0:T(8,128)(2,1)S(1)} %collective-permute-done.1.refs_1_), channel_id=1, source_target_pairs={{0,32},{32,64},{64,96},{96,128},{128,160},{160,192},{192,224},{224... | collective-permute-start | bytes 1572872 | tf_op jit(solution)/shard_map/ppermute | solution.py:42
  28.2 8.0 %collective-permute-done.2.refs_2_ = bf16[256,1024]{1,0:T(8,128)(2,1)S(1)} collective-permute-done((bf16[256,1024]{1,0:T(8,128)(2,1)S(1)}, bf16[256,1024]{1,0:T(8,128)(2,1)S(1)}, u32[]{:S(2)}, u32[]{:S(2)}) %collective-permute-start.2) | collective-permute-done | bytes 524320 | tf_op jit(solution)/shard_map/ppermute | solution.py:42
  36.2 3.4 %collective-permute-start.3 = (bf16[256,1024]{1,0:T(8,128)(2,1)S(1)}, bf16[256,1024]{1,0:T(8,128)(2,1)S(1)}, u32[]{:S(2)}, u32[]{:S(2)}) collective-permute-start(bf16[256,1024]{1,0:T(8,128)(2,1)S(1)} %collective-permute-done.2.refs_2_), channel_id=1, source_target_pairs={{0,32},{32,64},{64,96},{96,128},{128,160},{160,192},{192,224},{224... | collective-permute-start | bytes 1572872 | tf_op jit(solution)/shard_map/ppermute | solution.py:42
  39.6 3.6 %all-to-all-done = bf16[16,128,128]{2,1,0:T(8,128)(2,1)S(1)} async-done(((bf16[16,128,128]{2,1,0:T(8,128)(2,1)}), bf16[16,128,128]{2,1,0:T(8,128)(2,1)S(1)}, u32[]{:S(2)}, u32[]{:S(2)}) %all-to-all-start) | async-done | bytes 524320 | tf_op jit(solution)/shard_map/all_to_all | solution.py:35
  43.2 1.2 broadcast_in_dim.8
  44.5 4.0 %all-to-all-start.1 = ((bf16[4,4,2,128,128]{4,3,2,1,0:T(8,128)(2,1)}), bf16[4,4,2,128,128]{4,3,2,1,0:T(8,128)(2,1)S(1)}, u32[]{:S(2)}, u32[]{:S(2)}) async-start(bf16[4,4,2,128,128]{4,3,2,1,0:T(8,128)(2,1)} %bitcast.10), calls=%async_computation.1 | async-start | bytes 2097152 | tf_op jit(solution)/shard_map/all_to_all | solution.py:35
  48.5 1.9 %collective-permute-start.5 = (bf16[256,1024]{1,0:T(8,128)(2,1)S(1)}, bf16[256,1024]{1,0:T(8,128)(2,1)}, u32[]{:S(2)}, u32[]{:S(2)}) collective-permute-start(bf16[256,1024]{1,0:T(8,128)(2,1)S(1)} %collective-permute-done.1.refs_1_), channel_id=1, source_target_pairs={{0,1},{1,0},{2,3},{3,2},{4,5},{5,4},{6,7},{7,6},{8,9},{9,8},{10,11... | collective-permute-start | bytes 1572872 | tf_op jit(solution)/shard_map/ppermute | solution.py:31
  50.4 2.4 %collective-permute-start.6 = (bf16[256,1024]{1,0:T(8,128)(2,1)S(1)}, bf16[256,1024]{1,0:T(8,128)(2,1)}, u32[]{:S(2)}, u32[]{:S(2)}) collective-permute-start(bf16[256,1024]{1,0:T(8,128)(2,1)S(1)} %collective-permute-done.2.refs_2_), channel_id=1, source_target_pairs={{0,1},{1,0},{2,3},{3,2},{4,5},{5,4},{6,7},{7,6},{8,9},{9,8},{10,11... | collective-permute-start | bytes 1572872 | tf_op jit(solution)/shard_map/ppermute | solution.py:31
  52.8 0.0 collective-permute-done.3.refs_3_
  52.8 1.9 %collective-permute-start.7 = (bf16[256,1024]{1,0:T(8,128)(2,1)S(1)}, bf16[256,1024]{1,0:T(8,128)(2,1)}, u32[]{:S(2)}, u32[]{:S(2)}) collective-permute-start(bf16[256,1024]{1,0:T(8,128)(2,1)S(1)} %collective-permute-done.3.refs_3_), channel_id=1, source_target_pairs={{0,1},{1,0},{2,3},{3,2},{4,5},{5,4},{6,7},{7,6},{8,9},{9,8},{10,11... | collective-permute-start | bytes 1572872 | tf_op jit(solution)/shard_map/ppermute | solution.py:31
  54.7 2.2 %collective-permute-start.4 = (bf16[256,1024]{1,0:T(8,128)(2,1)S(1)}, bf16[256,1024]{1,0:T(8,128)(2,1)}, u32[]{:S(2)}, u32[]{:S(2)}) collective-permute-start(bf16[256,1024]{1,0:T(8,128)(2,1)S(1)} %collective-permute-done.3.refs_3_), channel_id=1, source_target_pairs={{0,32},{32,64},{64,96},{96,128},{128,160},{160,192},{192,224},{224... | collective-permute-start | bytes 1572872 | tf_op jit(solution)/shard_map/ppermute | solution.py:42
  57.0 0.0 collective-permute-done.5.refs_5_
  57.0 6.5 %all-to-all-done.1 = bf16[4,4,2,128,128]{4,3,2,1,0:T(8,128)(2,1)S(1)} async-done(((bf16[4,4,2,128,128]{4,3,2,1,0:T(8,128)(2,1)}), bf16[4,4,2,128,128]{4,3,2,1,0:T(8,128)(2,1)S(1)}, u32[]{:S(2)}, u32[]{:S(2)}) %all-to-all-start.1) | async-done | bytes 1048608 | tf_op jit(solution)/shard_map/all_to_all | solution.py:35
  63.5 0.0 collective-permute-done.6.refs_6_
  63.5 0.0 collective-permute-done.7.refs_7_
  63.5 1.6 %collective-permute-done.4.refs_4_ = bf16[256,1024]{1,0:T(8,128)(2,1)} collective-permute-done((bf16[256,1024]{1,0:T(8,128)(2,1)S(1)}, bf16[256,1024]{1,0:T(8,128)(2,1)}, u32[]{:S(2)}, u32[]{:S(2)}) %collective-permute-start.4) | collective-permute-done | bytes 524320 | tf_op jit(solution)/shard_map/ppermute | solution.py:42
  65.1 3.6 %shard_map.52 = (f32[128,1024]{1,0:T(8,128)S(1)}, f32[128,1024]{1,0:T(8,128)}, bf16[128,1024]{1,0:T(8,128)(2,1)S(1)}, bf16[128,1024]{1,0:T(8,128)(2,1)S(1)}) custom-call(bf16[2,2,4,2,128,128]{5,4,3,2,1,0:T(8,128)(2,1)S(1)} %bitcast.8, bf16[256,1024]{1,0:T(8,128)(2,1)S(1)} %shard_map.51.refs_0_, bf16[256,1024]{1,0:T(8,128)(2,1)S(1)} %collective-permute-done.1.refs_1_, ...), custom_call_target="tpu_custom_call" | custom-call | tf_op jit(solution)/shard_map/pallas_call | solution.py:173
  68.7 3.4 %collective-permute-start.8 = (bf16[128,1024]{1,0:T(8,128)(2,1)S(1)}, bf16[128,1024]{1,0:T(8,128)(2,1)S(1)}, u32[]{:S(2)}, u32[]{:S(2)}) collective-permute-start(bf16[128,1024]{1,0:T(8,128)(2,1)S(1)} %get-tuple-element.11), channel_id=1, source_target_pairs={{0,256},{256,0},{1,257},{257,1},{2,258},{258,2},{3,259},{259,3},{4... | collective-permute-start | bytes 786440 | tf_op jit(solution)/shard_map/ppermute | solution.py:31
  72.0 1.9 %collective-permute-start.9 = (bf16[128,1024]{1,0:T(8,128)(2,1)S(1)}, bf16[128,1024]{1,0:T(8,128)(2,1)S(1)}, u32[]{:S(2)}, u32[]{:S(2)}) collective-permute-start(bf16[128,1024]{1,0:T(8,128)(2,1)S(1)} %get-tuple-element.13), channel_id=1, source_target_pairs={{0,256},{256,0},{1,257},{257,1},{2,258},{258,2},{3,259},{259,3},{4... | collective-permute-start | bytes 786440 | tf_op jit(solution)/shard_map/ppermute | solution.py:31
  74.0 1.8 %collective-permute-done.8.arrived_ref = bf16[128,1024]{1,0:T(8,128)(2,1)S(1)} collective-permute-done((bf16[128,1024]{1,0:T(8,128)(2,1)S(1)}, bf16[128,1024]{1,0:T(8,128)(2,1)S(1)}, u32[]{:S(2)}, u32[]{:S(2)}) %collective-permute-start.8) | collective-permute-done | bytes 262176 | tf_op jit(solution)/shard_map/ppermute | solution.py:31
  75.8 0.7 shard_map.53.own_ref
  76.5 9.1 %all-to-all-start.3 = ((bf16[16,8,1024]{2,1,0:T(8,128)(2,1)}), bf16[16,8,1024]{2,1,0:T(8,128)(2,1)S(1)}, u32[]{:S(2)}, u32[]{:S(2)}) async-start(bf16[16,8,1024]{2,1,0:T(8,128)(2,1)} %bitcast.7), calls=%async_computation.3 | async-start | bytes 524288 | tf_op jit(solution)/shard_map/all_to_all | solution.py:35
  85.7 0.0 collective-permute-done.9.arrived_ref
  85.7 3.2 %shard_map.54 = (bf16[4,2,128,128]{3,2,1,0:T(8,128)(2,1)S(1)}, bf16[4,2,128,128]{3,2,1,0:T(8,128)(2,1)S(1)}, bf16[4,2,128,128]{3,2,1,0:T(8,128)(2,1)S(1)}, bf16[4,2,128,128]{3,2,1,0:T(8,128)(2,1)S(1)}) custom-call(bf16[128,1024]{1,0:T(8,128)(2,1)} %shard_map.53.own_ref, f32[128,1024]{1,0:T(8,128)} %get-tuple-element.12.other_ref, ...), custom_call_target="tpu_custom_call" | custom-call | tf_op jit(solution)/shard_map/pallas_call | solution.py:173
  88.8 4.8 %collective-permute-start.10 = (bf16[4,2,128,128]{3,2,1,0:T(8,128)(2,1)S(1)}, bf16[4,2,128,128]{3,2,1,0:T(8,128)(2,1)S(1)}, u32[]{:S(2)}, u32[]{:S(2)}) collective-permute-start(bf16[4,2,128,128]{3,2,1,0:T(8,128)(2,1)S(1)} %get-tuple-element.15), channel_id=1, source_target_pairs={{0,2},{256,258},{2,0},{258,256},{1,3},{257,259},{3,1},{259,257},{4... | collective-permute-start | bytes 786440 | tf_op jit(solution)/shard_map/ppermute | solution.py:47
  93.6 1.9 %collective-permute-start.11 = (bf16[4,2,128,128]{3,2,1,0:T(8,128)(2,1)S(1)}, bf16[4,2,128,128]{3,2,1,0:T(8,128)(2,1)S(1)}, u32[]{:S(2)}, u32[]{:S(2)}) collective-permute-start(bf16[4,2,128,128]{3,2,1,0:T(8,128)(2,1)S(1)} %get-tuple-element.16), channel_id=1, source_target_pairs={{0,258},{256,0},{2,256},{258,2},{1,259},{257,1},{3,257},{259,3},{4... | collective-permute-start | bytes 786440 | tf_op jit(solution)/shard_map/ppermute | solution.py:47
  95.5 3.4 %collective-permute-start.12 = (bf16[4,2,128,128]{3,2,1,0:T(8,128)(2,1)S(1)}, bf16[4,2,128,128]{3,2,1,0:T(8,128)(2,1)S(1)}, u32[]{:S(2)}, u32[]{:S(2)}) collective-permute-start(bf16[4,2,128,128]{3,2,1,0:T(8,128)(2,1)S(1)} %get-tuple-element.17), channel_id=1, source_target_pairs={{0,256},{256,2},{2,258},{258,0},{1,257},{257,3},{3,259},{259,1},{4... | collective-permute-start | bytes 786440 | tf_op jit(solution)/shard_map/ppermute | solution.py:47
  98.9 0.0 collective-permute-done.10.far_ref
  98.9 5.0 %collective-permute-done.11.left_ref = bf16[4,2,128,128]{3,2,1,0:T(8,128)(2,1)S(1)} collective-permute-done((bf16[4,2,128,128]{3,2,1,0:T(8,128)(2,1)S(1)}, bf16[4,2,128,128]{3,2,1,0:T(8,128)(2,1)S(1)}, u32[]{:S(2)}, u32[]{:S(2)}) %collective-permute-start.11) | collective-permute-done | bytes 262176 | tf_op jit(solution)/shard_map/ppermute | solution.py:47
  104.0 1.7 %collective-permute-done.12.right_ref = bf16[4,2,128,128]{3,2,1,0:T(8,128)(2,1)S(1)} collective-permute-done((bf16[4,2,128,128]{3,2,1,0:T(8,128)(2,1)S(1)}, bf16[4,2,128,128]{3,2,1,0:T(8,128)(2,1)S(1)}, u32[]{:S(2)}, u32[]{:S(2)}) %collective-permute-start.12) | collective-permute-done | bytes 262176 | tf_op jit(solution)/shard_map/ppermute | solution.py:47
  105.7 0.9 shard_map.55
  106.6 0.0 all-to-all-done.3.got_ref
  106.6 11.3 %all-to-all-start.2 = ((bf16[16,128,128]{2,1,0:T(8,128)(2,1)}), bf16[16,128,128]{2,1,0:T(8,128)(2,1)S(1)}, u32[]{:S(2)}, u32[]{:S(2)}) async-start(bf16[16,128,128]{2,1,0:T(8,128)(2,1)} %bitcast.4), calls=%async_computation.2 | async-start | bytes 1048576 | tf_op jit(solution)/shard_map/all_to_all | solution.py:35
  117.9 3.0 %shard_map.57 = bf16[8,20480]{1,0:T(8,128)(2,1)} custom-call(bf16[16,8,1024]{2,1,0:T(8,128)(2,1)S(1)} %all-to-all-done.3.got_ref, bf16[1024,1280]{1,0:T(8,128)(2,1)} %coef_ref.1), custom_call_target="tpu_custom_call" | custom-call | tf_op jit(solution)/shard_map/pallas_call | solution.py:211
  120.9 14.2 %all-to-all-done.2 = bf16[16,128,128]{2,1,0:T(8,128)(2,1)S(1)} async-done(((bf16[16,128,128]{2,1,0:T(8,128)(2,1)}), bf16[16,128,128]{2,1,0:T(8,128)(2,1)S(1)}, u32[]{:S(2)}, u32[]{:S(2)}) %all-to-all-start.2) | async-done | bytes 524320 | tf_op jit(solution)/shard_map/all_to_all | solution.py:35
  135.1 0.8 shard_map.56
Async XLA Ops:
  0.6 10.1 %collective-permute-start = (bf16[256,512]{1,0:T(8,128)(2,1)}, bf16[256,512]{1,0:T(8,128)(2,1)S(1)}, u32[]{:S(2)}, u32[]{:S(2)}) collective-permute-start(bf16[256,512]{1,0:T(8,128)(2,1)} %amp_ref.1), channel_id=1, source_target_pairs={{0,1},{1,0},{2,3},{3,2},{4,5},{5,4},{6,7},{7,6},{8,9},{9,8},{10,11... | collective-permute-start | bytes 786440 | tf_op jit(solution)/shard_map/ppermute | solution.py:31
  10.7 0.9 copy-start
  11.7 14.3 %collective-permute-start.1 = (bf16[256,1024]{1,0:T(8,128)(2,1)S(1)}, bf16[256,1024]{1,0:T(8,128)(2,1)S(1)}, u32[]{:S(2)}, u32[]{:S(2)}) collective-permute-start(bf16[256,1024]{1,0:T(8,128)(2,1)S(1)} %shard_map.51.refs_0_), channel_id=1, source_target_pairs={{0,32},{32,64},{64,96},{96,128},{128,160},{160,192},{192,224},{224... | collective-permute-start | bytes 1572872 | tf_op jit(solution)/shard_map/ppermute | solution.py:42
  17.1 0.8 copy-start.1
  18.8 24.4 %all-to-all-start = ((bf16[16,128,128]{2,1,0:T(8,128)(2,1)}), bf16[16,128,128]{2,1,0:T(8,128)(2,1)S(1)}, u32[]{:S(2)}, u32[]{:S(2)}) async-start(bf16[16,128,128]{2,1,0:T(8,128)(2,1)} %bitcast), calls=%async_computation | async-start | bytes 1048576 | tf_op jit(solution)/shard_map/all_to_all | solution.py:35
  26.0 10.2 %collective-permute-start.2 = (bf16[256,1024]{1,0:T(8,128)(2,1)S(1)}, bf16[256,1024]{1,0:T(8,128)(2,1)S(1)}, u32[]{:S(2)}, u32[]{:S(2)}) collective-permute-start(bf16[256,1024]{1,0:T(8,128)(2,1)S(1)} %collective-permute-done.1.refs_1_), channel_id=1, source_target_pairs={{0,32},{32,64},{64,96},{96,128},{128,160},{160,192},{192,224},{224... | collective-permute-start | bytes 1572872 | tf_op jit(solution)/shard_map/ppermute | solution.py:42
  36.2 16.6 %collective-permute-start.3 = (bf16[256,1024]{1,0:T(8,128)(2,1)S(1)}, bf16[256,1024]{1,0:T(8,128)(2,1)S(1)}, u32[]{:S(2)}, u32[]{:S(2)}) collective-permute-start(bf16[256,1024]{1,0:T(8,128)(2,1)S(1)} %collective-permute-done.2.refs_2_), channel_id=1, source_target_pairs={{0,32},{32,64},{64,96},{96,128},{128,160},{160,192},{192,224},{224... | collective-permute-start | bytes 1572872 | tf_op jit(solution)/shard_map/ppermute | solution.py:42
  44.5 19.1 %all-to-all-start.1 = ((bf16[4,4,2,128,128]{4,3,2,1,0:T(8,128)(2,1)}), bf16[4,4,2,128,128]{4,3,2,1,0:T(8,128)(2,1)S(1)}, u32[]{:S(2)}, u32[]{:S(2)}) async-start(bf16[4,4,2,128,128]{4,3,2,1,0:T(8,128)(2,1)} %bitcast.10), calls=%async_computation.1 | async-start | bytes 2097152 | tf_op jit(solution)/shard_map/all_to_all | solution.py:35
  48.5 8.5 %collective-permute-start.5 = (bf16[256,1024]{1,0:T(8,128)(2,1)S(1)}, bf16[256,1024]{1,0:T(8,128)(2,1)}, u32[]{:S(2)}, u32[]{:S(2)}) collective-permute-start(bf16[256,1024]{1,0:T(8,128)(2,1)S(1)} %collective-permute-done.1.refs_1_), channel_id=1, source_target_pairs={{0,1},{1,0},{2,3},{3,2},{4,5},{5,4},{6,7},{7,6},{8,9},{9,8},{10,11... | collective-permute-start | bytes 1572872 | tf_op jit(solution)/shard_map/ppermute | solution.py:31
  50.4 13.1 %collective-permute-start.6 = (bf16[256,1024]{1,0:T(8,128)(2,1)S(1)}, bf16[256,1024]{1,0:T(8,128)(2,1)}, u32[]{:S(2)}, u32[]{:S(2)}) collective-permute-start(bf16[256,1024]{1,0:T(8,128)(2,1)S(1)} %collective-permute-done.2.refs_2_), channel_id=1, source_target_pairs={{0,1},{1,0},{2,3},{3,2},{4,5},{5,4},{6,7},{7,6},{8,9},{9,8},{10,11... | collective-permute-start | bytes 1572872 | tf_op jit(solution)/shard_map/ppermute | solution.py:31
  52.8 10.7 %collective-permute-start.7 = (bf16[256,1024]{1,0:T(8,128)(2,1)S(1)}, bf16[256,1024]{1,0:T(8,128)(2,1)}, u32[]{:S(2)}, u32[]{:S(2)}) collective-permute-start(bf16[256,1024]{1,0:T(8,128)(2,1)S(1)} %collective-permute-done.3.refs_3_), channel_id=1, source_target_pairs={{0,1},{1,0},{2,3},{3,2},{4,5},{5,4},{6,7},{7,6},{8,9},{9,8},{10,11... | collective-permute-start | bytes 1572872 | tf_op jit(solution)/shard_map/ppermute | solution.py:31
  54.7 10.3 %collective-permute-start.4 = (bf16[256,1024]{1,0:T(8,128)(2,1)S(1)}, bf16[256,1024]{1,0:T(8,128)(2,1)}, u32[]{:S(2)}, u32[]{:S(2)}) collective-permute-start(bf16[256,1024]{1,0:T(8,128)(2,1)S(1)} %collective-permute-done.3.refs_3_), channel_id=1, source_target_pairs={{0,32},{32,64},{64,96},{96,128},{128,160},{160,192},{192,224},{224... | collective-permute-start | bytes 1572872 | tf_op jit(solution)/shard_map/ppermute | solution.py:42
  68.7 7.1 %collective-permute-start.8 = (bf16[128,1024]{1,0:T(8,128)(2,1)S(1)}, bf16[128,1024]{1,0:T(8,128)(2,1)S(1)}, u32[]{:S(2)}, u32[]{:S(2)}) collective-permute-start(bf16[128,1024]{1,0:T(8,128)(2,1)S(1)} %get-tuple-element.11), channel_id=1, source_target_pairs={{0,256},{256,0},{1,257},{257,1},{2,258},{258,2},{3,259},{259,3},{4... | collective-permute-start | bytes 786440 | tf_op jit(solution)/shard_map/ppermute | solution.py:31
  72.0 13.6 %collective-permute-start.9 = (bf16[128,1024]{1,0:T(8,128)(2,1)S(1)}, bf16[128,1024]{1,0:T(8,128)(2,1)S(1)}, u32[]{:S(2)}, u32[]{:S(2)}) collective-permute-start(bf16[128,1024]{1,0:T(8,128)(2,1)S(1)} %get-tuple-element.13), channel_id=1, source_target_pairs={{0,256},{256,0},{1,257},{257,1},{2,258},{258,2},{3,259},{259,3},{4... | collective-permute-start | bytes 786440 | tf_op jit(solution)/shard_map/ppermute | solution.py:31
  76.5 30.1 %all-to-all-start.3 = ((bf16[16,8,1024]{2,1,0:T(8,128)(2,1)}), bf16[16,8,1024]{2,1,0:T(8,128)(2,1)S(1)}, u32[]{:S(2)}, u32[]{:S(2)}) async-start(bf16[16,8,1024]{2,1,0:T(8,128)(2,1)} %bitcast.7), calls=%async_computation.3 | async-start | bytes 524288 | tf_op jit(solution)/shard_map/all_to_all | solution.py:35
  88.8 10.1 %collective-permute-start.10 = (bf16[4,2,128,128]{3,2,1,0:T(8,128)(2,1)S(1)}, bf16[4,2,128,128]{3,2,1,0:T(8,128)(2,1)S(1)}, u32[]{:S(2)}, u32[]{:S(2)}) collective-permute-start(bf16[4,2,128,128]{3,2,1,0:T(8,128)(2,1)S(1)} %get-tuple-element.15), channel_id=1, source_target_pairs={{0,2},{256,258},{2,0},{258,256},{1,3},{257,259},{3,1},{259,257},{4... | collective-permute-start | bytes 786440 | tf_op jit(solution)/shard_map/ppermute | solution.py:47
  93.6 10.4 %collective-permute-start.11 = (bf16[4,2,128,128]{3,2,1,0:T(8,128)(2,1)S(1)}, bf16[4,2,128,128]{3,2,1,0:T(8,128)(2,1)S(1)}, u32[]{:S(2)}, u32[]{:S(2)}) collective-permute-start(bf16[4,2,128,128]{3,2,1,0:T(8,128)(2,1)S(1)} %get-tuple-element.16), channel_id=1, source_target_pairs={{0,258},{256,0},{2,256},{258,2},{1,259},{257,1},{3,257},{259,3},{4... | collective-permute-start | bytes 786440 | tf_op jit(solution)/shard_map/ppermute | solution.py:47
  95.5 10.1 %collective-permute-start.12 = (bf16[4,2,128,128]{3,2,1,0:T(8,128)(2,1)S(1)}, bf16[4,2,128,128]{3,2,1,0:T(8,128)(2,1)S(1)}, u32[]{:S(2)}, u32[]{:S(2)}) collective-permute-start(bf16[4,2,128,128]{3,2,1,0:T(8,128)(2,1)S(1)} %get-tuple-element.17), channel_id=1, source_target_pairs={{0,256},{256,2},{2,258},{258,0},{1,257},{257,3},{3,259},{259,1},{4... | collective-permute-start | bytes 786440 | tf_op jit(solution)/shard_map/ppermute | solution.py:47
  106.6 28.5 %all-to-all-start.2 = ((bf16[16,128,128]{2,1,0:T(8,128)(2,1)}), bf16[16,128,128]{2,1,0:T(8,128)(2,1)S(1)}, u32[]{:S(2)}, u32[]{:S(2)}) async-start(bf16[16,128,128]{2,1,0:T(8,128)(2,1)} %bitcast.4), calls=%async_computation.2 | async-start | bytes 1048576 | tf_op jit(solution)/shard_map/all_to_all | solution.py:35

commit v9 on v8

--- a/solution.py
+++ b/solution.py
@@ -56,6 +56,12 @@
 def place(offset):
     at = lax.rem(lax.axis_index("z") + offset + 8, 8)
     return lax.rem(at, 2), lax.div(at, 2)
+
+
+def twice_kernel(in_ref, out_ref):
+    for h in range(2):
+        for i in range(2):
+            out_ref[h, i] = in_ref[h]
 
 
 def pack_kernel(amp_ref, got_ref, out_ref):
@@ -151,15 +157,29 @@
         out_specs=VMEM,
         out_shape=jax.ShapeDtypeStruct((8, 2, half, width), BF16),
         compiler_params=PARAMS,
-    )(metric)
+    )(pltpu.with_memory_space_constraint(metric, pltpu.HBM))
     ys = exchange(by_core.reshape(16, half, width), ("y", "c"))
-    ys = ys.reshape(2, 1, 4, 2, half, width)
-    wanted = jnp.broadcast_to(ys, (2, 2, 4, 2, half, width))
+    wanted = pl.pallas_call(
+        twice_kernel,
+        in_specs=[VMEM],
+        out_specs=VMEM,
+        out_shape=jax.ShapeDtypeStruct((2, 2, 4, 2, half, width), BF16),
+        compiler_params=PARAMS,
+    )(ys.reshape(2, 4, 2, half, width))
     part = exchange(wanted.reshape(4, 4, 2, half, width), ("xl", "xh"))
     part = part.reshape(2, 2, 4, 2, half, width)
 
     got = shifted(amplitudes, "c", 1)
-    (packed,) = in_vmem(pack_kernel, [((rows, 2 * cols), BF16)], amplitudes, got)
+    packed = pl.pallas_call(
+        pack_kernel,
+        in_specs=[VMEM] * 2,
+        out_specs=VMEM,
+        out_shape=pltpu.VMEM((rows, 2 * cols), BF16),
+        compiler_params=PARAMS,
+    )(
+        pltpu.with_memory_space_constraint(amplitudes, pltpu.HBM),
+        pltpu.with_memory_space_constraint(got, pltpu.VMEM),
+    )
     steps = [packed]
     for _ in range(1, 4):
         steps.append(ring_step(steps[-1]))

time: 137 us -> 137 us (level)
  local copies, waits for them, and re-layouts: 3.01 us -> 0 us
  Pallas kernels: 13.1 us -> 16.1 us
    pallas_call x0 -> x2, Pallas kernels: none -> 2.13 us  [the longest x1 1.14 us: work(): pl.pallas_call(twice_kernel, in_specs=[VMEM], out_specs=VMEM, out_shape=j...]
    unnamed x4 -> x0, local copies, waits for them, and re-layouts: 1.78 us -> none
  transfers between devices with their start and end apart: 17 -> 17, of which waited for: 9 -> 10; matrix products, arithmetic and copies ran while one was open for 1% -> 0% of each run, Pallas kernels for 6% -> 8%
where the time goes in v9:
time: 137 us; the launch traced here: 136 us
  starting transfers between devices  75 us (55%)
  waiting for transfers between devices  44 us (32%)
  Pallas kernels  16.1 us (12%)
    all_to_all x4, starting transfers between devices, exchange(): return lax.all_to_all(x, axes, split_axis=0, concat_axis=0, tiled=True)  31.6 us
    all_to_all x4, waiting for transfers between devices, exchange(): return lax.all_to_all(x, axes, split_axis=0, concat_axis=0, tiled=True)  24.3 us
    ppermute x6, starting transfers between devices, shifted(): return lax.ppermute(x, axis, [(i, (i + by) % n) for i in range(n)])  20.3 us
    ppermute x4, starting transfers between devices, ring_step(): return lax.ppermute(x, ('z', 'c'), moves)  13.1 us
    ppermute x3, starting transfers between devices, shifted_x(): lax.ppermute(x, ('xl', 'xh'), [(at(i), at((i + by) % 4)) for i in range(4)])  10.1 us
    ppermute x4, waiting for transfers between devices, ring_step(): return lax.ppermute(x, ('z', 'c'), moves)  9.59 us
    ppermute x3, waiting for transfers between devices, shifted_x(): lax.ppermute(x, ('xl', 'xh'), [(at(i), at((i + by) % 4)) for i in range(4)])  6.89 us
    pallas_call x2, Pallas kernels, on_blocks(): pl.pallas_call(kernel, in_specs=[VMEM] * len(args), out_specs=[VMEM] * le...  6.77 us
  transfers between devices with their start and end apart: 17, of which 10 were waited for; matrix products, arithmetic and copies ran while one was open for 0% of the time, Pallas kernels for 8%

profile of v9, /device:TPU:1, one launch (start us, length us, event | category | flops | bytes accessed | tf_op | source)
XLA Modules:
  0.0 135.9 jit_solution(14375723344096048931)
XLA Ops:
  0.6 8.7 %collective-permute-start = (bf16[256,512]{1,0:T(8,128)(2,1)}, bf16[256,512]{1,0:T(8,128)(2,1)S(1)}, u32[]{:S(2)}, u32[]{:S(2)}) collective-permute-start(bf16[256,512]{1,0:T(8,128)(2,1)} %amp_ref.1), channel_id=1, source_target_pairs={{0,1},{1,0},{2,3},{3,2},{4,5},{5,4},{6,7},{7,6},{8,9},{9,8},{10,11... | collective-permute-start | bytes 786440 | tf_op jit(solution)/shard_map/ppermute | solution.py:31
  9.4 1.4 collective-permute-done.got_ref
  10.7 1.0 shard_map.52.refs_0_
  11.7 5.3 %collective-permute-start.1 = (bf16[256,1024]{1,0:T(8,128)(2,1)S(1)}, bf16[256,1024]{1,0:T(8,128)(2,1)S(1)}, u32[]{:S(2)}, u32[]{:S(2)}) collective-permute-start(bf16[256,1024]{1,0:T(8,128)(2,1)S(1)} %shard_map.52.refs_0_), channel_id=1, source_target_pairs={{0,32},{32,64},{64,96},{96,128},{128,160},{160,192},{192,224},{224... | collective-permute-start | bytes 1572872 | tf_op jit(solution)/shard_map/ppermute | solution.py:42
  17.1 1.7 %shard_map.50 = bf16[8,2,128,128]{3,2,1,0:T(8,128)(2,1)} custom-call(bf16[256,128]{1,0:T(8,128)(2,1)} %in_ref.1), custom_call_target="tpu_custom_call" | custom-call | tf_op jit(solution)/shard_map/pallas_call | solution.py:154
  18.8 7.2 %all-to-all-start = ((bf16[16,128,128]{2,1,0:T(8,128)(2,1)}), bf16[16,128,128]{2,1,0:T(8,128)(2,1)S(1)}, u32[]{:S(2)}, u32[]{:S(2)}) async-start(bf16[16,128,128]{2,1,0:T(8,128)(2,1)} %bitcast), calls=%async_computation | async-start | bytes 1048576 | tf_op jit(solution)/shard_map/all_to_all | solution.py:35
  26.0 0.0 collective-permute-done.1.refs_1_
  26.0 2.2 %collective-permute-start.2 = (bf16[256,1024]{1,0:T(8,128)(2,1)S(1)}, bf16[256,1024]{1,0:T(8,128)(2,1)S(1)}, u32[]{:S(2)}, u32[]{:S(2)}) collective-permute-start(bf16[256,1024]{1,0:T(8,128)(2,1)S(1)} %collective-permute-done.1.refs_1_), channel_id=1, source_target_pairs={{0,32},{32,64},{64,96},{96,128},{128,160},{160,192},{192,224},{224... | collective-permute-start | bytes 1572872 | tf_op jit(solution)/shard_map/ppermute | solution.py:42
  28.2 8.0 %collective-permute-done.2.refs_2_ = bf16[256,1024]{1,0:T(8,128)(2,1)S(1)} collective-permute-done((bf16[256,1024]{1,0:T(8,128)(2,1)S(1)}, bf16[256,1024]{1,0:T(8,128)(2,1)S(1)}, u32[]{:S(2)}, u32[]{:S(2)}) %collective-permute-start.2) | collective-permute-done | bytes 524320 | tf_op jit(solution)/shard_map/ppermute | solution.py:42
  36.2 3.4 %collective-permute-start.3 = (bf16[256,1024]{1,0:T(8,128)(2,1)S(1)}, bf16[256,1024]{1,0:T(8,128)(2,1)S(1)}, u32[]{:S(2)}, u32[]{:S(2)}) collective-permute-start(bf16[256,1024]{1,0:T(8,128)(2,1)S(1)} %collective-permute-done.2.refs_2_), channel_id=1, source_target_pairs={{0,32},{32,64},{64,96},{96,128},{128,160},{160,192},{192,224},{224... | collective-permute-start | bytes 1572872 | tf_op jit(solution)/shard_map/ppermute | solution.py:42
  39.6 3.6 %all-to-all-done = bf16[16,128,128]{2,1,0:T(8,128)(2,1)S(1)} async-done(((bf16[16,128,128]{2,1,0:T(8,128)(2,1)}), bf16[16,128,128]{2,1,0:T(8,128)(2,1)S(1)}, u32[]{:S(2)}, u32[]{:S(2)}) %all-to-all-start) | async-done | bytes 524320 | tf_op jit(solution)/shard_map/all_to_all | solution.py:35
  43.2 1.1 shard_map.51
  44.4 4.0 %all-to-all-start.1 = ((bf16[4,4,2,128,128]{4,3,2,1,0:T(8,128)(2,1)}), bf16[4,4,2,128,128]{4,3,2,1,0:T(8,128)(2,1)S(1)}, u32[]{:S(2)}, u32[]{:S(2)}) async-start(bf16[4,4,2,128,128]{4,3,2,1,0:T(8,128)(2,1)} %bitcast.2), calls=%async_computation.1 | async-start | bytes 2097152 | tf_op jit(solution)/shard_map/all_to_all | solution.py:35
  48.4 1.9 %collective-permute-start.5 = (bf16[256,1024]{1,0:T(8,128)(2,1)S(1)}, bf16[256,1024]{1,0:T(8,128)(2,1)}, u32[]{:S(2)}, u32[]{:S(2)}) collective-permute-start(bf16[256,1024]{1,0:T(8,128)(2,1)S(1)} %collective-permute-done.1.refs_1_), channel_id=1, source_target_pairs={{0,1},{1,0},{2,3},{3,2},{4,5},{5,4},{6,7},{7,6},{8,9},{9,8},{10,11... | collective-permute-start | bytes 1572872 | tf_op jit(solution)/shard_map/ppermute | solution.py:31
  50.3 2.4 %collective-permute-start.6 = (bf16[256,1024]{1,0:T(8,128)(2,1)S(1)}, bf16[256,1024]{1,0:T(8,128)(2,1)}, u32[]{:S(2)}, u32[]{:S(2)}) collective-permute-start(bf16[256,1024]{1,0:T(8,128)(2,1)S(1)} %collective-permute-done.2.refs_2_), channel_id=1, source_target_pairs={{0,1},{1,0},{2,3},{3,2},{4,5},{5,4},{6,7},{7,6},{8,9},{9,8},{10,11... | collective-permute-start | bytes 1572872 | tf_op jit(solution)/shard_map/ppermute | solution.py:31
  52.7 0.0 collective-permute-done.3.refs_3_
  52.7 1.9 %collective-permute-start.7 = (bf16[256,1024]{1,0:T(8,128)(2,1)S(1)}, bf16[256,1024]{1,0:T(8,128)(2,1)}, u32[]{:S(2)}, u32[]{:S(2)}) collective-permute-start(bf16[256,1024]{1,0:T(8,128)(2,1)S(1)} %collective-permute-done.3.refs_3_), channel_id=1, source_target_pairs={{0,1},{1,0},{2,3},{3,2},{4,5},{5,4},{6,7},{7,6},{8,9},{9,8},{10,11... | collective-permute-start | bytes 1572872 | tf_op jit(solution)/shard_map/ppermute | solution.py:31
  54.6 2.2 %collective-permute-start.4 = (bf16[256,1024]{1,0:T(8,128)(2,1)S(1)}, bf16[256,1024]{1,0:T(8,128)(2,1)}, u32[]{:S(2)}, u32[]{:S(2)}) collective-permute-start(bf16[256,1024]{1,0:T(8,128)(2,1)S(1)} %collective-permute-done.3.refs_3_), channel_id=1, source_target_pairs={{0,32},{32,64},{64,96},{96,128},{128,160},{160,192},{192,224},{224... | collective-permute-start | bytes 1572872 | tf_op jit(solution)/shard_map/ppermute | solution.py:42
  56.9 0.0 collective-permute-done.5.refs_5_
  56.9 6.5 %all-to-all-done.1 = bf16[4,4,2,128,128]{4,3,2,1,0:T(8,128)(2,1)S(1)} async-done(((bf16[4,4,2,128,128]{4,3,2,1,0:T(8,128)(2,1)}), bf16[4,4,2,128,128]{4,3,2,1,0:T(8,128)(2,1)S(1)}, u32[]{:S(2)}, u32[]{:S(2)}) %all-to-all-start.1) | async-done | bytes 1048608 | tf_op jit(solution)/shard_map/all_to_all | solution.py:35
  63.4 0.0 collective-permute-done.6.refs_6_
  63.4 0.0 collective-permute-done.7.refs_7_
  63.4 1.6 %collective-permute-done.4.refs_4_ = bf16[256,1024]{1,0:T(8,128)(2,1)} collective-permute-done((bf16[256,1024]{1,0:T(8,128)(2,1)S(1)}, bf16[256,1024]{1,0:T(8,128)(2,1)}, u32[]{:S(2)}, u32[]{:S(2)}) %collective-permute-start.4) | collective-permute-done | bytes 524320 | tf_op jit(solution)/shard_map/ppermute | solution.py:42
  65.0 3.6 %shard_map.53 = (f32[128,1024]{1,0:T(8,128)S(1)}, f32[128,1024]{1,0:T(8,128)}, bf16[128,1024]{1,0:T(8,128)(2,1)S(1)}, bf16[128,1024]{1,0:T(8,128)(2,1)S(1)}) custom-call(bf16[2,2,4,2,128,128]{5,4,3,2,1,0:T(8,128)(2,1)S(1)} %bitcast.8, bf16[256,1024]{1,0:T(8,128)(2,1)S(1)} %shard_map.52.refs_0_, bf16[256,1024]{1,0:T(8,128)(2,1)S(1)} %collective-permute-done.1.refs_1_, ...), custom_call_target="tpu_custom_call" | custom-call | tf_op jit(solution)/shard_map/pallas_call | solution.py:193
  68.6 3.4 %collective-permute-start.8 = (bf16[128,1024]{1,0:T(8,128)(2,1)S(1)}, bf16[128,1024]{1,0:T(8,128)(2,1)S(1)}, u32[]{:S(2)}, u32[]{:S(2)}) collective-permute-start(bf16[128,1024]{1,0:T(8,128)(2,1)S(1)} %get-tuple-element.11), channel_id=1, source_target_pairs={{0,256},{256,0},{1,257},{257,1},{2,258},{258,2},{3,259},{259,3},{4... | collective-permute-start | bytes 786440 | tf_op jit(solution)/shard_map/ppermute | solution.py:31
  71.9 1.9 %collective-permute-start.9 = (bf16[128,1024]{1,0:T(8,128)(2,1)S(1)}, bf16[128,1024]{1,0:T(8,128)(2,1)S(1)}, u32[]{:S(2)}, u32[]{:S(2)}) collective-permute-start(bf16[128,1024]{1,0:T(8,128)(2,1)S(1)} %get-tuple-element.13), channel_id=1, source_target_pairs={{0,256},{256,0},{1,257},{257,1},{2,258},{258,2},{3,259},{259,3},{4... | collective-permute-start | bytes 786440 | tf_op jit(solution)/shard_map/ppermute | solution.py:31
  73.9 1.8 %collective-permute-done.8.arrived_ref = bf16[128,1024]{1,0:T(8,128)(2,1)S(1)} collective-permute-done((bf16[128,1024]{1,0:T(8,128)(2,1)S(1)}, bf16[128,1024]{1,0:T(8,128)(2,1)S(1)}, u32[]{:S(2)}, u32[]{:S(2)}) %collective-permute-start.8) | collective-permute-done | bytes 262176 | tf_op jit(solution)/shard_map/ppermute | solution.py:31
  75.7 0.7 shard_map.54.own_ref
  76.4 9.1 %all-to-all-start.3 = ((bf16[16,8,1024]{2,1,0:T(8,128)(2,1)}), bf16[16,8,1024]{2,1,0:T(8,128)(2,1)S(1)}, u32[]{:S(2)}, u32[]{:S(2)}) async-start(bf16[16,8,1024]{2,1,0:T(8,128)(2,1)} %bitcast.7), calls=%async_computation.3 | async-start | bytes 524288 | tf_op jit(solution)/shard_map/all_to_all | solution.py:35
  85.5 0.0 collective-permute-done.9.arrived_ref
  85.5 3.2 %shard_map.55 = (bf16[4,2,128,128]{3,2,1,0:T(8,128)(2,1)S(1)}, bf16[4,2,128,128]{3,2,1,0:T(8,128)(2,1)S(1)}, bf16[4,2,128,128]{3,2,1,0:T(8,128)(2,1)S(1)}, bf16[4,2,128,128]{3,2,1,0:T(8,128)(2,1)S(1)}) custom-call(bf16[128,1024]{1,0:T(8,128)(2,1)} %shard_map.54.own_ref, f32[128,1024]{1,0:T(8,128)} %get-tuple-element.12.other_ref, ...), custom_call_target="tpu_custom_call" | custom-call | tf_op jit(solution)/shard_map/pallas_call | solution.py:193
  88.7 4.8 %collective-permute-start.10 = (bf16[4,2,128,128]{3,2,1,0:T(8,128)(2,1)S(1)}, bf16[4,2,128,128]{3,2,1,0:T(8,128)(2,1)S(1)}, u32[]{:S(2)}, u32[]{:S(2)}) collective-permute-start(bf16[4,2,128,128]{3,2,1,0:T(8,128)(2,1)S(1)} %get-tuple-element.15), channel_id=1, source_target_pairs={{0,2},{256,258},{2,0},{258,256},{1,3},{257,259},{3,1},{259,257},{4... | collective-permute-start | bytes 786440 | tf_op jit(solution)/shard_map/ppermute | solution.py:47
  93.5 1.9 %collective-permute-start.11 = (bf16[4,2,128,128]{3,2,1,0:T(8,128)(2,1)S(1)}, bf16[4,2,128,128]{3,2,1,0:T(8,128)(2,1)S(1)}, u32[]{:S(2)}, u32[]{:S(2)}) collective-permute-start(bf16[4,2,128,128]{3,2,1,0:T(8,128)(2,1)S(1)} %get-tuple-element.16), channel_id=1, source_target_pairs={{0,258},{256,0},{2,256},{258,2},{1,259},{257,1},{3,257},{259,3},{4... | collective-permute-start | bytes 786440 | tf_op jit(solution)/shard_map/ppermute | solution.py:47
  95.4 3.4 %collective-permute-start.12 = (bf16[4,2,128,128]{3,2,1,0:T(8,128)(2,1)S(1)}, bf16[4,2,128,128]{3,2,1,0:T(8,128)(2,1)S(1)}, u32[]{:S(2)}, u32[]{:S(2)}) collective-permute-start(bf16[4,2,128,128]{3,2,1,0:T(8,128)(2,1)S(1)} %get-tuple-element.17), channel_id=1, source_target_pairs={{0,256},{256,2},{2,258},{258,0},{1,257},{257,3},{3,259},{259,1},{4... | collective-permute-start | bytes 786440 | tf_op jit(solution)/shard_map/ppermute | solution.py:47
  98.8 0.1 collective-permute-done.10.far_ref
  98.8 5.1 %collective-permute-done.11.left_ref = bf16[4,2,128,128]{3,2,1,0:T(8,128)(2,1)S(1)} collective-permute-done((bf16[4,2,128,128]{3,2,1,0:T(8,128)(2,1)S(1)}, bf16[4,2,128,128]{3,2,1,0:T(8,128)(2,1)S(1)}, u32[]{:S(2)}, u32[]{:S(2)}) %collective-permute-start.11) | collective-permute-done | bytes 262176 | tf_op jit(solution)/shard_map/ppermute | solution.py:47
  104.0 1.7 %collective-permute-done.12.right_ref = bf16[4,2,128,128]{3,2,1,0:T(8,128)(2,1)S(1)} collective-permute-done((bf16[4,2,128,128]{3,2,1,0:T(8,128)(2,1)S(1)}, bf16[4,2,128,128]{3,2,1,0:T(8,128)(2,1)S(1)}, u32[]{:S(2)}, u32[]{:S(2)}) %collective-permute-start.12) | collective-permute-done | bytes 262176 | tf_op jit(solution)/shard_map/ppermute | solution.py:47
  105.6 0.9 shard_map.56
  106.6 0.0 all-to-all-done.3.got_ref
  106.6 11.3 %all-to-all-start.2 = ((bf16[16,128,128]{2,1,0:T(8,128)(2,1)}), bf16[16,128,128]{2,1,0:T(8,128)(2,1)S(1)}, u32[]{:S(2)}, u32[]{:S(2)}) async-start(bf16[16,128,128]{2,1,0:T(8,128)(2,1)} %bitcast.4), calls=%async_computation.2 | async-start | bytes 1048576 | tf_op jit(solution)/shard_map/all_to_all | solution.py:35
  117.9 3.0 %shard_map.58 = bf16[8,20480]{1,0:T(8,128)(2,1)} custom-call(bf16[16,8,1024]{2,1,0:T(8,128)(2,1)S(1)} %all-to-all-done.3.got_ref, bf16[1024,1280]{1,0:T(8,128)(2,1)} %coef_ref.1), custom_call_target="tpu_custom_call" | custom-call | tf_op jit(solution)/shard_map/pallas_call | solution.py:231
  120.9 14.2 %all-to-all-done.2 = bf16[16,128,128]{2,1,0:T(8,128)(2,1)S(1)} async-done(((bf16[16,128,128]{2,1,0:T(8,128)(2,1)}), bf16[16,128,128]{2,1,0:T(8,128)(2,1)S(1)}, u32[]{:S(2)}, u32[]{:S(2)}) %all-to-all-start.2) | async-done | bytes 524320 | tf_op jit(solution)/shard_map/all_to_all | solution.py:35
  135.1 0.8 shard_map.57
Async XLA Ops:
  0.6 10.1 %collective-permute-start = (bf16[256,512]{1,0:T(8,128)(2,1)}, bf16[256,512]{1,0:T(8,128)(2,1)S(1)}, u32[]{:S(2)}, u32[]{:S(2)}) collective-permute-start(bf16[256,512]{1,0:T(8,128)(2,1)} %amp_ref.1), channel_id=1, source_target_pairs={{0,1},{1,0},{2,3},{3,2},{4,5},{5,4},{6,7},{7,6},{8,9},{9,8},{10,11... | collective-permute-start | bytes 786440 | tf_op jit(solution)/shard_map/ppermute | solution.py:31
  11.7 14.3 %collective-permute-start.1 = (bf16[256,1024]{1,0:T(8,128)(2,1)S(1)}, bf16[256,1024]{1,0:T(8,128)(2,1)S(1)}, u32[]{:S(2)}, u32[]{:S(2)}) collective-permute-start(bf16[256,1024]{1,0:T(8,128)(2,1)S(1)} %shard_map.52.refs_0_), channel_id=1, source_target_pairs={{0,32},{32,64},{64,96},{96,128},{128,160},{160,192},{192,224},{224... | collective-permute-start | bytes 1572872 | tf_op jit(solution)/shard_map/ppermute | solution.py:42
  18.8 24.4 %all-to-all-start = ((bf16[16,128,128]{2,1,0:T(8,128)(2,1)}), bf16[16,128,128]{2,1,0:T(8,128)(2,1)S(1)}, u32[]{:S(2)}, u32[]{:S(2)}) async-start(bf16[16,128,128]{2,1,0:T(8,128)(2,1)} %bitcast), calls=%async_computation | async-start | bytes 1048576 | tf_op jit(solution)/shard_map/all_to_all | solution.py:35
  26.0 10.2 %collective-permute-start.2 = (bf16[256,1024]{1,0:T(8,128)(2,1)S(1)}, bf16[256,1024]{1,0:T(8,128)(2,1)S(1)}, u32[]{:S(2)}, u32[]{:S(2)}) collective-permute-start(bf16[256,1024]{1,0:T(8,128)(2,1)S(1)} %collective-permute-done.1.refs_1_), channel_id=1, source_target_pairs={{0,32},{32,64},{64,96},{96,128},{128,160},{160,192},{192,224},{224... | collective-permute-start | bytes 1572872 | tf_op jit(solution)/shard_map/ppermute | solution.py:42
  36.2 16.5 %collective-permute-start.3 = (bf16[256,1024]{1,0:T(8,128)(2,1)S(1)}, bf16[256,1024]{1,0:T(8,128)(2,1)S(1)}, u32[]{:S(2)}, u32[]{:S(2)}) collective-permute-start(bf16[256,1024]{1,0:T(8,128)(2,1)S(1)} %collective-permute-done.2.refs_2_), channel_id=1, source_target_pairs={{0,32},{32,64},{64,96},{96,128},{128,160},{160,192},{192,224},{224... | collective-permute-start | bytes 1572872 | tf_op jit(solution)/shard_map/ppermute | solution.py:42
  44.4 19.1 %all-to-all-start.1 = ((bf16[4,4,2,128,128]{4,3,2,1,0:T(8,128)(2,1)}), bf16[4,4,2,128,128]{4,3,2,1,0:T(8,128)(2,1)S(1)}, u32[]{:S(2)}, u32[]{:S(2)}) async-start(bf16[4,4,2,128,128]{4,3,2,1,0:T(8,128)(2,1)} %bitcast.2), calls=%async_computation.1 | async-start | bytes 2097152 | tf_op jit(solution)/shard_map/all_to_all | solution.py:35
  48.4 8.5 %collective-permute-start.5 = (bf16[256,1024]{1,0:T(8,128)(2,1)S(1)}, bf16[256,1024]{1,0:T(8,128)(2,1)}, u32[]{:S(2)}, u32[]{:S(2)}) collective-permute-start(bf16[256,1024]{1,0:T(8,128)(2,1)S(1)} %collective-permute-done.1.refs_1_), channel_id=1, source_target_pairs={{0,1},{1,0},{2,3},{3,2},{4,5},{5,4},{6,7},{7,6},{8,9},{9,8},{10,11... | collective-permute-start | bytes 1572872 | tf_op jit(solution)/shard_map/ppermute | solution.py:31
  50.3 13.1 %collective-permute-start.6 = (bf16[256,1024]{1,0:T(8,128)(2,1)S(1)}, bf16[256,1024]{1,0:T(8,128)(2,1)}, u32[]{:S(2)}, u32[]{:S(2)}) collective-permute-start(bf16[256,1024]{1,0:T(8,128)(2,1)S(1)} %collective-permute-done.2.refs_2_), channel_id=1, source_target_pairs={{0,1},{1,0},{2,3},{3,2},{4,5},{5,4},{6,7},{7,6},{8,9},{9,8},{10,11... | collective-permute-start | bytes 1572872 | tf_op jit(solution)/shard_map/ppermute | solution.py:31
  52.7 10.7 %collective-permute-start.7 = (bf16[256,1024]{1,0:T(8,128)(2,1)S(1)}, bf16[256,1024]{1,0:T(8,128)(2,1)}, u32[]{:S(2)}, u32[]{:S(2)}) collective-permute-start(bf16[256,1024]{1,0:T(8,128)(2,1)S(1)} %collective-permute-done.3.refs_3_), channel_id=1, source_target_pairs={{0,1},{1,0},{2,3},{3,2},{4,5},{5,4},{6,7},{7,6},{8,9},{9,8},{10,11... | collective-permute-start | bytes 1572872 | tf_op jit(solution)/shard_map/ppermute | solution.py:31
  54.6 10.3 %collective-permute-start.4 = (bf16[256,1024]{1,0:T(8,128)(2,1)S(1)}, bf16[256,1024]{1,0:T(8,128)(2,1)}, u32[]{:S(2)}, u32[]{:S(2)}) collective-permute-start(bf16[256,1024]{1,0:T(8,128)(2,1)S(1)} %collective-permute-done.3.refs_3_), channel_id=1, source_target_pairs={{0,32},{32,64},{64,96},{96,128},{128,160},{160,192},{192,224},{224... | collective-permute-start | bytes 1572872 | tf_op jit(solution)/shard_map/ppermute | solution.py:42
  68.6 7.1 %collective-permute-start.8 = (bf16[128,1024]{1,0:T(8,128)(2,1)S(1)}, bf16[128,1024]{1,0:T(8,128)(2,1)S(1)}, u32[]{:S(2)}, u32[]{:S(2)}) collective-permute-start(bf16[128,1024]{1,0:T(8,128)(2,1)S(1)} %get-tuple-element.11), channel_id=1, source_target_pairs={{0,256},{256,0},{1,257},{257,1},{2,258},{258,2},{3,259},{259,3},{4... | collective-permute-start | bytes 786440 | tf_op jit(solution)/shard_map/ppermute | solution.py:31
  71.9 13.6 %collective-permute-start.9 = (bf16[128,1024]{1,0:T(8,128)(2,1)S(1)}, bf16[128,1024]{1,0:T(8,128)(2,1)S(1)}, u32[]{:S(2)}, u32[]{:S(2)}) collective-permute-start(bf16[128,1024]{1,0:T(8,128)(2,1)S(1)} %get-tuple-element.13), channel_id=1, source_target_pairs={{0,256},{256,0},{1,257},{257,1},{2,258},{258,2},{3,259},{259,3},{4... | collective-permute-start | bytes 786440 | tf_op jit(solution)/shard_map/ppermute | solution.py:31
  76.4 30.1 %all-to-all-start.3 = ((bf16[16,8,1024]{2,1,0:T(8,128)(2,1)}), bf16[16,8,1024]{2,1,0:T(8,128)(2,1)S(1)}, u32[]{:S(2)}, u32[]{:S(2)}) async-start(bf16[16,8,1024]{2,1,0:T(8,128)(2,1)} %bitcast.7), calls=%async_computation.3 | async-start | bytes 524288 | tf_op jit(solution)/shard_map/all_to_all | solution.py:35
  88.7 10.1 %collective-permute-start.10 = (bf16[4,2,128,128]{3,2,1,0:T(8,128)(2,1)S(1)}, bf16[4,2,128,128]{3,2,1,0:T(8,128)(2,1)S(1)}, u32[]{:S(2)}, u32[]{:S(2)}) collective-permute-start(bf16[4,2,128,128]{3,2,1,0:T(8,128)(2,1)S(1)} %get-tuple-element.15), channel_id=1, source_target_pairs={{0,2},{256,258},{2,0},{258,256},{1,3},{257,259},{3,1},{259,257},{4... | collective-permute-start | bytes 786440 | tf_op jit(solution)/shard_map/ppermute | solution.py:47
  93.5 10.5 %collective-permute-start.11 = (bf16[4,2,128,128]{3,2,1,0:T(8,128)(2,1)S(1)}, bf16[4,2,128,128]{3,2,1,0:T(8,128)(2,1)S(1)}, u32[]{:S(2)}, u32[]{:S(2)}) collective-permute-start(bf16[4,2,128,128]{3,2,1,0:T(8,128)(2,1)S(1)} %get-tuple-element.16), channel_id=1, source_target_pairs={{0,258},{256,0},{2,256},{258,2},{1,259},{257,1},{3,257},{259,3},{4... | collective-permute-start | bytes 786440 | tf_op jit(solution)/shard_map/ppermute | solution.py:47
  95.4 10.3 %collective-permute-start.12 = (bf16[4,2,128,128]{3,2,1,0:T(8,128)(2,1)S(1)}, bf16[4,2,128,128]{3,2,1,0:T(8,128)(2,1)S(1)}, u32[]{:S(2)}, u32[]{:S(2)}) collective-permute-start(bf16[4,2,128,128]{3,2,1,0:T(8,128)(2,1)S(1)} %get-tuple-element.17), channel_id=1, source_target_pairs={{0,256},{256,2},{2,258},{258,0},{1,257},{257,3},{3,259},{259,1},{4... | collective-permute-start | bytes 786440 | tf_op jit(solution)/shard_map/ppermute | solution.py:47
  106.6 28.5 %all-to-all-start.2 = ((bf16[16,128,128]{2,1,0:T(8,128)(2,1)}), bf16[16,128,128]{2,1,0:T(8,128)(2,1)S(1)}, u32[]{:S(2)}, u32[]{:S(2)}) async-start(bf16[16,128,128]{2,1,0:T(8,128)(2,1)} %bitcast.4), calls=%async_computation.2 | async-start | bytes 1048576 | tf_op jit(solution)/shard_map/all_to_all | solution.py:35

commit v10 on v9

--- a/solution.py
+++ b/solution.py
@@ -47,10 +47,21 @@
     return lax.ppermute(x, ("xl", "xh"), [(at(i), at((i + by) % 4)) for i in range(4)])
 
 
-def blocks_of(refs):
-    toward = 2 * lax.axis_index("c") - 1
-    near = [(toward * s, ref[...]) for s, ref in enumerate(refs[:5])]
-    return near + [(-toward * (i + 1), ref[...]) for i, ref in enumerate(refs[5:])]
+NEAR = 4
+
+
+def toward(s):
+    return (2 * lax.axis_index("c") - 1) * s
+
+
+FAR_STEPS = (4, -1, -2, -3)
+
+
+def copies_of(refs, bufs, sems):
+    copies = [pltpu.make_async_copy(ref, bufs.at[i], sems.at[i]) for i, ref in enumerate(refs)]
+    for copy in copies:
+        copy.start()
+    return copies
 
 
 def place(offset):
@@ -82,13 +93,23 @@
 
 
 def fitted_kernel(metric_ref, *refs):
-    blocks = blocks_of(refs[:8])
-    wide_refs, narrow_refs = refs[8:10], refs[10:12]
+    near_refs, far_refs = refs[:NEAR], refs[NEAR : 2 * NEAR]
+    wide_refs, narrow_refs, (bufs, sems) = refs[8:10], refs[10:12], refs[12:]
+    copies = copies_of(far_refs, bufs, sems)
     xl = lax.axis_index("xl")
-    rhs = jnp.concatenate([b for _, b in blocks], axis=0)
-    for i, h in enumerate((xl, 1 - xl)):
-        lhs = [metric_ref[(h, *place(o), j)] for o, _ in blocks for j in range(2)]
-        out = jnp.dot(jnp.concatenate(lhs, axis=1), rhs, preferred_element_type=F32)
+
+    def product(h, steps, blocks):
+        lhs = [metric_ref[(h, *place(toward(s)), j)] for s in steps for j in range(2)]
+        rhs = jnp.concatenate(blocks, axis=0)
+        return jnp.dot(jnp.concatenate(lhs, axis=1), rhs, preferred_element_type=F32)
+
+    halves = (xl, 1 - xl)
+    for i, h in enumerate(halves):
+        wide_refs[i][...] = product(h, range(NEAR), [ref[...] for ref in near_refs])
+    for copy in copies:
+        copy.wait()
+    for i, h in enumerate(halves):
+        out = wide_refs[i][...] + product(h, FAR_STEPS, [bufs[k] for k in range(NEAR)])
         wide_refs[i][...] = out
         narrow_refs[i][...] = out.astype(BF16)
 
@@ -97,23 +118,40 @@
     out_ref[...] = (own_ref[...] + arrived_ref[...].astype(F32)).astype(BF16)
 
 
-def density_kernel(own_ref, other_ref, arrived_ref, *refs):
-    blocks, outs, all_ref = blocks_of(refs[:8]), refs[8:12], refs[12]
+def density_kernel(own_ref, arrived_ref, *refs):
+    near_refs, far_refs, other_ref = refs[:NEAR], refs[NEAR : 2 * NEAR], refs[8]
+    outs, (all_ref, bufs, sems, other_buf, other_sem) = refs[9:13], refs[13:]
+    other_copy = pltpu.make_async_copy(other_ref, other_buf, other_sem)
+    other_copy.start()
+    copies = copies_of(far_refs, bufs, sems)
     xl = lax.axis_index("xl")
     x = 2 * lax.axis_index("xh") + xl
-    other = (other_ref[...] + arrived_ref[...].astype(F32)).astype(BF16)
-    fitted = jnp.concatenate([own_ref[...], other], axis=0)
     rows = own_ref.shape[0]
-    for offset, block in blocks:
+
+    def put(step, block, fitted, halves):
         out = lax.dot_general(
             block, fitted, (((1,), (1,)), ((), ())), preferred_element_type=F32
         ).astype(BF16)
-        far, near = place(offset)
+        far, near = place(toward(step))
         half = out.shape[0] // 2
-        for h, part in ((xl, out[:, :rows]), (1 - xl, out[:, rows:])):
+        for i, h in enumerate(halves):
             slot = lax.rem(2 * far + h + 4 - x, 4)
             for j in range(2):
-                all_ref[slot, near, j] = part[j * half : (j + 1) * half]
+                part = out[j * half : (j + 1) * half, i * rows : (i + 1) * rows]
+                all_ref[slot, near, j] = part
+
+    own = own_ref[...]
+    for s, ref in enumerate(near_refs):
+        put(s, ref[...], own, (xl,))
+    other_copy.wait()
+    other = (other_buf[...] + arrived_ref[...].astype(F32)).astype(BF16)
+    for s, ref in enumerate(near_refs):
+        put(s, ref[...], other, (1 - xl,))
+    for copy in copies:
+        copy.wait()
+    both = jnp.concatenate([own, other], axis=0)
+    for i, s in enumerate(FAR_STEPS):
+        put(s, bufs[i], both, (xl, 1 - xl))
     for s in range(4):
         outs[s][...] = all_ref[s]
 
@@ -187,23 +225,26 @@
     steps.append(ring_step(steps[3]))
     shape = (half, 2 * cols)
 
-    def on_blocks(kernel, outs, scratch, *args):
-        spaces = [pltpu.HBM if a.dtype == F32 else pltpu.VMEM for a in args] + [pltpu.VMEM] * 5 + [pltpu.HBM] * 3
-        args = list(map(pltpu.with_memory_space_constraint, (*args, *steps, *swaps), spaces))
+    near, far = steps[:NEAR], [steps[NEAR], *swaps]
+
+    def on_blocks(kernel, outs, scratch, args, last=()):
+        in_near = [pltpu.with_memory_space_constraint(a, pltpu.VMEM) for a in (*args, *near)]
+        in_far = [pltpu.with_memory_space_constraint(a, pltpu.HBM) for a in (*far, *last)]
+        buffers = [pltpu.VMEM((NEAR, rows, 2 * cols), BF16), pltpu.SemaphoreType.DMA((NEAR,))]
         return pl.pallas_call(
             kernel,
-            in_specs=[VMEM] * len(args),
+            in_specs=[VMEM] * len(in_near) + [pl.BlockSpec(memory_space=pl.ANY)] * len(in_far),
             out_specs=[VMEM] * len(outs),
             out_shape=[space(shape, dtype) for space, shape, dtype in outs],
-            scratch_shapes=scratch,
+            scratch_shapes=scratch[:1] + buffers + scratch[1:],
             compiler_params=PARAMS,
-        )(*args)
+        )(*in_near, *in_far)
 
     own, other, own_sent, other_sent = on_blocks(
         fitted_kernel,
         [(pltpu.VMEM, shape, F32), (pltpu.HBM, shape, F32)] + [(pltpu.VMEM, shape, BF16)] * 2,
         [],
-        part,
+        [part],
     )
     own_arrived = shifted(other_sent, "xl", 1)
     other_arrived = shifted(own_sent, "xl", 1)
@@ -212,8 +253,9 @@
     slots = on_blocks(
         density_kernel,
         [(pltpu.VMEM, piece, BF16)] * 4,
-        [pltpu.VMEM((4, *piece), BF16)],
-        fitted, other, other_arrived,
+        [pltpu.VMEM((4, *piece), BF16), pltpu.VMEM(shape, F32), pltpu.SemaphoreType.DMA],
+        [fitted, other_arrived],
+        [other],
     )
     arrived = [shifted_x(slots[s], s) for s in (2, 3, 1)]
     (xs,) = in_vmem(half_sum_kernel, [((8, 2, half, half), BF16)], slots[0], *arrived)

time: 137 us -> 138 us (level)
  transfers between devices with their start and end apart: 17 -> 17, of which waited for: 10 -> 10; matrix products, arithmetic and copies ran while one was open for 0% -> 0% of each run, Pallas kernels for 8% -> 9%
where the time goes in v10:
time: 138 us; the launch traced here: 137 us
  starting transfers between devices  75.1 us (54%)
  waiting for transfers between devices  43.9 us (32%)
  Pallas kernels  17.2 us (12%)
    all_to_all x4, starting transfers between devices, exchange(): return lax.all_to_all(x, axes, split_axis=0, concat_axis=0, tiled=True)  31.6 us
    all_to_all x4, waiting for transfers between devices, exchange(): return lax.all_to_all(x, axes, split_axis=0, concat_axis=0, tiled=True)  24.3 us
    ppermute x6, starting transfers between devices, shifted(): return lax.ppermute(x, axis, [(i, (i + by) % n) for i in range(n)])  20.3 us
    ppermute x4, starting transfers between devices, ring_step(): return lax.ppermute(x, ('z', 'c'), moves)  13.1 us
    ppermute x3, starting transfers between devices, shifted_x(): lax.ppermute(x, ('xl', 'xh'), [(at(i), at((i + by) % 4)) for i in range(4)])  10.1 us
    ppermute x4, waiting for transfers between devices, ring_step(): return lax.ppermute(x, ('z', 'c'), moves)  9.59 us
    pallas_call x2, Pallas kernels, on_blocks(): pl.pallas_call(kernel, in_specs=[VMEM] * len(in_near) + [pl.BlockSpec(mem...  7.87 us
    ppermute x3, waiting for transfers between devices, shifted_x(): lax.ppermute(x, ('xl', 'xh'), [(at(i), at((i + by) % 4)) for i in range(4)])  6.84 us
  transfers between devices with their start and end apart: 17, of which 10 were waited for; matrix products, arithmetic and copies ran while one was open for 0% of the time, Pallas kernels for 9%

profile of v10, /device:TPU:1, one launch (start us, length us, event | category | flops | bytes accessed | tf_op | source)
XLA Modules:
  0.0 137.0 jit_solution(5867582011433887570)
XLA Ops:
  0.6 8.7 %collective-permute-start = (bf16[256,512]{1,0:T(8,128)(2,1)}, bf16[256,512]{1,0:T(8,128)(2,1)S(1)}, u32[]{:S(2)}, u32[]{:S(2)}) collective-permute-start(bf16[256,512]{1,0:T(8,128)(2,1)} %amp_ref.1), channel_id=1, source_target_pairs={{0,1},{1,0},{2,3},{3,2},{4,5},{5,4},{6,7},{7,6},{8,9},{9,8},{10,11... | collective-permute-start | bytes 786440 | tf_op jit(solution)/shard_map/ppermute | solution.py:31
  9.4 1.4 collective-permute-done.got_ref
  10.7 1.0 shard_map.52.refs_0_
  11.7 5.3 %collective-permute-start.1 = (bf16[256,1024]{1,0:T(8,128)(2,1)S(1)}, bf16[256,1024]{1,0:T(8,128)(2,1)S(1)}, u32[]{:S(2)}, u32[]{:S(2)}) collective-permute-start(bf16[256,1024]{1,0:T(8,128)(2,1)S(1)} %shard_map.52.refs_0_), channel_id=1, source_target_pairs={{0,32},{32,64},{64,96},{96,128},{128,160},{160,192},{192,224},{224... | collective-permute-start | bytes 1572872 | tf_op jit(solution)/shard_map/ppermute | solution.py:42
  17.1 1.7 %shard_map.50 = bf16[8,2,128,128]{3,2,1,0:T(8,128)(2,1)} custom-call(bf16[256,128]{1,0:T(8,128)(2,1)} %in_ref.1), custom_call_target="tpu_custom_call" | custom-call | tf_op jit(solution)/shard_map/pallas_call | solution.py:192
  18.8 7.2 %all-to-all-start = ((bf16[16,128,128]{2,1,0:T(8,128)(2,1)}), bf16[16,128,128]{2,1,0:T(8,128)(2,1)S(1)}, u32[]{:S(2)}, u32[]{:S(2)}) async-start(bf16[16,128,128]{2,1,0:T(8,128)(2,1)} %bitcast), calls=%async_computation | async-start | bytes 1048576 | tf_op jit(solution)/shard_map/all_to_all | solution.py:35
  26.0 0.0 collective-permute-done.1.refs_1_
  26.0 2.2 %collective-permute-start.2 = (bf16[256,1024]{1,0:T(8,128)(2,1)S(1)}, bf16[256,1024]{1,0:T(8,128)(2,1)S(1)}, u32[]{:S(2)}, u32[]{:S(2)}) collective-permute-start(bf16[256,1024]{1,0:T(8,128)(2,1)S(1)} %collective-permute-done.1.refs_1_), channel_id=1, source_target_pairs={{0,32},{32,64},{64,96},{96,128},{128,160},{160,192},{192,224},{224... | collective-permute-start | bytes 1572872 | tf_op jit(solution)/shard_map/ppermute | solution.py:42
  28.2 8.0 %collective-permute-done.2.refs_2_ = bf16[256,1024]{1,0:T(8,128)(2,1)S(1)} collective-permute-done((bf16[256,1024]{1,0:T(8,128)(2,1)S(1)}, bf16[256,1024]{1,0:T(8,128)(2,1)S(1)}, u32[]{:S(2)}, u32[]{:S(2)}) %collective-permute-start.2) | collective-permute-done | bytes 524320 | tf_op jit(solution)/shard_map/ppermute | solution.py:42
  36.2 3.4 %collective-permute-start.3 = (bf16[256,1024]{1,0:T(8,128)(2,1)S(1)}, bf16[256,1024]{1,0:T(8,128)(2,1)S(1)}, u32[]{:S(2)}, u32[]{:S(2)}) collective-permute-start(bf16[256,1024]{1,0:T(8,128)(2,1)S(1)} %collective-permute-done.2.refs_2_), channel_id=1, source_target_pairs={{0,32},{32,64},{64,96},{96,128},{128,160},{160,192},{192,224},{224... | collective-permute-start | bytes 1572872 | tf_op jit(solution)/shard_map/ppermute | solution.py:42
  39.6 3.6 %all-to-all-done = bf16[16,128,128]{2,1,0:T(8,128)(2,1)S(1)} async-done(((bf16[16,128,128]{2,1,0:T(8,128)(2,1)}), bf16[16,128,128]{2,1,0:T(8,128)(2,1)S(1)}, u32[]{:S(2)}, u32[]{:S(2)}) %all-to-all-start) | async-done | bytes 524320 | tf_op jit(solution)/shard_map/all_to_all | solution.py:35
  43.2 1.1 shard_map.51
  44.4 4.0 %all-to-all-start.1 = ((bf16[4,4,2,128,128]{4,3,2,1,0:T(8,128)(2,1)}), bf16[4,4,2,128,128]{4,3,2,1,0:T(8,128)(2,1)S(1)}, u32[]{:S(2)}, u32[]{:S(2)}) async-start(bf16[4,4,2,128,128]{4,3,2,1,0:T(8,128)(2,1)} %bitcast.2), calls=%async_computation.1 | async-start | bytes 2097152 | tf_op jit(solution)/shard_map/all_to_all | solution.py:35
  48.4 1.9 %collective-permute-start.5 = (bf16[256,1024]{1,0:T(8,128)(2,1)S(1)}, bf16[256,1024]{1,0:T(8,128)(2,1)}, u32[]{:S(2)}, u32[]{:S(2)}) collective-permute-start(bf16[256,1024]{1,0:T(8,128)(2,1)S(1)} %collective-permute-done.1.refs_1_), channel_id=1, source_target_pairs={{0,1},{1,0},{2,3},{3,2},{4,5},{5,4},{6,7},{7,6},{8,9},{9,8},{10,11... | collective-permute-start | bytes 1572872 | tf_op jit(solution)/shard_map/ppermute | solution.py:31
  50.3 2.4 %collective-permute-start.6 = (bf16[256,1024]{1,0:T(8,128)(2,1)S(1)}, bf16[256,1024]{1,0:T(8,128)(2,1)}, u32[]{:S(2)}, u32[]{:S(2)}) collective-permute-start(bf16[256,1024]{1,0:T(8,128)(2,1)S(1)} %collective-permute-done.2.refs_2_), channel_id=1, source_target_pairs={{0,1},{1,0},{2,3},{3,2},{4,5},{5,4},{6,7},{7,6},{8,9},{9,8},{10,11... | collective-permute-start | bytes 1572872 | tf_op jit(solution)/shard_map/ppermute | solution.py:31
  52.7 0.0 collective-permute-done.3.refs_3_
  52.7 1.9 %collective-permute-start.7 = (bf16[256,1024]{1,0:T(8,128)(2,1)S(1)}, bf16[256,1024]{1,0:T(8,128)(2,1)}, u32[]{:S(2)}, u32[]{:S(2)}) collective-permute-start(bf16[256,1024]{1,0:T(8,128)(2,1)S(1)} %collective-permute-done.3.refs_3_), channel_id=1, source_target_pairs={{0,1},{1,0},{2,3},{3,2},{4,5},{5,4},{6,7},{7,6},{8,9},{9,8},{10,11... | collective-permute-start | bytes 1572872 | tf_op jit(solution)/shard_map/ppermute | solution.py:31
  54.6 2.2 %collective-permute-start.4 = (bf16[256,1024]{1,0:T(8,128)(2,1)S(1)}, bf16[256,1024]{1,0:T(8,128)(2,1)}, u32[]{:S(2)}, u32[]{:S(2)}) collective-permute-start(bf16[256,1024]{1,0:T(8,128)(2,1)S(1)} %collective-permute-done.3.refs_3_), channel_id=1, source_target_pairs={{0,32},{32,64},{64,96},{96,128},{128,160},{160,192},{192,224},{224... | collective-permute-start | bytes 1572872 | tf_op jit(solution)/shard_map/ppermute | solution.py:42
  56.9 0.0 collective-permute-done.5.refs_5_
  56.9 6.5 %all-to-all-done.1 = bf16[4,4,2,128,128]{4,3,2,1,0:T(8,128)(2,1)S(1)} async-done(((bf16[4,4,2,128,128]{4,3,2,1,0:T(8,128)(2,1)}), bf16[4,4,2,128,128]{4,3,2,1,0:T(8,128)(2,1)S(1)}, u32[]{:S(2)}, u32[]{:S(2)}) %all-to-all-start.1) | async-done | bytes 1048608 | tf_op jit(solution)/shard_map/all_to_all | solution.py:35
  63.4 0.0 collective-permute-done.6.refs_6_
  63.4 0.0 collective-permute-done.7.refs_7_
  63.4 1.6 %collective-permute-done.4.refs_4_ = bf16[256,1024]{1,0:T(8,128)(2,1)} collective-permute-done((bf16[256,1024]{1,0:T(8,128)(2,1)S(1)}, bf16[256,1024]{1,0:T(8,128)(2,1)}, u32[]{:S(2)}, u32[]{:S(2)}) %collective-permute-start.4) | collective-permute-done | bytes 524320 | tf_op jit(solution)/shard_map/ppermute | solution.py:42
  65.0 3.3 %shard_map.53 = (f32[128,1024]{1,0:T(8,128)S(1)}, f32[128,1024]{1,0:T(8,128)}, bf16[128,1024]{1,0:T(8,128)(2,1)S(1)}, bf16[128,1024]{1,0:T(8,128)(2,1)S(1)}) custom-call(bf16[2,2,4,2,128,128]{5,4,3,2,1,0:T(8,128)(2,1)S(1)} %bitcast.8, bf16[256,1024]{1,0:T(8,128)(2,1)S(1)} %shard_map.52.refs_0_, bf16[256,1024]{1,0:T(8,128)(2,1)S(1)} %collective-permute-done.1.refs_1_, ...), custom_call_target="tpu_custom_call" | custom-call | tf_op jit(solution)/shard_map/pallas_call | solution.py:234
  68.3 3.4 %collective-permute-start.8 = (bf16[128,1024]{1,0:T(8,128)(2,1)S(1)}, bf16[128,1024]{1,0:T(8,128)(2,1)S(1)}, u32[]{:S(2)}, u32[]{:S(2)}) collective-permute-start(bf16[128,1024]{1,0:T(8,128)(2,1)S(1)} %get-tuple-element.11), channel_id=1, source_target_pairs={{0,256},{256,0},{1,257},{257,1},{2,258},{258,2},{3,259},{259,3},{4... | collective-permute-start | bytes 786440 | tf_op jit(solution)/shard_map/ppermute | solution.py:31
  71.7 1.9 %collective-permute-start.9 = (bf16[128,1024]{1,0:T(8,128)(2,1)S(1)}, bf16[128,1024]{1,0:T(8,128)(2,1)S(1)}, u32[]{:S(2)}, u32[]{:S(2)}) collective-permute-start(bf16[128,1024]{1,0:T(8,128)(2,1)S(1)} %get-tuple-element.12), channel_id=1, source_target_pairs={{0,256},{256,0},{1,257},{257,1},{2,258},{258,2},{3,259},{259,3},{4... | collective-permute-start | bytes 786440 | tf_op jit(solution)/shard_map/ppermute | solution.py:31
  73.6 1.8 %collective-permute-done.8.arrived_ref = bf16[128,1024]{1,0:T(8,128)(2,1)S(1)} collective-permute-done((bf16[128,1024]{1,0:T(8,128)(2,1)S(1)}, bf16[128,1024]{1,0:T(8,128)(2,1)S(1)}, u32[]{:S(2)}, u32[]{:S(2)}) %collective-permute-start.8) | collective-permute-done | bytes 262176 | tf_op jit(solution)/shard_map/ppermute | solution.py:31
  75.4 0.7 shard_map.54.own_ref
  76.2 9.1 %all-to-all-start.3 = ((bf16[16,8,1024]{2,1,0:T(8,128)(2,1)}), bf16[16,8,1024]{2,1,0:T(8,128)(2,1)S(1)}, u32[]{:S(2)}, u32[]{:S(2)}) async-start(bf16[16,8,1024]{2,1,0:T(8,128)(2,1)} %bitcast.7), calls=%async_computation.3 | async-start | bytes 524288 | tf_op jit(solution)/shard_map/all_to_all | solution.py:35
  85.2 0.0 collective-permute-done.9.arrived_ref
  85.2 4.5 %shard_map.55 = (bf16[4,2,128,128]{3,2,1,0:T(8,128)(2,1)S(1)}, bf16[4,2,128,128]{3,2,1,0:T(8,128)(2,1)S(1)}, bf16[4,2,128,128]{3,2,1,0:T(8,128)(2,1)S(1)}, bf16[4,2,128,128]{3,2,1,0:T(8,128)(2,1)S(1)}) custom-call(bf16[128,1024]{1,0:T(8,128)(2,1)} %shard_map.54.own_ref, bf16[128,1024]{1,0:T(8,128)(2,1)S(1)} %collective-permute-done.9.arrived_ref, ...), custom_call_target="tpu_custom_call" | custom-call | tf_op jit(solution)/shard_map/pallas_call | solution.py:234
  89.8 4.8 %collective-permute-start.10 = (bf16[4,2,128,128]{3,2,1,0:T(8,128)(2,1)S(1)}, bf16[4,2,128,128]{3,2,1,0:T(8,128)(2,1)S(1)}, u32[]{:S(2)}, u32[]{:S(2)}) collective-permute-start(bf16[4,2,128,128]{3,2,1,0:T(8,128)(2,1)S(1)} %get-tuple-element.15), channel_id=1, source_target_pairs={{0,2},{256,258},{2,0},{258,256},{1,3},{257,259},{3,1},{259,257},{4... | collective-permute-start | bytes 786440 | tf_op jit(solution)/shard_map/ppermute | solution.py:47
  94.6 1.9 %collective-permute-start.11 = (bf16[4,2,128,128]{3,2,1,0:T(8,128)(2,1)S(1)}, bf16[4,2,128,128]{3,2,1,0:T(8,128)(2,1)S(1)}, u32[]{:S(2)}, u32[]{:S(2)}) collective-permute-start(bf16[4,2,128,128]{3,2,1,0:T(8,128)(2,1)S(1)} %get-tuple-element.16), channel_id=1, source_target_pairs={{0,258},{256,0},{2,256},{258,2},{1,259},{257,1},{3,257},{259,3},{4... | collective-permute-start | bytes 786440 | tf_op jit(solution)/shard_map/ppermute | solution.py:47
  96.5 3.4 %collective-permute-start.12 = (bf16[4,2,128,128]{3,2,1,0:T(8,128)(2,1)S(1)}, bf16[4,2,128,128]{3,2,1,0:T(8,128)(2,1)S(1)}, u32[]{:S(2)}, u32[]{:S(2)}) collective-permute-start(bf16[4,2,128,128]{3,2,1,0:T(8,128)(2,1)S(1)} %get-tuple-element.17), channel_id=1, source_target_pairs={{0,256},{256,2},{2,258},{258,0},{1,257},{257,3},{3,259},{259,1},{4... | collective-permute-start | bytes 786440 | tf_op jit(solution)/shard_map/ppermute | solution.py:47
  99.9 0.1 collective-permute-done.10.far_ref
  99.9 2.9 %collective-permute-done.11.left_ref = bf16[4,2,128,128]{3,2,1,0:T(8,128)(2,1)S(1)} collective-permute-done((bf16[4,2,128,128]{3,2,1,0:T(8,128)(2,1)S(1)}, bf16[4,2,128,128]{3,2,1,0:T(8,128)(2,1)S(1)}, u32[]{:S(2)}, u32[]{:S(2)}) %collective-permute-start.11) | collective-permute-done | bytes 262176 | tf_op jit(solution)/shard_map/ppermute | solution.py:47
  102.8 3.9 %collective-permute-done.12.right_ref = bf16[4,2,128,128]{3,2,1,0:T(8,128)(2,1)S(1)} collective-permute-done((bf16[4,2,128,128]{3,2,1,0:T(8,128)(2,1)S(1)}, bf16[4,2,128,128]{3,2,1,0:T(8,128)(2,1)S(1)}, u32[]{:S(2)}, u32[]{:S(2)}) %collective-permute-start.12) | collective-permute-done | bytes 262176 | tf_op jit(solution)/shard_map/ppermute | solution.py:47
  106.7 0.9 shard_map.56
  107.7 0.0 all-to-all-done.3.got_ref
  107.7 11.3 %all-to-all-start.2 = ((bf16[16,128,128]{2,1,0:T(8,128)(2,1)}), bf16[16,128,128]{2,1,0:T(8,128)(2,1)S(1)}, u32[]{:S(2)}, u32[]{:S(2)}) async-start(bf16[16,128,128]{2,1,0:T(8,128)(2,1)} %bitcast.4), calls=%async_computation.2 | async-start | bytes 1048576 | tf_op jit(solution)/shard_map/all_to_all | solution.py:35
  119.0 3.0 %shard_map.58 = bf16[8,20480]{1,0:T(8,128)(2,1)} custom-call(bf16[16,8,1024]{2,1,0:T(8,128)(2,1)S(1)} %all-to-all-done.3.got_ref, bf16[1024,1280]{1,0:T(8,128)(2,1)} %coef_ref.1), custom_call_target="tpu_custom_call" | custom-call | tf_op jit(solution)/shard_map/pallas_call | solution.py:273
  122.0 14.2 %all-to-all-done.2 = bf16[16,128,128]{2,1,0:T(8,128)(2,1)S(1)} async-done(((bf16[16,128,128]{2,1,0:T(8,128)(2,1)}), bf16[16,128,128]{2,1,0:T(8,128)(2,1)S(1)}, u32[]{:S(2)}, u32[]{:S(2)}) %all-to-all-start.2) | async-done | bytes 524320 | tf_op jit(solution)/shard_map/all_to_all | solution.py:35
  136.2 0.8 shard_map.57
Async XLA Ops:
  0.6 10.1 %collective-permute-start = (bf16[256,512]{1,0:T(8,128)(2,1)}, bf16[256,512]{1,0:T(8,128)(2,1)S(1)}, u32[]{:S(2)}, u32[]{:S(2)}) collective-permute-start(bf16[256,512]{1,0:T(8,128)(2,1)} %amp_ref.1), channel_id=1, source_target_pairs={{0,1},{1,0},{2,3},{3,2},{4,5},{5,4},{6,7},{7,6},{8,9},{9,8},{10,11... | collective-permute-start | bytes 786440 | tf_op jit(solution)/shard_map/ppermute | solution.py:31
  11.7 14.3 %collective-permute-start.1 = (bf16[256,1024]{1,0:T(8,128)(2,1)S(1)}, bf16[256,1024]{1,0:T(8,128)(2,1)S(1)}, u32[]{:S(2)}, u32[]{:S(2)}) collective-permute-start(bf16[256,1024]{1,0:T(8,128)(2,1)S(1)} %shard_map.52.refs_0_), channel_id=1, source_target_pairs={{0,32},{32,64},{64,96},{96,128},{128,160},{160,192},{192,224},{224... | collective-permute-start | bytes 1572872 | tf_op jit(solution)/shard_map/ppermute | solution.py:42
  18.8 24.4 %all-to-all-start = ((bf16[16,128,128]{2,1,0:T(8,128)(2,1)}), bf16[16,128,128]{2,1,0:T(8,128)(2,1)S(1)}, u32[]{:S(2)}, u32[]{:S(2)}) async-start(bf16[16,128,128]{2,1,0:T(8,128)(2,1)} %bitcast), calls=%async_computation | async-start | bytes 1048576 | tf_op jit(solution)/shard_map/all_to_all | solution.py:35
  26.0 10.2 %collective-permute-start.2 = (bf16[256,1024]{1,0:T(8,128)(2,1)S(1)}, bf16[256,1024]{1,0:T(8,128)(2,1)S(1)}, u32[]{:S(2)}, u32[]{:S(2)}) collective-permute-start(bf16[256,1024]{1,0:T(8,128)(2,1)S(1)} %collective-permute-done.1.refs_1_), channel_id=1, source_target_pairs={{0,32},{32,64},{64,96},{96,128},{128,160},{160,192},{192,224},{224... | collective-permute-start | bytes 1572872 | tf_op jit(solution)/shard_map/ppermute | solution.py:42
  36.2 16.5 %collective-permute-start.3 = (bf16[256,1024]{1,0:T(8,128)(2,1)S(1)}, bf16[256,1024]{1,0:T(8,128)(2,1)S(1)}, u32[]{:S(2)}, u32[]{:S(2)}) collective-permute-start(bf16[256,1024]{1,0:T(8,128)(2,1)S(1)} %collective-permute-done.2.refs_2_), channel_id=1, source_target_pairs={{0,32},{32,64},{64,96},{96,128},{128,160},{160,192},{192,224},{224... | collective-permute-start | bytes 1572872 | tf_op jit(solution)/shard_map/ppermute | solution.py:42
  44.4 19.1 %all-to-all-start.1 = ((bf16[4,4,2,128,128]{4,3,2,1,0:T(8,128)(2,1)}), bf16[4,4,2,128,128]{4,3,2,1,0:T(8,128)(2,1)S(1)}, u32[]{:S(2)}, u32[]{:S(2)}) async-start(bf16[4,4,2,128,128]{4,3,2,1,0:T(8,128)(2,1)} %bitcast.2), calls=%async_computation.1 | async-start | bytes 2097152 | tf_op jit(solution)/shard_map/all_to_all | solution.py:35
  48.4 8.5 %collective-permute-start.5 = (bf16[256,1024]{1,0:T(8,128)(2,1)S(1)}, bf16[256,1024]{1,0:T(8,128)(2,1)}, u32[]{:S(2)}, u32[]{:S(2)}) collective-permute-start(bf16[256,1024]{1,0:T(8,128)(2,1)S(1)} %collective-permute-done.1.refs_1_), channel_id=1, source_target_pairs={{0,1},{1,0},{2,3},{3,2},{4,5},{5,4},{6,7},{7,6},{8,9},{9,8},{10,11... | collective-permute-start | bytes 1572872 | tf_op jit(solution)/shard_map/ppermute | solution.py:31
  50.3 13.1 %collective-permute-start.6 = (bf16[256,1024]{1,0:T(8,128)(2,1)S(1)}, bf16[256,1024]{1,0:T(8,128)(2,1)}, u32[]{:S(2)}, u32[]{:S(2)}) collective-permute-start(bf16[256,1024]{1,0:T(8,128)(2,1)S(1)} %collective-permute-done.2.refs_2_), channel_id=1, source_target_pairs={{0,1},{1,0},{2,3},{3,2},{4,5},{5,4},{6,7},{7,6},{8,9},{9,8},{10,11... | collective-permute-start | bytes 1572872 | tf_op jit(solution)/shard_map/ppermute | solution.py:31
  52.7 10.7 %collective-permute-start.7 = (bf16[256,1024]{1,0:T(8,128)(2,1)S(1)}, bf16[256,1024]{1,0:T(8,128)(2,1)}, u32[]{:S(2)}, u32[]{:S(2)}) collective-permute-start(bf16[256,1024]{1,0:T(8,128)(2,1)S(1)} %collective-permute-done.3.refs_3_), channel_id=1, source_target_pairs={{0,1},{1,0},{2,3},{3,2},{4,5},{5,4},{6,7},{7,6},{8,9},{9,8},{10,11... | collective-permute-start | bytes 1572872 | tf_op jit(solution)/shard_map/ppermute | solution.py:31
  54.6 10.3 %collective-permute-start.4 = (bf16[256,1024]{1,0:T(8,128)(2,1)S(1)}, bf16[256,1024]{1,0:T(8,128)(2,1)}, u32[]{:S(2)}, u32[]{:S(2)}) collective-permute-start(bf16[256,1024]{1,0:T(8,128)(2,1)S(1)} %collective-permute-done.3.refs_3_), channel_id=1, source_target_pairs={{0,32},{32,64},{64,96},{96,128},{128,160},{160,192},{192,224},{224... | collective-permute-start | bytes 1572872 | tf_op jit(solution)/shard_map/ppermute | solution.py:42
  68.3 7.1 %collective-permute-start.8 = (bf16[128,1024]{1,0:T(8,128)(2,1)S(1)}, bf16[128,1024]{1,0:T(8,128)(2,1)S(1)}, u32[]{:S(2)}, u32[]{:S(2)}) collective-permute-start(bf16[128,1024]{1,0:T(8,128)(2,1)S(1)} %get-tuple-element.11), channel_id=1, source_target_pairs={{0,256},{256,0},{1,257},{257,1},{2,258},{258,2},{3,259},{259,3},{4... | collective-permute-start | bytes 786440 | tf_op jit(solution)/shard_map/ppermute | solution.py:31
  71.7 13.6 %collective-permute-start.9 = (bf16[128,1024]{1,0:T(8,128)(2,1)S(1)}, bf16[128,1024]{1,0:T(8,128)(2,1)S(1)}, u32[]{:S(2)}, u32[]{:S(2)}) collective-permute-start(bf16[128,1024]{1,0:T(8,128)(2,1)S(1)} %get-tuple-element.12), channel_id=1, source_target_pairs={{0,256},{256,0},{1,257},{257,1},{2,258},{258,2},{3,259},{259,3},{4... | collective-permute-start | bytes 786440 | tf_op jit(solution)/shard_map/ppermute | solution.py:31
  76.2 31.5 %all-to-all-start.3 = ((bf16[16,8,1024]{2,1,0:T(8,128)(2,1)}), bf16[16,8,1024]{2,1,0:T(8,128)(2,1)S(1)}, u32[]{:S(2)}, u32[]{:S(2)}) async-start(bf16[16,8,1024]{2,1,0:T(8,128)(2,1)} %bitcast.7), calls=%async_computation.3 | async-start | bytes 524288 | tf_op jit(solution)/shard_map/all_to_all | solution.py:35
  89.8 10.1 %collective-permute-start.10 = (bf16[4,2,128,128]{3,2,1,0:T(8,128)(2,1)S(1)}, bf16[4,2,128,128]{3,2,1,0:T(8,128)(2,1)S(1)}, u32[]{:S(2)}, u32[]{:S(2)}) collective-permute-start(bf16[4,2,128,128]{3,2,1,0:T(8,128)(2,1)S(1)} %get-tuple-element.15), channel_id=1, source_target_pairs={{0,2},{256,258},{2,0},{258,256},{1,3},{257,259},{3,1},{259,257},{4... | collective-permute-start | bytes 786440 | tf_op jit(solution)/shard_map/ppermute | solution.py:47
  94.6 8.2 %collective-permute-start.11 = (bf16[4,2,128,128]{3,2,1,0:T(8,128)(2,1)S(1)}, bf16[4,2,128,128]{3,2,1,0:T(8,128)(2,1)S(1)}, u32[]{:S(2)}, u32[]{:S(2)}) collective-permute-start(bf16[4,2,128,128]{3,2,1,0:T(8,128)(2,1)S(1)} %get-tuple-element.16), channel_id=1, source_target_pairs={{0,258},{256,0},{2,256},{258,2},{1,259},{257,1},{3,257},{259,3},{4... | collective-permute-start | bytes 786440 | tf_op jit(solution)/shard_map/ppermute | solution.py:47
  96.5 10.2 %collective-permute-start.12 = (bf16[4,2,128,128]{3,2,1,0:T(8,128)(2,1)S(1)}, bf16[4,2,128,128]{3,2,1,0:T(8,128)(2,1)S(1)}, u32[]{:S(2)}, u32[]{:S(2)}) collective-permute-start(bf16[4,2,128,128]{3,2,1,0:T(8,128)(2,1)S(1)} %get-tuple-element.17), channel_id=1, source_target_pairs={{0,256},{256,2},{2,258},{258,0},{1,257},{257,3},{3,259},{259,1},{4... | collective-permute-start | bytes 786440 | tf_op jit(solution)/shard_map/ppermute | solution.py:47
  107.7 28.5 %all-to-all-start.2 = ((bf16[16,128,128]{2,1,0:T(8,128)(2,1)}), bf16[16,128,128]{2,1,0:T(8,128)(2,1)S(1)}, u32[]{:S(2)}, u32[]{:S(2)}) async-start(bf16[16,128,128]{2,1,0:T(8,128)(2,1)} %bitcast.4), calls=%async_computation.2 | async-start | bytes 1048576 | tf_op jit(solution)/shard_map/all_to_all | solution.py:35

commit v11 on v9

--- a/solution.py
+++ b/solution.py
@@ -86,11 +86,16 @@
     wide_refs, narrow_refs = refs[8:10], refs[10:12]
     xl = lax.axis_index("xl")
     rhs = jnp.concatenate([b for _, b in blocks], axis=0)
-    for i, h in enumerate((xl, 1 - xl)):
-        lhs = [metric_ref[(h, *place(o), j)] for o, _ in blocks for j in range(2)]
-        out = jnp.dot(jnp.concatenate(lhs, axis=1), rhs, preferred_element_type=F32)
-        wide_refs[i][...] = out
-        narrow_refs[i][...] = out.astype(BF16)
+    lhs = [
+        jnp.concatenate([metric_ref[(h, *place(o), j)] for o, _ in blocks for j in range(2)], axis=1)
+        for h in (xl, 1 - xl)
+    ]
+    out = jnp.dot(jnp.concatenate(lhs, axis=0), rhs, preferred_element_type=F32)
+    rows = out.shape[0] // 2
+    for i in range(2):
+        part = out[i * rows : (i + 1) * rows]
+        wide_refs[i][...] = part
+        narrow_refs[i][...] = part.astype(BF16)
 
 
 def join_kernel(own_ref, arrived_ref, out_ref):
@@ -104,12 +109,13 @@
     other = (other_ref[...] + arrived_ref[...].astype(F32)).astype(BF16)
     fitted = jnp.concatenate([own_ref[...], other], axis=0)
     rows = own_ref.shape[0]
-    for offset, block in blocks:
-        out = lax.dot_general(
-            block, fitted, (((1,), (1,)), ((), ())), preferred_element_type=F32
-        ).astype(BF16)
+    amp = jnp.concatenate([b for _, b in blocks], axis=0)
+    whole = lax.dot_general(amp, fitted, (((1,), (1,)), ((), ())), preferred_element_type=F32)
+    height = blocks[0][1].shape[0]
+    half = height // 2
+    for i, (offset, _) in enumerate(blocks):
+        out = whole[i * height : (i + 1) * height].astype(BF16)
         far, near = place(offset)
-        half = out.shape[0] // 2
         for h, part in ((xl, out[:, :rows]), (1 - xl, out[:, rows:])):
             slot = lax.rem(2 * far + h + 4 - x, 4)
             for j in range(2):
@@ -188,7 +194,9 @@
     shape = (half, 2 * cols)
 
     def on_blocks(kernel, outs, scratch, *args):
-        spaces = [pltpu.HBM if a.dtype == F32 else pltpu.VMEM for a in args] + [pltpu.VMEM] * 5 + [pltpu.HBM] * 3
+        small = (a.dtype == BF16 and a.ndim == 2 for a in args)
+        spaces = [pltpu.VMEM if fits else pltpu.HBM for fits in small]
+        spaces += [pltpu.VMEM] * 4 + [pltpu.HBM] + [pltpu.VMEM] * 2 + [pltpu.HBM]
         args = list(map(pltpu.with_memory_space_constraint, (*args, *steps, *swaps), spaces))
         return pl.pallas_call(
             kernel,
@@ -211,7 +219,7 @@
     piece = (4, 2, half, half)
     slots = on_blocks(
         density_kernel,
-        [(pltpu.VMEM, piece, BF16)] * 4,
+        [(space, piece, BF16) for space in (pltpu.HBM, pltpu.VMEM) * 2],
         [pltpu.VMEM((4, *piece), BF16)],
         fitted, other, other_arrived,
     )

time: 137 us -> 138 us (level)
  no operation moved by 1% of the time
where the time goes in v11:
time: 138 us; the launch traced here: 137 us
  starting transfers between devices  74.7 us (54%)
  waiting for transfers between devices  44.3 us (32%)
  Pallas kernels  16.5 us (12%)
    all_to_all x4, starting transfers between devices, exchange(): return lax.all_to_all(x, axes, split_axis=0, concat_axis=0, tiled=True)  31.4 us
    all_to_all x4, waiting for transfers between devices, exchange(): return lax.all_to_all(x, axes, split_axis=0, concat_axis=0, tiled=True)  24.1 us
    ppermute x6, starting transfers between devices, shifted(): return lax.ppermute(x, axis, [(i, (i + by) % n) for i in range(n)])  20.3 us
    ppermute x4, starting transfers between devices, ring_step(): return lax.ppermute(x, ('z', 'c'), moves)  13.1 us
    ppermute x3, starting transfers between devices, shifted_x(): lax.ppermute(x, ('xl', 'xh'), [(at(i), at((i + by) % 4)) for i in range(4)])  10 us
    ppermute x4, waiting for transfers between devices, ring_step(): return lax.ppermute(x, ('z', 'c'), moves)  9.83 us
    pallas_call x2, Pallas kernels, on_blocks(): pl.pallas_call(kernel, in_specs=[VMEM] * len(args), out_specs=[VMEM] * le...  7.24 us
    ppermute x3, waiting for transfers between devices, shifted_x(): lax.ppermute(x, ('xl', 'xh'), [(at(i), at((i + by) % 4)) for i in range(4)])  7.17 us
  transfers between devices with their start and end apart: 17, of which 10 were waited for; matrix products, arithmetic and copies ran while one was open for 0% of the time, Pallas kernels for 8%

profile of v11, /device:TPU:1, one launch (start us, length us, event | category | flops | bytes accessed | tf_op | source)
XLA Modules:
  0.0 137.3 jit_solution(3510329329908911237)
XLA Ops:
  0.6 8.7 %collective-permute-start = (bf16[256,512]{1,0:T(8,128)(2,1)}, bf16[256,512]{1,0:T(8,128)(2,1)S(1)}, u32[]{:S(2)}, u32[]{:S(2)}) collective-permute-start(bf16[256,512]{1,0:T(8,128)(2,1)} %amp_ref.1), channel_id=1, source_target_pairs={{0,1},{1,0},{2,3},{3,2},{4,5},{5,4},{6,7},{7,6},{8,9},{9,8},{10,11... | collective-permute-start | bytes 786440 | tf_op jit(solution)/shard_map/ppermute | solution.py:31
  9.4 1.4 collective-permute-done.got_ref
  10.7 1.0 shard_map.52.refs_0_
  11.7 5.3 %collective-permute-start.1 = (bf16[256,1024]{1,0:T(8,128)(2,1)S(1)}, bf16[256,1024]{1,0:T(8,128)(2,1)S(1)}, u32[]{:S(2)}, u32[]{:S(2)}) collective-permute-start(bf16[256,1024]{1,0:T(8,128)(2,1)S(1)} %shard_map.52.refs_0_), channel_id=1, source_target_pairs={{0,32},{32,64},{64,96},{96,128},{128,160},{160,192},{192,224},{224... | collective-permute-start | bytes 1572872 | tf_op jit(solution)/shard_map/ppermute | solution.py:42
  17.1 1.7 %shard_map.50 = bf16[8,2,128,128]{3,2,1,0:T(8,128)(2,1)} custom-call(bf16[256,128]{1,0:T(8,128)(2,1)} %in_ref.1), custom_call_target="tpu_custom_call" | custom-call | tf_op jit(solution)/shard_map/pallas_call | solution.py:160
  18.8 7.2 %all-to-all-start = ((bf16[16,128,128]{2,1,0:T(8,128)(2,1)}), bf16[16,128,128]{2,1,0:T(8,128)(2,1)S(1)}, u32[]{:S(2)}, u32[]{:S(2)}) async-start(bf16[16,128,128]{2,1,0:T(8,128)(2,1)} %bitcast), calls=%async_computation | async-start | bytes 1048576 | tf_op jit(solution)/shard_map/all_to_all | solution.py:35
  26.0 0.0 collective-permute-done.1.refs_1_
  26.0 2.2 %collective-permute-start.2 = (bf16[256,1024]{1,0:T(8,128)(2,1)S(1)}, bf16[256,1024]{1,0:T(8,128)(2,1)S(1)}, u32[]{:S(2)}, u32[]{:S(2)}) collective-permute-start(bf16[256,1024]{1,0:T(8,128)(2,1)S(1)} %collective-permute-done.1.refs_1_), channel_id=1, source_target_pairs={{0,32},{32,64},{64,96},{96,128},{128,160},{160,192},{192,224},{224... | collective-permute-start | bytes 1572872 | tf_op jit(solution)/shard_map/ppermute | solution.py:42
  28.2 8.0 %collective-permute-done.2.refs_2_ = bf16[256,1024]{1,0:T(8,128)(2,1)S(1)} collective-permute-done((bf16[256,1024]{1,0:T(8,128)(2,1)S(1)}, bf16[256,1024]{1,0:T(8,128)(2,1)S(1)}, u32[]{:S(2)}, u32[]{:S(2)}) %collective-permute-start.2) | collective-permute-done | bytes 524320 | tf_op jit(solution)/shard_map/ppermute | solution.py:42
  36.2 3.4 %collective-permute-start.3 = (bf16[256,1024]{1,0:T(8,128)(2,1)S(1)}, bf16[256,1024]{1,0:T(8,128)(2,1)S(1)}, u32[]{:S(2)}, u32[]{:S(2)}) collective-permute-start(bf16[256,1024]{1,0:T(8,128)(2,1)S(1)} %collective-permute-done.2.refs_2_), channel_id=1, source_target_pairs={{0,32},{32,64},{64,96},{96,128},{128,160},{160,192},{192,224},{224... | collective-permute-start | bytes 1572872 | tf_op jit(solution)/shard_map/ppermute | solution.py:42
  39.6 3.6 %all-to-all-done = bf16[16,128,128]{2,1,0:T(8,128)(2,1)S(1)} async-done(((bf16[16,128,128]{2,1,0:T(8,128)(2,1)}), bf16[16,128,128]{2,1,0:T(8,128)(2,1)S(1)}, u32[]{:S(2)}, u32[]{:S(2)}) %all-to-all-start) | async-done | bytes 524320 | tf_op jit(solution)/shard_map/all_to_all | solution.py:35
  43.2 1.1 shard_map.51
  44.3 4.2 %all-to-all-start.1 = ((bf16[4,4,2,128,128]{4,3,2,1,0:T(8,128)(2,1)}), bf16[4,4,2,128,128]{4,3,2,1,0:T(8,128)(2,1)}, u32[]{:S(2)}, u32[]{:S(2)}) async-start(bf16[4,4,2,128,128]{4,3,2,1,0:T(8,128)(2,1)} %bitcast.2), calls=%async_computation.1 | async-start | bytes 2097152 | tf_op jit(solution)/shard_map/all_to_all | solution.py:35
  48.6 1.9 %collective-permute-start.5 = (bf16[256,1024]{1,0:T(8,128)(2,1)S(1)}, bf16[256,1024]{1,0:T(8,128)(2,1)S(1)}, u32[]{:S(2)}, u32[]{:S(2)}) collective-permute-start(bf16[256,1024]{1,0:T(8,128)(2,1)S(1)} %collective-permute-done.1.refs_1_), channel_id=1, source_target_pairs={{0,1},{1,0},{2,3},{3,2},{4,5},{5,4},{6,7},{7,6},{8,9},{9,8},{10,11... | collective-permute-start | bytes 1572872 | tf_op jit(solution)/shard_map/ppermute | solution.py:31
  50.5 2.4 %collective-permute-start.6 = (bf16[256,1024]{1,0:T(8,128)(2,1)S(1)}, bf16[256,1024]{1,0:T(8,128)(2,1)S(1)}, u32[]{:S(2)}, u32[]{:S(2)}) collective-permute-start(bf16[256,1024]{1,0:T(8,128)(2,1)S(1)} %collective-permute-done.2.refs_2_), channel_id=1, source_target_pairs={{0,1},{1,0},{2,3},{3,2},{4,5},{5,4},{6,7},{7,6},{8,9},{9,8},{10,11... | collective-permute-start | bytes 1572872 | tf_op jit(solution)/shard_map/ppermute | solution.py:31
  52.9 0.0 collective-permute-done.3.refs_3_
  52.9 1.9 %collective-permute-start.7 = (bf16[256,1024]{1,0:T(8,128)(2,1)S(1)}, bf16[256,1024]{1,0:T(8,128)(2,1)}, u32[]{:S(2)}, u32[]{:S(2)}) collective-permute-start(bf16[256,1024]{1,0:T(8,128)(2,1)S(1)} %collective-permute-done.3.refs_3_), channel_id=1, source_target_pairs={{0,1},{1,0},{2,3},{3,2},{4,5},{5,4},{6,7},{7,6},{8,9},{9,8},{10,11... | collective-permute-start | bytes 1572872 | tf_op jit(solution)/shard_map/ppermute | solution.py:31
  54.8 2.2 %collective-permute-start.4 = (bf16[256,1024]{1,0:T(8,128)(2,1)S(1)}, bf16[256,1024]{1,0:T(8,128)(2,1)}, u32[]{:S(2)}, u32[]{:S(2)}) collective-permute-start(bf16[256,1024]{1,0:T(8,128)(2,1)S(1)} %collective-permute-done.3.refs_3_), channel_id=1, source_target_pairs={{0,32},{32,64},{64,96},{96,128},{128,160},{160,192},{192,224},{224... | collective-permute-start | bytes 1572872 | tf_op jit(solution)/shard_map/ppermute | solution.py:42
  57.0 0.0 collective-permute-done.5.refs_5_
  57.0 6.3 %all-to-all-done.1 = bf16[4,4,2,128,128]{4,3,2,1,0:T(8,128)(2,1)} async-done(((bf16[4,4,2,128,128]{4,3,2,1,0:T(8,128)(2,1)}), bf16[4,4,2,128,128]{4,3,2,1,0:T(8,128)(2,1)}, u32[]{:S(2)}, u32[]{:S(2)}) %all-to-all-start.1) | async-done | bytes 1048608 | tf_op jit(solution)/shard_map/all_to_all | solution.py:35
  63.4 0.0 collective-permute-done.6.refs_6_
  63.4 0.0 collective-permute-done.7.refs_7_
  63.4 1.8 %collective-permute-done.4.refs_4_ = bf16[256,1024]{1,0:T(8,128)(2,1)} collective-permute-done((bf16[256,1024]{1,0:T(8,128)(2,1)S(1)}, bf16[256,1024]{1,0:T(8,128)(2,1)}, u32[]{:S(2)}, u32[]{:S(2)}) %collective-permute-start.4) | collective-permute-done | bytes 524320 | tf_op jit(solution)/shard_map/ppermute | solution.py:42
  65.2 3.6 %shard_map.53 = (f32[128,1024]{1,0:T(8,128)S(1)}, f32[128,1024]{1,0:T(8,128)}, bf16[128,1024]{1,0:T(8,128)(2,1)}, bf16[128,1024]{1,0:T(8,128)(2,1)S(1)}) custom-call(bf16[2,2,4,2,128,128]{5,4,3,2,1,0:T(8,128)(2,1)} %bitcast.3.metric_ref, bf16[256,1024]{1,0:T(8,128)(2,1)S(1)} %shard_map.52.refs_0_, bf16[256,1024]{1,0:T(8,128)(2,1)S(1)} %collective-permute-done.1.refs_1_, ...), custom_call_target="tpu_custom_call" | custom-call | tf_op jit(solution)/shard_map/pallas_call | solution.py:201
  68.8 3.3 %collective-permute-start.8 = (bf16[128,1024]{1,0:T(8,128)(2,1)S(1)}, bf16[128,1024]{1,0:T(8,128)(2,1)S(1)}, u32[]{:S(2)}, u32[]{:S(2)}) collective-permute-start(bf16[128,1024]{1,0:T(8,128)(2,1)S(1)} %get-tuple-element.11), channel_id=1, source_target_pairs={{0,256},{256,0},{1,257},{257,1},{2,258},{258,2},{3,259},{259,3},{4... | collective-permute-start | bytes 786440 | tf_op jit(solution)/shard_map/ppermute | solution.py:31
  72.1 2.0 %collective-permute-start.9 = (bf16[128,1024]{1,0:T(8,128)(2,1)}, bf16[128,1024]{1,0:T(8,128)(2,1)}, u32[]{:S(2)}, u32[]{:S(2)}) collective-permute-start(bf16[128,1024]{1,0:T(8,128)(2,1)} %get-tuple-element.13), channel_id=1, source_target_pairs={{0,256},{256,0},{1,257},{257,1},{2,258},{258,2},{3,259},{259,3},{4... | collective-permute-start | bytes 786440 | tf_op jit(solution)/shard_map/ppermute | solution.py:31
  74.1 1.8 %collective-permute-done.8.arrived_ref = bf16[128,1024]{1,0:T(8,128)(2,1)S(1)} collective-permute-done((bf16[128,1024]{1,0:T(8,128)(2,1)S(1)}, bf16[128,1024]{1,0:T(8,128)(2,1)S(1)}, u32[]{:S(2)}, u32[]{:S(2)}) %collective-permute-start.8) | collective-permute-done | bytes 262176 | tf_op jit(solution)/shard_map/ppermute | solution.py:31
  75.9 0.7 shard_map.54.own_ref
  76.6 8.8 %all-to-all-start.3 = ((bf16[16,8,1024]{2,1,0:T(8,128)(2,1)}), bf16[16,8,1024]{2,1,0:T(8,128)(2,1)S(1)}, u32[]{:S(2)}, u32[]{:S(2)}) async-start(bf16[16,8,1024]{2,1,0:T(8,128)(2,1)} %bitcast.7), calls=%async_computation.3 | async-start | bytes 524288 | tf_op jit(solution)/shard_map/all_to_all | solution.py:35
  85.4 0.0 collective-permute-done.9.arrived_ref
  85.4 3.6 %shard_map.55 = (bf16[4,2,128,128]{3,2,1,0:T(8,128)(2,1)}, bf16[4,2,128,128]{3,2,1,0:T(8,128)(2,1)S(1)}, bf16[4,2,128,128]{3,2,1,0:T(8,128)(2,1)}, bf16[4,2,128,128]{3,2,1,0:T(8,128)(2,1)S(1)}) custom-call(bf16[128,1024]{1,0:T(8,128)(2,1)} %shard_map.54.own_ref, f32[128,1024]{1,0:T(8,128)} %get-tuple-element.12.other_ref, ...), custom_call_target="tpu_custom_call" | custom-call | tf_op jit(solution)/shard_map/pallas_call | solution.py:201
  89.1 4.8 %collective-permute-start.10 = (bf16[4,2,128,128]{3,2,1,0:T(8,128)(2,1)}, bf16[4,2,128,128]{3,2,1,0:T(8,128)(2,1)S(1)}, u32[]{:S(2)}, u32[]{:S(2)}) collective-permute-start(bf16[4,2,128,128]{3,2,1,0:T(8,128)(2,1)} %get-tuple-element.15), channel_id=1, source_target_pairs={{0,2},{256,258},{2,0},{258,256},{1,3},{257,259},{3,1},{259,257},{4... | collective-permute-start | bytes 786440 | tf_op jit(solution)/shard_map/ppermute | solution.py:47
  93.8 1.9 %collective-permute-start.11 = (bf16[4,2,128,128]{3,2,1,0:T(8,128)(2,1)S(1)}, bf16[4,2,128,128]{3,2,1,0:T(8,128)(2,1)S(1)}, u32[]{:S(2)}, u32[]{:S(2)}) collective-permute-start(bf16[4,2,128,128]{3,2,1,0:T(8,128)(2,1)S(1)} %get-tuple-element.16), channel_id=1, source_target_pairs={{0,258},{256,0},{2,256},{258,2},{1,259},{257,1},{3,257},{259,3},{4... | collective-permute-start | bytes 786440 | tf_op jit(solution)/shard_map/ppermute | solution.py:47
  95.7 3.4 %collective-permute-start.12 = (bf16[4,2,128,128]{3,2,1,0:T(8,128)(2,1)S(1)}, bf16[4,2,128,128]{3,2,1,0:T(8,128)(2,1)S(1)}, u32[]{:S(2)}, u32[]{:S(2)}) collective-permute-start(bf16[4,2,128,128]{3,2,1,0:T(8,128)(2,1)S(1)} %get-tuple-element.17), channel_id=1, source_target_pairs={{0,256},{256,2},{2,258},{258,0},{1,257},{257,3},{3,259},{259,1},{4... | collective-permute-start | bytes 786440 | tf_op jit(solution)/shard_map/ppermute | solution.py:47
  99.1 0.1 collective-permute-done.10.far_ref
  99.2 3.9 %collective-permute-done.11.left_ref = bf16[4,2,128,128]{3,2,1,0:T(8,128)(2,1)S(1)} collective-permute-done((bf16[4,2,128,128]{3,2,1,0:T(8,128)(2,1)S(1)}, bf16[4,2,128,128]{3,2,1,0:T(8,128)(2,1)S(1)}, u32[]{:S(2)}, u32[]{:S(2)}) %collective-permute-start.11) | collective-permute-done | bytes 262176 | tf_op jit(solution)/shard_map/ppermute | solution.py:47
  103.1 3.2 %collective-permute-done.12.right_ref = bf16[4,2,128,128]{3,2,1,0:T(8,128)(2,1)S(1)} collective-permute-done((bf16[4,2,128,128]{3,2,1,0:T(8,128)(2,1)S(1)}, bf16[4,2,128,128]{3,2,1,0:T(8,128)(2,1)S(1)}, u32[]{:S(2)}, u32[]{:S(2)}) %collective-permute-start.12) | collective-permute-done | bytes 262176 | tf_op jit(solution)/shard_map/ppermute | solution.py:47
  106.3 0.0 copy-start
  106.3 0.9 copy-done
  107.2 0.9 shard_map.56
  108.2 0.0 all-to-all-done.3.got_ref
  108.2 11.1 %all-to-all-start.2 = ((bf16[16,128,128]{2,1,0:T(8,128)(2,1)}), bf16[16,128,128]{2,1,0:T(8,128)(2,1)S(1)}, u32[]{:S(2)}, u32[]{:S(2)}) async-start(bf16[16,128,128]{2,1,0:T(8,128)(2,1)} %bitcast.4), calls=%async_computation.2 | async-start | bytes 1048576 | tf_op jit(solution)/shard_map/all_to_all | solution.py:35
  119.3 3.0 %shard_map.58 = bf16[8,20480]{1,0:T(8,128)(2,1)} custom-call(bf16[16,8,1024]{2,1,0:T(8,128)(2,1)S(1)} %all-to-all-done.3.got_ref, bf16[1024,1280]{1,0:T(8,128)(2,1)} %coef_ref.1), custom_call_target="tpu_custom_call" | custom-call | tf_op jit(solution)/shard_map/pallas_call | solution.py:239
  122.3 14.2 %all-to-all-done.2 = bf16[16,128,128]{2,1,0:T(8,128)(2,1)S(1)} async-done(((bf16[16,128,128]{2,1,0:T(8,128)(2,1)}), bf16[16,128,128]{2,1,0:T(8,128)(2,1)S(1)}, u32[]{:S(2)}, u32[]{:S(2)}) %all-to-all-start.2) | async-done | bytes 524320 | tf_op jit(solution)/shard_map/all_to_all | solution.py:35
  136.5 0.8 shard_map.57
Async XLA Ops:
  0.6 10.1 %collective-permute-start = (bf16[256,512]{1,0:T(8,128)(2,1)}, bf16[256,512]{1,0:T(8,128)(2,1)S(1)}, u32[]{:S(2)}, u32[]{:S(2)}) collective-permute-start(bf16[256,512]{1,0:T(8,128)(2,1)} %amp_ref.1), channel_id=1, source_target_pairs={{0,1},{1,0},{2,3},{3,2},{4,5},{5,4},{6,7},{7,6},{8,9},{9,8},{10,11... | collective-permute-start | bytes 786440 | tf_op jit(solution)/shard_map/ppermute | solution.py:31
  11.7 14.3 %collective-permute-start.1 = (bf16[256,1024]{1,0:T(8,128)(2,1)S(1)}, bf16[256,1024]{1,0:T(8,128)(2,1)S(1)}, u32[]{:S(2)}, u32[]{:S(2)}) collective-permute-start(bf16[256,1024]{1,0:T(8,128)(2,1)S(1)} %shard_map.52.refs_0_), channel_id=1, source_target_pairs={{0,32},{32,64},{64,96},{96,128},{128,160},{160,192},{192,224},{224... | collective-permute-start | bytes 1572872 | tf_op jit(solution)/shard_map/ppermute | solution.py:42
  18.8 24.4 %all-to-all-start = ((bf16[16,128,128]{2,1,0:T(8,128)(2,1)}), bf16[16,128,128]{2,1,0:T(8,128)(2,1)S(1)}, u32[]{:S(2)}, u32[]{:S(2)}) async-start(bf16[16,128,128]{2,1,0:T(8,128)(2,1)} %bitcast), calls=%async_computation | async-start | bytes 1048576 | tf_op jit(solution)/shard_map/all_to_all | solution.py:35
  26.0 10.2 %collective-permute-start.2 = (bf16[256,1024]{1,0:T(8,128)(2,1)S(1)}, bf16[256,1024]{1,0:T(8,128)(2,1)S(1)}, u32[]{:S(2)}, u32[]{:S(2)}) collective-permute-start(bf16[256,1024]{1,0:T(8,128)(2,1)S(1)} %collective-permute-done.1.refs_1_), channel_id=1, source_target_pairs={{0,32},{32,64},{64,96},{96,128},{128,160},{160,192},{192,224},{224... | collective-permute-start | bytes 1572872 | tf_op jit(solution)/shard_map/ppermute | solution.py:42
  36.2 16.7 %collective-permute-start.3 = (bf16[256,1024]{1,0:T(8,128)(2,1)S(1)}, bf16[256,1024]{1,0:T(8,128)(2,1)S(1)}, u32[]{:S(2)}, u32[]{:S(2)}) collective-permute-start(bf16[256,1024]{1,0:T(8,128)(2,1)S(1)} %collective-permute-done.2.refs_2_), channel_id=1, source_target_pairs={{0,32},{32,64},{64,96},{96,128},{128,160},{160,192},{192,224},{224... | collective-permute-start | bytes 1572872 | tf_op jit(solution)/shard_map/ppermute | solution.py:42
  44.3 19.1 %all-to-all-start.1 = ((bf16[4,4,2,128,128]{4,3,2,1,0:T(8,128)(2,1)}), bf16[4,4,2,128,128]{4,3,2,1,0:T(8,128)(2,1)}, u32[]{:S(2)}, u32[]{:S(2)}) async-start(bf16[4,4,2,128,128]{4,3,2,1,0:T(8,128)(2,1)} %bitcast.2), calls=%async_computation.1 | async-start | bytes 2097152 | tf_op jit(solution)/shard_map/all_to_all | solution.py:35
  48.6 8.5 %collective-permute-start.5 = (bf16[256,1024]{1,0:T(8,128)(2,1)S(1)}, bf16[256,1024]{1,0:T(8,128)(2,1)S(1)}, u32[]{:S(2)}, u32[]{:S(2)}) collective-permute-start(bf16[256,1024]{1,0:T(8,128)(2,1)S(1)} %collective-permute-done.1.refs_1_), channel_id=1, source_target_pairs={{0,1},{1,0},{2,3},{3,2},{4,5},{5,4},{6,7},{7,6},{8,9},{9,8},{10,11... | collective-permute-start | bytes 1572872 | tf_op jit(solution)/shard_map/ppermute | solution.py:31
  50.5 12.9 %collective-permute-start.6 = (bf16[256,1024]{1,0:T(8,128)(2,1)S(1)}, bf16[256,1024]{1,0:T(8,128)(2,1)S(1)}, u32[]{:S(2)}, u32[]{:S(2)}) collective-permute-start(bf16[256,1024]{1,0:T(8,128)(2,1)S(1)} %collective-permute-done.2.refs_2_), channel_id=1, source_target_pairs={{0,1},{1,0},{2,3},{3,2},{4,5},{5,4},{6,7},{7,6},{8,9},{9,8},{10,11... | collective-permute-start | bytes 1572872 | tf_op jit(solution)/shard_map/ppermute | solution.py:31
  52.9 10.5 %collective-permute-start.7 = (bf16[256,1024]{1,0:T(8,128)(2,1)S(1)}, bf16[256,1024]{1,0:T(8,128)(2,1)}, u32[]{:S(2)}, u32[]{:S(2)}) collective-permute-start(bf16[256,1024]{1,0:T(8,128)(2,1)S(1)} %collective-permute-done.3.refs_3_), channel_id=1, source_target_pairs={{0,1},{1,0},{2,3},{3,2},{4,5},{5,4},{6,7},{7,6},{8,9},{9,8},{10,11... | collective-permute-start | bytes 1572872 | tf_op jit(solution)/shard_map/ppermute | solution.py:31
  54.8 10.3 %collective-permute-start.4 = (bf16[256,1024]{1,0:T(8,128)(2,1)S(1)}, bf16[256,1024]{1,0:T(8,128)(2,1)}, u32[]{:S(2)}, u32[]{:S(2)}) collective-permute-start(bf16[256,1024]{1,0:T(8,128)(2,1)S(1)} %collective-permute-done.3.refs_3_), channel_id=1, source_target_pairs={{0,32},{32,64},{64,96},{96,128},{128,160},{160,192},{192,224},{224... | collective-permute-start | bytes 1572872 | tf_op jit(solution)/shard_map/ppermute | solution.py:42
  68.8 7.1 %collective-permute-start.8 = (bf16[128,1024]{1,0:T(8,128)(2,1)S(1)}, bf16[128,1024]{1,0:T(8,128)(2,1)S(1)}, u32[]{:S(2)}, u32[]{:S(2)}) collective-permute-start(bf16[128,1024]{1,0:T(8,128)(2,1)S(1)} %get-tuple-element.11), channel_id=1, source_target_pairs={{0,256},{256,0},{1,257},{257,1},{2,258},{258,2},{3,259},{259,3},{4... | collective-permute-start | bytes 786440 | tf_op jit(solution)/shard_map/ppermute | solution.py:31
  72.1 13.3 %collective-permute-start.9 = (bf16[128,1024]{1,0:T(8,128)(2,1)}, bf16[128,1024]{1,0:T(8,128)(2,1)}, u32[]{:S(2)}, u32[]{:S(2)}) collective-permute-start(bf16[128,1024]{1,0:T(8,128)(2,1)} %get-tuple-element.13), channel_id=1, source_target_pairs={{0,256},{256,0},{1,257},{257,1},{2,258},{258,2},{3,259},{259,3},{4... | collective-permute-start | bytes 786440 | tf_op jit(solution)/shard_map/ppermute | solution.py:31
  76.6 31.5 %all-to-all-start.3 = ((bf16[16,8,1024]{2,1,0:T(8,128)(2,1)}), bf16[16,8,1024]{2,1,0:T(8,128)(2,1)S(1)}, u32[]{:S(2)}, u32[]{:S(2)}) async-start(bf16[16,8,1024]{2,1,0:T(8,128)(2,1)} %bitcast.7), calls=%async_computation.3 | async-start | bytes 524288 | tf_op jit(solution)/shard_map/all_to_all | solution.py:35
  89.1 10.2 %collective-permute-start.10 = (bf16[4,2,128,128]{3,2,1,0:T(8,128)(2,1)}, bf16[4,2,128,128]{3,2,1,0:T(8,128)(2,1)S(1)}, u32[]{:S(2)}, u32[]{:S(2)}) collective-permute-start(bf16[4,2,128,128]{3,2,1,0:T(8,128)(2,1)} %get-tuple-element.15), channel_id=1, source_target_pairs={{0,2},{256,258},{2,0},{258,256},{1,3},{257,259},{3,1},{259,257},{4... | collective-permute-start | bytes 786440 | tf_op jit(solution)/shard_map/ppermute | solution.py:47
  93.8 9.3 %collective-permute-start.11 = (bf16[4,2,128,128]{3,2,1,0:T(8,128)(2,1)S(1)}, bf16[4,2,128,128]{3,2,1,0:T(8,128)(2,1)S(1)}, u32[]{:S(2)}, u32[]{:S(2)}) collective-permute-start(bf16[4,2,128,128]{3,2,1,0:T(8,128)(2,1)S(1)} %get-tuple-element.16), channel_id=1, source_target_pairs={{0,258},{256,0},{2,256},{258,2},{1,259},{257,1},{3,257},{259,3},{4... | collective-permute-start | bytes 786440 | tf_op jit(solution)/shard_map/ppermute | solution.py:47
  95.7 10.5 %collective-permute-start.12 = (bf16[4,2,128,128]{3,2,1,0:T(8,128)(2,1)S(1)}, bf16[4,2,128,128]{3,2,1,0:T(8,128)(2,1)S(1)}, u32[]{:S(2)}, u32[]{:S(2)}) collective-permute-start(bf16[4,2,128,128]{3,2,1,0:T(8,128)(2,1)S(1)} %get-tuple-element.17), channel_id=1, source_target_pairs={{0,256},{256,2},{2,258},{258,0},{1,257},{257,3},{3,259},{259,1},{4... | collective-permute-start | bytes 786440 | tf_op jit(solution)/shard_map/ppermute | solution.py:47
  106.3 1.0 copy-start
  108.2 28.3 %all-to-all-start.2 = ((bf16[16,128,128]{2,1,0:T(8,128)(2,1)}), bf16[16,128,128]{2,1,0:T(8,128)(2,1)S(1)}, u32[]{:S(2)}, u32[]{:S(2)}) async-start(bf16[16,128,128]{2,1,0:T(8,128)(2,1)} %bitcast.4), calls=%async_computation.2 | async-start | bytes 1048576 | tf_op jit(solution)/shard_map/all_to_all | solution.py:35

commit v12 on v11

--- a/solution.py
+++ b/solution.py
@@ -144,14 +144,24 @@
             out_ref[g, c] = total[g * rows : (g + 1) * rows]
 
 
-def ao_kernel(got_ref, coef_ref, out_ref):
-    n, rows, _ = got_ref.shape
-    lhs = jnp.concatenate([got_ref[i].astype(F32) for i in range(n)], axis=0).astype(BF16)
+def pick_kernel(got_ref, keep_ref, send_ref):
+    xh = lax.axis_index("xh")
+    for y in range(got_ref.shape[0]):
+        keep_ref[y] = got_ref[y, xh]
+        send_ref[y] = got_ref[y, 1 - xh]
+
+
+def ao_kernel(keep_ref, got_ref, coef_ref, out_ref):
+    n, rows, _ = keep_ref.shape
+    xh = lax.axis_index("xh")
+    parts = [ref[y].astype(F32) for ref in (keep_ref, got_ref) for y in range(n)]
+    lhs = jnp.concatenate(parts, axis=0).astype(BF16)
     out = jnp.dot(lhs, coef_ref[...], preferred_element_type=F32)
     count = out.shape[1]
-    for i in range(n):
+    for i in range(2 * n):
         part = out[i * rows : (i + 1) * rows].astype(BF16)
-        out_ref[:, i * count : (i + 1) * count] = part
+        orbital = 2 * (i % n) + (xh if i < n else 1 - xh)
+        out_ref[:, pl.ds(pl.multiple_of(orbital * count, 128), count)] = part
 
 
 def work(metric, amplitudes, virt_coef):
@@ -194,9 +204,7 @@
     shape = (half, 2 * cols)
 
     def on_blocks(kernel, outs, scratch, *args):
-        small = (a.dtype == BF16 and a.ndim == 2 for a in args)
-        spaces = [pltpu.VMEM if fits else pltpu.HBM for fits in small]
-        spaces += [pltpu.VMEM] * 4 + [pltpu.HBM] + [pltpu.VMEM] * 2 + [pltpu.HBM]
+        spaces = [pltpu.HBM if a.dtype == F32 else pltpu.VMEM for a in args] + [pltpu.VMEM] * 5 + [pltpu.HBM] * 3
         args = list(map(pltpu.with_memory_space_constraint, (*args, *steps, *swaps), spaces))
         return pl.pallas_call(
             kernel,
@@ -219,7 +227,7 @@
     piece = (4, 2, half, half)
     slots = on_blocks(
         density_kernel,
-        [(space, piece, BF16) for space in (pltpu.HBM, pltpu.VMEM) * 2],
+        [(pltpu.VMEM, piece, BF16)] * 4,
         [pltpu.VMEM((4, *piece), BF16)],
         fitted, other, other_arrived,
     )
@@ -234,15 +242,17 @@
         compiler_params=PARAMS,
     )(got.reshape(8, 2, half, half))
 
-    got = exchange(fitted.reshape(16, 8, 2 * cols), ("y", "xh"))
+    got = exchange(fitted.reshape(8, 2, 8, 2 * cols), "y")
+    kept, sent = in_vmem(pick_kernel, [((8, 8, 2 * cols), BF16)] * 2, got)
+    came = shifted(sent, "xh", 1)
     ao_count = virt_coef.shape[1]
     ao = pl.pallas_call(
         ao_kernel,
-        in_specs=[VMEM] * 2,
+        in_specs=[VMEM] * 3,
         out_specs=VMEM,
         out_shape=jax.ShapeDtypeStruct((8, 16 * ao_count), BF16),
         compiler_params=PARAMS,
-    )(got, pltpu.with_memory_space_constraint(virt_coef, pltpu.HBM))
+    )(kept, came, pltpu.with_memory_space_constraint(virt_coef, pltpu.HBM))
     return density.reshape(rows, half), ao
 
 

time: 138 us -> 135 us (0.978)
  waiting for transfers between devices: 44.3 us -> 42.1 us
    all_to_all x4, waiting for transfers between devices: 24.1 us -> 16 us  [exchange(): return lax.all_to_all(x, axes, split_axis=0, concat_axis=0, tiled=True)]
    ppermute x6 -> x7, waiting for transfers between devices: 3.18 us -> 9.25 us  [shifted(): return lax.ppermute(x, axis, [(i, (i + by) % n) for i in range(n)])]
    ppermute x6 -> x7, starting transfers between devices: 20.3 us -> 22.5 us  [shifted(): return lax.ppermute(x, axis, [(i, (i + by) % n) for i in range(n)])]
    all_to_all x4, starting transfers between devices: 31.4 us -> 29.3 us  [exchange(): return lax.all_to_all(x, axes, split_axis=0, concat_axis=0, tiled=True)]
  transfers between devices with their start and end apart: 17 -> 18, of which waited for: 10 -> 10; matrix products, arithmetic and copies ran while one was open for 0% -> 0% of each run, Pallas kernels for 8% -> 8%
where the time goes in v12:
time: 135 us; the launch traced here: 134 us
  starting transfers between devices  75.4 us (56%)
  waiting for transfers between devices  42.1 us (31%)
  Pallas kernels  16 us (12%)
    all_to_all x4, starting transfers between devices, exchange(): return lax.all_to_all(x, axes, split_axis=0, concat_axis=0, tiled=True)  29.3 us
    ppermute x7, starting transfers between devices, shifted(): return lax.ppermute(x, axis, [(i, (i + by) % n) for i in range(n)])  22.5 us
    all_to_all x4, waiting for transfers between devices, exchange(): return lax.all_to_all(x, axes, split_axis=0, concat_axis=0, tiled=True)  16 us
    ppermute x4, starting transfers between devices, ring_step(): return lax.ppermute(x, ('z', 'c'), moves)  13.1 us
    ppermute x3, starting transfers between devices, shifted_x(): lax.ppermute(x, ('xl', 'xh'), [(at(i), at((i + by) % 4)) for i in range(4)])  10.4 us
    ppermute x4, waiting for transfers between devices, ring_step(): return lax.ppermute(x, ('z', 'c'), moves)  9.59 us
    ppermute x7, waiting for transfers between devices, shifted(): return lax.ppermute(x, axis, [(i, (i + by) % n) for i in range(n)])  9.25 us
    ppermute x3, waiting for transfers between devices, shifted_x(): lax.ppermute(x, ('xl', 'xh'), [(at(i), at((i + by) % 4)) for i in range(4)])  7.26 us
  transfers between devices with their start and end apart: 18, of which 10 were waited for; matrix products, arithmetic and copies ran while one was open for 0% of the time, Pallas kernels for 8%

profile of v12, /device:TPU:1, one launch (start us, length us, event | category | flops | bytes accessed | tf_op | source)
XLA Modules:
  0.0 134.2 jit_solution(10771096663283668653)
XLA Ops:
  0.6 8.7 %collective-permute-start = (bf16[256,512]{1,0:T(8,128)(2,1)}, bf16[256,512]{1,0:T(8,128)(2,1)S(1)}, u32[]{:S(2)}, u32[]{:S(2)}) collective-permute-start(bf16[256,512]{1,0:T(8,128)(2,1)} %amp_ref.1), channel_id=1, source_target_pairs={{0,1},{1,0},{2,3},{3,2},{4,5},{5,4},{6,7},{7,6},{8,9},{9,8},{10,11... | collective-permute-start | bytes 786440 | tf_op jit(solution)/shard_map/ppermute | solution.py:31
  9.4 1.4 %collective-permute-done.got_ref = bf16[256,512]{1,0:T(8,128)(2,1)S(1)} collective-permute-done((bf16[256,512]{1,0:T(8,128)(2,1)}, bf16[256,512]{1,0:T(8,128)(2,1)S(1)}, u32[]{:S(2)}, u32[]{:S(2)}) %collective-permute-start) | collective-permute-done | bytes 262176 | tf_op jit(solution)/shard_map/ppermute | solution.py:31
  10.7 1.0 shard_map.52.refs_0_
  11.7 5.3 %collective-permute-start.1 = (bf16[256,1024]{1,0:T(8,128)(2,1)S(1)}, bf16[256,1024]{1,0:T(8,128)(2,1)S(1)}, u32[]{:S(2)}, u32[]{:S(2)}) collective-permute-start(bf16[256,1024]{1,0:T(8,128)(2,1)S(1)} %shard_map.52.refs_0_), channel_id=1, source_target_pairs={{0,32},{32,64},{64,96},{96,128},{128,160},{160,192},{192,224},{224... | collective-permute-start | bytes 1572872 | tf_op jit(solution)/shard_map/ppermute | solution.py:42
  17.1 1.7 %shard_map.50 = bf16[8,2,128,128]{3,2,1,0:T(8,128)(2,1)} custom-call(bf16[256,128]{1,0:T(8,128)(2,1)} %in_ref.1), custom_call_target="tpu_custom_call" | custom-call | tf_op jit(solution)/shard_map/pallas_call | solution.py:170
  18.8 7.2 %all-to-all-start = ((bf16[16,128,128]{2,1,0:T(8,128)(2,1)}), bf16[16,128,128]{2,1,0:T(8,128)(2,1)S(1)}, u32[]{:S(2)}, u32[]{:S(2)}) async-start(bf16[16,128,128]{2,1,0:T(8,128)(2,1)} %bitcast), calls=%async_computation | async-start | bytes 1048576 | tf_op jit(solution)/shard_map/all_to_all | solution.py:35
  26.0 0.0 collective-permute-done.1.refs_1_
  26.0 2.2 %collective-permute-start.2 = (bf16[256,1024]{1,0:T(8,128)(2,1)S(1)}, bf16[256,1024]{1,0:T(8,128)(2,1)S(1)}, u32[]{:S(2)}, u32[]{:S(2)}) collective-permute-start(bf16[256,1024]{1,0:T(8,128)(2,1)S(1)} %collective-permute-done.1.refs_1_), channel_id=1, source_target_pairs={{0,32},{32,64},{64,96},{96,128},{128,160},{160,192},{192,224},{224... | collective-permute-start | bytes 1572872 | tf_op jit(solution)/shard_map/ppermute | solution.py:42
  28.2 8.0 %collective-permute-done.2.refs_2_ = bf16[256,1024]{1,0:T(8,128)(2,1)S(1)} collective-permute-done((bf16[256,1024]{1,0:T(8,128)(2,1)S(1)}, bf16[256,1024]{1,0:T(8,128)(2,1)S(1)}, u32[]{:S(2)}, u32[]{:S(2)}) %collective-permute-start.2) | collective-permute-done | bytes 524320 | tf_op jit(solution)/shard_map/ppermute | solution.py:42
  36.2 3.4 %collective-permute-start.3 = (bf16[256,1024]{1,0:T(8,128)(2,1)S(1)}, bf16[256,1024]{1,0:T(8,128)(2,1)S(1)}, u32[]{:S(2)}, u32[]{:S(2)}) collective-permute-start(bf16[256,1024]{1,0:T(8,128)(2,1)S(1)} %collective-permute-done.2.refs_2_), channel_id=1, source_target_pairs={{0,32},{32,64},{64,96},{96,128},{128,160},{160,192},{192,224},{224... | collective-permute-start | bytes 1572872 | tf_op jit(solution)/shard_map/ppermute | solution.py:42
  39.6 3.6 %all-to-all-done = bf16[16,128,128]{2,1,0:T(8,128)(2,1)S(1)} async-done(((bf16[16,128,128]{2,1,0:T(8,128)(2,1)}), bf16[16,128,128]{2,1,0:T(8,128)(2,1)S(1)}, u32[]{:S(2)}, u32[]{:S(2)}) %all-to-all-start) | async-done | bytes 524320 | tf_op jit(solution)/shard_map/all_to_all | solution.py:35
  43.2 1.1 shard_map.51
  44.3 4.0 %all-to-all-start.1 = ((bf16[4,4,2,128,128]{4,3,2,1,0:T(8,128)(2,1)}), bf16[4,4,2,128,128]{4,3,2,1,0:T(8,128)(2,1)S(1)}, u32[]{:S(2)}, u32[]{:S(2)}) async-start(bf16[4,4,2,128,128]{4,3,2,1,0:T(8,128)(2,1)} %bitcast.2), calls=%async_computation.1 | async-start | bytes 2097152 | tf_op jit(solution)/shard_map/all_to_all | solution.py:35
  48.4 1.9 %collective-permute-start.5 = (bf16[256,1024]{1,0:T(8,128)(2,1)S(1)}, bf16[256,1024]{1,0:T(8,128)(2,1)}, u32[]{:S(2)}, u32[]{:S(2)}) collective-permute-start(bf16[256,1024]{1,0:T(8,128)(2,1)S(1)} %collective-permute-done.1.refs_1_), channel_id=1, source_target_pairs={{0,1},{1,0},{2,3},{3,2},{4,5},{5,4},{6,7},{7,6},{8,9},{9,8},{10,11... | collective-permute-start | bytes 1572872 | tf_op jit(solution)/shard_map/ppermute | solution.py:31
  50.3 2.4 %collective-permute-start.6 = (bf16[256,1024]{1,0:T(8,128)(2,1)S(1)}, bf16[256,1024]{1,0:T(8,128)(2,1)}, u32[]{:S(2)}, u32[]{:S(2)}) collective-permute-start(bf16[256,1024]{1,0:T(8,128)(2,1)S(1)} %collective-permute-done.2.refs_2_), channel_id=1, source_target_pairs={{0,1},{1,0},{2,3},{3,2},{4,5},{5,4},{6,7},{7,6},{8,9},{9,8},{10,11... | collective-permute-start | bytes 1572872 | tf_op jit(solution)/shard_map/ppermute | solution.py:31
  52.7 0.0 collective-permute-done.3.refs_3_
  52.7 1.9 %collective-permute-start.7 = (bf16[256,1024]{1,0:T(8,128)(2,1)S(1)}, bf16[256,1024]{1,0:T(8,128)(2,1)}, u32[]{:S(2)}, u32[]{:S(2)}) collective-permute-start(bf16[256,1024]{1,0:T(8,128)(2,1)S(1)} %collective-permute-done.3.refs_3_), channel_id=1, source_target_pairs={{0,1},{1,0},{2,3},{3,2},{4,5},{5,4},{6,7},{7,6},{8,9},{9,8},{10,11... | collective-permute-start | bytes 1572872 | tf_op jit(solution)/shard_map/ppermute | solution.py:31
  54.6 2.2 %collective-permute-start.4 = (bf16[256,1024]{1,0:T(8,128)(2,1)S(1)}, bf16[256,1024]{1,0:T(8,128)(2,1)}, u32[]{:S(2)}, u32[]{:S(2)}) collective-permute-start(bf16[256,1024]{1,0:T(8,128)(2,1)S(1)} %collective-permute-done.3.refs_3_), channel_id=1, source_target_pairs={{0,32},{32,64},{64,96},{96,128},{128,160},{160,192},{192,224},{224... | collective-permute-start | bytes 1572872 | tf_op jit(solution)/shard_map/ppermute | solution.py:42
  56.9 0.0 collective-permute-done.5.refs_5_
  56.9 6.5 %all-to-all-done.1 = bf16[4,4,2,128,128]{4,3,2,1,0:T(8,128)(2,1)S(1)} async-done(((bf16[4,4,2,128,128]{4,3,2,1,0:T(8,128)(2,1)}), bf16[4,4,2,128,128]{4,3,2,1,0:T(8,128)(2,1)S(1)}, u32[]{:S(2)}, u32[]{:S(2)}) %all-to-all-start.1) | async-done | bytes 1048608 | tf_op jit(solution)/shard_map/all_to_all | solution.py:35
  63.4 0.0 collective-permute-done.6.refs_6_
  63.4 0.0 collective-permute-done.7.refs_7_
  63.4 1.6 %collective-permute-done.4.refs_4_ = bf16[256,1024]{1,0:T(8,128)(2,1)} collective-permute-done((bf16[256,1024]{1,0:T(8,128)(2,1)S(1)}, bf16[256,1024]{1,0:T(8,128)(2,1)}, u32[]{:S(2)}, u32[]{:S(2)}) %collective-permute-start.4) | collective-permute-done | bytes 524320 | tf_op jit(solution)/shard_map/ppermute | solution.py:42
  65.0 3.6 %shard_map.53 = (f32[128,1024]{1,0:T(8,128)S(1)}, f32[128,1024]{1,0:T(8,128)}, bf16[128,1024]{1,0:T(8,128)(2,1)S(1)}, bf16[128,1024]{1,0:T(8,128)(2,1)S(1)}) custom-call(bf16[2,2,4,2,128,128]{5,4,3,2,1,0:T(8,128)(2,1)S(1)} %bitcast.8, bf16[256,1024]{1,0:T(8,128)(2,1)S(1)} %shard_map.52.refs_0_, bf16[256,1024]{1,0:T(8,128)(2,1)S(1)} %collective-permute-done.1.refs_1_, ...), custom_call_target="tpu_custom_call" | custom-call | tf_op jit(solution)/shard_map/pallas_call | solution.py:209
  68.5 3.4 %collective-permute-start.8 = (bf16[128,1024]{1,0:T(8,128)(2,1)S(1)}, bf16[128,1024]{1,0:T(8,128)(2,1)S(1)}, u32[]{:S(2)}, u32[]{:S(2)}) collective-permute-start(bf16[128,1024]{1,0:T(8,128)(2,1)S(1)} %get-tuple-element.13), channel_id=1, source_target_pairs={{0,256},{256,0},{1,257},{257,1},{2,258},{258,2},{3,259},{259,3},{4... | collective-permute-start | bytes 786440 | tf_op jit(solution)/shard_map/ppermute | solution.py:31
  71.9 1.9 %collective-permute-start.9 = (bf16[128,1024]{1,0:T(8,128)(2,1)S(1)}, bf16[128,1024]{1,0:T(8,128)(2,1)S(1)}, u32[]{:S(2)}, u32[]{:S(2)}) collective-permute-start(bf16[128,1024]{1,0:T(8,128)(2,1)S(1)} %get-tuple-element.15), channel_id=1, source_target_pairs={{0,256},{256,0},{1,257},{257,1},{2,258},{258,2},{3,259},{259,3},{4... | collective-permute-start | bytes 786440 | tf_op jit(solution)/shard_map/ppermute | solution.py:31
  73.8 1.8 %collective-permute-done.8.arrived_ref = bf16[128,1024]{1,0:T(8,128)(2,1)S(1)} collective-permute-done((bf16[128,1024]{1,0:T(8,128)(2,1)S(1)}, bf16[128,1024]{1,0:T(8,128)(2,1)S(1)}, u32[]{:S(2)}, u32[]{:S(2)}) %collective-permute-start.8) | collective-permute-done | bytes 262176 | tf_op jit(solution)/shard_map/ppermute | solution.py:31
  75.6 0.7 shard_map.54.own_ref
  76.4 6.1 %all-to-all-start.3 = ((bf16[8,2,8,1024]{3,2,1,0:T(8,128)(2,1)}), bf16[8,2,8,1024]{3,2,1,0:T(8,128)(2,1)S(1)}, u32[]{:S(2)}, u32[]{:S(2)}) async-start(bf16[8,2,8,1024]{3,2,1,0:T(8,128)(2,1)} %bitcast.7), calls=%async_computation.3 | async-start | bytes 524288 | tf_op jit(solution)/shard_map/all_to_all | solution.py:35
  82.4 0.0 collective-permute-done.9.arrived_ref
  82.5 3.1 %shard_map.55 = (bf16[4,2,128,128]{3,2,1,0:T(8,128)(2,1)S(1)}, bf16[4,2,128,128]{3,2,1,0:T(8,128)(2,1)S(1)}, bf16[4,2,128,128]{3,2,1,0:T(8,128)(2,1)S(1)}, bf16[4,2,128,128]{3,2,1,0:T(8,128)(2,1)S(1)}) custom-call(bf16[128,1024]{1,0:T(8,128)(2,1)} %shard_map.54.own_ref, f32[128,1024]{1,0:T(8,128)} %get-tuple-element.14.other_ref, ...), custom_call_target="tpu_custom_call" | custom-call | tf_op jit(solution)/shard_map/pallas_call | solution.py:209
  85.6 5.1 %collective-permute-start.10 = (bf16[4,2,128,128]{3,2,1,0:T(8,128)(2,1)S(1)}, bf16[4,2,128,128]{3,2,1,0:T(8,128)(2,1)S(1)}, u32[]{:S(2)}, u32[]{:S(2)}) collective-permute-start(bf16[4,2,128,128]{3,2,1,0:T(8,128)(2,1)S(1)} %get-tuple-element.17), channel_id=1, source_target_pairs={{0,2},{256,258},{2,0},{258,256},{1,3},{257,259},{3,1},{259,257},{4... | collective-permute-start | bytes 786440 | tf_op jit(solution)/shard_map/ppermute | solution.py:47
  90.7 2.8 %collective-permute-start.11 = (bf16[4,2,128,128]{3,2,1,0:T(8,128)(2,1)S(1)}, bf16[4,2,128,128]{3,2,1,0:T(8,128)(2,1)S(1)}, u32[]{:S(2)}, u32[]{:S(2)}) collective-permute-start(bf16[4,2,128,128]{3,2,1,0:T(8,128)(2,1)S(1)} %get-tuple-element.18), channel_id=1, source_target_pairs={{0,258},{256,0},{2,256},{258,2},{1,259},{257,1},{3,257},{259,3},{4... | collective-permute-start | bytes 786440 | tf_op jit(solution)/shard_map/ppermute | solution.py:47
  93.5 2.5 %collective-permute-start.12 = (bf16[4,2,128,128]{3,2,1,0:T(8,128)(2,1)S(1)}, bf16[4,2,128,128]{3,2,1,0:T(8,128)(2,1)S(1)}, u32[]{:S(2)}, u32[]{:S(2)}) collective-permute-start(bf16[4,2,128,128]{3,2,1,0:T(8,128)(2,1)S(1)} %get-tuple-element.19), channel_id=1, source_target_pairs={{0,256},{256,2},{2,258},{258,0},{1,257},{257,3},{3,259},{259,1},{4... | collective-permute-start | bytes 786440 | tf_op jit(solution)/shard_map/ppermute | solution.py:47
  96.0 0.0 collective-permute-done.10.far_ref
  96.0 2.9 %collective-permute-done.11.left_ref = bf16[4,2,128,128]{3,2,1,0:T(8,128)(2,1)S(1)} collective-permute-done((bf16[4,2,128,128]{3,2,1,0:T(8,128)(2,1)S(1)}, bf16[4,2,128,128]{3,2,1,0:T(8,128)(2,1)S(1)}, u32[]{:S(2)}, u32[]{:S(2)}) %collective-permute-start.11) | collective-permute-done | bytes 262176 | tf_op jit(solution)/shard_map/ppermute | solution.py:47
  98.9 4.3 %collective-permute-done.12.right_ref = bf16[4,2,128,128]{3,2,1,0:T(8,128)(2,1)S(1)} collective-permute-done((bf16[4,2,128,128]{3,2,1,0:T(8,128)(2,1)S(1)}, bf16[4,2,128,128]{3,2,1,0:T(8,128)(2,1)S(1)}, u32[]{:S(2)}, u32[]{:S(2)}) %collective-permute-start.12) | collective-permute-done | bytes 262176 | tf_op jit(solution)/shard_map/ppermute | solution.py:47
  103.2 0.9 shard_map.56
  104.2 0.0 all-to-all-done.3.got_ref
  104.2 12.1 %all-to-all-start.2 = ((bf16[16,128,128]{2,1,0:T(8,128)(2,1)}), bf16[16,128,128]{2,1,0:T(8,128)(2,1)S(1)}, u32[]{:S(2)}, u32[]{:S(2)}) async-start(bf16[16,128,128]{2,1,0:T(8,128)(2,1)} %bitcast.4), calls=%async_computation.2 | async-start | bytes 1048576 | tf_op jit(solution)/shard_map/all_to_all | solution.py:35
  116.2 2.3 %collective-permute-start.13 = (bf16[8,8,1024]{2,1,0:T(8,128)(2,1)S(1)}, bf16[8,8,1024]{2,1,0:T(8,128)(2,1)S(1)}, u32[]{:S(2)}, u32[]{:S(2)}) collective-permute-start(bf16[8,8,1024]{2,1,0:T(8,128)(2,1)S(1)} %get-tuple-element.21), channel_id=1, source_target_pairs={{0,2},{2,0},{1,3},{3,1},{4,6},{6,4},{5,7},{7,5},{8,10},{10,8},{9,1... | collective-permute-start | bytes 393224 | tf_op jit(solution)/shard_map/ppermute | solution.py:31
  118.5 6.1 %collective-permute-done.13.got_ref = bf16[8,8,1024]{2,1,0:T(8,128)(2,1)S(1)} collective-permute-done((bf16[8,8,1024]{2,1,0:T(8,128)(2,1)S(1)}, bf16[8,8,1024]{2,1,0:T(8,128)(2,1)S(1)}, u32[]{:S(2)}, u32[]{:S(2)}) %collective-permute-start.13) | collective-permute-done | bytes 131104 | tf_op jit(solution)/shard_map/ppermute | solution.py:31
  124.6 3.0 %shard_map.59 = bf16[8,20480]{1,0:T(8,128)(2,1)} custom-call(bf16[8,8,1024]{2,1,0:T(8,128)(2,1)S(1)} %get-tuple-element.20.keep_ref, bf16[8,8,1024]{2,1,0:T(8,128)(2,1)S(1)} %collective-permute-done.13.got_ref, bf16[1024,1280]{1,0:T(8,128)(2,1)} %coef_ref.1), custom_call_target="tpu_custom_call" | custom-call | tf_op jit(solution)/shard_map/pallas_call | solution.py:249
  127.6 5.9 %all-to-all-done.2 = bf16[16,128,128]{2,1,0:T(8,128)(2,1)S(1)} async-done(((bf16[16,128,128]{2,1,0:T(8,128)(2,1)}), bf16[16,128,128]{2,1,0:T(8,128)(2,1)S(1)}, u32[]{:S(2)}, u32[]{:S(2)}) %all-to-all-start.2) | async-done | bytes 524320 | tf_op jit(solution)/shard_map/all_to_all | solution.py:35
  133.4 0.8 shard_map.57
  (1 shorter events, 0.0 us)
Async XLA Ops:
  0.6 10.1 %collective-permute-start = (bf16[256,512]{1,0:T(8,128)(2,1)}, bf16[256,512]{1,0:T(8,128)(2,1)S(1)}, u32[]{:S(2)}, u32[]{:S(2)}) collective-permute-start(bf16[256,512]{1,0:T(8,128)(2,1)} %amp_ref.1), channel_id=1, source_target_pairs={{0,1},{1,0},{2,3},{3,2},{4,5},{5,4},{6,7},{7,6},{8,9},{9,8},{10,11... | collective-permute-start | bytes 786440 | tf_op jit(solution)/shard_map/ppermute | solution.py:31
  11.7 14.3 %collective-permute-start.1 = (bf16[256,1024]{1,0:T(8,128)(2,1)S(1)}, bf16[256,1024]{1,0:T(8,128)(2,1)S(1)}, u32[]{:S(2)}, u32[]{:S(2)}) collective-permute-start(bf16[256,1024]{1,0:T(8,128)(2,1)S(1)} %shard_map.52.refs_0_), channel_id=1, source_target_pairs={{0,32},{32,64},{64,96},{96,128},{128,160},{160,192},{192,224},{224... | collective-permute-start | bytes 1572872 | tf_op jit(solution)/shard_map/ppermute | solution.py:42
  18.8 24.4 %all-to-all-start = ((bf16[16,128,128]{2,1,0:T(8,128)(2,1)}), bf16[16,128,128]{2,1,0:T(8,128)(2,1)S(1)}, u32[]{:S(2)}, u32[]{:S(2)}) async-start(bf16[16,128,128]{2,1,0:T(8,128)(2,1)} %bitcast), calls=%async_computation | async-start | bytes 1048576 | tf_op jit(solution)/shard_map/all_to_all | solution.py:35
  26.0 10.2 %collective-permute-start.2 = (bf16[256,1024]{1,0:T(8,128)(2,1)S(1)}, bf16[256,1024]{1,0:T(8,128)(2,1)S(1)}, u32[]{:S(2)}, u32[]{:S(2)}) collective-permute-start(bf16[256,1024]{1,0:T(8,128)(2,1)S(1)} %collective-permute-done.1.refs_1_), channel_id=1, source_target_pairs={{0,32},{32,64},{64,96},{96,128},{128,160},{160,192},{192,224},{224... | collective-permute-start | bytes 1572872 | tf_op jit(solution)/shard_map/ppermute | solution.py:42
  36.2 16.5 %collective-permute-start.3 = (bf16[256,1024]{1,0:T(8,128)(2,1)S(1)}, bf16[256,1024]{1,0:T(8,128)(2,1)S(1)}, u32[]{:S(2)}, u32[]{:S(2)}) collective-permute-start(bf16[256,1024]{1,0:T(8,128)(2,1)S(1)} %collective-permute-done.2.refs_2_), channel_id=1, source_target_pairs={{0,32},{32,64},{64,96},{96,128},{128,160},{160,192},{192,224},{224... | collective-permute-start | bytes 1572872 | tf_op jit(solution)/shard_map/ppermute | solution.py:42
  44.3 19.1 %all-to-all-start.1 = ((bf16[4,4,2,128,128]{4,3,2,1,0:T(8,128)(2,1)}), bf16[4,4,2,128,128]{4,3,2,1,0:T(8,128)(2,1)S(1)}, u32[]{:S(2)}, u32[]{:S(2)}) async-start(bf16[4,4,2,128,128]{4,3,2,1,0:T(8,128)(2,1)} %bitcast.2), calls=%async_computation.1 | async-start | bytes 2097152 | tf_op jit(solution)/shard_map/all_to_all | solution.py:35
  48.4 8.5 %collective-permute-start.5 = (bf16[256,1024]{1,0:T(8,128)(2,1)S(1)}, bf16[256,1024]{1,0:T(8,128)(2,1)}, u32[]{:S(2)}, u32[]{:S(2)}) collective-permute-start(bf16[256,1024]{1,0:T(8,128)(2,1)S(1)} %collective-permute-done.1.refs_1_), channel_id=1, source_target_pairs={{0,1},{1,0},{2,3},{3,2},{4,5},{5,4},{6,7},{7,6},{8,9},{9,8},{10,11... | collective-permute-start | bytes 1572872 | tf_op jit(solution)/shard_map/ppermute | solution.py:31
  50.3 13.1 %collective-permute-start.6 = (bf16[256,1024]{1,0:T(8,128)(2,1)S(1)}, bf16[256,1024]{1,0:T(8,128)(2,1)}, u32[]{:S(2)}, u32[]{:S(2)}) collective-permute-start(bf16[256,1024]{1,0:T(8,128)(2,1)S(1)} %collective-permute-done.2.refs_2_), channel_id=1, source_target_pairs={{0,1},{1,0},{2,3},{3,2},{4,5},{5,4},{6,7},{7,6},{8,9},{9,8},{10,11... | collective-permute-start | bytes 1572872 | tf_op jit(solution)/shard_map/ppermute | solution.py:31
  52.7 10.7 %collective-permute-start.7 = (bf16[256,1024]{1,0:T(8,128)(2,1)S(1)}, bf16[256,1024]{1,0:T(8,128)(2,1)}, u32[]{:S(2)}, u32[]{:S(2)}) collective-permute-start(bf16[256,1024]{1,0:T(8,128)(2,1)S(1)} %collective-permute-done.3.refs_3_), channel_id=1, source_target_pairs={{0,1},{1,0},{2,3},{3,2},{4,5},{5,4},{6,7},{7,6},{8,9},{9,8},{10,11... | collective-permute-start | bytes 1572872 | tf_op jit(solution)/shard_map/ppermute | solution.py:31
  54.6 10.3 %collective-permute-start.4 = (bf16[256,1024]{1,0:T(8,128)(2,1)S(1)}, bf16[256,1024]{1,0:T(8,128)(2,1)}, u32[]{:S(2)}, u32[]{:S(2)}) collective-permute-start(bf16[256,1024]{1,0:T(8,128)(2,1)S(1)} %collective-permute-done.3.refs_3_), channel_id=1, source_target_pairs={{0,32},{32,64},{64,96},{96,128},{128,160},{160,192},{192,224},{224... | collective-permute-start | bytes 1572872 | tf_op jit(solution)/shard_map/ppermute | solution.py:42
  68.5 7.1 %collective-permute-start.8 = (bf16[128,1024]{1,0:T(8,128)(2,1)S(1)}, bf16[128,1024]{1,0:T(8,128)(2,1)S(1)}, u32[]{:S(2)}, u32[]{:S(2)}) collective-permute-start(bf16[128,1024]{1,0:T(8,128)(2,1)S(1)} %get-tuple-element.13), channel_id=1, source_target_pairs={{0,256},{256,0},{1,257},{257,1},{2,258},{258,2},{3,259},{259,3},{4... | collective-permute-start | bytes 786440 | tf_op jit(solution)/shard_map/ppermute | solution.py:31
  71.9 10.6 %collective-permute-start.9 = (bf16[128,1024]{1,0:T(8,128)(2,1)S(1)}, bf16[128,1024]{1,0:T(8,128)(2,1)S(1)}, u32[]{:S(2)}, u32[]{:S(2)}) collective-permute-start(bf16[128,1024]{1,0:T(8,128)(2,1)S(1)} %get-tuple-element.15), channel_id=1, source_target_pairs={{0,256},{256,0},{1,257},{257,1},{2,258},{258,2},{3,259},{259,3},{4... | collective-permute-start | bytes 786440 | tf_op jit(solution)/shard_map/ppermute | solution.py:31
  76.4 27.8 %all-to-all-start.3 = ((bf16[8,2,8,1024]{3,2,1,0:T(8,128)(2,1)}), bf16[8,2,8,1024]{3,2,1,0:T(8,128)(2,1)S(1)}, u32[]{:S(2)}, u32[]{:S(2)}) async-start(bf16[8,2,8,1024]{3,2,1,0:T(8,128)(2,1)} %bitcast.7), calls=%async_computation.3 | async-start | bytes 524288 | tf_op jit(solution)/shard_map/all_to_all | solution.py:35
  85.6 10.4 %collective-permute-start.10 = (bf16[4,2,128,128]{3,2,1,0:T(8,128)(2,1)S(1)}, bf16[4,2,128,128]{3,2,1,0:T(8,128)(2,1)S(1)}, u32[]{:S(2)}, u32[]{:S(2)}) collective-permute-start(bf16[4,2,128,128]{3,2,1,0:T(8,128)(2,1)S(1)} %get-tuple-element.17), channel_id=1, source_target_pairs={{0,2},{256,258},{2,0},{258,256},{1,3},{257,259},{3,1},{259,257},{4... | collective-permute-start | bytes 786440 | tf_op jit(solution)/shard_map/ppermute | solution.py:47
  90.7 8.2 %collective-permute-start.11 = (bf16[4,2,128,128]{3,2,1,0:T(8,128)(2,1)S(1)}, bf16[4,2,128,128]{3,2,1,0:T(8,128)(2,1)S(1)}, u32[]{:S(2)}, u32[]{:S(2)}) collective-permute-start(bf16[4,2,128,128]{3,2,1,0:T(8,128)(2,1)S(1)} %get-tuple-element.18), channel_id=1, source_target_pairs={{0,258},{256,0},{2,256},{258,2},{1,259},{257,1},{3,257},{259,3},{4... | collective-permute-start | bytes 786440 | tf_op jit(solution)/shard_map/ppermute | solution.py:47
  93.5 9.7 %collective-permute-start.12 = (bf16[4,2,128,128]{3,2,1,0:T(8,128)(2,1)S(1)}, bf16[4,2,128,128]{3,2,1,0:T(8,128)(2,1)S(1)}, u32[]{:S(2)}, u32[]{:S(2)}) collective-permute-start(bf16[4,2,128,128]{3,2,1,0:T(8,128)(2,1)S(1)} %get-tuple-element.19), channel_id=1, source_target_pairs={{0,256},{256,2},{2,258},{258,0},{1,257},{257,3},{3,259},{259,1},{4... | collective-permute-start | bytes 786440 | tf_op jit(solution)/shard_map/ppermute | solution.py:47
  104.2 29.3 %all-to-all-start.2 = ((bf16[16,128,128]{2,1,0:T(8,128)(2,1)}), bf16[16,128,128]{2,1,0:T(8,128)(2,1)S(1)}, u32[]{:S(2)}, u32[]{:S(2)}) async-start(bf16[16,128,128]{2,1,0:T(8,128)(2,1)} %bitcast.4), calls=%async_computation.2 | async-start | bytes 1048576 | tf_op jit(solution)/shard_map/all_to_all | solution.py:35
  116.2 8.3 %collective-permute-start.13 = (bf16[8,8,1024]{2,1,0:T(8,128)(2,1)S(1)}, bf16[8,8,1024]{2,1,0:T(8,128)(2,1)S(1)}, u32[]{:S(2)}, u32[]{:S(2)}) collective-permute-start(bf16[8,8,1024]{2,1,0:T(8,128)(2,1)S(1)} %get-tuple-element.21), channel_id=1, source_target_pairs={{0,2},{2,0},{1,3},{3,1},{4,6},{6,4},{5,7},{7,5},{8,10},{10,8},{9,1... | collective-permute-start | bytes 393224 | tf_op jit(solution)/shard_map/ppermute | solution.py:31

commit v13 on v11

--- a/solution.py
+++ b/solution.py
@@ -194,9 +194,7 @@
     shape = (half, 2 * cols)
 
     def on_blocks(kernel, outs, scratch, *args):
-        small = (a.dtype == BF16 and a.ndim == 2 for a in args)
-        spaces = [pltpu.VMEM if fits else pltpu.HBM for fits in small]
-        spaces += [pltpu.VMEM] * 4 + [pltpu.HBM] + [pltpu.VMEM] * 2 + [pltpu.HBM]
+        spaces = [pltpu.HBM if a.dtype == F32 else pltpu.VMEM for a in args] + [pltpu.VMEM] * 5 + [pltpu.HBM] * 3
         args = list(map(pltpu.with_memory_space_constraint, (*args, *steps, *swaps), spaces))
         return pl.pallas_call(
             kernel,
@@ -219,7 +217,7 @@
     piece = (4, 2, half, half)
     slots = on_blocks(
         density_kernel,
-        [(space, piece, BF16) for space in (pltpu.HBM, pltpu.VMEM) * 2],
+        [(pltpu.HBM, piece, BF16)] * 4,
         [pltpu.VMEM((4, *piece), BF16)],
         fitted, other, other_arrived,
     )

time: 138 us -> 139 us (level)
  no operation moved by 1% of the time
where the time goes in v13:
time: 139 us; the launch traced here: 138 us
  starting transfers between devices  75.1 us (54%)
  waiting for transfers between devices  44.1 us (32%)
  Pallas kernels  16.9 us (12%)
    all_to_all x4, starting transfers between devices, exchange(): return lax.all_to_all(x, axes, split_axis=0, concat_axis=0, tiled=True)  31.7 us
    all_to_all x4, waiting for transfers between devices, exchange(): return lax.all_to_all(x, axes, split_axis=0, concat_axis=0, tiled=True)  24.3 us
    ppermute x6, starting transfers between devices, shifted(): return lax.ppermute(x, axis, [(i, (i + by) % n) for i in range(n)])  20.3 us
    ppermute x4, starting transfers between devices, ring_step(): return lax.ppermute(x, ('z', 'c'), moves)  13.1 us
    ppermute x3, starting transfers between devices, shifted_x(): lax.ppermute(x, ('xl', 'xh'), [(at(i), at((i + by) % 4)) for i in range(4)])  10 us
    ppermute x4, waiting for transfers between devices, ring_step(): return lax.ppermute(x, ('z', 'c'), moves)  9.59 us
    pallas_call x2, Pallas kernels, on_blocks(): pl.pallas_call(kernel, in_specs=[VMEM] * len(args), out_specs=[VMEM] * le...  7.62 us
    ppermute x3, waiting for transfers between devices, shifted_x(): lax.ppermute(x, ('xl', 'xh'), [(at(i), at((i + by) % 4)) for i in range(4)])  7.02 us
  transfers between devices with their start and end apart: 17, of which 10 were waited for; matrix products, arithmetic and copies ran while one was open for 0% of the time, Pallas kernels for 8%

profile of v13, /device:TPU:1, one launch (start us, length us, event | category | flops | bytes accessed | tf_op | source)
XLA Modules:
  0.0 137.9 jit_solution(17171799867438511524)
XLA Ops:
  0.6 8.7 %collective-permute-start = (bf16[256,512]{1,0:T(8,128)(2,1)}, bf16[256,512]{1,0:T(8,128)(2,1)S(1)}, u32[]{:S(2)}, u32[]{:S(2)}) collective-permute-start(bf16[256,512]{1,0:T(8,128)(2,1)} %amp_ref.1), channel_id=1, source_target_pairs={{0,1},{1,0},{2,3},{3,2},{4,5},{5,4},{6,7},{7,6},{8,9},{9,8},{10,11... | collective-permute-start | bytes 786440 | tf_op jit(solution)/shard_map/ppermute | solution.py:31
  9.4 1.4 collective-permute-done.got_ref
  10.7 1.0 shard_map.52.refs_0_
  11.7 5.3 %collective-permute-start.1 = (bf16[256,1024]{1,0:T(8,128)(2,1)S(1)}, bf16[256,1024]{1,0:T(8,128)(2,1)S(1)}, u32[]{:S(2)}, u32[]{:S(2)}) collective-permute-start(bf16[256,1024]{1,0:T(8,128)(2,1)S(1)} %shard_map.52.refs_0_), channel_id=1, source_target_pairs={{0,32},{32,64},{64,96},{96,128},{128,160},{160,192},{192,224},{224... | collective-permute-start | bytes 1572872 | tf_op jit(solution)/shard_map/ppermute | solution.py:42
  17.1 1.7 %shard_map.50 = bf16[8,2,128,128]{3,2,1,0:T(8,128)(2,1)} custom-call(bf16[256,128]{1,0:T(8,128)(2,1)} %in_ref.1), custom_call_target="tpu_custom_call" | custom-call | tf_op jit(solution)/shard_map/pallas_call | solution.py:160
  18.8 7.2 %all-to-all-start = ((bf16[16,128,128]{2,1,0:T(8,128)(2,1)}), bf16[16,128,128]{2,1,0:T(8,128)(2,1)S(1)}, u32[]{:S(2)}, u32[]{:S(2)}) async-start(bf16[16,128,128]{2,1,0:T(8,128)(2,1)} %bitcast), calls=%async_computation | async-start | bytes 1048576 | tf_op jit(solution)/shard_map/all_to_all | solution.py:35
  26.0 0.0 collective-permute-done.1.refs_1_
  26.0 2.2 %collective-permute-start.2 = (bf16[256,1024]{1,0:T(8,128)(2,1)S(1)}, bf16[256,1024]{1,0:T(8,128)(2,1)S(1)}, u32[]{:S(2)}, u32[]{:S(2)}) collective-permute-start(bf16[256,1024]{1,0:T(8,128)(2,1)S(1)} %collective-permute-done.1.refs_1_), channel_id=1, source_target_pairs={{0,32},{32,64},{64,96},{96,128},{128,160},{160,192},{192,224},{224... | collective-permute-start | bytes 1572872 | tf_op jit(solution)/shard_map/ppermute | solution.py:42
  28.2 8.0 %collective-permute-done.2.refs_2_ = bf16[256,1024]{1,0:T(8,128)(2,1)S(1)} collective-permute-done((bf16[256,1024]{1,0:T(8,128)(2,1)S(1)}, bf16[256,1024]{1,0:T(8,128)(2,1)S(1)}, u32[]{:S(2)}, u32[]{:S(2)}) %collective-permute-start.2) | collective-permute-done | bytes 524320 | tf_op jit(solution)/shard_map/ppermute | solution.py:42
  36.2 3.4 %collective-permute-start.3 = (bf16[256,1024]{1,0:T(8,128)(2,1)S(1)}, bf16[256,1024]{1,0:T(8,128)(2,1)S(1)}, u32[]{:S(2)}, u32[]{:S(2)}) collective-permute-start(bf16[256,1024]{1,0:T(8,128)(2,1)S(1)} %collective-permute-done.2.refs_2_), channel_id=1, source_target_pairs={{0,32},{32,64},{64,96},{96,128},{128,160},{160,192},{192,224},{224... | collective-permute-start | bytes 1572872 | tf_op jit(solution)/shard_map/ppermute | solution.py:42
  39.6 3.6 %all-to-all-done = bf16[16,128,128]{2,1,0:T(8,128)(2,1)S(1)} async-done(((bf16[16,128,128]{2,1,0:T(8,128)(2,1)}), bf16[16,128,128]{2,1,0:T(8,128)(2,1)S(1)}, u32[]{:S(2)}, u32[]{:S(2)}) %all-to-all-start) | async-done | bytes 524320 | tf_op jit(solution)/shard_map/all_to_all | solution.py:35
  43.2 1.1 shard_map.51
  44.3 4.0 %all-to-all-start.1 = ((bf16[4,4,2,128,128]{4,3,2,1,0:T(8,128)(2,1)}), bf16[4,4,2,128,128]{4,3,2,1,0:T(8,128)(2,1)S(1)}, u32[]{:S(2)}, u32[]{:S(2)}) async-start(bf16[4,4,2,128,128]{4,3,2,1,0:T(8,128)(2,1)} %bitcast.2), calls=%async_computation.1 | async-start | bytes 2097152 | tf_op jit(solution)/shard_map/all_to_all | solution.py:35
  48.4 1.9 %collective-permute-start.5 = (bf16[256,1024]{1,0:T(8,128)(2,1)S(1)}, bf16[256,1024]{1,0:T(8,128)(2,1)}, u32[]{:S(2)}, u32[]{:S(2)}) collective-permute-start(bf16[256,1024]{1,0:T(8,128)(2,1)S(1)} %collective-permute-done.1.refs_1_), channel_id=1, source_target_pairs={{0,1},{1,0},{2,3},{3,2},{4,5},{5,4},{6,7},{7,6},{8,9},{9,8},{10,11... | collective-permute-start | bytes 1572872 | tf_op jit(solution)/shard_map/ppermute | solution.py:31
  50.3 2.4 %collective-permute-start.6 = (bf16[256,1024]{1,0:T(8,128)(2,1)S(1)}, bf16[256,1024]{1,0:T(8,128)(2,1)}, u32[]{:S(2)}, u32[]{:S(2)}) collective-permute-start(bf16[256,1024]{1,0:T(8,128)(2,1)S(1)} %collective-permute-done.2.refs_2_), channel_id=1, source_target_pairs={{0,1},{1,0},{2,3},{3,2},{4,5},{5,4},{6,7},{7,6},{8,9},{9,8},{10,11... | collective-permute-start | bytes 1572872 | tf_op jit(solution)/shard_map/ppermute | solution.py:31
  52.7 0.0 collective-permute-done.3.refs_3_
  52.7 1.9 %collective-permute-start.7 = (bf16[256,1024]{1,0:T(8,128)(2,1)S(1)}, bf16[256,1024]{1,0:T(8,128)(2,1)}, u32[]{:S(2)}, u32[]{:S(2)}) collective-permute-start(bf16[256,1024]{1,0:T(8,128)(2,1)S(1)} %collective-permute-done.3.refs_3_), channel_id=1, source_target_pairs={{0,1},{1,0},{2,3},{3,2},{4,5},{5,4},{6,7},{7,6},{8,9},{9,8},{10,11... | collective-permute-start | bytes 1572872 | tf_op jit(solution)/shard_map/ppermute | solution.py:31
  54.6 2.2 %collective-permute-start.4 = (bf16[256,1024]{1,0:T(8,128)(2,1)S(1)}, bf16[256,1024]{1,0:T(8,128)(2,1)}, u32[]{:S(2)}, u32[]{:S(2)}) collective-permute-start(bf16[256,1024]{1,0:T(8,128)(2,1)S(1)} %collective-permute-done.3.refs_3_), channel_id=1, source_target_pairs={{0,32},{32,64},{64,96},{96,128},{128,160},{160,192},{192,224},{224... | collective-permute-start | bytes 1572872 | tf_op jit(solution)/shard_map/ppermute | solution.py:42
  56.9 0.0 collective-permute-done.5.refs_5_
  56.9 6.5 %all-to-all-done.1 = bf16[4,4,2,128,128]{4,3,2,1,0:T(8,128)(2,1)S(1)} async-done(((bf16[4,4,2,128,128]{4,3,2,1,0:T(8,128)(2,1)}), bf16[4,4,2,128,128]{4,3,2,1,0:T(8,128)(2,1)S(1)}, u32[]{:S(2)}, u32[]{:S(2)}) %all-to-all-start.1) | async-done | bytes 1048608 | tf_op jit(solution)/shard_map/all_to_all | solution.py:35
  63.4 0.0 collective-permute-done.6.refs_6_
  63.4 0.0 collective-permute-done.7.refs_7_
  63.4 1.6 %collective-permute-done.4.refs_4_ = bf16[256,1024]{1,0:T(8,128)(2,1)} collective-permute-done((bf16[256,1024]{1,0:T(8,128)(2,1)S(1)}, bf16[256,1024]{1,0:T(8,128)(2,1)}, u32[]{:S(2)}, u32[]{:S(2)}) %collective-permute-start.4) | collective-permute-done | bytes 524320 | tf_op jit(solution)/shard_map/ppermute | solution.py:42
  65.0 3.6 %shard_map.53 = (f32[128,1024]{1,0:T(8,128)S(1)}, f32[128,1024]{1,0:T(8,128)}, bf16[128,1024]{1,0:T(8,128)(2,1)S(1)}, bf16[128,1024]{1,0:T(8,128)(2,1)S(1)}) custom-call(bf16[2,2,4,2,128,128]{5,4,3,2,1,0:T(8,128)(2,1)S(1)} %bitcast.8, bf16[256,1024]{1,0:T(8,128)(2,1)S(1)} %shard_map.52.refs_0_, bf16[256,1024]{1,0:T(8,128)(2,1)S(1)} %collective-permute-done.1.refs_1_, ...), custom_call_target="tpu_custom_call" | custom-call | tf_op jit(solution)/shard_map/pallas_call | solution.py:199
  68.5 3.4 %collective-permute-start.8 = (bf16[128,1024]{1,0:T(8,128)(2,1)S(1)}, bf16[128,1024]{1,0:T(8,128)(2,1)S(1)}, u32[]{:S(2)}, u32[]{:S(2)}) collective-permute-start(bf16[128,1024]{1,0:T(8,128)(2,1)S(1)} %get-tuple-element.11), channel_id=1, source_target_pairs={{0,256},{256,0},{1,257},{257,1},{2,258},{258,2},{3,259},{259,3},{4... | collective-permute-start | bytes 786440 | tf_op jit(solution)/shard_map/ppermute | solution.py:31
  71.9 1.9 %collective-permute-start.9 = (bf16[128,1024]{1,0:T(8,128)(2,1)S(1)}, bf16[128,1024]{1,0:T(8,128)(2,1)S(1)}, u32[]{:S(2)}, u32[]{:S(2)}) collective-permute-start(bf16[128,1024]{1,0:T(8,128)(2,1)S(1)} %get-tuple-element.13), channel_id=1, source_target_pairs={{0,256},{256,0},{1,257},{257,1},{2,258},{258,2},{3,259},{259,3},{4... | collective-permute-start | bytes 786440 | tf_op jit(solution)/shard_map/ppermute | solution.py:31
  73.8 1.8 %collective-permute-done.8.arrived_ref = bf16[128,1024]{1,0:T(8,128)(2,1)S(1)} collective-permute-done((bf16[128,1024]{1,0:T(8,128)(2,1)S(1)}, bf16[128,1024]{1,0:T(8,128)(2,1)S(1)}, u32[]{:S(2)}, u32[]{:S(2)}) %collective-permute-start.8) | collective-permute-done | bytes 262176 | tf_op jit(solution)/shard_map/ppermute | solution.py:31
  75.6 0.7 shard_map.54.own_ref
  76.4 9.1 %all-to-all-start.3 = ((bf16[16,8,1024]{2,1,0:T(8,128)(2,1)}), bf16[16,8,1024]{2,1,0:T(8,128)(2,1)S(1)}, u32[]{:S(2)}, u32[]{:S(2)}) async-start(bf16[16,8,1024]{2,1,0:T(8,128)(2,1)} %bitcast.7), calls=%async_computation.3 | async-start | bytes 524288 | tf_op jit(solution)/shard_map/all_to_all | solution.py:35
  85.4 0.0 collective-permute-done.9.arrived_ref
  85.5 4.1 %shard_map.55 = (bf16[4,2,128,128]{3,2,1,0:T(8,128)(2,1)}, bf16[4,2,128,128]{3,2,1,0:T(8,128)(2,1)}, bf16[4,2,128,128]{3,2,1,0:T(8,128)(2,1)}, bf16[4,2,128,128]{3,2,1,0:T(8,128)(2,1)}) custom-call(bf16[128,1024]{1,0:T(8,128)(2,1)} %shard_map.54.own_ref, f32[128,1024]{1,0:T(8,128)} %get-tuple-element.12.other_ref, ...), custom_call_target="tpu_custom_call" | custom-call | tf_op jit(solution)/shard_map/pallas_call | solution.py:199
  89.5 4.8 %collective-permute-start.10 = (bf16[4,2,128,128]{3,2,1,0:T(8,128)(2,1)}, bf16[4,2,128,128]{3,2,1,0:T(8,128)(2,1)S(1)}, u32[]{:S(2)}, u32[]{:S(2)}) collective-permute-start(bf16[4,2,128,128]{3,2,1,0:T(8,128)(2,1)} %get-tuple-element.15), channel_id=1, source_target_pairs={{0,2},{256,258},{2,0},{258,256},{1,3},{257,259},{3,1},{259,257},{4... | collective-permute-start | bytes 786440 | tf_op jit(solution)/shard_map/ppermute | solution.py:47
  94.3 1.9 %collective-permute-start.11 = (bf16[4,2,128,128]{3,2,1,0:T(8,128)(2,1)}, bf16[4,2,128,128]{3,2,1,0:T(8,128)(2,1)S(1)}, u32[]{:S(2)}, u32[]{:S(2)}) collective-permute-start(bf16[4,2,128,128]{3,2,1,0:T(8,128)(2,1)} %get-tuple-element.16), channel_id=1, source_target_pairs={{0,258},{256,0},{2,256},{258,2},{1,259},{257,1},{3,257},{259,3},{4... | collective-permute-start | bytes 786440 | tf_op jit(solution)/shard_map/ppermute | solution.py:47
  96.2 3.4 %collective-permute-start.12 = (bf16[4,2,128,128]{3,2,1,0:T(8,128)(2,1)}, bf16[4,2,128,128]{3,2,1,0:T(8,128)(2,1)S(1)}, u32[]{:S(2)}, u32[]{:S(2)}) collective-permute-start(bf16[4,2,128,128]{3,2,1,0:T(8,128)(2,1)} %get-tuple-element.17), channel_id=1, source_target_pairs={{0,256},{256,2},{2,258},{258,0},{1,257},{257,3},{3,259},{259,1},{4... | collective-permute-start | bytes 786440 | tf_op jit(solution)/shard_map/ppermute | solution.py:47
  99.6 0.3 collective-permute-done.10.far_ref
  99.8 3.4 %collective-permute-done.11.left_ref = bf16[4,2,128,128]{3,2,1,0:T(8,128)(2,1)S(1)} collective-permute-done((bf16[4,2,128,128]{3,2,1,0:T(8,128)(2,1)}, bf16[4,2,128,128]{3,2,1,0:T(8,128)(2,1)S(1)}, u32[]{:S(2)}, u32[]{:S(2)}) %collective-permute-start.11) | collective-permute-done | bytes 262176 | tf_op jit(solution)/shard_map/ppermute | solution.py:47
  103.2 3.4 %collective-permute-done.12.right_ref = bf16[4,2,128,128]{3,2,1,0:T(8,128)(2,1)S(1)} collective-permute-done((bf16[4,2,128,128]{3,2,1,0:T(8,128)(2,1)}, bf16[4,2,128,128]{3,2,1,0:T(8,128)(2,1)S(1)}, u32[]{:S(2)}, u32[]{:S(2)}) %collective-permute-start.12) | collective-permute-done | bytes 262176 | tf_op jit(solution)/shard_map/ppermute | solution.py:47
  106.6 0.0 copy-start
  106.6 0.9 copy-done
  107.5 0.9 shard_map.56
  108.5 0.0 all-to-all-done.3.got_ref
  108.5 11.4 %all-to-all-start.2 = ((bf16[16,128,128]{2,1,0:T(8,128)(2,1)}), bf16[16,128,128]{2,1,0:T(8,128)(2,1)S(1)}, u32[]{:S(2)}, u32[]{:S(2)}) async-start(bf16[16,128,128]{2,1,0:T(8,128)(2,1)} %bitcast.4), calls=%async_computation.2 | async-start | bytes 1048576 | tf_op jit(solution)/shard_map/all_to_all | solution.py:35
  119.9 3.0 %shard_map.58 = bf16[8,20480]{1,0:T(8,128)(2,1)} custom-call(bf16[16,8,1024]{2,1,0:T(8,128)(2,1)S(1)} %all-to-all-done.3.got_ref, bf16[1024,1280]{1,0:T(8,128)(2,1)} %coef_ref.1), custom_call_target="tpu_custom_call" | custom-call | tf_op jit(solution)/shard_map/pallas_call | solution.py:237
  122.9 14.2 %all-to-all-done.2 = bf16[16,128,128]{2,1,0:T(8,128)(2,1)S(1)} async-done(((bf16[16,128,128]{2,1,0:T(8,128)(2,1)}), bf16[16,128,128]{2,1,0:T(8,128)(2,1)S(1)}, u32[]{:S(2)}, u32[]{:S(2)}) %all-to-all-start.2) | async-done | bytes 524320 | tf_op jit(solution)/shard_map/all_to_all | solution.py:35
  137.1 0.8 shard_map.57
Async XLA Ops:
  0.6 10.1 %collective-permute-start = (bf16[256,512]{1,0:T(8,128)(2,1)}, bf16[256,512]{1,0:T(8,128)(2,1)S(1)}, u32[]{:S(2)}, u32[]{:S(2)}) collective-permute-start(bf16[256,512]{1,0:T(8,128)(2,1)} %amp_ref.1), channel_id=1, source_target_pairs={{0,1},{1,0},{2,3},{3,2},{4,5},{5,4},{6,7},{7,6},{8,9},{9,8},{10,11... | collective-permute-start | bytes 786440 | tf_op jit(solution)/shard_map/ppermute | solution.py:31
  11.7 14.3 %collective-permute-start.1 = (bf16[256,1024]{1,0:T(8,128)(2,1)S(1)}, bf16[256,1024]{1,0:T(8,128)(2,1)S(1)}, u32[]{:S(2)}, u32[]{:S(2)}) collective-permute-start(bf16[256,1024]{1,0:T(8,128)(2,1)S(1)} %shard_map.52.refs_0_), channel_id=1, source_target_pairs={{0,32},{32,64},{64,96},{96,128},{128,160},{160,192},{192,224},{224... | collective-permute-start | bytes 1572872 | tf_op jit(solution)/shard_map/ppermute | solution.py:42
  18.8 24.4 %all-to-all-start = ((bf16[16,128,128]{2,1,0:T(8,128)(2,1)}), bf16[16,128,128]{2,1,0:T(8,128)(2,1)S(1)}, u32[]{:S(2)}, u32[]{:S(2)}) async-start(bf16[16,128,128]{2,1,0:T(8,128)(2,1)} %bitcast), calls=%async_computation | async-start | bytes 1048576 | tf_op jit(solution)/shard_map/all_to_all | solution.py:35
  26.0 10.2 %collective-permute-start.2 = (bf16[256,1024]{1,0:T(8,128)(2,1)S(1)}, bf16[256,1024]{1,0:T(8,128)(2,1)S(1)}, u32[]{:S(2)}, u32[]{:S(2)}) collective-permute-start(bf16[256,1024]{1,0:T(8,128)(2,1)S(1)} %collective-permute-done.1.refs_1_), channel_id=1, source_target_pairs={{0,32},{32,64},{64,96},{96,128},{128,160},{160,192},{192,224},{224... | collective-permute-start | bytes 1572872 | tf_op jit(solution)/shard_map/ppermute | solution.py:42
  36.2 16.5 %collective-permute-start.3 = (bf16[256,1024]{1,0:T(8,128)(2,1)S(1)}, bf16[256,1024]{1,0:T(8,128)(2,1)S(1)}, u32[]{:S(2)}, u32[]{:S(2)}) collective-permute-start(bf16[256,1024]{1,0:T(8,128)(2,1)S(1)} %collective-permute-done.2.refs_2_), channel_id=1, source_target_pairs={{0,32},{32,64},{64,96},{96,128},{128,160},{160,192},{192,224},{224... | collective-permute-start | bytes 1572872 | tf_op jit(solution)/shard_map/ppermute | solution.py:42
  44.3 19.1 %all-to-all-start.1 = ((bf16[4,4,2,128,128]{4,3,2,1,0:T(8,128)(2,1)}), bf16[4,4,2,128,128]{4,3,2,1,0:T(8,128)(2,1)S(1)}, u32[]{:S(2)}, u32[]{:S(2)}) async-start(bf16[4,4,2,128,128]{4,3,2,1,0:T(8,128)(2,1)} %bitcast.2), calls=%async_computation.1 | async-start | bytes 2097152 | tf_op jit(solution)/shard_map/all_to_all | solution.py:35
  48.4 8.5 %collective-permute-start.5 = (bf16[256,1024]{1,0:T(8,128)(2,1)S(1)}, bf16[256,1024]{1,0:T(8,128)(2,1)}, u32[]{:S(2)}, u32[]{:S(2)}) collective-permute-start(bf16[256,1024]{1,0:T(8,128)(2,1)S(1)} %collective-permute-done.1.refs_1_), channel_id=1, source_target_pairs={{0,1},{1,0},{2,3},{3,2},{4,5},{5,4},{6,7},{7,6},{8,9},{9,8},{10,11... | collective-permute-start | bytes 1572872 | tf_op jit(solution)/shard_map/ppermute | solution.py:31
  50.3 13.1 %collective-permute-start.6 = (bf16[256,1024]{1,0:T(8,128)(2,1)S(1)}, bf16[256,1024]{1,0:T(8,128)(2,1)}, u32[]{:S(2)}, u32[]{:S(2)}) collective-permute-start(bf16[256,1024]{1,0:T(8,128)(2,1)S(1)} %collective-permute-done.2.refs_2_), channel_id=1, source_target_pairs={{0,1},{1,0},{2,3},{3,2},{4,5},{5,4},{6,7},{7,6},{8,9},{9,8},{10,11... | collective-permute-start | bytes 1572872 | tf_op jit(solution)/shard_map/ppermute | solution.py:31
  52.7 10.7 %collective-permute-start.7 = (bf16[256,1024]{1,0:T(8,128)(2,1)S(1)}, bf16[256,1024]{1,0:T(8,128)(2,1)}, u32[]{:S(2)}, u32[]{:S(2)}) collective-permute-start(bf16[256,1024]{1,0:T(8,128)(2,1)S(1)} %collective-permute-done.3.refs_3_), channel_id=1, source_target_pairs={{0,1},{1,0},{2,3},{3,2},{4,5},{5,4},{6,7},{7,6},{8,9},{9,8},{10,11... | collective-permute-start | bytes 1572872 | tf_op jit(solution)/shard_map/ppermute | solution.py:31
  54.6 10.3 %collective-permute-start.4 = (bf16[256,1024]{1,0:T(8,128)(2,1)S(1)}, bf16[256,1024]{1,0:T(8,128)(2,1)}, u32[]{:S(2)}, u32[]{:S(2)}) collective-permute-start(bf16[256,1024]{1,0:T(8,128)(2,1)S(1)} %collective-permute-done.3.refs_3_), channel_id=1, source_target_pairs={{0,32},{32,64},{64,96},{96,128},{128,160},{160,192},{192,224},{224... | collective-permute-start | bytes 1572872 | tf_op jit(solution)/shard_map/ppermute | solution.py:42
  68.5 7.1 %collective-permute-start.8 = (bf16[128,1024]{1,0:T(8,128)(2,1)S(1)}, bf16[128,1024]{1,0:T(8,128)(2,1)S(1)}, u32[]{:S(2)}, u32[]{:S(2)}) collective-permute-start(bf16[128,1024]{1,0:T(8,128)(2,1)S(1)} %get-tuple-element.11), channel_id=1, source_target_pairs={{0,256},{256,0},{1,257},{257,1},{2,258},{258,2},{3,259},{259,3},{4... | collective-permute-start | bytes 786440 | tf_op jit(solution)/shard_map/ppermute | solution.py:31
  71.9 13.6 %collective-permute-start.9 = (bf16[128,1024]{1,0:T(8,128)(2,1)S(1)}, bf16[128,1024]{1,0:T(8,128)(2,1)S(1)}, u32[]{:S(2)}, u32[]{:S(2)}) collective-permute-start(bf16[128,1024]{1,0:T(8,128)(2,1)S(1)} %get-tuple-element.13), channel_id=1, source_target_pairs={{0,256},{256,0},{1,257},{257,1},{2,258},{258,2},{3,259},{259,3},{4... | collective-permute-start | bytes 786440 | tf_op jit(solution)/shard_map/ppermute | solution.py:31
  76.4 32.1 %all-to-all-start.3 = ((bf16[16,8,1024]{2,1,0:T(8,128)(2,1)}), bf16[16,8,1024]{2,1,0:T(8,128)(2,1)S(1)}, u32[]{:S(2)}, u32[]{:S(2)}) async-start(bf16[16,8,1024]{2,1,0:T(8,128)(2,1)} %bitcast.7), calls=%async_computation.3 | async-start | bytes 524288 | tf_op jit(solution)/shard_map/all_to_all | solution.py:35
  89.5 10.3 %collective-permute-start.10 = (bf16[4,2,128,128]{3,2,1,0:T(8,128)(2,1)}, bf16[4,2,128,128]{3,2,1,0:T(8,128)(2,1)S(1)}, u32[]{:S(2)}, u32[]{:S(2)}) collective-permute-start(bf16[4,2,128,128]{3,2,1,0:T(8,128)(2,1)} %get-tuple-element.15), channel_id=1, source_target_pairs={{0,2},{256,258},{2,0},{258,256},{1,3},{257,259},{3,1},{259,257},{4... | collective-permute-start | bytes 786440 | tf_op jit(solution)/shard_map/ppermute | solution.py:47
  94.3 9.0 %collective-permute-start.11 = (bf16[4,2,128,128]{3,2,1,0:T(8,128)(2,1)}, bf16[4,2,128,128]{3,2,1,0:T(8,128)(2,1)S(1)}, u32[]{:S(2)}, u32[]{:S(2)}) collective-permute-start(bf16[4,2,128,128]{3,2,1,0:T(8,128)(2,1)} %get-tuple-element.16), channel_id=1, source_target_pairs={{0,258},{256,0},{2,256},{258,2},{1,259},{257,1},{3,257},{259,3},{4... | collective-permute-start | bytes 786440 | tf_op jit(solution)/shard_map/ppermute | solution.py:47
  96.2 10.4 %collective-permute-start.12 = (bf16[4,2,128,128]{3,2,1,0:T(8,128)(2,1)}, bf16[4,2,128,128]{3,2,1,0:T(8,128)(2,1)S(1)}, u32[]{:S(2)}, u32[]{:S(2)}) collective-permute-start(bf16[4,2,128,128]{3,2,1,0:T(8,128)(2,1)} %get-tuple-element.17), channel_id=1, source_target_pairs={{0,256},{256,2},{2,258},{258,0},{1,257},{257,3},{3,259},{259,1},{4... | collective-permute-start | bytes 786440 | tf_op jit(solution)/shard_map/ppermute | solution.py:47
  106.6 1.0 copy-start
  108.5 28.6 %all-to-all-start.2 = ((bf16[16,128,128]{2,1,0:T(8,128)(2,1)}), bf16[16,128,128]{2,1,0:T(8,128)(2,1)S(1)}, u32[]{:S(2)}, u32[]{:S(2)}) async-start(bf16[16,128,128]{2,1,0:T(8,128)(2,1)} %bitcast.4), calls=%async_computation.2 | async-start | bytes 1048576 | tf_op jit(solution)/shard_map/all_to_all | solution.py:35
